TPU v7x, 256 devices: a whole 4x4x8 slice. The times are simulated.
256 devices in a mesh: seq: 16 (over x, y_hi, core), head: 16 (over y_lo, z).
Axes of the slice: x: 4, y: 4 (y_hi: 2, y_lo: 2; y = y_hi * 2 + y_lo), z: 8, core: 2. Of those that a mesh axis runs over, the one named last changes fastest.
Arguments:
- tokens: bfloat16 [4096, 8192], P('seq', 'head'), may hold values from -12 to 12
- w_query: bfloat16 [8192, 4096], P(None, 'head'), may hold values from -0.100097656 to 0.100097656
- w_keyval: bfloat16 [8192, 512], P(None, 'head'), may hold values from -0.15039062 to 0.15039062
- w_out: bfloat16 [4096, 8192], P('head'), may hold values from -0.125 to 0.125
Outputs:
- layer_out: bfloat16 [4096, 8192], P('seq', 'head')
All inputs are finite; a program needn't handle non-finite values.
Results may differ from a plain program's by a relative error of at most 0.0075.
The roundings to bfloat16 on the way count: a program that leaves them out, or rounds other values in their place, can miss the bound.
Values may be sent and summed in bfloat16 or wider, within the bound.
No kernel may reach another device: no remote copies, remote signals or barrier semaphores. Data moves between devices by JAX's collectives and lax.ppermute only.
A program may use at most 64 MiB of HBM per device.

v0:
```python
import jax
import jax.numpy as jnp
from jax import lax
from jax.sharding import PartitionSpec as P

HEAD = 128
WIN1 = 512
WIN2 = 32


def in_order(blocks, dim):
    blocks = jnp.moveaxis(blocks, 0, dim)
    dims = blocks.shape
    return blocks.reshape(*dims[:dim], dims[dim] * dims[dim + 1], *dims[dim + 2 :])


def sent_to_all(value, axis):
    size = lax.axis_size(axis)
    return lax.all_to_all(
        jnp.broadcast_to(value[None], (size, *value.shape)), axis, 0, 0, tiled=True
    )


def gather_directly(value, axis, dim):
    return in_order(sent_to_all(value, axis), dim)


def passed_along(value, axis, steps):
    count = lax.axis_size(axis)
    leading, last = (max(0, -steps), min(count, count - steps))
    return lax.ppermute(value, axis, [(source, source + steps) for source in range(leading, last)])


def window_rows(source, window, amount):
    return jnp.stack(
        [
            source[window - 1 - lag_index : window - 1 - lag_index + amount]
            for lag_index in range(window)
        ],
        axis=1,
    )


def attend_block(query_rows, key_rows, value_rows, second_keys, second_values, first_pos):
    amount = query_rows.shape[0]
    window = second_keys.shape[0] - amount + 1
    lead = key_rows.shape[0] - amount
    key_two = window_rows(second_keys, window, amount)
    value_two = window_rows(second_values, window, amount)
    product = (query_rows.astype(jnp.float32)[:, None, :] * key_two.astype(jnp.float32)).astype(
        jnp.bfloat16
    )
    scores = jnp.einsum(
        "ird,jd->irj", product, key_rows, preferred_element_type=jnp.float32
    ) * query_rows.shape[1] ** (-0.5)
    row_ids = jnp.arange(amount, dtype=jnp.int32)[:, None, None]
    lag_ids = jnp.arange(window, dtype=jnp.int32)[None, :, None]
    column = jnp.arange(amount + lead, dtype=jnp.int32)[None, None, :]
    usable = (
        (column >= row_ids)
        & (column <= row_ids + lead)
        & (first_pos - lead + column >= 0)
        & (first_pos + row_ids - lag_ids >= 0)
    )
    row_peak = jnp.max(jnp.where(usable, scores, -jnp.inf), axis=(1, 2))
    raised = jnp.where(usable, jnp.exp(scores - row_peak[:, None, None]), 0.0)
    row_total = jnp.sum(raised, axis=(1, 2))
    weights = raised.astype(jnp.bfloat16)
    mixture = jnp.einsum("irj,jd->ird", weights, value_rows, preferred_element_type=jnp.float32)
    combined = jnp.sum(mixture * value_two.astype(jnp.float32), axis=1)
    return (combined / row_total[:, None]).astype(jnp.bfloat16)


def body(tokens, w_query, w_keyval, w_out):
    tok_rows = tokens.shape[0]
    out_columns = lax.all_to_all(w_out, "head", split_axis=1, concat_axis=0, tiled=True)
    piece = lax.all_gather(tokens, "head", axis=1, tiled=True)
    query_sum = jnp.dot(piece, w_query, preferred_element_type=jnp.float32)
    keyval_sum = jnp.dot(piece, w_keyval, preferred_element_type=jnp.float32)
    queries = query_sum.astype(jnp.bfloat16)
    keyval = gather_directly(keyval_sum.astype(jnp.bfloat16), "head", 1)
    first_pair = keyval[:, : 2 * HEAD]
    second_pair = keyval[:, 2 * HEAD :]
    tail_pair = second_pair[tok_rows - WIN2 :]
    near_pair, near_tail = passed_along((first_pair, tail_pair), "seq", 1)
    reach = (WIN1 - 1 + tok_rows - 1) // tok_rows
    earlier = [near_pair]
    earlier.append(passed_along(first_pair, "seq", 2))
    first_ext = jnp.concatenate(earlier[::-1] + [first_pair], axis=0)
    second_ext = jnp.concatenate([near_tail, second_pair], axis=0)
    seq_index = lax.axis_index("seq")
    block = min(tok_rows, 128)
    lead = WIN1 - 1
    head_count = queries.shape[1] // HEAD
    head_pieces = []
    for head_index in range(head_count):
        block_pieces = []
        for block_index in range(tok_rows // block):
            offset = block_index * block
            query_rows = queries[
                offset : offset + block, head_index * HEAD : (head_index + 1) * HEAD
            ]
            low_first = reach * tok_rows + offset - lead
            first_rows = first_ext[low_first : low_first + block + lead]
            second_rows = second_ext[offset + 1 : offset + block + WIN2]
            first_pos = seq_index * tok_rows + offset
            block_pieces.append(
                attend_block(
                    query_rows,
                    first_rows[:, :HEAD],
                    first_rows[:, HEAD:],
                    second_rows[:, :HEAD],
                    second_rows[:, HEAD:],
                    first_pos,
                )
            )
        head_pieces.append(jnp.concatenate(block_pieces, axis=0))
    attended = jnp.concatenate(head_pieces, axis=1)
    result = jnp.dot(
        lax.all_gather(attended, "head", axis=1, tiled=True),
        out_columns,
        preferred_element_type=jnp.float32,
    )
    return result.astype(jnp.bfloat16)


def solution(mesh):
    return jax.shard_map(
        body,
        mesh=mesh,
        in_specs=(P("seq", "head"), P(None, "head"), P(None, "head"), P("head", None)),
        out_specs=P("seq", "head"),
        check_vma=False,
    )
```

profile of v0, /device:TPU:2, one launch (start us, length us, event | category | flops | bytes accessed | tf_op | source)
XLA Modules:
  0.0 300.9 jit_solution(11767990637845947500)
XLA Ops:
  6.5 0.7 all-gather.3.cloned.1.call-update
  7.3 6.4 %copy.56 = bf16[256,8192]{0,1:T(8,128)(2,1)} copy(bf16[256,8192]{1,0:T(8,128)(2,1)} %param.7) | data formatting | bytes 8388608 | tf_op args[3]
  13.9 74.4 %all-gather.3.cloned.1.call-done = bf16[256,8192]{1,0:T(8,128)(2,1)} async-done(((bf16[256,512]{1,0:T(8,128)(2,1)}), bf16[256,8192]{1,0:T(8,128)(2,1)}) %all-gather.3.cloned.1.call-update) | async-done | bytes 4194320 | tf_op jit(solution)/shard_map/all_gather | solution.py:77
  88.3 3.5 %convolution_convert_fusion.2 = bf16[256,32]{0,1:T(8,128)(2,1)S(1)} fusion(bf16[256,8192]{1,0:T(8,128)(2,1)} %all-gather.3.cloned.1.call-done, bf16[8192,32]{0,1:T(8,128)(2,1)S(1)} %copy-done), kind=kOutput, calls=%fused_computation.111 | convolution fusion | flops 134225920 | bytes 4734976 | tf_op jit(solution)/shard_map/dot_general | solution.py:79
  91.8 0.7 broadcast_in_dim.15
  92.5 4.2 %all-to-all-start = ((bf16[16,256,32]{1,2,0:T(8,128)(2,1)}), bf16[16,256,32]{1,2,0:T(8,128)(2,1)S(1)}, u32[]{:S(2)}, u32[]{:S(2)}) async-start(bf16[16,256,32]{1,2,0:T(8,128)(2,1)} %broadcast_in_dim.15), calls=%async_computation | async-start | bytes 524288 | tf_op jit(solution)/shard_map/all_to_all | solution.py:19
  96.8 4.7 %convolution_convert_fusion.1 = bf16[256,256]{1,0:T(8,128)(2,1)S(1)} fusion(bf16[256,8192]{1,0:T(8,128)(2,1)} %all-gather.3.cloned.1.call-done, bf16[8192,256]{1,0:T(8,128)(2,1)} %param.5), kind=kOutput, calls=%fused_computation.110 | convolution fusion | flops 1073807360 | bytes 8519680 | tf_op jit(solution)/shard_map/dot_general | solution.py:78
  101.7 5.8 %all-to-all-done = bf16[16,256,32]{1,2,0:T(8,128)(2,1)S(1)} async-done(((bf16[16,256,32]{1,2,0:T(8,128)(2,1)}), bf16[16,256,32]{1,2,0:T(8,128)(2,1)S(1)}, u32[]{:S(2)}, u32[]{:S(2)}) %all-to-all-start) | async-done | bytes 262176 | tf_op jit(solution)/shard_map/all_to_all | solution.py:19
  107.6 8.0 %all-to-all-start.1 = ((bf16[256,16,512]{0,2,1:T(8,128)(2,1)}), bf16[256,16,512]{0,2,1:T(8,128)(2,1)}, u32[]{:S(2)}, u32[]{:S(2)}) async-start(bf16[256,16,512]{0,2,1:T(8,128)(2,1)} %bitcast.516), calls=%async_computation.1 | async-start | bytes 8388608 | tf_op jit(solution)/shard_map/all_to_all | solution.py:76
  115.9 1.9 collective-permute-start.2
  117.8 4.6 %collective-permute-start.1 = (bf16[256,256]{1,0:T(8,128)(2,1)S(1)}, bf16[256,256]{1,0:T(8,128)(2,1)S(1)}, u32[]{:S(2)}, u32[]{:S(2)}) collective-permute-start(bf16[256,256]{1,0:T(8,128)(2,1)S(1)} %copy.63), channel_id=1, source_target_pairs={{0,32},{16,48},{32,64},{48,80},{64,96},{80,112},{96,128},{112,144}... | collective-permute-start | bytes 393224 | tf_op jit(solution)/shard_map/ppermute | solution.py:31
  123.5 3.5 %collective-permute-start = (bf16[32,256]{1,0:T(8,128)(2,1)S(1)}, bf16[32,256]{1,0:T(8,128)(2,1)S(1)}, u32[]{:S(2)}, u32[]{:S(2)}) collective-permute-start(bf16[32,256]{1,0:T(8,128)(2,1)S(1)} %copy.61), channel_id=1, source_target_pairs={{0,16},{16,32},{32,48},{48,64},{64,80},{80,96},{96,112},{112,128},... | collective-permute-start | bytes 49160 | tf_op jit(solution)/shard_map/ppermute | solution.py:31
  131.8 0.7 constant_dynamic-update-slice_fusion.94
  132.5 0.7 constant_dynamic-update-slice_fusion.93
  133.2 0.7 constant_dynamic-update-slice_fusion.92
  133.9 0.7 constant_dynamic-update-slice_fusion.91
  134.6 0.7 constant_dynamic-update-slice_fusion.90
  135.3 0.7 constant_dynamic-update-slice_fusion.89
  135.9 0.7 constant_dynamic-update-slice_fusion.88
  136.6 0.7 constant_dynamic-update-slice_fusion.87
  137.3 0.7 constant_dynamic-update-slice_fusion.86
  138.0 0.7 constant_dynamic-update-slice_fusion.85
  138.7 0.7 constant_dynamic-update-slice_fusion.84
  139.3 0.7 constant_dynamic-update-slice_fusion.83
  140.0 0.7 constant_dynamic-update-slice_fusion.82
  140.7 0.7 constant_dynamic-update-slice_fusion.81
  141.4 0.7 constant_dynamic-update-slice_fusion.80
  142.1 0.7 constant_dynamic-update-slice_fusion.79
  142.7 0.7 constant_dynamic-update-slice_fusion.78
  143.4 0.7 constant_dynamic-update-slice_fusion.77
  144.1 0.7 constant_dynamic-update-slice_fusion.76
  144.8 0.7 constant_dynamic-update-slice_fusion.75
  145.5 0.7 constant_dynamic-update-slice_fusion.74
  146.2 0.7 constant_dynamic-update-slice_fusion.73
  146.9 0.7 constant_dynamic-update-slice_fusion.72
  147.5 0.7 constant_dynamic-update-slice_fusion.71
  148.2 0.7 constant_dynamic-update-slice_fusion.70
  148.9 0.7 constant_dynamic-update-slice_fusion.69
  149.6 0.7 constant_dynamic-update-slice_fusion.68
  150.3 0.7 constant_dynamic-update-slice_fusion.67
  151.0 0.7 constant_dynamic-update-slice_fusion.66
  151.6 0.7 constant_dynamic-update-slice_fusion.65
  152.3 0.7 constant_dynamic-update-slice_fusion.64
  153.5 1.0 copy-done.4
  154.6 0.6 constant_dynamic-update-slice_fusion.30
  158.2 0.6 constant_dynamic-update-slice_fusion.24
  165.6 0.6 constant_dynamic-update-slice_fusion.12
  169.3 0.6 constant_dynamic-update-slice_fusion.6
  170.5 0.6 constant_dynamic-update-slice_fusion.4
  172.9 0.6 constant_dynamic-update-slice_fusion
  174.4 3.5 %fusion.2 = (f32[128]{0:T(128)S(1)}, f32[128,32,639]{2,0,1:T(8,128)S(1)}) fusion(pred[128,32]{0,1:T(8,128)(4,1)S(1)} %subtract_compare_fusion, pred[128,639]{1,0:T(8,128)(4,1)S(1)} %get-tuple-element.52, bf16[768,256]{1,0:T(8,128)(2,1)S(1)} %pad_maximum_fusion, bf16[128,32,128]{0,2,1:T(8,128)(2,1)S(1)} %copy-done.3, f32[128,128]{0,1:T(8,128)S(1)} %copy.20), kind=kOutput, calls=%fused_computation.10 | convolution fusion | flops 682082176 | bytes 11833856 | tf_op jit(solution)/shard_map/ird,jd->irj/dot_general | solution.py:53
  177.9 3.6 %fusion.34 = f32[128,128]{1,0:T(8,128)S(1)} fusion(bf16[128,32,128]{2,0,1:T(8,128)(2,1)S(1)} %copy-done.5, f32[128,32,639]{2,0,1:T(8,128)S(1)} %get-tuple-element.54, f32[128]{0:T(128)S(1)} %get-tuple-element.53, pred[128,32]{0,1:T(8,128)(4,1)S(1)} %subtract_compare_fusion, pred[128,639]{1,0:T(8,128)(4,1)S(1)} %get-tuple-element.52, ...), kind=kOutput, calls=%fused_computation.107 | convolution fusion | flops 684683264 | bytes 11850240 | tf_op jit(solution)/shard_map/irj,jd->ird/dot_general | solution.py:69
  181.5 6.4 %fusion.8 = (f32[128]{0:T(128)S(1)}, f32[128]{0:T(128)S(1)}, f32[128,32,639]{2,0,1:T(8,128)S(1)}) fusion(f32[128,32,639]{2,0,1:T(8,128)S(1)} %get-tuple-element.54, f32[128]{0:T(128)S(1)} %get-tuple-element.53, pred[128,32]{0,1:T(8,128)(4,1)S(1)} %subtract_compare_fusion, pred[128,639]{1,0:T(8,128)(4,1)S(1)} %get-tuple-element.52, ...), kind=kOutput, calls=%fused_computation.16 | convolution fusion | flops 692551424 | bytes 22320640 | tf_op jit(solution)/shard_map/ird,jd->irj/dot_general | solution.py:53
  188.0 3.5 %fusion.35 = f32[128,128]{1,0:T(8,128)S(1)} fusion(bf16[128,32,128]{2,0,1:T(8,128)(2,1)S(1)} %copy-done.5, f32[128,32,639]{2,0,1:T(8,128)S(1)} %get-tuple-element.55, f32[128]{0:T(128)S(1)} %get-tuple-element.8, pred[128,32]{0,1:T(8,128)(4,1)S(1)} %subtract_compare_fusion, pred[128,639]{1,0:T(8,128)(4,1)S(1)} %get-tuple-element.52, ...), kind=kOutput, calls=%fused_computation.108 | convolution fusion | flops 684683264 | bytes 11850240 | tf_op jit(solution)/shard_map/irj,jd->ird/dot_general | solution.py:69
  191.4 4.4 %fusion.10 = f32[128]{0:T(128)S(1)} fusion(f32[128,32,639]{2,0,1:T(8,128)S(1)} %get-tuple-element.55, f32[128]{0:T(128)S(1)} %get-tuple-element.8, pred[128,32]{0,1:T(8,128)(4,1)S(1)} %subtract_compare_fusion, pred[128,639]{1,0:T(8,128)(4,1)S(1)} %get-tuple-element.52), kind=kLoop, calls=%fused_computation.18 | loop fusion | flops 13086592 | bytes 10556288 | tf_op jit(solution)/shard_map/reduce_sum | solution.py:67
  196.0 2.8 fusion
  198.8 6.0 %fusion.4 = (f32[128]{0:T(128)S(1)}, f32[128]{0:T(128)S(1)}, f32[128,32,639]{2,0,1:T(8,128)S(1)}) fusion(f32[128,32,639]{2,0,1:T(8,128)S(1)} %get-tuple-element.57, f32[128]{0:T(128)S(1)} %get-tuple-element.56, pred[128,32]{0,1:T(8,128)(4,1)S(1)} %subtract_compare_fusion.1, pred[128,639]{1,0:T(8,128)(4,1)S(1)} %get-tuple-element.51, ...), kind=kOutput, calls=%fused_computation.12 | convolution fusion | flops 692551424 | bytes 22320640 | tf_op jit(solution)/shard_map/ird,jd->irj/dot_general | solution.py:53
  204.8 4.2 %fusion.6 = f32[128]{0:T(128)S(1)} fusion(f32[128,32,639]{2,0,1:T(8,128)S(1)} %get-tuple-element.58, f32[128]{0:T(128)S(1)} %get-tuple-element.6, pred[128,32]{0,1:T(8,128)(4,1)S(1)} %subtract_compare_fusion.1, pred[128,639]{1,0:T(8,128)(4,1)S(1)} %get-tuple-element.51), kind=kLoop, calls=%fused_computation.14 | loop fusion | flops 13086592 | bytes 10556288 | tf_op jit(solution)/shard_map/reduce_sum | solution.py:67
  209.0 3.4 %fusion.31 = f32[128,128]{1,0:T(8,128)S(1)} fusion(bf16[128,32,128]{2,0,1:T(8,128)(2,1)S(1)} %constant_dynamic-update-slice_fusion.32, f32[128,32,639]{2,0,1:T(8,128)S(1)} %get-tuple-element.58, f32[128]{0:T(128)S(1)} %get-tuple-element.6, pred[128,32]{0,1:T(8,128)(4,1)S(1)} %subtract_compare_fusion.1, pred[128,639]{1,0:T(8,128)(4,1)S(1)} %get-tuple-element.51, ...), kind=kOutput, calls=%fused_computation.104 | convolution fusion | flops 684683264 | bytes 11850240 | tf_op jit(solution)/shard_map/irj,jd->ird/dot_general | solution.py:69
  212.5 3.5 %fusion.30 = f32[128,128]{1,0:T(8,128)S(1)} fusion(bf16[128,32,128]{2,0,1:T(8,128)(2,1)S(1)} %constant_dynamic-update-slice_fusion.32, f32[128,32,639]{2,0,1:T(8,128)S(1)} %get-tuple-element.57, f32[128]{0:T(128)S(1)} %get-tuple-element.56, pred[128,32]{0,1:T(8,128)(4,1)S(1)} %subtract_compare_fusion.1, pred[128,639]{1,0:T(8,128)(4,1)S(1)} %get-tuple-element.51, ...), kind=kOutput, calls=%fused_computation.103 | convolution fusion | flops 684683264 | bytes 11850240 | tf_op jit(solution)/shard_map/irj,jd->ird/dot_general | solution.py:69
  216.1 0.7 maximum_maximum_fusion
  216.8 6.4 %copy.57 = bf16[16,256,512]{2,1,0:T(8,128)(2,1)} copy(bf16[16,256,512]{1,2,0:T(8,128)(2,1)} %bitcast.136) | data formatting | bytes 8388608 | tf_op jit(solution)/shard_map/all_to_all | solution.py:76
  223.2 66.0 %all-gather.5.cloned.1.call-done = bf16[256,4096]{1,0:T(8,128)(2,1)} async-done(((bf16[256,256]{1,0:T(8,128)(2,1)}), bf16[256,4096]{1,0:T(8,128)(2,1)}) %all-gather.5.cloned.1.call-update) | async-done | bytes 2097168 | tf_op jit(solution)/shard_map/all_gather | solution.py:120
  289.3 4.8 %convolution_convert_fusion = bf16[256,512]{1,0:T(8,128)(2,1)} fusion(bf16[256,4096]{1,0:T(8,128)(2,1)} %all-gather.5.cloned.1.call-done, bf16[4096,512]{1,0:T(8,128)(2,1)} %bitcast.517), kind=kOutput, calls=%fused_computation.109 | convolution fusion | flops 1073872896 | bytes 6553600 | tf_op jit(solution)/shard_map/dot_general | solution.py:119
  (164 shorter events, 23.2 us)
Async XLA Ops:
  6.5 81.7 %copy-start = (bf16[8192,32]{0,1:T(8,128)(2,1)S(1)}, bf16[8192,32]{0,1:T(8,128)(2,1)}, u32[]{:S(2)}) copy-start(bf16[8192,32]{0,1:T(8,128)(2,1)} %param.6) | copy-start | bytes 1572868
  6.5 81.7 %all-gather.3.cloned.1.call-start = ((), (), s32[]{:S(2)}) async-start(), calls=%async_computation.2 | async-start | bytes 4456448 | tf_op jit(solution)/shard_map/all_gather | solution.py:77
  92.5 15.0 %all-to-all-start = ((bf16[16,256,32]{1,2,0:T(8,128)(2,1)}), bf16[16,256,32]{1,2,0:T(8,128)(2,1)S(1)}, u32[]{:S(2)}, u32[]{:S(2)}) async-start(bf16[16,256,32]{1,2,0:T(8,128)(2,1)} %broadcast_in_dim.15), calls=%async_computation | async-start | bytes 524288 | tf_op jit(solution)/shard_map/all_to_all | solution.py:19
  107.6 109.2 %all-to-all-start.1 = ((bf16[256,16,512]{0,2,1:T(8,128)(2,1)}), bf16[256,16,512]{0,2,1:T(8,128)(2,1)}, u32[]{:S(2)}, u32[]{:S(2)}) async-start(bf16[256,16,512]{0,2,1:T(8,128)(2,1)} %bitcast.516), calls=%async_computation.1 | async-start | bytes 8388608 | tf_op jit(solution)/shard_map/all_to_all | solution.py:76
  115.6 173.6 %all-gather.5.cloned.1.call-start = ((), (), s32[]{:S(2)}) async-start(), calls=%async_computation.3 | async-start | bytes 2228224 | tf_op jit(solution)/shard_map/all_gather | solution.py:120
  115.9 58.4 %collective-permute-start.2 = (bf16[256,256]{1,0:T(8,128)(2,1)S(1)}, bf16[256,256]{1,0:T(8,128)(2,1)S(1)}, u32[]{:S(2)}, u32[]{:S(2)}) collective-permute-start(bf16[256,256]{1,0:T(8,128)(2,1)S(1)} %copy.63), channel_id=1, source_target_pairs={{0,16},{16,32},{32,48},{48,64},{64,80},{80,96},{96,112},{112,128},... | collective-permute-start | bytes 393224 | tf_op jit(solution)/shard_map/ppermute | solution.py:31
  117.8 56.5 %collective-permute-start.1 = (bf16[256,256]{1,0:T(8,128)(2,1)S(1)}, bf16[256,256]{1,0:T(8,128)(2,1)S(1)}, u32[]{:S(2)}, u32[]{:S(2)}) collective-permute-start(bf16[256,256]{1,0:T(8,128)(2,1)S(1)} %copy.63), channel_id=1, source_target_pairs={{0,32},{16,48},{32,64},{48,80},{64,96},{80,112},{96,128},{112,144}... | collective-permute-start | bytes 393224 | tf_op jit(solution)/shard_map/ppermute | solution.py:31
  123.5 31.1 %collective-permute-start = (bf16[32,256]{1,0:T(8,128)(2,1)S(1)}, bf16[32,256]{1,0:T(8,128)(2,1)S(1)}, u32[]{:S(2)}, u32[]{:S(2)}) collective-permute-start(bf16[32,256]{1,0:T(8,128)(2,1)S(1)} %copy.61), channel_id=1, source_target_pairs={{0,16},{16,32},{32,48},{48,64},{64,80},{80,96},{96,112},{112,128},... | collective-permute-start | bytes 49160 | tf_op jit(solution)/shard_map/ppermute | solution.py:31
  153.5 1.0 copy-start.4
  154.5 19.8 %copy-start.3 = (bf16[128,32,128]{0,2,1:T(8,128)(2,1)S(1)}, bf16[128,32,128]{0,2,1:T(8,128)(2,1)}, u32[]{:S(2)}) copy-start(bf16[128,32,128]{0,2,1:T(8,128)(2,1)} %constant_dynamic-update-slice_fusion.64) | copy-start | bytes 3145732
  171.7 6.1 %copy-start.5 = (bf16[128,32,128]{2,0,1:T(8,128)(2,1)S(1)}, bf16[128,32,128]{2,0,1:T(8,128)(2,1)}, u32[]{:S(2)}) copy-start(bf16[128,32,128]{2,0,1:T(8,128)(2,1)} %copy-done.4) | copy-start | bytes 3145732
  188.0 8.1 %copy-start.2 = (bf16[128,32,128]{2,0,1:T(8,128)(2,1)S(1)}, bf16[128,32,128]{2,0,1:T(8,128)(2,1)}, u32[]{:S(2)}) copy-start(bf16[128,32,128]{2,0,1:T(8,128)(2,1)} %get-tuple-element.45) | copy-start | bytes 3145732
  212.5 81.5 %copy-start.1 = (bf16[8192,32]{0,1:T(8,128)(2,1)S(1)}, bf16[8192,32]{0,1:T(8,128)(2,1)}, u32[]{:S(2)}) copy-start(bf16[8192,32]{0,1:T(8,128)(2,1)} %param.6) | copy-start | bytes 1572868
Sparse Core Ops, SparseCore 0:
  9.1 79.0 all-gather.2
  216.9 72.2 all-gather.4
where the time goes:
time: 301 us
  waiting for transfers between devices  147 us (49%)
  matrix products  45.7 us (15%)
  local copies, waits for them, and re-layouts  42.3 us (14%)
  other arithmetic  29.4 us (10%)
  starting transfers between devices  22.3 us (7%)
  between operations  14.2 us (5%)
    all_gather x1, waiting for transfers between devices, body(): piece = lax.all_gather(tokens, 'head', axis=1, tiled=True)  74.4 us
    all_gather x1, waiting for transfers between devices, body(): lax.all_gather(attended, 'head', axis=1, tiled=True)  66 us
    unnamed x114, local copies, waits for them, and re-layouts  33.7 us
    unnamed x59, other arithmetic  19 us
    dot_general x4, matrix products, attend_block(): jnp.einsum('ird,jd->irj', product, key_rows, preferred_element_type=jnp.f...  18.7 us
    dot_general x4, matrix products, attend_block(): jnp.einsum('irj,jd->ird', weights, value_rows, preferred_element_type=jnp...  14 us
    ppermute x3, starting transfers between devices, passed_along(): lax.ppermute(value, axis, [(source, source + steps) for source in range(l...  9.96 us
    reduce_sum x2, other arithmetic, attend_block(): row_total = jnp.sum(raised, axis=(1, 2))  8.53 us
  transfers between devices with their start and end apart: 7, of which 3 were waited for; matrix products, arithmetic and copies ran while one was open for 36% of the time, Pallas kernels for 0%

commit v1 on v0

v1 whole, which is shorter than its diff:
```python
import jax, jax.numpy as jnp, functools
from jax import lax
from jax.experimental import pallas as pl
from jax.experimental.pallas import tpu as pltpu
from jax.sharding import PartitionSpec as P
HEAD = 128
WIN1 = 512
WIN2 = 32
BLK = 128
def attend_kernel(group, seq_ref, q_ref, first_ref, second_ref, out_ref, k2f, v2f, kpair, vtile, s_scr, mx_scr, mcb_scr):
    heads = q_ref.shape[1] // HEAD
    blocks = q_ref.shape[0] // BLK
    seq = seq_ref[0]
    tok = q_ref.shape[0]
    coef = (HEAD ** -0.5) * 1.4426950408889634
    start = seq == 0
    k2f[...] = second_ref[:, :HEAD].astype(jnp.float32)
    v2f[...] = second_ref[:, HEAD:].astype(jnp.float32)

    @pl.when(start)
    def _():
        k2f[:WIN2] = jnp.broadcast_to(k2f[WIN2:WIN2 + 1], (WIN2, HEAD))
        v2f[:WIN2] = jnp.zeros((WIN2, HEAD), jnp.float32)

    row = lax.broadcasted_iota(jnp.int32, (BLK, BLK), 0)
    col = lax.broadcasted_iota(jnp.int32, (BLK, BLK), 1)
    early = col > row
    absent = jnp.maximum(WIN1 - seq * tok, 0) // BLK
    low = jnp.float32(-1e30)

    def one(combo, _):
        h = combo // blocks
        b = combo % blocks
        base = pl.multiple_of(b * BLK, BLK)
        hcol = pl.multiple_of(h * HEAD, HEAD)
        qf = q_ref[pl.ds(base, BLK), pl.ds(hcol, HEAD)].astype(jnp.float32)
        kpair[:BLK] = first_ref[pl.ds(base, BLK), :HEAD]
        kpair[BLK:2 * BLK] = first_ref[pl.ds(base + 4 * BLK, BLK), :HEAD]
        kpair[2 * BLK:] = first_ref[pl.ds(base + BLK, 3 * BLK), :HEAD]
        vtile[:BLK] = first_ref[pl.ds(base, BLK), HEAD:]
        vtile[BLK:2 * BLK] = first_ref[pl.ds(base + 4 * BLK, BLK), HEAD:]
        vtile[2 * BLK:] = first_ref[pl.ds(base + BLK, 3 * BLK), HEAD:]
        mx_scr[...] = jnp.full(mx_scr.shape, low, jnp.float32)

        def scores(step, _):
            lag0 = step * group
            prods = []
            for g in range(group):
                k2 = k2f[pl.ds(WIN2 + base - lag0 - g, BLK), :]
                prods.append((qf * k2).astype(jnp.bfloat16))
            prod = jnp.concatenate(prods, axis=0)
            dims = (((1,), (1,)), ((), ()))
            for t in range(3):
                width = 2 * BLK if t < 2 else BLK
                s = lax.dot_general(prod, kpair[2 * BLK * t: 2 * BLK * t + width], dims, preferred_element_type=jnp.float32)
                s = s.reshape(group, BLK, width)
                if t == 0:
                    parts = [(0, jnp.where(early[None], s[:, :, :BLK], s[:, :, BLK:]))]
                elif t == 1:
                    parts = [(1, s[:, :, :BLK]), (2, s[:, :, BLK:])]
                else:
                    parts = [(3, s)]
                for place, value in parts:
                    s_scr[pl.ds(lag0, group), :, place * BLK:(place + 1) * BLK] = value
                    top = value[0]
                    for g in range(1, group):
                        top = jnp.maximum(top, value[g])
                    mx_scr[place] = jnp.maximum(mx_scr[place], top)
            return 0

        lax.fori_loop(0, WIN2 // group, scores, 0)
        tops = []
        gone = []
        for place in range(4):
            hide = (b + place) < absent
            if place == 0:
                gone.append(jnp.logical_and(early, hide))
            else:
                gone.append(jnp.logical_and(row >= 0, hide))
            tops.append(jnp.where(gone[place], low, mx_scr[place]))
        peak = jnp.max(jnp.maximum(jnp.maximum(tops[0], tops[1]), jnp.maximum(tops[2], tops[3])), axis=1, keepdims=True) * coef
        for place in range(4):
            mcb_scr[place] = jnp.where(gone[place], -low, jnp.broadcast_to(peak, (BLK, BLK)))

        def mix(lag, carry):
            acc, tot = carry
            raised = [jnp.exp2(s_scr[lag, :, p * BLK:(p + 1) * BLK] * coef - mcb_scr[p]) for p in range(4)]
            tot = tot + ((raised[0] + raised[1]) + (raised[2] + raised[3]))
            w = jnp.concatenate([
                jnp.where(early, raised[0], 0.0).astype(jnp.bfloat16),
                jnp.where(early, 0.0, raised[0]).astype(jnp.bfloat16),
                raised[1].astype(jnp.bfloat16), raised[2].astype(jnp.bfloat16), raised[3].astype(jnp.bfloat16)], axis=1)
            m = jnp.dot(w, vtile[...], preferred_element_type=jnp.float32)
            acc = acc + m * v2f[pl.ds(WIN2 + base - lag, BLK), :]
            return acc, tot

        zero = jnp.zeros((BLK, HEAD), jnp.float32)
        acc, tot = lax.fori_loop(0, WIN2, mix, (zero, zero), unroll=4)
        last = [jnp.exp2(s_scr[WIN2 - 1, :, p * BLK:(p + 1) * BLK] * coef - mcb_scr[p]) for p in range(4)]
        twice = jnp.where(jnp.logical_and(start, b == 0), jnp.maximum(WIN2 - 1 - row, 0), 0).astype(jnp.float32)
        tot = tot - twice * ((last[0] + last[1]) + (last[2] + last[3]))
        total = jnp.sum(tot, axis=1, keepdims=True)
        out_ref[pl.ds(base, BLK), pl.ds(hcol, HEAD)] = (acc / total).astype(jnp.bfloat16)
        return 0

    lax.fori_loop(0, heads * blocks, one, 0)

def attend(seq, q, first, second, group=8):
    rows = second.shape[0]
    return pl.pallas_call(
        functools.partial(attend_kernel, group),
        out_shape=jax.ShapeDtypeStruct(q.shape, jnp.bfloat16),
        in_specs=[pl.BlockSpec(memory_space=pltpu.SMEM)]+[pl.BlockSpec(memory_space=pltpu.VMEM)]*3,
        out_specs=pl.BlockSpec(memory_space=pltpu.VMEM),
        scratch_shapes=[pltpu.VMEM((rows, HEAD), jnp.float32), pltpu.VMEM((rows, HEAD), jnp.float32),
            pltpu.VMEM((5*BLK, HEAD), jnp.bfloat16), pltpu.VMEM((5*BLK, HEAD), jnp.bfloat16),
            pltpu.VMEM((WIN2, BLK, 4*BLK), jnp.float32), pltpu.VMEM((4, BLK, BLK), jnp.float32), pltpu.VMEM((4, BLK, BLK), jnp.float32)],
        compiler_params=pltpu.CompilerParams(vmem_limit_bytes=40*1024*1024),
    )(seq, q, first, second)


def swap_rows(value):
    return lax.ppermute(value, "head", [(i, (i + 8) % 16) for i in range(16)])


def along_z(value, step):
    return lax.ppermute(
        value, "head", [(i, (i // 8) * 8 + (i + step) % 8) for i in range(16)]
    )


def along_seq(value, step):
    return lax.ppermute(value, "seq", [(i, i + step) for i in range(16 - step)])


def round_x(value, step):
    return lax.ppermute(value, "seq", [(i, (i + 4 * step) % 16) for i in range(16)])


def other_core(value):
    return lax.ppermute(value, "seq", [(i, i ^ 1) for i in range(16)])


def ring_sum(mine, add):
    other = swap_rows(mine)
    total = add(None, 0, mine, other)
    pair = jnp.concatenate([mine[None], other[None]], axis=0)
    up = down = pair
    for step in range(1, 5):
        up = along_z(up, 1)
        if step < 4:
            down = along_z(down, -1)
        total = add(total, -step, up[0], up[1])
        if step < 4:
            total = add(total, step, down[0], down[1])
    return total


def sent_to_all(value, axis):
    size = lax.axis_size(axis)
    return lax.all_to_all(
        jnp.broadcast_to(value[None], (size, *value.shape)), axis, 0, 0, tiled=True
    )


def owned_columns(w_out):
    seq = lax.axis_index("seq")
    x, core = seq >> 2, seq & 1
    rows, width = w_out.shape
    part = rows // 8
    piece = lax.dynamic_slice_in_dim(w_out, (2 * x + core) * part, part, 0)
    piece = piece.reshape(part, 16, width // 16).transpose(1, 0, 2)
    piece = lax.all_to_all(piece, "head", 0, 0, tiled=True)
    held = jnp.zeros((4, *piece.shape), piece.dtype)
    held = lax.dynamic_update_slice_in_dim(held, piece[None], x, 0)
    for step in (1, 3, 2):
        moved = round_x(piece, step)
        held = lax.dynamic_update_slice_in_dim(held, moved[None], (x - step) & 3, 0)
    twin = other_core(held)
    first = jnp.where(core == 0, held, twin)
    second = jnp.where(core == 0, twin, held)
    both = jnp.stack([first, second], axis=0)
    return both.transpose(2, 1, 0, 3, 4).reshape(rows * 16, width // 16)


def body(tokens, w_query, w_keyval, w_out):
    tok_rows, depth = tokens.shape
    head = lax.axis_index("head")
    far_row = (head & 8) ^ 8

    def places(offset):
        spot = (head + offset) & 7
        return (head & 8) | spot, far_row | spot

    def rows_of(matrix, place, count):
        return lax.dynamic_slice_in_dim(matrix, place * count, count, 0)

    def dot(a, b):
        return jnp.dot(a, b, preferred_element_type=jnp.float32)

    def project(total, offset, mine, other):
        near, far = places(offset)
        new = [
            dot(mine, rows_of(w, near, depth)) + dot(other, rows_of(w, far, depth))
            for w in (w_query, w_keyval)
        ]
        return new if total is None else [a + b for a, b in zip(total, new)]

    query_sum, keyval_sum = ring_sum(tokens, project)
    queries = query_sum.astype(jnp.bfloat16)
    own = keyval_sum.astype(jnp.bfloat16)
    keyval = sent_to_all(own, "head").transpose(1, 0, 2).reshape(tok_rows, 4 * HEAD)
    first_pair = keyval[:, : 2 * HEAD]
    second_pair = keyval[:, 2 * HEAD :]
    near_first = along_seq(first_pair, 1)
    near_tail = along_seq(second_pair[tok_rows - WIN2 :], 1)
    far_first = along_seq(first_pair, 2)
    first_ext = jnp.concatenate([far_first, near_first, first_pair], axis=0)
    second_ext = jnp.concatenate([near_tail, second_pair], axis=0)
    seq = lax.axis_index("seq").astype(jnp.int32).reshape(1)
    attended = attend(seq, queries, first_ext, second_ext)
    columns = owned_columns(w_out)
    feats = attended.shape[1]

    def finish(total, offset, mine, other):
        near, far = places(offset)
        new = dot(mine, rows_of(columns, near, feats)) + dot(other, rows_of(columns, far, feats))
        return new if total is None else total + new

    return ring_sum(attended, finish).astype(jnp.bfloat16)


def solution(mesh):
    return jax.shard_map(
        body,
        mesh=mesh,
        in_specs=(P("seq", "head"), P(None, "head"), P(None, "head"), P("head", None)),
        out_specs=P("seq", "head"),
        check_vma=False,
    )
```

time: 301 us -> 200 us (0.66)
  waiting for transfers between devices: 147 us -> 75.1 us
  local copies, waits for them, and re-layouts: 42.3 us -> 8.49 us
  starting transfers between devices: 22.3 us -> 51.5 us
  other arithmetic: 29.4 us -> 4.07 us
  Pallas kernels: 0 us -> 21.1 us
  between operations: 14.2 us -> 0.65 us
  matrix products: 45.7 us -> 38.1 us
    all_gather x2 -> x0, waiting for transfers between devices: 140 us -> none  [the longest x1 74.4 us: body(): piece = lax.all_gather(tokens, 'head', axis=1, tiled=True)]
    ppermute x3 -> x23, waiting for transfers between devices: 0.01 us -> 67.9 us  [the longest x14 52.1 us: along_z(): lax.ppermute(value, 'head', [(i, i // 8 * 8 + (i + step) % 8) for i in ra...]
    unnamed x114 -> x12, local copies, waits for them, and re-layouts: 33.7 us -> 3.73 us
    ppermute x3 -> x23, starting transfers between devices: 9.96 us -> 34.9 us  [the longest x14 19.4 us: along_z(): lax.ppermute(value, 'head', [(i, i // 8 * 8 + (i + step) % 8) for i in ra...]
    pallas_call x0 -> x1, Pallas kernels: none -> 21.1 us  [attend(): pl.pallas_call(functools.partial(attend_kernel, group), out_shape=jax.Sha...]
    unnamed x59 -> x0, other arithmetic: 19 us -> none
    reduce_sum x2 -> x0, other arithmetic: 8.53 us -> none  [attend_block(): row_total = jnp.sum(raised, axis=(1, 2))]
    dot_general x11 -> x48, matrix products: 45.7 us -> 38.1 us  [dot(): return jnp.dot(a, b, preferred_element_type=jnp.float32)]
  transfers between devices with their start and end apart: 7 -> 25, of which waited for: 3 -> 12; matrix products, arithmetic and copies ran while one was open for 36% -> 25% of each run, Pallas kernels for 0% -> 11%
where the time goes in v1:
time: 200 us; the launch traced here: 199 us
  waiting for transfers between devices  75.1 us (38%)
  starting transfers between devices  51.5 us (26%)
  matrix products  38.1 us (19%)
  Pallas kernels  21.1 us (11%)
  local copies, waits for them, and re-layouts  8.49 us (4%)
  other arithmetic  4.07 us (2%)
    ppermute x14, waiting for transfers between devices, along_z(): lax.ppermute(value, 'head', [(i, i // 8 * 8 + (i + step) % 8) for i in ra...  52.1 us
    dot_general x48, matrix products, dot(): return jnp.dot(a, b, preferred_element_type=jnp.float32)  38.1 us
    pallas_call x1, Pallas kernels, attend(): pl.pallas_call(functools.partial(attend_kernel, group), out_shape=jax.Sha...  21.1 us
    ppermute x14, starting transfers between devices, along_z(): lax.ppermute(value, 'head', [(i, i // 8 * 8 + (i + step) % 8) for i in ra...  19.4 us
    ppermute x3, starting transfers between devices, along_seq(): return lax.ppermute(value, 'seq', [(i, i + step) for i in range(16 - step)])  8.95 us
    all_to_all x1, starting transfers between devices, owned_columns(): piece = lax.all_to_all(piece, 'head', 0, 0, tiled=True)  8.57 us
    ppermute x3, waiting for transfers between devices, round_x(): lax.ppermute(value, 'seq', [(i, (i + 4 * step) % 16) for i in range(16)])  8.28 us
    all_to_all x1, starting transfers between devices, sent_to_all(): lax.all_to_all(jnp.broadcast_to(value[None], (size, *value.shape)), axis,...  8.01 us
  transfers between devices with their start and end apart: 25, of which 12 were waited for; matrix products, arithmetic and copies ran while one was open for 25% of the time, Pallas kernels for 11%

profile of v1, /device:TPU:2, one launch (start us, length us, event | category | flops | bytes accessed | tf_op | source)
XLA Modules:
  0.0 199.0 jit_solution(14053996302774696324)
XLA Ops:
  0.0 1.6 collective-permute-start
  1.6 1.1 constant_dynamic-slice_fusion
  2.8 1.1 copy.32
  3.9 8.6 %all-to-all-start.1 = ((bf16[16,32,512]{2,1,0:T(8,128)(2,1)}), bf16[16,32,512]{2,1,0:T(8,128)(2,1)S(1)}, u32[]{:S(2)}, u32[]{:S(2)}) async-start(bf16[16,32,512]{2,1,0:T(8,128)(2,1)} %copy.32), calls=%async_computation.1 | async-start | bytes 1048576 | tf_op jit(solution)/shard_map/all_to_all | solution.py:173
  12.6 3.2 %collective-permute-start.2 = (bf16[2,256,512]{2,1,0:T(8,128)(2,1)S(1)}, bf16[2,256,512]{2,1,0:T(8,128)(2,1)}, u32[]{:S(2)}, u32[]{:S(2)}) collective-permute-start(bf16[2,256,512]{2,1,0:T(8,128)(2,1)S(1)} %pad_maximum_fusion.1), channel_id=1, source_target_pairs={{0,7},{1,0},{2,1},{3,2},{4,3},{5,4},{6,5},{7,6},{8,15},{9,8},{10,9... | collective-permute-start | bytes 1572872 | tf_op jit(solution)/shard_map/ppermute | solution.py:127
  16.0 1.2 fusion.72
  17.4 19.6 %collective-permute-done.2 = bf16[2,256,512]{2,1,0:T(8,128)(2,1)} collective-permute-done((bf16[2,256,512]{2,1,0:T(8,128)(2,1)S(1)}, bf16[2,256,512]{2,1,0:T(8,128)(2,1)}, u32[]{:S(2)}, u32[]{:S(2)}) %collective-permute-start.2) | collective-permute-done | bytes 524320 | tf_op jit(solution)/shard_map/ppermute | solution.py:127
  37.1 1.5 collective-permute-start.4
  38.6 1.2 fusion.75
  39.7 1.3 fusion.65
  41.6 1.3 fusion.68
  42.9 1.1 convolution_add_fusion.21
  44.0 1.1 fusion.74
  45.1 1.3 convolution_add_fusion.14
  46.4 1.3 convolution_add_fusion.15
  47.7 1.1 fusion.22
  48.8 1.2 fusion.15
  50.1 1.6 collective-permute-start.11
  52.2 2.1 %collective-permute-start.13 = (bf16[16,32,512]{2,1,0:T(8,128)(2,1)S(1)}, bf16[16,32,512]{2,1,0:T(8,128)(2,1)S(1)}, u32[]{:S(2)}, u32[]{:S(2)}) collective-permute-start(bf16[16,32,512]{2,1,0:T(8,128)(2,1)S(1)} %all-to-all-done.1), channel_id=1, source_target_pairs={{0,128},{16,144},{32,160},{48,176},{64,192},{80,208},{96,224},{112... | collective-permute-start | bytes 1572872 | tf_op jit(solution)/shard_map/ppermute | solution.py:137
  54.6 2.8 %collective-permute-start.6 = (bf16[2,256,512]{2,1,0:T(8,128)(2,1)}, bf16[2,256,512]{2,1,0:T(8,128)(2,1)S(1)}, u32[]{:S(2)}, u32[]{:S(2)}) collective-permute-start(bf16[2,256,512]{2,1,0:T(8,128)(2,1)} %collective-permute-done.4), channel_id=1, source_target_pairs={{0,7},{1,0},{2,1},{3,2},{4,3},{5,4},{6,5},{7,6},{8,15},{9,8},{10,9... | collective-permute-start | bytes 1572872 | tf_op jit(solution)/shard_map/ppermute | solution.py:127
  57.4 1.2 fusion.77
  58.5 1.3 fusion.59
  59.9 1.3 fusion.62
  61.2 1.3 fusion.13
  62.5 1.3 fusion.12
  63.7 1.1 convolution_add_fusion.19
  64.9 1.1 fusion.76
  66.0 1.2 fusion.23
  67.3 8.3 %collective-permute-done.13 = bf16[16,32,512]{2,1,0:T(8,128)(2,1)S(1)} collective-permute-done((bf16[16,32,512]{2,1,0:T(8,128)(2,1)S(1)}, bf16[16,32,512]{2,1,0:T(8,128)(2,1)S(1)}, u32[]{:S(2)}, u32[]{:S(2)}) %collective-permute-start.13) | collective-permute-done | bytes 524320 | tf_op jit(solution)/shard_map/ppermute | solution.py:137
  75.9 1.2 fusion.53
  77.1 1.8 collective-permute-start.7
  79.5 1.9 fusion.56
  81.4 1.9 convolution_add_fusion.10
  83.3 9.7 %collective-permute-done.7 = bf16[2,256,512]{2,1,0:T(8,128)(2,1)S(1)} collective-permute-done((bf16[2,256,512]{2,1,0:T(8,128)(2,1)S(1)}, bf16[2,256,512]{2,1,0:T(8,128)(2,1)S(1)}, u32[]{:S(2)}, u32[]{:S(2)}) %collective-permute-start.7) | collective-permute-done | bytes 524320 | tf_op jit(solution)/shard_map/ppermute | solution.py:127
  93.9 0.7 broadcast_in_dim.35
  94.7 8.0 %all-to-all-start = ((bf16[16,256,32]{1,2,0:T(8,128)(2,1)}), bf16[16,256,32]{1,2,0:T(8,128)(2,1)S(1)}, u32[]{:S(2)}, u32[]{:S(2)}) async-start(bf16[16,256,32]{1,2,0:T(8,128)(2,1)} %broadcast_in_dim.35), calls=%async_computation | async-start | bytes 524288 | tf_op jit(solution)/shard_map/all_to_all | solution.py:161
  102.7 1.4 fusion.14
  104.1 1.3 fusion.50
  105.4 7.2 %all-to-all-done = bf16[16,256,32]{1,2,0:T(8,128)(2,1)S(1)} async-done(((bf16[16,256,32]{1,2,0:T(8,128)(2,1)}), bf16[16,256,32]{1,2,0:T(8,128)(2,1)S(1)}, u32[]{:S(2)}, u32[]{:S(2)}) %all-to-all-start) | async-done | bytes 262176 | tf_op jit(solution)/shard_map/all_to_all | solution.py:161
  113.3 1.0 copy.36
  114.3 1.9 collective-permute-start.9
  116.2 5.0 %collective-permute-start.8 = (bf16[256,256]{1,0:T(8,128)(2,1)S(1)}, bf16[256,256]{1,0:T(8,128)(2,1)}, u32[]{:S(2)}, u32[]{:S(2)}) collective-permute-start(bf16[256,256]{1,0:T(8,128)(2,1)S(1)} %copy.36), channel_id=1, source_target_pairs={{0,32},{16,48},{32,64},{48,80},{64,96},{80,112},{96,128},{112,144}... | collective-permute-start | bytes 393224 | tf_op jit(solution)/shard_map/ppermute | solution.py:133
  121.2 0.7 slice.140
  121.9 0.9 copy.37
  122.8 2.0 %collective-permute-start.10 = (bf16[32,256]{1,0:T(8,128)(2,1)S(1)}, bf16[32,256]{1,0:T(8,128)(2,1)}, u32[]{:S(2)}, u32[]{:S(2)}) collective-permute-start(bf16[32,256]{1,0:T(8,128)(2,1)S(1)} %copy.37), channel_id=1, source_target_pairs={{0,16},{16,32},{32,48},{48,64},{64,80},{80,96},{96,112},{112,128},... | collective-permute-start | bytes 49160 | tf_op jit(solution)/shard_map/ppermute | solution.py:133
  124.9 1.3 fusion.16.q_ref
  126.1 1.0 copy.38
  127.2 3.3 %collective-permute-done.10 = bf16[32,256]{1,0:T(8,128)(2,1)} collective-permute-done((bf16[32,256]{1,0:T(8,128)(2,1)S(1)}, bf16[32,256]{1,0:T(8,128)(2,1)}, u32[]{:S(2)}, u32[]{:S(2)}) %collective-permute-start.10) | collective-permute-done | bytes 16416 | tf_op jit(solution)/shard_map/ppermute | solution.py:133
  130.4 0.7 pad_maximum_fusion.4.second_ref
  131.2 1.0 pad_maximum_fusion.2.first_ref
  132.2 21.1 %shard_map.46 = bf16[256,256]{1,0:T(8,128)(2,1)S(1)} custom-call(s32[1]{0:T(128)} %bitcast.seq_ref, bf16[256,256]{1,0:T(8,128)(2,1)S(1)} %fusion.16.q_ref, bf16[768,256]{1,0:T(8,128)(2,1)S(1)} %pad_maximum_fusion.2.first_ref, bf16[288,256]{1,0:T(8,128)(2,1)S(1)} %pad_maximum_fusion.4.second_ref), custom_call_target="tpu_custom_call" | custom-call | tf_op jit(solution)/shard_map/pallas_call | solution.py:110
  153.2 0.7 collective-permute-start.15
  154.0 4.3 %collective-permute-done.15 = bf16[256,256]{1,0:T(8,128)(2,1)S(1)} collective-permute-done((bf16[256,256]{1,0:T(8,128)(2,1)S(1)}, bf16[256,256]{1,0:T(8,128)(2,1)S(1)}, u32[]{:S(2)}, u32[]{:S(2)}) %collective-permute-start.15) | collective-permute-done | bytes 131104 | tf_op jit(solution)/shard_map/ppermute | solution.py:123
  158.3 2.7 %collective-permute-start.17 = (bf16[2,256,256]{2,1,0:T(8,128)(2,1)S(1)}, bf16[2,256,256]{2,1,0:T(8,128)(2,1)S(1)}, u32[]{:S(2)}, u32[]{:S(2)}) collective-permute-start(bf16[2,256,256]{2,1,0:T(8,128)(2,1)S(1)} %pad_maximum_fusion.3), channel_id=1, source_target_pairs={{0,7},{1,0},{2,1},{3,2},{4,3},{5,4},{6,5},{7,6},{8,15},{9,8},{10,9... | collective-permute-start | bytes 786440 | tf_op jit(solution)/shard_map/ppermute | solution.py:127
  161.0 6.3 %collective-permute-done.17 = bf16[2,256,256]{2,1,0:T(8,128)(2,1)S(1)} collective-permute-done((bf16[2,256,256]{2,1,0:T(8,128)(2,1)S(1)}, bf16[2,256,256]{2,1,0:T(8,128)(2,1)S(1)}, u32[]{:S(2)}, u32[]{:S(2)}) %collective-permute-start.17) | collective-permute-done | bytes 262176 | tf_op jit(solution)/shard_map/ppermute | solution.py:127
  167.3 3.0 %collective-permute-start.19 = (bf16[2,256,256]{2,1,0:T(8,128)(2,1)S(1)}, bf16[2,256,256]{2,1,0:T(8,128)(2,1)S(1)}, u32[]{:S(2)}, u32[]{:S(2)}) collective-permute-start(bf16[2,256,256]{2,1,0:T(8,128)(2,1)S(1)} %collective-permute-done.17), channel_id=1, source_target_pairs={{0,7},{1,0},{2,1},{3,2},{4,3},{5,4},{6,5},{7,6},{8,15},{9,8},{10,9... | collective-permute-start | bytes 786440 | tf_op jit(solution)/shard_map/ppermute | solution.py:127
  170.4 1.9 select_bitcast_fusion.1
  172.7 1.1 fusion.44
  174.0 1.1 convolution_add_fusion.6
  175.9 1.0 collective-permute-done.19
  176.9 3.7 %collective-permute-start.21 = (bf16[2,256,256]{2,1,0:T(8,128)(2,1)S(1)}, bf16[2,256,256]{2,1,0:T(8,128)(2,1)S(1)}, u32[]{:S(2)}, u32[]{:S(2)}) collective-permute-start(bf16[2,256,256]{2,1,0:T(8,128)(2,1)S(1)} %collective-permute-done.19), channel_id=1, source_target_pairs={{0,7},{1,0},{2,1},{3,2},{4,3},{5,4},{6,5},{7,6},{8,15},{9,8},{10,9... | collective-permute-start | bytes 786440 | tf_op jit(solution)/shard_map/ppermute | solution.py:127
  181.6 8.7 %collective-permute-done.20 = bf16[2,256,256]{2,1,0:T(8,128)(2,1)S(1)} collective-permute-done((bf16[2,256,256]{2,1,0:T(8,128)(2,1)S(1)}, bf16[2,256,256]{2,1,0:T(8,128)(2,1)S(1)}, u32[]{:S(2)}, u32[]{:S(2)}) %collective-permute-start.20) | collective-permute-done | bytes 262176 | tf_op jit(solution)/shard_map/ppermute | solution.py:127
  191.2 6.6 %collective-permute-done.22 = bf16[2,256,256]{2,1,0:T(8,128)(2,1)S(1)} collective-permute-done((bf16[2,256,256]{2,1,0:T(8,128)(2,1)S(1)}, bf16[2,256,256]{2,1,0:T(8,128)(2,1)S(1)}, u32[]{:S(2)}, u32[]{:S(2)}) %collective-permute-start.22) | collective-permute-done | bytes 262176 | tf_op jit(solution)/shard_map/ppermute | solution.py:127
  198.1 0.9 fusion.7
  (63 shorter events, 8.4 us)
Async XLA Ops:
  0.0 15.8 %copy-start = (bf16[8192,32]{0,1:T(8,128)(2,1)S(1)}, bf16[8192,32]{0,1:T(8,128)(2,1)}, u32[]{:S(2)}) copy-start(bf16[8192,32]{0,1:T(8,128)(2,1)} %param.6) | copy-start | bytes 1572868
  0.0 12.5 %copy-start.1 = (bf16[256,512]{1,0:T(8,128)(2,1)S(1)}, bf16[256,512]{1,0:T(8,128)(2,1)}, u32[]{:S(2)}) copy-start(bf16[256,512]{1,0:T(8,128)(2,1)} %param.4) | copy-start | bytes 786436
  0.0 12.5 %collective-permute-start = (bf16[256,512]{1,0:T(8,128)(2,1)}, bf16[256,512]{1,0:T(8,128)(2,1)S(1)}, u32[]{:S(2)}, u32[]{:S(2)}) collective-permute-start(bf16[256,512]{1,0:T(8,128)(2,1)} %param.4), channel_id=1, source_target_pairs={{0,8},{1,9},{2,10},{3,11},{4,12},{5,13},{6,14},{7,15},{8,0},{9,1},... | collective-permute-start | bytes 786440 | tf_op jit(solution)/shard_map/ppermute | solution.py:123
  3.9 46.1 %all-to-all-start.1 = ((bf16[16,32,512]{2,1,0:T(8,128)(2,1)}), bf16[16,32,512]{2,1,0:T(8,128)(2,1)S(1)}, u32[]{:S(2)}, u32[]{:S(2)}) async-start(bf16[16,32,512]{2,1,0:T(8,128)(2,1)} %copy.32), calls=%async_computation.1 | async-start | bytes 1048576 | tf_op jit(solution)/shard_map/all_to_all | solution.py:173
  12.6 24.5 %collective-permute-start.2 = (bf16[2,256,512]{2,1,0:T(8,128)(2,1)S(1)}, bf16[2,256,512]{2,1,0:T(8,128)(2,1)}, u32[]{:S(2)}, u32[]{:S(2)}) collective-permute-start(bf16[2,256,512]{2,1,0:T(8,128)(2,1)S(1)} %pad_maximum_fusion.1), channel_id=1, source_target_pairs={{0,7},{1,0},{2,1},{3,2},{4,3},{5,4},{6,5},{7,6},{8,15},{9,8},{10,9... | collective-permute-start | bytes 1572872 | tf_op jit(solution)/shard_map/ppermute | solution.py:127
  17.2 23.8 %collective-permute-start.1 = (bf16[2,256,512]{2,1,0:T(8,128)(2,1)S(1)}, bf16[2,256,512]{2,1,0:T(8,128)(2,1)}, u32[]{:S(2)}, u32[]{:S(2)}) collective-permute-start(bf16[2,256,512]{2,1,0:T(8,128)(2,1)S(1)} %pad_maximum_fusion.1), channel_id=1, source_target_pairs={{0,1},{1,2},{2,3},{3,4},{4,5},{5,6},{6,7},{7,0},{8,9},{9,10},{10,1... | collective-permute-start | bytes 1572872 | tf_op jit(solution)/shard_map/ppermute | solution.py:127
  37.1 17.5 %collective-permute-start.4 = (bf16[2,256,512]{2,1,0:T(8,128)(2,1)}, bf16[2,256,512]{2,1,0:T(8,128)(2,1)}, u32[]{:S(2)}, u32[]{:S(2)}) collective-permute-start(bf16[2,256,512]{2,1,0:T(8,128)(2,1)} %collective-permute-done.2), channel_id=1, source_target_pairs={{0,7},{1,0},{2,1},{3,2},{4,3},{5,4},{6,5},{7,6},{8,15},{9,8},{10,9... | collective-permute-start | bytes 1572872 | tf_op jit(solution)/shard_map/ppermute | solution.py:127
  41.0 18.8 %collective-permute-start.3 = (bf16[2,256,512]{2,1,0:T(8,128)(2,1)}, bf16[2,256,512]{2,1,0:T(8,128)(2,1)}, u32[]{:S(2)}, u32[]{:S(2)}) collective-permute-start(bf16[2,256,512]{2,1,0:T(8,128)(2,1)} %collective-permute-done.1), channel_id=1, source_target_pairs={{0,1},{1,2},{2,3},{3,4},{4,5},{5,6},{6,7},{7,0},{8,9},{9,10},{10,1... | collective-permute-start | bytes 1572872 | tf_op jit(solution)/shard_map/ppermute | solution.py:127
  50.1 17.1 %collective-permute-start.11 = (bf16[16,32,512]{2,1,0:T(8,128)(2,1)S(1)}, bf16[16,32,512]{2,1,0:T(8,128)(2,1)S(1)}, u32[]{:S(2)}, u32[]{:S(2)}) collective-permute-start(bf16[16,32,512]{2,1,0:T(8,128)(2,1)S(1)} %all-to-all-done.1), channel_id=1, source_target_pairs={{0,64},{16,80},{32,96},{48,112},{64,128},{80,144},{96,160},{112,17... | collective-permute-start | bytes 1572872 | tf_op jit(solution)/shard_map/ppermute | solution.py:137
  51.6 15.6 %collective-permute-start.12 = (bf16[16,32,512]{2,1,0:T(8,128)(2,1)S(1)}, bf16[16,32,512]{2,1,0:T(8,128)(2,1)S(1)}, u32[]{:S(2)}, u32[]{:S(2)}) collective-permute-start(bf16[16,32,512]{2,1,0:T(8,128)(2,1)S(1)} %all-to-all-done.1), channel_id=1, source_target_pairs={{0,192},{16,208},{32,224},{48,240},{64,0},{80,16},{96,32},{112,48}... | collective-permute-start | bytes 1572872 | tf_op jit(solution)/shard_map/ppermute | solution.py:137
  52.2 23.4 %collective-permute-start.13 = (bf16[16,32,512]{2,1,0:T(8,128)(2,1)S(1)}, bf16[16,32,512]{2,1,0:T(8,128)(2,1)S(1)}, u32[]{:S(2)}, u32[]{:S(2)}) collective-permute-start(bf16[16,32,512]{2,1,0:T(8,128)(2,1)S(1)} %all-to-all-done.1), channel_id=1, source_target_pairs={{0,128},{16,144},{32,160},{48,176},{64,192},{80,208},{96,224},{112... | collective-permute-start | bytes 1572872 | tf_op jit(solution)/shard_map/ppermute | solution.py:137
  54.6 21.1 %collective-permute-start.6 = (bf16[2,256,512]{2,1,0:T(8,128)(2,1)}, bf16[2,256,512]{2,1,0:T(8,128)(2,1)S(1)}, u32[]{:S(2)}, u32[]{:S(2)}) collective-permute-start(bf16[2,256,512]{2,1,0:T(8,128)(2,1)} %collective-permute-done.4), channel_id=1, source_target_pairs={{0,7},{1,0},{2,1},{3,2},{4,3},{5,4},{6,5},{7,6},{8,15},{9,8},{10,9... | collective-permute-start | bytes 1572872 | tf_op jit(solution)/shard_map/ppermute | solution.py:127
  59.8 17.3 %collective-permute-start.5 = (bf16[2,256,512]{2,1,0:T(8,128)(2,1)}, bf16[2,256,512]{2,1,0:T(8,128)(2,1)S(1)}, u32[]{:S(2)}, u32[]{:S(2)}) collective-permute-start(bf16[2,256,512]{2,1,0:T(8,128)(2,1)} %collective-permute-done.3), channel_id=1, source_target_pairs={{0,1},{1,2},{2,3},{3,4},{4,5},{5,6},{6,7},{7,0},{8,9},{9,10},{10,1... | collective-permute-start | bytes 1572872 | tf_op jit(solution)/shard_map/ppermute | solution.py:127
  75.6 94.7 %collective-permute-start.14 = (bf16[4,16,32,512]{3,2,0,1:T(8,128)(2,1)S(1)}, bf16[4,16,32,512]{3,2,0,1:T(8,128)(2,1)}, u32[]{:S(2)}, u32[]{:S(2)}) collective-permute-start(bf16[4,16,32,512]{3,2,0,1:T(8,128)(2,1)S(1)} %bitcast_dynamic-update-slice_fusion), channel_id=1, source_target_pairs={{0,16},{16,0},{32,48},{48,32},{64,80},{80,64},{96,112},{112,96},{1... | collective-permute-start | bytes 6291464 | tf_op jit(solution)/shard_map/ppermute | solution.py:141
  77.1 2.4 %copy-start.2 = (bf16[2,256,512]{2,1,0:T(8,128)(2,1)}, bf16[2,256,512]{2,1,0:T(8,128)(2,1)S(1)}, u32[]{:S(2)}) copy-start(bf16[2,256,512]{2,1,0:T(8,128)(2,1)S(1)} %collective-permute-done.5) | copy-start | bytes 1572868
  77.1 15.8 %collective-permute-start.7 = (bf16[2,256,512]{2,1,0:T(8,128)(2,1)S(1)}, bf16[2,256,512]{2,1,0:T(8,128)(2,1)S(1)}, u32[]{:S(2)}, u32[]{:S(2)}) collective-permute-start(bf16[2,256,512]{2,1,0:T(8,128)(2,1)S(1)} %collective-permute-done.5), channel_id=1, source_target_pairs={{0,1},{1,2},{2,3},{3,4},{4,5},{5,6},{6,7},{7,0},{8,9},{9,10},{10,1... | collective-permute-start | bytes 1572872 | tf_op jit(solution)/shard_map/ppermute | solution.py:127
  92.9 0.8 copy-start.3
  94.7 17.9 %all-to-all-start = ((bf16[16,256,32]{1,2,0:T(8,128)(2,1)}), bf16[16,256,32]{1,2,0:T(8,128)(2,1)S(1)}, u32[]{:S(2)}, u32[]{:S(2)}) async-start(bf16[16,256,32]{1,2,0:T(8,128)(2,1)} %broadcast_in_dim.35), calls=%async_computation | async-start | bytes 524288 | tf_op jit(solution)/shard_map/all_to_all | solution.py:161
  114.3 16.9 %collective-permute-start.9 = (bf16[256,256]{1,0:T(8,128)(2,1)S(1)}, bf16[256,256]{1,0:T(8,128)(2,1)}, u32[]{:S(2)}, u32[]{:S(2)}) collective-permute-start(bf16[256,256]{1,0:T(8,128)(2,1)S(1)} %copy.36), channel_id=1, source_target_pairs={{0,16},{16,32},{32,48},{48,64},{64,80},{80,96},{96,112},{112,128},... | collective-permute-start | bytes 393224 | tf_op jit(solution)/shard_map/ppermute | solution.py:133
  116.2 14.9 %collective-permute-start.8 = (bf16[256,256]{1,0:T(8,128)(2,1)S(1)}, bf16[256,256]{1,0:T(8,128)(2,1)}, u32[]{:S(2)}, u32[]{:S(2)}) collective-permute-start(bf16[256,256]{1,0:T(8,128)(2,1)S(1)} %copy.36), channel_id=1, source_target_pairs={{0,32},{16,48},{32,64},{48,80},{64,96},{80,112},{96,128},{112,144}... | collective-permute-start | bytes 393224 | tf_op jit(solution)/shard_map/ppermute | solution.py:133
  122.8 7.6 %collective-permute-start.10 = (bf16[32,256]{1,0:T(8,128)(2,1)S(1)}, bf16[32,256]{1,0:T(8,128)(2,1)}, u32[]{:S(2)}, u32[]{:S(2)}) collective-permute-start(bf16[32,256]{1,0:T(8,128)(2,1)S(1)} %copy.37), channel_id=1, source_target_pairs={{0,16},{16,32},{32,48},{48,64},{64,80},{80,96},{96,112},{112,128},... | collective-permute-start | bytes 49160 | tf_op jit(solution)/shard_map/ppermute | solution.py:133
  153.2 5.1 %collective-permute-start.15 = (bf16[256,256]{1,0:T(8,128)(2,1)S(1)}, bf16[256,256]{1,0:T(8,128)(2,1)S(1)}, u32[]{:S(2)}, u32[]{:S(2)}) collective-permute-start(bf16[256,256]{1,0:T(8,128)(2,1)S(1)} %shard_map.46), channel_id=1, source_target_pairs={{0,8},{1,9},{2,10},{3,11},{4,12},{5,13},{6,14},{7,15},{8,0},{9,1},... | collective-permute-start | bytes 393224 | tf_op jit(solution)/shard_map/ppermute | solution.py:123
  158.3 9.0 %collective-permute-start.17 = (bf16[2,256,256]{2,1,0:T(8,128)(2,1)S(1)}, bf16[2,256,256]{2,1,0:T(8,128)(2,1)S(1)}, u32[]{:S(2)}, u32[]{:S(2)}) collective-permute-start(bf16[2,256,256]{2,1,0:T(8,128)(2,1)S(1)} %pad_maximum_fusion.3), channel_id=1, source_target_pairs={{0,7},{1,0},{2,1},{3,2},{4,3},{5,4},{6,5},{7,6},{8,15},{9,8},{10,9... | collective-permute-start | bytes 786440 | tf_op jit(solution)/shard_map/ppermute | solution.py:127
  161.0 9.4 %collective-permute-start.16 = (bf16[2,256,256]{2,1,0:T(8,128)(2,1)S(1)}, bf16[2,256,256]{2,1,0:T(8,128)(2,1)}, u32[]{:S(2)}, u32[]{:S(2)}) collective-permute-start(bf16[2,256,256]{2,1,0:T(8,128)(2,1)S(1)} %pad_maximum_fusion.3), channel_id=1, source_target_pairs={{0,1},{1,2},{2,3},{3,4},{4,5},{5,6},{6,7},{7,0},{8,9},{9,10},{10,1... | collective-permute-start | bytes 786440 | tf_op jit(solution)/shard_map/ppermute | solution.py:127
  167.3 9.5 %collective-permute-start.19 = (bf16[2,256,256]{2,1,0:T(8,128)(2,1)S(1)}, bf16[2,256,256]{2,1,0:T(8,128)(2,1)S(1)}, u32[]{:S(2)}, u32[]{:S(2)}) collective-permute-start(bf16[2,256,256]{2,1,0:T(8,128)(2,1)S(1)} %collective-permute-done.17), channel_id=1, source_target_pairs={{0,7},{1,0},{2,1},{3,2},{4,3},{5,4},{6,5},{7,6},{8,15},{9,8},{10,9... | collective-permute-start | bytes 786440 | tf_op jit(solution)/shard_map/ppermute | solution.py:127
  170.4 10.5 %collective-permute-start.18 = (bf16[2,256,256]{2,1,0:T(8,128)(2,1)}, bf16[2,256,256]{2,1,0:T(8,128)(2,1)S(1)}, u32[]{:S(2)}, u32[]{:S(2)}) collective-permute-start(bf16[2,256,256]{2,1,0:T(8,128)(2,1)} %collective-permute-done.16), channel_id=1, source_target_pairs={{0,1},{1,2},{2,3},{3,4},{4,5},{5,6},{6,7},{7,0},{8,9},{9,10},{10,1... | collective-permute-start | bytes 786440 | tf_op jit(solution)/shard_map/ppermute | solution.py:127
  176.9 13.6 %collective-permute-start.21 = (bf16[2,256,256]{2,1,0:T(8,128)(2,1)S(1)}, bf16[2,256,256]{2,1,0:T(8,128)(2,1)S(1)}, u32[]{:S(2)}, u32[]{:S(2)}) collective-permute-start(bf16[2,256,256]{2,1,0:T(8,128)(2,1)S(1)} %collective-permute-done.19), channel_id=1, source_target_pairs={{0,7},{1,0},{2,1},{3,2},{4,3},{5,4},{6,5},{7,6},{8,15},{9,8},{10,9... | collective-permute-start | bytes 786440 | tf_op jit(solution)/shard_map/ppermute | solution.py:127
  180.9 9.4 %collective-permute-start.20 = (bf16[2,256,256]{2,1,0:T(8,128)(2,1)S(1)}, bf16[2,256,256]{2,1,0:T(8,128)(2,1)S(1)}, u32[]{:S(2)}, u32[]{:S(2)}) collective-permute-start(bf16[2,256,256]{2,1,0:T(8,128)(2,1)S(1)} %collective-permute-done.18), channel_id=1, source_target_pairs={{0,1},{1,2},{2,3},{3,4},{4,5},{5,6},{6,7},{7,0},{8,9},{9,10},{10,1... | collective-permute-start | bytes 786440 | tf_op jit(solution)/shard_map/ppermute | solution.py:127
  190.3 7.6 %collective-permute-start.22 = (bf16[2,256,256]{2,1,0:T(8,128)(2,1)S(1)}, bf16[2,256,256]{2,1,0:T(8,128)(2,1)S(1)}, u32[]{:S(2)}, u32[]{:S(2)}) collective-permute-start(bf16[2,256,256]{2,1,0:T(8,128)(2,1)S(1)} %collective-permute-done.20), channel_id=1, source_target_pairs={{0,1},{1,2},{2,3},{3,4},{4,5},{5,6},{6,7},{7,0},{8,9},{9,10},{10,1... | collective-permute-start | bytes 786440 | tf_op jit(solution)/shard_map/ppermute | solution.py:127

commit v2 on v1

v2 whole, which is shorter than its diff:
```python
import jax
import jax.numpy as jnp
from jax import lax
from jax.experimental import pallas as pl
from jax.experimental.pallas import tpu as pltpu
from jax.sharding import PartitionSpec as P


HEAD = 128
WIN1 = 512
WIN2 = 32
BLK = 128
GROUP = 8
LOW = -1e30
LANES = (((1,), (1,)), ((), ()))


def attend_kernel(
    seq_ref, mine_ref, sent_ref, far_ref, near_ref, own_ref, out_ref,
    k2f, v2f, ktile, vtile, kpair, vpair, s_scr, mx_scr, mcb_scr,
):
    tok = mine_ref.shape[0]
    heads = mine_ref.shape[1] // HEAD
    blocks = tok // BLK
    seq = seq_ref[0]
    coef = (HEAD ** -0.5) * 1.4426950408889634
    start = seq == 0

    for t in range(6):
        source = (far_ref, near_ref, own_ref)[t // 2]
        lanes = slice((t % 2) * BLK, (t % 2 + 1) * BLK)
        ktile[t] = source[:HEAD, lanes]
        vtile[t] = source[HEAD:2 * HEAD, lanes].astype(jnp.float32).T.astype(jnp.bfloat16)
    for scr, low in ((k2f, 2 * HEAD), (v2f, 3 * HEAD)):
        scr[:BLK] = near_ref[low:low + HEAD, tok - BLK:].astype(jnp.float32).T
        for t in range(blocks):
            scr[(t + 1) * BLK:(t + 2) * BLK] = own_ref[low:low + HEAD, t * BLK:(t + 1) * BLK].astype(jnp.float32).T

    @pl.when(start)
    def _():
        k2f[:BLK] = jnp.broadcast_to(k2f[BLK:BLK + 1], (BLK, HEAD))
        v2f[:BLK] = jnp.zeros((BLK, HEAD), jnp.float32)

    row = lax.broadcasted_iota(jnp.int32, (BLK, BLK), 0)
    col = lax.broadcasted_iota(jnp.int32, (BLK, BLK), 1)
    early = col > row
    absent = jnp.maximum(WIN1 - seq * tok, 0) // BLK

    def one(combo, _):
        h = combo // blocks
        b = combo % blocks
        base = pl.multiple_of(b * BLK, BLK)
        hcol = pl.multiple_of(h * HEAD, HEAD)
        at = (pl.ds(base, BLK), pl.ds(hcol, HEAD))
        qf = (mine_ref[at] + sent_ref[at]).astype(jnp.bfloat16).astype(jnp.float32)
        for slot, t in enumerate((0, 4, 1, 2, 3)):
            kpair[:, slot * BLK:(slot + 1) * BLK] = ktile[b + t]
            vpair[slot * BLK:(slot + 1) * BLK] = vtile[b + t]
        mx_scr[...] = jnp.full(mx_scr.shape, LOW, jnp.float32)

        def scores(step, _):
            lag0 = step * GROUP
            prods = []
            for g in range(GROUP):
                k2 = k2f[pl.ds(BLK + base - lag0 - g, BLK), :]
                prods.append((qf * k2).astype(jnp.bfloat16))
            prod = jnp.concatenate(prods, axis=0)
            for t in range(3):
                width = 2 * BLK if t < 2 else BLK
                s = jnp.dot(prod, kpair[:, 2 * BLK * t:2 * BLK * t + width], preferred_element_type=jnp.float32)
                s = s.reshape(GROUP, BLK, width)
                if t == 0:
                    parts = [(0, jnp.where(early[None], s[:, :, :BLK], s[:, :, BLK:]))]
                elif t == 1:
                    parts = [(1, s[:, :, :BLK]), (2, s[:, :, BLK:])]
                else:
                    parts = [(3, s)]
                for place, value in parts:
                    s_scr[pl.ds(lag0, GROUP), :, place * BLK:(place + 1) * BLK] = value
                    top = value[0]
                    for g in range(1, GROUP):
                        top = jnp.maximum(top, value[g])
                    mx_scr[place] = jnp.maximum(mx_scr[place], top)
            return 0

        lax.fori_loop(0, WIN2 // GROUP, scores, 0)
        tops = []
        gone = []
        for place in range(4):
            hide = (b + place) < absent
            mask = early if place == 0 else row >= 0
            gone.append(jnp.logical_and(mask, hide))
            tops.append(jnp.where(gone[place], LOW, mx_scr[place]))
        top = jnp.maximum(jnp.maximum(tops[0], tops[1]), jnp.maximum(tops[2], tops[3]))
        peak = jnp.max(top, axis=1, keepdims=True) * coef
        for place in range(4):
            mcb_scr[place] = jnp.where(gone[place], -LOW, jnp.broadcast_to(peak, (BLK, BLK)))

        def raised_at(lag):
            return [
                jnp.exp2(s_scr[lag, :, p * BLK:(p + 1) * BLK] * coef - mcb_scr[p])
                for p in range(4)
            ]

        def mix(lag, carry):
            acc, tot = carry
            raised = raised_at(lag)
            tot = tot + ((raised[0] + raised[1]) + (raised[2] + raised[3]))
            split = [jnp.where(early, raised[0], 0.0), jnp.where(early, 0.0, raised[0])]
            w = jnp.concatenate([part.astype(jnp.bfloat16) for part in split + raised[1:]], axis=1)
            m = jnp.dot(w, vpair[...], preferred_element_type=jnp.float32)
            acc = acc + m * v2f[pl.ds(BLK + base - lag, BLK), :]
            return acc, tot

        zero = jnp.zeros((BLK, HEAD), jnp.float32)
        acc, tot = lax.fori_loop(0, WIN2, mix, (zero, zero), unroll=4)
        last = raised_at(WIN2 - 1)
        spare = jnp.where(jnp.logical_and(start, b == 0), jnp.maximum(WIN2 - 1 - row, 0), 0)
        tot = tot - spare.astype(jnp.float32) * ((last[0] + last[1]) + (last[2] + last[3]))
        total = jnp.sum(tot, axis=1, keepdims=True)
        out_ref[at] = (acc / total).astype(jnp.bfloat16)
        return 0

    lax.fori_loop(0, heads * blocks, one, 0)


def in_vmem(count):
    return [pl.BlockSpec(memory_space=pltpu.VMEM)] * count


def attend(seq, mine, sent, far, near, own):
    tok = mine.shape[0]
    return pl.pallas_call(
        attend_kernel,
        out_shape=jax.ShapeDtypeStruct(mine.shape, jnp.bfloat16),
        in_specs=[pl.BlockSpec(memory_space=pltpu.SMEM)] + in_vmem(5),
        out_specs=in_vmem(1)[0],
        scratch_shapes=[
            pltpu.VMEM((BLK + tok, HEAD), jnp.float32),
            pltpu.VMEM((BLK + tok, HEAD), jnp.float32),
            pltpu.VMEM((6, HEAD, BLK), jnp.bfloat16),
            pltpu.VMEM((6, BLK, HEAD), jnp.bfloat16),
            pltpu.VMEM((HEAD, 5 * BLK), jnp.bfloat16),
            pltpu.VMEM((5 * BLK, HEAD), jnp.bfloat16),
            pltpu.VMEM((WIN2, BLK, 4 * BLK), jnp.float32),
            pltpu.VMEM((4, BLK, BLK), jnp.float32),
            pltpu.VMEM((4, BLK, BLK), jnp.float32),
        ],
        compiler_params=pltpu.CompilerParams(vmem_limit_bytes=24 * 1024 * 1024),
    )(seq, mine, sent, far, near, own)


OFFSETS = (0, -1, 1, -2, 2, -3, 3, -4)


def project_kernel(spot_ref, *refs):
    shards, kv_own, kv_part, own_ref, same_ref, twin_ref = refs[:8], *refs[8:13]
    kv_mine, kv_theirs, mine_out, theirs_out = refs[13:]
    depth = shards[0].shape[1]
    core = spot_ref[1]

    def from_place(offset, count):
        spot = (spot_ref[0] + offset) & (count - 1)
        return pl.ds(pl.multiple_of(spot * depth, depth), depth)

    for weight, out in ((kv_own, kv_mine), (kv_part, kv_theirs)):
        total = None
        for offset, shard in zip(OFFSETS, shards):
            cols = weight[:, from_place(offset, 8)]
            new = lax.dot_general(cols, shard[...], LANES, preferred_element_type=jnp.float32)
            total = new if total is None else total + new
        out[...] = total
    total = None
    for offset, shard in zip(OFFSETS, shards):
        new = jnp.dot(shard[...], own_ref[from_place(offset, 8), :], preferred_element_type=jnp.float32)
        total = new if total is None else total + new
    mine_out[...] = total
    theirs_out[...] = jnp.zeros(theirs_out.shape, jnp.float32)
    for offset, shard in zip(OFFSETS, shards):
        low = from_place(offset, 4)
        upper = ((spot_ref[0] + offset) & 7) >> 2
        for ref, side in ((same_ref, core), (twin_ref, 1 - core)):

            @pl.when(upper == side)
            def _():
                theirs_out[...] += jnp.dot(shard[...], ref[low, :], preferred_element_type=jnp.float32)


def project(spots, arrays, shapes):
    return pl.pallas_call(
        project_kernel,
        out_shape=tuple(jax.ShapeDtypeStruct(shape, jnp.float32) for shape in shapes),
        in_specs=[pl.BlockSpec(memory_space=pltpu.SMEM)] + in_vmem(len(arrays)),
        out_specs=tuple(in_vmem(len(shapes))),
        compiler_params=pltpu.CompilerParams(vmem_limit_bytes=24 * 1024 * 1024),
    )(spots, *arrays)


def swap_rows(value):
    return lax.ppermute(value, "head", [(i, (i + 8) % 16) for i in range(16)])


def along_z(value, step):
    return lax.ppermute(
        value, "head", [(i, (i // 8) * 8 + (i + step) % 8) for i in range(16)]
    )


def along_seq(value, step):
    return lax.ppermute(value, "seq", [(i, i + step) for i in range(16 - step)])


def round_x(value, step):
    return lax.ppermute(value, "seq", [(i, (i + 4 * step) % 16) for i in range(16)])


def other_core(value):
    return lax.ppermute(value, "seq", [(i, i ^ 1) for i in range(16)])


def z_ring(value):
    found = [value]
    up = down = value
    for step in range(1, 5):
        up = along_z(up, 1)
        if step < 4:
            down = along_z(down, -1)
        if step < 4:
            up, down = lax.optimization_barrier((up, down))
            found += [up, down]
        else:
            found.append(up)
    return found


def sent_to_all(value, axis):
    size = lax.axis_size(axis)
    return lax.all_to_all(
        jnp.broadcast_to(value[None], (size, *value.shape)), axis, 0, 0, tiled=True
    )


def owned_piece(w_out, seq):
    x, core = seq >> 2, seq & 1
    rows, width = w_out.shape
    part = rows // 8
    piece = lax.dynamic_slice_in_dim(w_out, (2 * x + core) * part, part, 0)
    return piece.reshape(part, 16, width // 16).transpose(1, 0, 2)


def owned_columns(piece, seq):
    x = seq >> 2
    piece = lax.all_to_all(piece, "head", 0, 0, tiled=True)
    held = jnp.zeros((4, *piece.shape), piece.dtype)
    held = lax.dynamic_update_slice_in_dim(held, piece[None], x, 0)
    for step in (1, 3, 2):
        moved = round_x(piece, step)
        held = lax.dynamic_update_slice_in_dim(held, moved[None], (x - step) & 3, 0)
    return held, other_core(held)


def gather_rows(spot_ref, held, twin, place, out, slot):
    core = spot_ref[1]
    part = held.shape[2]
    for x in range(4):
        for source, side in ((held, core), (twin, 1 - core)):
            low = pl.multiple_of(x * 2 * part + side * part, part)
            out[slot, pl.ds(low, part), :] = source[x, place]


def finish_kernel(spot_ref, *refs):
    near, far, pairs, held, twin = refs[0], refs[1], refs[2:8], refs[8], refs[9]
    part_out, tail_out, w_scr = refs[10:]
    total = None
    values = [(near, far)] + [(pair.at[0], pair.at[1]) for pair in pairs]
    for k, offset in enumerate(OFFSETS):
        spot = (spot_ref[0] + offset) & 7
        for side in range(2):
            place = ((spot_ref[0] & 8) ^ (8 * side)) | spot
            if k == 7:
                gather_rows(spot_ref, held, twin, place, tail_out, side)
                continue
            gather_rows(spot_ref, held, twin, place, w_scr, 2 * k + side)
            new = jnp.dot(values[k][side][...], w_scr[2 * k + side], preferred_element_type=jnp.float32)
            total = new if total is None else total + new
    part_out[...] = total


def close_kernel(part_ref, tail_ref, pair_ref, out_ref):
    total = part_ref[...]
    for side in range(2):
        total = total + jnp.dot(pair_ref[side], tail_ref[side], preferred_element_type=jnp.float32)
    out_ref[...] = total.astype(jnp.bfloat16)


def finish(spots, near, pairs, held, twin):
    tok, feats = near.shape
    cols = held.shape[-1]
    limit = pltpu.CompilerParams(vmem_limit_bytes=24 * 1024 * 1024)
    part, tail = pl.pallas_call(
        finish_kernel,
        out_shape=(
            jax.ShapeDtypeStruct((tok, cols), jnp.float32),
            jax.ShapeDtypeStruct((2, feats, cols), held.dtype),
        ),
        in_specs=[pl.BlockSpec(memory_space=pltpu.SMEM)] + in_vmem(10),
        out_specs=tuple(in_vmem(2)),
        scratch_shapes=[pltpu.VMEM((14, feats, cols), held.dtype)],
        compiler_params=limit,
    )(spots, *near_and(near, pairs), held, twin)
    return pl.pallas_call(
        close_kernel,
        out_shape=jax.ShapeDtypeStruct((tok, cols), jnp.bfloat16),
        in_specs=in_vmem(3),
        out_specs=in_vmem(1)[0],
        compiler_params=limit,
    )(part, tail, pairs[7])


def near_and(near, pairs):
    return (near, pairs[0][1], *pairs[1:7])


def body(tokens, w_query, w_keyval, w_out):
    tok_rows = tokens.shape[0]
    head = lax.axis_index("head").astype(jnp.int32)
    seq = lax.axis_index("seq").astype(jnp.int32)
    row, core = head >> 3, seq & 1
    spots = jnp.stack([head, core])
    half = w_query.shape[0] // 2
    quarter = half // 2
    kv_flat = w_keyval.T
    kv_part = swap_rows(lax.dynamic_slice_in_dim(kv_flat, (1 - row) * half, half, 1))
    q_same = swap_rows(
        lax.dynamic_slice_in_dim(w_query, (1 - row) * half + core * quarter, quarter, 0)
    )
    q_twin = other_core(q_same)
    kv_own = lax.dynamic_slice_in_dim(kv_flat, row * half, half, 1)
    q_own = lax.dynamic_slice_in_dim(w_query, row * half, half, 0)
    shards = z_ring(tokens)
    piece, shards[5], shards[6] = lax.optimization_barrier(
        (owned_piece(w_out, seq), shards[5], shards[6])
    )
    kv_mine, kv_theirs, q_mine, q_theirs = project(
        spots,
        (*shards, kv_own, kv_part, q_own, q_same, q_twin),
        ((kv_flat.shape[0], tok_rows),) * 2 + ((tok_rows, w_query.shape[1]),) * 2,
    )
    kv = (kv_mine + swap_rows(kv_theirs)).astype(jnp.bfloat16)
    q_sent = swap_rows(q_theirs)
    keyval = sent_to_all(kv, "head").reshape(4 * HEAD, tok_rows)
    near = along_seq(keyval, 1)
    far = along_seq(keyval[:2 * HEAD], 2)
    attended = attend(seq.reshape(1), q_mine, q_sent, far, near, keyval)
    held, twin = owned_columns(piece, seq)
    other = swap_rows(attended)
    pairs = z_ring(jnp.concatenate([attended[None], other[None]], axis=0))
    pairs[0] = (attended, other)
    return finish(spots, attended, pairs, held, twin)


def solution(mesh):
    return jax.shard_map(
        body,
        mesh=mesh,
        in_specs=(P("seq", "head"), P(None, "head"), P(None, "head"), P("head", None)),
        out_specs=P("seq", "head"),
        check_vma=False,
    )
```

time: 200 us -> 173 us (0.86)
  matrix products: 38.1 us -> 0 us
  local copies, waits for them, and re-layouts: 8.49 us -> 18.1 us
  Pallas kernels: 21.1 us -> 29.8 us
  waiting for transfers between devices: 75.1 us -> 67.3 us
  starting transfers between devices: 51.5 us -> 55.6 us
  other arithmetic: 4.07 us -> 0.11 us
    dot_general x48 -> x0, matrix products: 38.1 us -> none  [dot(): return jnp.dot(a, b, preferred_element_type=jnp.float32)]
    ppermute x14, waiting for transfers between devices: 52.1 us -> 36.4 us  [along_z(): lax.ppermute(value, 'head', [(i, i // 8 * 8 + (i + step) % 8) for i in ra...]
    ppermute x2 -> x5, waiting for transfers between devices: 4.33 us -> 14 us  [swap_rows(): return lax.ppermute(value, 'head', [(i, (i + 8) % 16) for i in range(16)])]
    pallas_call x1 -> x4, Pallas kernels: 21.1 us -> 29.8 us  [the longest x1 20.7 us: attend(): pl.pallas_call(attend_kernel, out_shape=jax.ShapeDtypeStruct(mine.shape,...]
    ppermute x2 -> x5, starting transfers between devices: 2.31 us -> 8.08 us  [swap_rows(): return lax.ppermute(value, 'head', [(i, (i + 8) % 16) for i in range(16)])]
    dynamic_slice x1 -> x4, local copies, waits for them, and re-layouts: 1.08 us -> 6.49 us  [the longest x1 3.06 us: body(): q_own = lax.dynamic_slice_in_dim(w_query, row * half, half, 0)]
    ppermute x3, waiting for transfers between devices: 8.28 us -> 3.43 us  [round_x(): lax.ppermute(value, 'seq', [(i, (i + 4 * step) % 16) for i in range(16)])]
    ppermute x14, starting transfers between devices: 19.4 us -> 24.1 us  [along_z(): lax.ppermute(value, 'head', [(i, i // 8 * 8 + (i + step) % 8) for i in ra...]
  transfers between devices with their start and end apart: 25 -> 28, of which waited for: 12 -> 16; matrix products, arithmetic and copies ran while one was open for 25% -> 7% of each run, Pallas kernels for 11% -> 17%
where the time goes in v2:
time: 173 us; the launch traced here: 171 us
  waiting for transfers between devices  67.3 us (39%)
  starting transfers between devices  55.6 us (32%)
  Pallas kernels  29.8 us (17%)
  local copies, waits for them, and re-layouts  18.1 us (10%)
    ppermute x14, waiting for transfers between devices, along_z(): lax.ppermute(value, 'head', [(i, i // 8 * 8 + (i + step) % 8) for i in ra...  36.4 us
    ppermute x14, starting transfers between devices, along_z(): lax.ppermute(value, 'head', [(i, i // 8 * 8 + (i + step) % 8) for i in ra...  24.1 us
    pallas_call x1, Pallas kernels, attend(): pl.pallas_call(attend_kernel, out_shape=jax.ShapeDtypeStruct(mine.shape,...  20.7 us
    ppermute x5, waiting for transfers between devices, swap_rows(): return lax.ppermute(value, 'head', [(i, (i + 8) % 16) for i in range(16)])  14 us
    all_to_all x1, waiting for transfers between devices, sent_to_all(): lax.all_to_all(jnp.broadcast_to(value[None], (size, *value.shape)), axis,...  8.73 us
    ppermute x5, starting transfers between devices, swap_rows(): return lax.ppermute(value, 'head', [(i, (i + 8) % 16) for i in range(16)])  8.08 us
    ppermute x2, starting transfers between devices, along_seq(): return lax.ppermute(value, 'seq', [(i, i + step) for i in range(16 - step)])  6.72 us
    all_to_all x1, starting transfers between devices, owned_columns(): piece = lax.all_to_all(piece, 'head', 0, 0, tiled=True)  6.48 us
  transfers between devices with their start and end apart: 28, of which 16 were waited for; matrix products, arithmetic and copies ran while one was open for 7% of the time, Pallas kernels for 17%

profile of v2, /device:TPU:2, one launch (start us, length us, event | category | flops | bytes accessed | tf_op | source)
XLA Modules:
  0.0 171.2 jit_solution(2508216192474764232)
XLA Ops:
  0.0 1.9 %collective-permute-start = (bf16[256,512]{1,0:T(8,128)(2,1)}, bf16[256,512]{1,0:T(8,128)(2,1)S(1)}, u32[]{:S(2)}, u32[]{:S(2)}) collective-permute-start(bf16[256,512]{1,0:T(8,128)(2,1)} %refs_0_.1), channel_id=1, source_target_pairs={{0,1},{1,2},{2,3},{3,4},{4,5},{5,6},{6,7},{7,0},{8,9},{9,10},{10,1... | collective-permute-start | bytes 786440 | tf_op jit(solution)/shard_map/ppermute | solution.py:204
  1.9 3.9 %collective-permute-start.1 = (bf16[256,512]{1,0:T(8,128)(2,1)}, bf16[256,512]{1,0:T(8,128)(2,1)S(1)}, u32[]{:S(2)}, u32[]{:S(2)}) collective-permute-start(bf16[256,512]{1,0:T(8,128)(2,1)} %refs_0_.1), channel_id=1, source_target_pairs={{0,7},{1,0},{2,1},{3,2},{4,3},{5,4},{6,5},{7,6},{8,15},{9,8},{10,9... | collective-permute-start | bytes 786440 | tf_op jit(solution)/shard_map/ppermute | solution.py:204
  5.9 6.5 %collective-permute-done.refs_1_ = bf16[256,512]{1,0:T(8,128)(2,1)S(1)} collective-permute-done((bf16[256,512]{1,0:T(8,128)(2,1)}, bf16[256,512]{1,0:T(8,128)(2,1)S(1)}, u32[]{:S(2)}, u32[]{:S(2)}) %collective-permute-start) | collective-permute-done | bytes 262176 | tf_op jit(solution)/shard_map/ppermute | solution.py:204
  12.4 0.1 collective-permute-start.2
  12.5 3.2 %collective-permute-start.3 = (bf16[256,512]{1,0:T(8,128)(2,1)S(1)}, bf16[256,512]{1,0:T(8,128)(2,1)S(1)}, u32[]{:S(2)}, u32[]{:S(2)}) collective-permute-start(bf16[256,512]{1,0:T(8,128)(2,1)S(1)} %collective-permute-done.1.refs_2_), channel_id=1, source_target_pairs={{0,7},{1,0},{2,1},{3,2},{4,3},{5,4},{6,5},{7,6},{8,15},{9,8},{10,9... | collective-permute-start | bytes 786440 | tf_op jit(solution)/shard_map/ppermute | solution.py:204
  15.7 1.3 constant_dynamic-slice_fusion
  17.0 1.7 collective-permute-start.8
  18.6 2.5 %collective-permute-done.2.refs_3_ = bf16[256,512]{1,0:T(8,128)(2,1)S(1)} collective-permute-done((bf16[256,512]{1,0:T(8,128)(2,1)S(1)}, bf16[256,512]{1,0:T(8,128)(2,1)S(1)}, u32[]{:S(2)}, u32[]{:S(2)}) %collective-permute-start.2) | collective-permute-done | bytes 262176 | tf_op jit(solution)/shard_map/ppermute | solution.py:204
  21.1 1.8 %collective-permute-start.4 = (bf16[256,512]{1,0:T(8,128)(2,1)S(1)}, bf16[256,512]{1,0:T(8,128)(2,1)}, u32[]{:S(2)}, u32[]{:S(2)}) collective-permute-start(bf16[256,512]{1,0:T(8,128)(2,1)S(1)} %collective-permute-done.2.refs_3_), channel_id=1, source_target_pairs={{0,1},{1,2},{2,3},{3,4},{4,5},{5,6},{6,7},{7,0},{8,9},{9,10},{10,1... | collective-permute-start | bytes 786440 | tf_op jit(solution)/shard_map/ppermute | solution.py:204
  23.0 1.5 collective-permute-start.5
  24.5 1.1 constant_dynamic-slice_fusion.2
  25.5 0.9 copy.8
  26.4 2.7 %collective-permute-done.4.refs_5_ = bf16[256,512]{1,0:T(8,128)(2,1)} collective-permute-done((bf16[256,512]{1,0:T(8,128)(2,1)S(1)}, bf16[256,512]{1,0:T(8,128)(2,1)}, u32[]{:S(2)}, u32[]{:S(2)}) %collective-permute-start.4) | collective-permute-done | bytes 262176 | tf_op jit(solution)/shard_map/ppermute | solution.py:204
  29.1 0.2 collective-permute-done.5.refs_6_
  29.3 6.5 %all-to-all-start.1 = ((bf16[16,32,512]{2,1,0:T(8,128)(2,1)}), bf16[16,32,512]{2,1,0:T(8,128)(2,1)}, u32[]{:S(2)}, u32[]{:S(2)}) async-start(bf16[16,32,512]{2,1,0:T(8,128)(2,1)} %bitcast.25), calls=%async_computation.1 | async-start | bytes 1048576 | tf_op jit(solution)/shard_map/all_to_all | solution.py:253
  35.8 9.1 %collective-permute-done.8.refs_11_ = bf16[2048,256]{1,0:T(8,128)(2,1)S(1)} collective-permute-done((bf16[2048,256]{1,0:T(8,128)(2,1)S(1)}, bf16[2048,256]{1,0:T(8,128)(2,1)S(1)}, u32[]{:S(2)}, u32[]{:S(2)}) %collective-permute-start.8) | collective-permute-done | bytes 1048608 | tf_op jit(solution)/shard_map/ppermute | solution.py:200
  44.9 1.1 dynamic-slice_bitcast_fusion
  46.0 2.5 %collective-permute-start.7 = (bf16[32,4096]{1,0:T(8,128)(2,1)S(1)}, bf16[32,4096]{1,0:T(8,128)(2,1)S(1)}, u32[]{:S(2)}, u32[]{:S(2)}) collective-permute-start(bf16[32,4096]{1,0:T(8,128)(2,1)S(1)} %get-tuple-element.47), channel_id=1, source_target_pairs={{0,8},{1,9},{2,10},{3,11},{4,12},{5,13},{6,14},{7,15},{8,0},{9,1},... | collective-permute-start | bytes 786440 | tf_op jit(solution)/shard_map/ppermute | solution.py:200
  48.5 1.5 collective-permute-start.21
  50.0 3.1 %constant_dynamic-slice_fusion.1.refs_10_ = bf16[4096,256]{1,0:T(8,128)(2,1)} fusion(bf16[8192,256]{1,0:T(8,128)(2,1)} %param.5, s32[]{:T(128)S(6)} %select_n.26), kind=kLoop, calls=%fused_computation.10 | loop fusion | bytes 4194308 | tf_op jit(solution)/shard_map/dynamic_slice | solution.py:339
  53.1 1.3 collective-permute-start.6
  54.3 0.5 collective-permute-start.22
  54.9 0.5 collective-permute-done.7.refs_9_
  55.5 0.7 copy-done.12
  56.2 2.1 %collective-permute-start.23 = (bf16[16,32,512]{2,1,0:T(8,128)(2,1)}, bf16[16,32,512]{2,1,0:T(8,128)(2,1)S(1)}, u32[]{:S(2)}, u32[]{:S(2)}) collective-permute-start(bf16[16,32,512]{2,1,0:T(8,128)(2,1)} %all-to-all-done.1), channel_id=1, source_target_pairs={{0,128},{16,144},{32,160},{48,176},{64,192},{80,208},{96,224},{112... | collective-permute-start | bytes 1572872 | tf_op jit(solution)/shard_map/ppermute | solution.py:214
  58.3 0.2 broadcast_in_dim.30
  58.6 1.1 bitcast_dynamic-update-slice_fusion.3
  59.7 3.1 %collective-permute-done.6.refs_7_ = bf16[256,512]{1,0:T(8,128)(2,1)} collective-permute-done((bf16[256,512]{1,0:T(8,128)(2,1)}, bf16[256,512]{1,0:T(8,128)(2,1)}, u32[]{:S(2)}, u32[]{:S(2)}) %collective-permute-start.6) | collective-permute-done | bytes 262176 | tf_op jit(solution)/shard_map/ppermute | solution.py:204
  62.8 0.9 copy-done.1
  63.7 0.9 copy-done.3
  64.7 0.9 copy-done.5
  65.6 0.9 copy-done.7
  66.6 0.9 copy-done.9
  67.5 5.3 %shard_map.46 = (f32[32,256]{1,0:T(8,128)S(1)}, f32[32,256]{1,0:T(8,128)S(1)}, f32[256,256]{1,0:T(8,128)S(1)}, f32[256,256]{1,0:T(8,128)S(1)}) custom-call(s32[2]{0:T(128)S(1)} %pad_add_fusion.spot_ref, bf16[256,512]{1,0:T(8,128)(2,1)S(1)} %copy-done.1, bf16[256,512]{1,0:T(8,128)(2,1)S(1)} %copy-done.3, bf16[256,512]{1,0:T(8,128)(2,1)S(1)} %copy-done.5, ...), custom_call_target="tpu_custom_call" | custom-call | tf_op jit(solution)/shard_map/pallas_call | solution.py:190
  72.8 0.5 collective-permute-start.11
  73.3 1.1 bitcast_dynamic-update-slice_fusion.2
  74.4 1.1 bitcast_dynamic-update-slice_fusion.1
  75.5 3.4 %collective-permute-done.23 = bf16[16,32,512]{2,1,0:T(8,128)(2,1)S(1)} collective-permute-done((bf16[16,32,512]{2,1,0:T(8,128)(2,1)}, bf16[16,32,512]{2,1,0:T(8,128)(2,1)S(1)}, u32[]{:S(2)}, u32[]{:S(2)}) %collective-permute-start.23) | collective-permute-done | bytes 524320 | tf_op jit(solution)/shard_map/ppermute | solution.py:214
  79.0 0.1 collective-permute-start.24
  79.1 0.7 broadcast_in_dim.27
  79.8 6.0 %all-to-all-start = ((bf16[16,32,256]{2,1,0:T(8,128)(2,1)}), bf16[16,32,256]{2,1,0:T(8,128)(2,1)S(1)}, u32[]{:S(2)}, u32[]{:S(2)}) async-start(bf16[16,32,256]{2,1,0:T(8,128)(2,1)} %broadcast_in_dim.27), calls=%async_computation | async-start | bytes 524288 | tf_op jit(solution)/shard_map/all_to_all | solution.py:238
  85.9 1.9 %collective-permute-start.10 = (f32[256,256]{1,0:T(8,128)}, f32[256,256]{1,0:T(8,128)S(1)}, u32[]{:S(2)}, u32[]{:S(2)}) collective-permute-start(f32[256,256]{1,0:T(8,128)} %copy-done.16), channel_id=1, source_target_pairs={{0,8},{1,9},{2,10},{3,11},{4,12},{5,13},{6,14},{7,15},{8,0},{9,1},... | collective-permute-start | bytes 786440 | tf_op jit(solution)/shard_map/ppermute | solution.py:200
  87.8 8.7 %all-to-all-done = bf16[16,32,256]{2,1,0:T(8,128)(2,1)S(1)} async-done(((bf16[16,32,256]{2,1,0:T(8,128)(2,1)}), bf16[16,32,256]{2,1,0:T(8,128)(2,1)S(1)}, u32[]{:S(2)}, u32[]{:S(2)}) %all-to-all-start) | async-done | bytes 262176 | tf_op jit(solution)/shard_map/all_to_all | solution.py:238
  96.5 1.9 %collective-permute-start.13 = (bf16[512,256]{1,0:T(8,128)(2,1)S(1)}, bf16[512,256]{1,0:T(8,128)(2,1)S(1)}, u32[]{:S(2)}, u32[]{:S(2)}) collective-permute-start(bf16[512,256]{1,0:T(8,128)(2,1)S(1)} %bitcast.26), channel_id=1, source_target_pairs={{0,16},{16,32},{32,48},{48,64},{64,80},{80,96},{96,112},{112,128},... | collective-permute-start | bytes 786440 | tf_op jit(solution)/shard_map/ppermute | solution.py:210
  98.5 4.8 %collective-permute-start.12 = (bf16[256,256]{1,0:T(8,128)(2,1)S(1)}, bf16[256,256]{1,0:T(8,128)(2,1)S(1)}, u32[]{:S(2)}, u32[]{:S(2)}) collective-permute-start(bf16[256,256]{1,0:T(8,128)(2,1)S(1)} %bitcast.31), channel_id=1, source_target_pairs={{0,32},{16,48},{32,64},{48,80},{64,96},{80,112},{96,128},{112,144}... | collective-permute-start | bytes 393224 | tf_op jit(solution)/shard_map/ppermute | solution.py:210
  103.3 4.7 %collective-permute-done.12.far_ref = bf16[256,256]{1,0:T(8,128)(2,1)S(1)} collective-permute-done((bf16[256,256]{1,0:T(8,128)(2,1)S(1)}, bf16[256,256]{1,0:T(8,128)(2,1)S(1)}, u32[]{:S(2)}, u32[]{:S(2)}) %collective-permute-start.12) | collective-permute-done | bytes 131104 | tf_op jit(solution)/shard_map/ppermute | solution.py:210
  108.0 0.9 copy-done.15
  109.0 20.7 %shard_map.47.refs_0_ = bf16[256,256]{1,0:T(8,128)(2,1)S(1)} custom-call(s32[1]{0:T(128)} %bitcast.2.seq_ref, f32[256,256]{1,0:T(8,128)S(1)} %copy-done.15, f32[256,256]{1,0:T(8,128)S(1)} %collective-permute-done.10.sent_ref, bf16[256,256]{1,0:T(8,128)(2,1)S(1)} %collective-permute-done.12.far_ref, bf16[512,256]{1,0:T(8,128)(2,1)S(1)} %collective-permute-done.13.near_ref, ...), custom_call_target="tpu_custom_call" | custom-call | tf_op jit(solution)/shard_map/pallas_call | solution.py:133
  129.7 1.5 collective-permute-start.14
  131.2 4.4 %collective-permute-done.14.refs_1_ = bf16[256,256]{1,0:T(8,128)(2,1)S(1)} collective-permute-done((bf16[256,256]{1,0:T(8,128)(2,1)S(1)}, bf16[256,256]{1,0:T(8,128)(2,1)S(1)}, u32[]{:S(2)}, u32[]{:S(2)}) %collective-permute-start.14) | collective-permute-done | bytes 131104 | tf_op jit(solution)/shard_map/ppermute | solution.py:200
  135.6 2.1 %collective-permute-start.15 = (bf16[2,256,256]{2,1,0:T(8,128)(2,1)S(1)}, bf16[2,256,256]{2,1,0:T(8,128)(2,1)S(1)}, u32[]{:S(2)}, u32[]{:S(2)}) collective-permute-start(bf16[2,256,256]{2,1,0:T(8,128)(2,1)S(1)} %pad_maximum_fusion), channel_id=1, source_target_pairs={{0,1},{1,2},{2,3},{3,4},{4,5},{5,6},{6,7},{7,0},{8,9},{9,10},{10,1... | collective-permute-start | bytes 786440 | tf_op jit(solution)/shard_map/ppermute | solution.py:204
  137.7 1.2 collective-permute-start.16
  138.9 6.7 %collective-permute-done.15.refs_2_ = bf16[2,256,256]{2,1,0:T(8,128)(2,1)S(1)} collective-permute-done((bf16[2,256,256]{2,1,0:T(8,128)(2,1)S(1)}, bf16[2,256,256]{2,1,0:T(8,128)(2,1)S(1)}, u32[]{:S(2)}, u32[]{:S(2)}) %collective-permute-start.15) | collective-permute-done | bytes 262176 | tf_op jit(solution)/shard_map/ppermute | solution.py:204
  145.6 0.4 collective-permute-done.16.refs_3_
  146.0 0.6 collective-permute-start.17
  146.6 2.7 %collective-permute-start.18 = (bf16[2,256,256]{2,1,0:T(8,128)(2,1)S(1)}, bf16[2,256,256]{2,1,0:T(8,128)(2,1)S(1)}, u32[]{:S(2)}, u32[]{:S(2)}) collective-permute-start(bf16[2,256,256]{2,1,0:T(8,128)(2,1)S(1)} %collective-permute-done.16.refs_3_), channel_id=1, source_target_pairs={{0,7},{1,0},{2,1},{3,2},{4,3},{5,4},{6,5},{7,6},{8,15},{9,8},{10,9... | collective-permute-start | bytes 786440 | tf_op jit(solution)/shard_map/ppermute | solution.py:204
  149.3 5.5 %collective-permute-done.17.refs_4_ = bf16[2,256,256]{2,1,0:T(8,128)(2,1)S(1)} collective-permute-done((bf16[2,256,256]{2,1,0:T(8,128)(2,1)S(1)}, bf16[2,256,256]{2,1,0:T(8,128)(2,1)S(1)}, u32[]{:S(2)}, u32[]{:S(2)}) %collective-permute-start.17) | collective-permute-done | bytes 262176 | tf_op jit(solution)/shard_map/ppermute | solution.py:204
  154.7 0.3 collective-permute-start.19
  155.0 2.9 %collective-permute-start.20 = (bf16[2,256,256]{2,1,0:T(8,128)(2,1)S(1)}, bf16[2,256,256]{2,1,0:T(8,128)(2,1)S(1)}, u32[]{:S(2)}, u32[]{:S(2)}) collective-permute-start(bf16[2,256,256]{2,1,0:T(8,128)(2,1)S(1)} %collective-permute-done.18.refs_5_), channel_id=1, source_target_pairs={{0,7},{1,0},{2,1},{3,2},{4,3},{5,4},{6,5},{7,6},{8,15},{9,8},{10,9... | collective-permute-start | bytes 786440 | tf_op jit(solution)/shard_map/ppermute | solution.py:204
  158.0 4.6 %collective-permute-done.19.refs_6_ = bf16[2,256,256]{2,1,0:T(8,128)(2,1)S(1)} collective-permute-done((bf16[2,256,256]{2,1,0:T(8,128)(2,1)S(1)}, bf16[2,256,256]{2,1,0:T(8,128)(2,1)S(1)}, u32[]{:S(2)}, u32[]{:S(2)}) %collective-permute-start.19) | collective-permute-done | bytes 262176 | tf_op jit(solution)/shard_map/ppermute | solution.py:204
  162.6 0.6 collective-permute-start.25
  163.2 2.8 %shard_map.48 = (f32[256,512]{1,0:T(8,128)S(1)}, bf16[2,256,512]{2,1,0:T(8,128)(2,1)S(1)}) custom-call(s32[2]{0:T(128)S(1)} %pad_add_fusion.spot_ref, bf16[256,256]{1,0:T(8,128)(2,1)S(1)} %shard_map.47.refs_0_, bf16[256,256]{1,0:T(8,128)(2,1)S(1)} %collective-permute-done.14.refs_1_, bf16[2,256,256]{2,1,0:T(8,128)(2,1)S(1)} %collective-permute-done.15.refs_2_, ...), custom_call_target="tpu_custom_call" | custom-call | tf_op jit(solution)/shard_map/pallas_call | solution.py:300
  165.9 4.2 %collective-permute-done.25.pair_ref = bf16[2,256,256]{2,1,0:T(8,128)(2,1)S(1)} collective-permute-done((bf16[2,256,256]{2,1,0:T(8,128)(2,1)S(1)}, bf16[2,256,256]{2,1,0:T(8,128)(2,1)S(1)}, u32[]{:S(2)}, u32[]{:S(2)}) %collective-permute-start.25) | collective-permute-done | bytes 262176 | tf_op jit(solution)/shard_map/ppermute | solution.py:204
  170.2 1.0 shard_map.49
  (45 shorter events, 0.3 us)
Async XLA Ops:
  0.0 12.4 %collective-permute-start = (bf16[256,512]{1,0:T(8,128)(2,1)}, bf16[256,512]{1,0:T(8,128)(2,1)S(1)}, u32[]{:S(2)}, u32[]{:S(2)}) collective-permute-start(bf16[256,512]{1,0:T(8,128)(2,1)} %refs_0_.1), channel_id=1, source_target_pairs={{0,1},{1,2},{2,3},{3,4},{4,5},{5,6},{6,7},{7,0},{8,9},{9,10},{10,1... | collective-permute-start | bytes 786440 | tf_op jit(solution)/shard_map/ppermute | solution.py:204
  1.9 10.5 %collective-permute-start.1 = (bf16[256,512]{1,0:T(8,128)(2,1)}, bf16[256,512]{1,0:T(8,128)(2,1)S(1)}, u32[]{:S(2)}, u32[]{:S(2)}) collective-permute-start(bf16[256,512]{1,0:T(8,128)(2,1)} %refs_0_.1), channel_id=1, source_target_pairs={{0,7},{1,0},{2,1},{3,2},{4,3},{5,4},{6,5},{7,6},{8,15},{9,8},{10,9... | collective-permute-start | bytes 786440 | tf_op jit(solution)/shard_map/ppermute | solution.py:204
  12.4 14.0 %copy-start.2 = (bf16[256,512]{1,0:T(8,128)(2,1)}, bf16[256,512]{1,0:T(8,128)(2,1)S(1)}, u32[]{:S(2)}) copy-start(bf16[256,512]{1,0:T(8,128)(2,1)S(1)} %collective-permute-done.refs_1_) | copy-start | bytes 786436
  12.4 14.0 %copy-start.4 = (bf16[256,512]{1,0:T(8,128)(2,1)}, bf16[256,512]{1,0:T(8,128)(2,1)S(1)}, u32[]{:S(2)}) copy-start(bf16[256,512]{1,0:T(8,128)(2,1)S(1)} %collective-permute-done.1.refs_2_) | copy-start | bytes 786436
  12.4 8.8 %collective-permute-start.2 = (bf16[256,512]{1,0:T(8,128)(2,1)S(1)}, bf16[256,512]{1,0:T(8,128)(2,1)S(1)}, u32[]{:S(2)}, u32[]{:S(2)}) collective-permute-start(bf16[256,512]{1,0:T(8,128)(2,1)S(1)} %collective-permute-done.refs_1_), channel_id=1, source_target_pairs={{0,1},{1,2},{2,3},{3,4},{4,5},{5,6},{6,7},{7,0},{8,9},{9,10},{10,1... | collective-permute-start | bytes 786440 | tf_op jit(solution)/shard_map/ppermute | solution.py:204
  12.5 8.7 %collective-permute-start.3 = (bf16[256,512]{1,0:T(8,128)(2,1)S(1)}, bf16[256,512]{1,0:T(8,128)(2,1)S(1)}, u32[]{:S(2)}, u32[]{:S(2)}) collective-permute-start(bf16[256,512]{1,0:T(8,128)(2,1)S(1)} %collective-permute-done.1.refs_2_), channel_id=1, source_target_pairs={{0,7},{1,0},{2,1},{3,2},{4,3},{5,4},{6,5},{7,6},{8,15},{9,8},{10,9... | collective-permute-start | bytes 786440 | tf_op jit(solution)/shard_map/ppermute | solution.py:204
  17.0 27.9 %collective-permute-start.8 = (bf16[2048,256]{1,0:T(8,128)(2,1)S(1)}, bf16[2048,256]{1,0:T(8,128)(2,1)S(1)}, u32[]{:S(2)}, u32[]{:S(2)}) collective-permute-start(bf16[2048,256]{1,0:T(8,128)(2,1)S(1)} %constant_dynamic-slice_fusion), channel_id=1, source_target_pairs={{0,8},{1,9},{2,10},{3,11},{4,12},{5,13},{6,14},{7,15},{8,0},{9,1},... | collective-permute-start | bytes 3145736 | tf_op jit(solution)/shard_map/ppermute | solution.py:200
  21.1 24.8 %copy-start.6 = (bf16[256,512]{1,0:T(8,128)(2,1)}, bf16[256,512]{1,0:T(8,128)(2,1)S(1)}, u32[]{:S(2)}) copy-start(bf16[256,512]{1,0:T(8,128)(2,1)S(1)} %collective-permute-done.2.refs_3_) | copy-start | bytes 786436
  21.1 24.8 %copy-start.8 = (bf16[256,512]{1,0:T(8,128)(2,1)}, bf16[256,512]{1,0:T(8,128)(2,1)S(1)}, u32[]{:S(2)}) copy-start(bf16[256,512]{1,0:T(8,128)(2,1)S(1)} %collective-permute-done.3.refs_4_) | copy-start | bytes 786436
  21.1 8.0 %collective-permute-start.4 = (bf16[256,512]{1,0:T(8,128)(2,1)S(1)}, bf16[256,512]{1,0:T(8,128)(2,1)}, u32[]{:S(2)}, u32[]{:S(2)}) collective-permute-start(bf16[256,512]{1,0:T(8,128)(2,1)S(1)} %collective-permute-done.2.refs_3_), channel_id=1, source_target_pairs={{0,1},{1,2},{2,3},{3,4},{4,5},{5,6},{6,7},{7,0},{8,9},{9,10},{10,1... | collective-permute-start | bytes 786440 | tf_op jit(solution)/shard_map/ppermute | solution.py:204
  23.0 6.4 %collective-permute-start.5 = (bf16[256,512]{1,0:T(8,128)(2,1)S(1)}, bf16[256,512]{1,0:T(8,128)(2,1)S(1)}, u32[]{:S(2)}, u32[]{:S(2)}) collective-permute-start(bf16[256,512]{1,0:T(8,128)(2,1)S(1)} %collective-permute-done.3.refs_4_), channel_id=1, source_target_pairs={{0,7},{1,0},{2,1},{3,2},{4,3},{5,4},{6,5},{7,6},{8,15},{9,8},{10,9... | collective-permute-start | bytes 786440 | tf_op jit(solution)/shard_map/ppermute | solution.py:204
  29.3 23.7 %copy-start.10 = (bf16[256,512]{1,0:T(8,128)(2,1)}, bf16[256,512]{1,0:T(8,128)(2,1)S(1)}, u32[]{:S(2)}) copy-start(bf16[256,512]{1,0:T(8,128)(2,1)S(1)} %collective-permute-done.5.refs_6_) | copy-start | bytes 786436
  29.3 19.2 %all-to-all-start.1 = ((bf16[16,32,512]{2,1,0:T(8,128)(2,1)}), bf16[16,32,512]{2,1,0:T(8,128)(2,1)}, u32[]{:S(2)}, u32[]{:S(2)}) async-start(bf16[16,32,512]{2,1,0:T(8,128)(2,1)} %bitcast.25), calls=%async_computation.1 | async-start | bytes 1048576 | tf_op jit(solution)/shard_map/all_to_all | solution.py:253
  44.9 17.9 %collective-permute-start.9 = (bf16[2048,256]{1,0:T(8,128)(2,1)S(1)}, bf16[2048,256]{1,0:T(8,128)(2,1)}, u32[]{:S(2)}, u32[]{:S(2)}) collective-permute-start(bf16[2048,256]{1,0:T(8,128)(2,1)S(1)} %collective-permute-done.8.refs_11_), channel_id=1, source_target_pairs={{0,16},{16,0},{32,48},{48,32},{64,80},{80,64},{96,112},{112,96},{1... | collective-permute-start | bytes 3145736 | tf_op jit(solution)/shard_map/ppermute | solution.py:218
  46.0 9.5 %collective-permute-start.7 = (bf16[32,4096]{1,0:T(8,128)(2,1)S(1)}, bf16[32,4096]{1,0:T(8,128)(2,1)S(1)}, u32[]{:S(2)}, u32[]{:S(2)}) collective-permute-start(bf16[32,4096]{1,0:T(8,128)(2,1)S(1)} %get-tuple-element.47), channel_id=1, source_target_pairs={{0,8},{1,9},{2,10},{3,11},{4,12},{5,13},{6,14},{7,15},{8,0},{9,1},... | collective-permute-start | bytes 786440 | tf_op jit(solution)/shard_map/ppermute | solution.py:200
  48.5 24.8 %collective-permute-start.21 = (bf16[16,32,512]{2,1,0:T(8,128)(2,1)}, bf16[16,32,512]{2,1,0:T(8,128)(2,1)}, u32[]{:S(2)}, u32[]{:S(2)}) collective-permute-start(bf16[16,32,512]{2,1,0:T(8,128)(2,1)} %all-to-all-done.1), channel_id=1, source_target_pairs={{0,64},{16,80},{32,96},{48,112},{64,128},{80,144},{96,160},{112,17... | collective-permute-start | bytes 1572872 | tf_op jit(solution)/shard_map/ppermute | solution.py:214
  53.1 9.7 %collective-permute-start.6 = (bf16[256,512]{1,0:T(8,128)(2,1)}, bf16[256,512]{1,0:T(8,128)(2,1)}, u32[]{:S(2)}, u32[]{:S(2)}) collective-permute-start(bf16[256,512]{1,0:T(8,128)(2,1)} %collective-permute-done.4.refs_5_), channel_id=1, source_target_pairs={{0,1},{1,2},{2,3},{3,4},{4,5},{5,6},{6,7},{7,0},{8,9},{9,10},{10,1... | collective-permute-start | bytes 786440 | tf_op jit(solution)/shard_map/ppermute | solution.py:204
  54.3 20.1 %collective-permute-start.22 = (bf16[16,32,512]{2,1,0:T(8,128)(2,1)}, bf16[16,32,512]{2,1,0:T(8,128)(2,1)}, u32[]{:S(2)}, u32[]{:S(2)}) collective-permute-start(bf16[16,32,512]{2,1,0:T(8,128)(2,1)} %all-to-all-done.1), channel_id=1, source_target_pairs={{0,192},{16,208},{32,224},{48,240},{64,0},{80,16},{96,32},{112,48}... | collective-permute-start | bytes 1572872 | tf_op jit(solution)/shard_map/ppermute | solution.py:214
  54.9 7.8 %copy-start = (bf16[4096,256]{1,0:T(8,128)(2,1)S(1)}, bf16[4096,256]{1,0:T(8,128)(2,1)}, u32[]{:S(2)}) copy-start(bf16[4096,256]{1,0:T(8,128)(2,1)} %constant_dynamic-slice_fusion.1.refs_10_) | copy-start | bytes 6291460
  54.9 7.8 %copy-start.11 = (bf16[256,512]{1,0:T(8,128)(2,1)S(1)}, bf16[256,512]{1,0:T(8,128)(2,1)}, u32[]{:S(2)}) copy-start(bf16[256,512]{1,0:T(8,128)(2,1)} %copy-done.10) | copy-start | bytes 786436
  55.5 0.7 copy-start.12
  56.2 22.7 %collective-permute-start.23 = (bf16[16,32,512]{2,1,0:T(8,128)(2,1)}, bf16[16,32,512]{2,1,0:T(8,128)(2,1)S(1)}, u32[]{:S(2)}, u32[]{:S(2)}) collective-permute-start(bf16[16,32,512]{2,1,0:T(8,128)(2,1)} %all-to-all-done.1), channel_id=1, source_target_pairs={{0,128},{16,144},{32,160},{48,176},{64,192},{80,208},{96,224},{112... | collective-permute-start | bytes 1572872 | tf_op jit(solution)/shard_map/ppermute | solution.py:214
  58.3 4.4 %copy-start.13 = (bf16[32,4096]{1,0:T(8,128)(2,1)S(1)}, bf16[32,4096]{1,0:T(8,128)(2,1)}, u32[]{:S(2)}) copy-start(bf16[32,4096]{1,0:T(8,128)(2,1)} %copy-done.12) | copy-start | bytes 786436
  62.8 1.0 copy-start.1
  63.7 0.9 copy-start.3
  64.7 0.9 copy-start.5
  65.6 0.9 copy-start.7
  66.6 0.9 copy-start.9
  72.8 6.2 %copy-start.14 = (f32[256,256]{1,0:T(8,128)}, f32[256,256]{1,0:T(8,128)S(1)}, u32[]{:S(2)}) copy-start(f32[256,256]{1,0:T(8,128)S(1)} %get-tuple-element.34.mine_ref) | copy-start | bytes 786436
  72.8 6.3 %copy-start.16 = (f32[256,256]{1,0:T(8,128)}, f32[256,256]{1,0:T(8,128)S(1)}, u32[]{:S(2)}) copy-start(f32[256,256]{1,0:T(8,128)S(1)} %get-tuple-element.35) | copy-start | bytes 786436
  72.8 6.2 %collective-permute-start.11 = (f32[32,256]{1,0:T(8,128)S(1)}, f32[32,256]{1,0:T(8,128)S(1)}, u32[]{:S(2)}, u32[]{:S(2)}) collective-permute-start(f32[32,256]{1,0:T(8,128)S(1)} %get-tuple-element.37), channel_id=1, source_target_pairs={{0,8},{1,9},{2,10},{3,11},{4,12},{5,13},{6,14},{7,15},{8,0},{9,1},... | collective-permute-start | bytes 98312 | tf_op jit(solution)/shard_map/ppermute | solution.py:200
  79.0 84.2 %collective-permute-start.24 = (bf16[4,16,32,512]{3,2,1,0:T(8,128)(2,1)S(1)}, bf16[4,16,32,512]{3,2,1,0:T(8,128)(2,1)}, u32[]{:S(2)}, u32[]{:S(2)}) collective-permute-start(bf16[4,16,32,512]{3,2,1,0:T(8,128)(2,1)S(1)} %bitcast_dynamic-update-slice_fusion.refs_8_), channel_id=1, source_target_pairs={{0,16},{16,0},{32,48},{48,32},{64,80},{80,64},{96,112},{112,96},{1... | collective-permute-start | bytes 6291464 | tf_op jit(solution)/shard_map/ppermute | solution.py:218
  79.8 16.7 %all-to-all-start = ((bf16[16,32,256]{2,1,0:T(8,128)(2,1)}), bf16[16,32,256]{2,1,0:T(8,128)(2,1)S(1)}, u32[]{:S(2)}, u32[]{:S(2)}) async-start(bf16[16,32,256]{2,1,0:T(8,128)(2,1)} %broadcast_in_dim.27), calls=%async_computation | async-start | bytes 524288 | tf_op jit(solution)/shard_map/all_to_all | solution.py:238
  85.9 17.4 %collective-permute-start.10 = (f32[256,256]{1,0:T(8,128)}, f32[256,256]{1,0:T(8,128)S(1)}, u32[]{:S(2)}, u32[]{:S(2)}) collective-permute-start(f32[256,256]{1,0:T(8,128)} %copy-done.16), channel_id=1, source_target_pairs={{0,8},{1,9},{2,10},{3,11},{4,12},{5,13},{6,14},{7,15},{8,0},{9,1},... | collective-permute-start | bytes 786440 | tf_op jit(solution)/shard_map/ppermute | solution.py:200
  96.5 11.5 %collective-permute-start.13 = (bf16[512,256]{1,0:T(8,128)(2,1)S(1)}, bf16[512,256]{1,0:T(8,128)(2,1)S(1)}, u32[]{:S(2)}, u32[]{:S(2)}) collective-permute-start(bf16[512,256]{1,0:T(8,128)(2,1)S(1)} %bitcast.26), channel_id=1, source_target_pairs={{0,16},{16,32},{32,48},{48,64},{64,80},{80,96},{96,112},{112,128},... | collective-permute-start | bytes 786440 | tf_op jit(solution)/shard_map/ppermute | solution.py:210
  98.5 9.6 %collective-permute-start.12 = (bf16[256,256]{1,0:T(8,128)(2,1)S(1)}, bf16[256,256]{1,0:T(8,128)(2,1)S(1)}, u32[]{:S(2)}, u32[]{:S(2)}) collective-permute-start(bf16[256,256]{1,0:T(8,128)(2,1)S(1)} %bitcast.31), channel_id=1, source_target_pairs={{0,32},{16,48},{32,64},{48,80},{64,96},{80,112},{96,128},{112,144}... | collective-permute-start | bytes 393224 | tf_op jit(solution)/shard_map/ppermute | solution.py:210
  108.0 1.0 copy-start.15
  129.7 5.9 %collective-permute-start.14 = (bf16[256,256]{1,0:T(8,128)(2,1)S(1)}, bf16[256,256]{1,0:T(8,128)(2,1)S(1)}, u32[]{:S(2)}, u32[]{:S(2)}) collective-permute-start(bf16[256,256]{1,0:T(8,128)(2,1)S(1)} %shard_map.47.refs_0_), channel_id=1, source_target_pairs={{0,8},{1,9},{2,10},{3,11},{4,12},{5,13},{6,14},{7,15},{8,0},{9,1},... | collective-permute-start | bytes 393224 | tf_op jit(solution)/shard_map/ppermute | solution.py:200
  135.6 10.0 %collective-permute-start.15 = (bf16[2,256,256]{2,1,0:T(8,128)(2,1)S(1)}, bf16[2,256,256]{2,1,0:T(8,128)(2,1)S(1)}, u32[]{:S(2)}, u32[]{:S(2)}) collective-permute-start(bf16[2,256,256]{2,1,0:T(8,128)(2,1)S(1)} %pad_maximum_fusion), channel_id=1, source_target_pairs={{0,1},{1,2},{2,3},{3,4},{4,5},{5,6},{6,7},{7,0},{8,9},{9,10},{10,1... | collective-permute-start | bytes 786440 | tf_op jit(solution)/shard_map/ppermute | solution.py:204
  137.7 8.3 %collective-permute-start.16 = (bf16[2,256,256]{2,1,0:T(8,128)(2,1)S(1)}, bf16[2,256,256]{2,1,0:T(8,128)(2,1)S(1)}, u32[]{:S(2)}, u32[]{:S(2)}) collective-permute-start(bf16[2,256,256]{2,1,0:T(8,128)(2,1)S(1)} %pad_maximum_fusion), channel_id=1, source_target_pairs={{0,7},{1,0},{2,1},{3,2},{4,3},{5,4},{6,5},{7,6},{8,15},{9,8},{10,9... | collective-permute-start | bytes 786440 | tf_op jit(solution)/shard_map/ppermute | solution.py:204
  146.0 8.7 %collective-permute-start.17 = (bf16[2,256,256]{2,1,0:T(8,128)(2,1)S(1)}, bf16[2,256,256]{2,1,0:T(8,128)(2,1)S(1)}, u32[]{:S(2)}, u32[]{:S(2)}) collective-permute-start(bf16[2,256,256]{2,1,0:T(8,128)(2,1)S(1)} %collective-permute-done.15.refs_2_), channel_id=1, source_target_pairs={{0,1},{1,2},{2,3},{3,4},{4,5},{5,6},{6,7},{7,0},{8,9},{9,10},{10,1... | collective-permute-start | bytes 786440 | tf_op jit(solution)/shard_map/ppermute | solution.py:204
  146.6 8.1 %collective-permute-start.18 = (bf16[2,256,256]{2,1,0:T(8,128)(2,1)S(1)}, bf16[2,256,256]{2,1,0:T(8,128)(2,1)S(1)}, u32[]{:S(2)}, u32[]{:S(2)}) collective-permute-start(bf16[2,256,256]{2,1,0:T(8,128)(2,1)S(1)} %collective-permute-done.16.refs_3_), channel_id=1, source_target_pairs={{0,7},{1,0},{2,1},{3,2},{4,3},{5,4},{6,5},{7,6},{8,15},{9,8},{10,9... | collective-permute-start | bytes 786440 | tf_op jit(solution)/shard_map/ppermute | solution.py:204
  154.7 7.8 %collective-permute-start.19 = (bf16[2,256,256]{2,1,0:T(8,128)(2,1)S(1)}, bf16[2,256,256]{2,1,0:T(8,128)(2,1)S(1)}, u32[]{:S(2)}, u32[]{:S(2)}) collective-permute-start(bf16[2,256,256]{2,1,0:T(8,128)(2,1)S(1)} %collective-permute-done.17.refs_4_), channel_id=1, source_target_pairs={{0,1},{1,2},{2,3},{3,4},{4,5},{5,6},{6,7},{7,0},{8,9},{9,10},{10,1... | collective-permute-start | bytes 786440 | tf_op jit(solution)/shard_map/ppermute | solution.py:204
  155.0 7.5 %collective-permute-start.20 = (bf16[2,256,256]{2,1,0:T(8,128)(2,1)S(1)}, bf16[2,256,256]{2,1,0:T(8,128)(2,1)S(1)}, u32[]{:S(2)}, u32[]{:S(2)}) collective-permute-start(bf16[2,256,256]{2,1,0:T(8,128)(2,1)S(1)} %collective-permute-done.18.refs_5_), channel_id=1, source_target_pairs={{0,7},{1,0},{2,1},{3,2},{4,3},{5,4},{6,5},{7,6},{8,15},{9,8},{10,9... | collective-permute-start | bytes 786440 | tf_op jit(solution)/shard_map/ppermute | solution.py:204
  162.6 7.6 %collective-permute-start.25 = (bf16[2,256,256]{2,1,0:T(8,128)(2,1)S(1)}, bf16[2,256,256]{2,1,0:T(8,128)(2,1)S(1)}, u32[]{:S(2)}, u32[]{:S(2)}) collective-permute-start(bf16[2,256,256]{2,1,0:T(8,128)(2,1)S(1)} %collective-permute-done.19.refs_6_), channel_id=1, source_target_pairs={{0,1},{1,2},{2,3},{3,4},{4,5},{5,6},{6,7},{7,0},{8,9},{9,10},{10,1... | collective-permute-start | bytes 786440 | tf_op jit(solution)/shard_map/ppermute | solution.py:204

commit v3 on v2

--- a/solution.py
+++ b/solution.py
@@ -13,6 +13,12 @@
 GROUP = 8
 LOW = -1e30
 LANES = (((1,), (1,)), ((), ()))
+
+
+def pick(source, which, lanes):
+    places = slice((which % 2) * 4, (which % 2) * 4 + 4)
+    found = source[places, :, lanes] if len(source.shape) == 3 else source[places, which // 2, :, lanes]
+    return found.reshape(HEAD, BLK)
 
 
 def attend_kernel(
@@ -29,12 +35,12 @@
     for t in range(6):
         source = (far_ref, near_ref, own_ref)[t // 2]
         lanes = slice((t % 2) * BLK, (t % 2 + 1) * BLK)
-        ktile[t] = source[:HEAD, lanes]
-        vtile[t] = source[HEAD:2 * HEAD, lanes].astype(jnp.float32).T.astype(jnp.bfloat16)
-    for scr, low in ((k2f, 2 * HEAD), (v2f, 3 * HEAD)):
-        scr[:BLK] = near_ref[low:low + HEAD, tok - BLK:].astype(jnp.float32).T
+        ktile[t] = pick(source, 0, lanes)
+        vtile[t] = pick(source, 1, lanes).astype(jnp.float32).T.astype(jnp.bfloat16)
+    for scr, which in ((k2f, 2), (v2f, 3)):
+        scr[:BLK] = pick(near_ref, which, slice(tok - BLK, tok)).astype(jnp.float32).T
         for t in range(blocks):
-            scr[(t + 1) * BLK:(t + 2) * BLK] = own_ref[low:low + HEAD, t * BLK:(t + 1) * BLK].astype(jnp.float32).T
+            scr[(t + 1) * BLK:(t + 2) * BLK] = pick(own_ref, which, slice(t * BLK, (t + 1) * BLK)).astype(jnp.float32).T
 
     @pl.when(start)
     def _():
@@ -154,44 +160,58 @@
 
 
 def project_kernel(spot_ref, *refs):
-    shards, kv_own, kv_part, own_ref, same_ref, twin_ref = refs[:8], *refs[8:13]
-    kv_mine, kv_theirs, mine_out, theirs_out = refs[13:]
+    shards, kv_own, kv_part, own_any, same_ref, twin_ref = refs[:8], *refs[8:13]
+    kv_out, mine_out, theirs_out, own_ref, sem = refs[13:]
     depth = shards[0].shape[1]
-    core = spot_ref[1]
+    half = own_ref.shape[0]
+    row, core = spot_ref[0] >> 3, spot_ref[1]
+    fetch = pltpu.make_async_copy(
+        own_any.at[pl.ds(pl.multiple_of(row * half, half), half), :], own_ref, sem
+    )
+    fetch.start()
 
     def from_place(offset, count):
         spot = (spot_ref[0] + offset) & (count - 1)
         return pl.ds(pl.multiple_of(spot * depth, depth), depth)
 
-    for weight, out in ((kv_own, kv_mine), (kv_part, kv_theirs)):
+    parts = kv_own.shape[0]
+    for weight, side in ((kv_own, row), (kv_part, 1 - row)):
         total = None
         for offset, shard in zip(OFFSETS, shards):
             cols = weight[:, from_place(offset, 8)]
             new = lax.dot_general(cols, shard[...], LANES, preferred_element_type=jnp.float32)
             total = new if total is None else total + new
-        out[...] = total
+        kv_out[pl.ds(pl.multiple_of(side * parts, parts), parts), :] = total
+    theirs_out[...] = jnp.zeros(theirs_out.shape, jnp.float32)
+    for offset, shard in zip(OFFSETS, shards):
+        low = from_place(offset, 4)
+        upper = ((spot_ref[0] + offset) & 7) >> 2
+        for ref, side in ((same_ref, core), (twin_ref, 1 - core)):
+
+            @pl.when(upper == side)
+            def _():
+                theirs_out[...] += jnp.dot(shard[...], ref[low, :], preferred_element_type=jnp.float32)
+    fetch.wait()
     total = None
     for offset, shard in zip(OFFSETS, shards):
         new = jnp.dot(shard[...], own_ref[from_place(offset, 8), :], preferred_element_type=jnp.float32)
         total = new if total is None else total + new
     mine_out[...] = total
-    theirs_out[...] = jnp.zeros(theirs_out.shape, jnp.float32)
-    for offset, shard in zip(OFFSETS, shards):
-        low = from_place(offset, 4)
-        upper = ((spot_ref[0] + offset) & 7) >> 2
-        for ref, side in ((same_ref, core), (twin_ref, 1 - core)):
-
-            @pl.when(upper == side)
-            def _():
-                theirs_out[...] += jnp.dot(shard[...], ref[low, :], preferred_element_type=jnp.float32)
 
 
 def project(spots, arrays, shapes):
+    specs = in_vmem(len(arrays))
+    specs[10] = pl.BlockSpec(memory_space=pl.ANY)
+    own = arrays[10]
     return pl.pallas_call(
         project_kernel,
         out_shape=tuple(jax.ShapeDtypeStruct(shape, jnp.float32) for shape in shapes),
-        in_specs=[pl.BlockSpec(memory_space=pltpu.SMEM)] + in_vmem(len(arrays)),
+        in_specs=[pl.BlockSpec(memory_space=pltpu.SMEM)] + specs,
         out_specs=tuple(in_vmem(len(shapes))),
+        scratch_shapes=[
+            pltpu.VMEM((own.shape[0] // 2, own.shape[1]), own.dtype),
+            pltpu.SemaphoreType.DMA,
+        ],
         compiler_params=pltpu.CompilerParams(vmem_limit_bytes=24 * 1024 * 1024),
     )(spots, *arrays)
 
@@ -233,10 +253,13 @@
     return found
 
 
-def sent_to_all(value, axis):
-    size = lax.axis_size(axis)
+ROWS = [list(range(8)), list(range(8, 16))]
+
+
+def sent_to_row(value):
     return lax.all_to_all(
-        jnp.broadcast_to(value[None], (size, *value.shape)), axis, 0, 0, tiled=True
+        jnp.broadcast_to(value[None], (8, *value.shape)),
+        "head", 0, 0, tiled=True, axis_index_groups=ROWS,
     )
 
 
@@ -248,15 +271,23 @@
     return piece.reshape(part, 16, width // 16).transpose(1, 0, 2)
 
 
-def owned_columns(piece, seq):
+def owned_columns(piece, seq, tie):
     x = seq >> 2
-    piece = lax.all_to_all(piece, "head", 0, 0, tiled=True)
+    moved = [round_x(piece, step) for step in (1, 3, 2)]
+    *moved, tie = lax.optimization_barrier((*moved, tie))
     held = jnp.zeros((4, *piece.shape), piece.dtype)
     held = lax.dynamic_update_slice_in_dim(held, piece[None], x, 0)
-    for step in (1, 3, 2):
-        moved = round_x(piece, step)
-        held = lax.dynamic_update_slice_in_dim(held, moved[None], (x - step) & 3, 0)
-    return held, other_core(held)
+    for step, part in zip((1, 3, 2), moved):
+        held = lax.dynamic_update_slice_in_dim(held, part[None], (x - step) & 3, 0)
+    return held, other_core(held), tie
+
+
+def two_rings(value):
+    other = swap_rows(value)
+    rings = []
+    for start in (value, other):
+        rings.append(z_ring(start))
+    return rings
 
 
 def gather_rows(spot_ref, held, twin, place, out, slot):
@@ -269,56 +300,48 @@
 
 
 def finish_kernel(spot_ref, *refs):
-    near, far, pairs, held, twin = refs[0], refs[1], refs[2:8], refs[8], refs[9]
-    part_out, tail_out, w_scr = refs[10:]
+    mine, other, held, twin = refs[:8], refs[8:15], refs[15], refs[16]
+    part_out, tail_out, w_scr = refs[17:]
     total = None
-    values = [(near, far)] + [(pair.at[0], pair.at[1]) for pair in pairs]
-    for k, offset in enumerate(OFFSETS):
-        spot = (spot_ref[0] + offset) & 7
-        for side in range(2):
-            place = ((spot_ref[0] & 8) ^ (8 * side)) | spot
-            if k == 7:
-                gather_rows(spot_ref, held, twin, place, tail_out, side)
-                continue
-            gather_rows(spot_ref, held, twin, place, w_scr, 2 * k + side)
-            new = jnp.dot(values[k][side][...], w_scr[2 * k + side], preferred_element_type=jnp.float32)
+    for side, values in enumerate((mine, other)):
+        for k, value in enumerate(values):
+            place = ((spot_ref[0] & 8) ^ (8 * side)) | ((spot_ref[0] + OFFSETS[k]) & 7)
+            slot = 8 * side + k
+            gather_rows(spot_ref, held, twin, place, w_scr, slot)
+            new = jnp.dot(value[...], w_scr[slot], preferred_element_type=jnp.float32)
             total = new if total is None else total + new
     part_out[...] = total
-
-
-def close_kernel(part_ref, tail_ref, pair_ref, out_ref):
-    total = part_ref[...]
-    for side in range(2):
-        total = total + jnp.dot(pair_ref[side], tail_ref[side], preferred_element_type=jnp.float32)
+    place = ((spot_ref[0] & 8) ^ 8) | ((spot_ref[0] + OFFSETS[7]) & 7)
+    gather_rows(spot_ref, held, twin, place, tail_out, 0)
+
+
+def close_kernel(part_ref, tail_ref, last_ref, out_ref):
+    total = part_ref[...] + jnp.dot(last_ref[...], tail_ref[0], preferred_element_type=jnp.float32)
     out_ref[...] = total.astype(jnp.bfloat16)
 
 
-def finish(spots, near, pairs, held, twin):
-    tok, feats = near.shape
+def finish(spots, mine, other, held, twin):
+    tok, feats = mine[0].shape
     cols = held.shape[-1]
     limit = pltpu.CompilerParams(vmem_limit_bytes=24 * 1024 * 1024)
     part, tail = pl.pallas_call(
         finish_kernel,
         out_shape=(
             jax.ShapeDtypeStruct((tok, cols), jnp.float32),
-            jax.ShapeDtypeStruct((2, feats, cols), held.dtype),
+            jax.ShapeDtypeStruct((1, feats, cols), held.dtype),
         ),
-        in_specs=[pl.BlockSpec(memory_space=pltpu.SMEM)] + in_vmem(10),
+        in_specs=[pl.BlockSpec(memory_space=pltpu.SMEM)] + in_vmem(17),
         out_specs=tuple(in_vmem(2)),
-        scratch_shapes=[pltpu.VMEM((14, feats, cols), held.dtype)],
+        scratch_shapes=[pltpu.VMEM((15, feats, cols), held.dtype)],
         compiler_params=limit,
-    )(spots, *near_and(near, pairs), held, twin)
+    )(spots, *mine, *other[:7], held, twin)
     return pl.pallas_call(
         close_kernel,
         out_shape=jax.ShapeDtypeStruct((tok, cols), jnp.bfloat16),
         in_specs=in_vmem(3),
         out_specs=in_vmem(1)[0],
         compiler_params=limit,
-    )(part, tail, pairs[7])
-
-
-def near_and(near, pairs):
-    return (near, pairs[0][1], *pairs[1:7])
+    )(part, tail, other[7])
 
 
 def body(tokens, w_query, w_keyval, w_out):
@@ -336,27 +359,26 @@
     )
     q_twin = other_core(q_same)
     kv_own = lax.dynamic_slice_in_dim(kv_flat, row * half, half, 1)
-    q_own = lax.dynamic_slice_in_dim(w_query, row * half, half, 0)
     shards = z_ring(tokens)
     piece, shards[5], shards[6] = lax.optimization_barrier(
         (owned_piece(w_out, seq), shards[5], shards[6])
     )
-    kv_mine, kv_theirs, q_mine, q_theirs = project(
+    piece = lax.all_to_all(piece, "head", 0, 0, tiled=True)
+    kv_part, q_mine, q_theirs = project(
         spots,
-        (*shards, kv_own, kv_part, q_own, q_same, q_twin),
-        ((kv_flat.shape[0], tok_rows),) * 2 + ((tok_rows, w_query.shape[1]),) * 2,
-    )
-    kv = (kv_mine + swap_rows(kv_theirs)).astype(jnp.bfloat16)
+        (*shards, kv_own, kv_part, w_query, q_same, q_twin),
+        ((2 * kv_flat.shape[0], tok_rows),) + ((tok_rows, w_query.shape[1]),) * 2,
+    )
+    kv = (kv_part + swap_rows(kv_part)).astype(jnp.bfloat16)
+    piece, kv = lax.optimization_barrier((piece, kv))
     q_sent = swap_rows(q_theirs)
-    keyval = sent_to_all(kv, "head").reshape(4 * HEAD, tok_rows)
+    keyval = sent_to_row(kv).reshape(8, 2, kv_flat.shape[0], tok_rows)
     near = along_seq(keyval, 1)
-    far = along_seq(keyval[:2 * HEAD], 2)
+    far = along_seq(keyval[:, 0], 2)
     attended = attend(seq.reshape(1), q_mine, q_sent, far, near, keyval)
-    held, twin = owned_columns(piece, seq)
-    other = swap_rows(attended)
-    pairs = z_ring(jnp.concatenate([attended[None], other[None]], axis=0))
-    pairs[0] = (attended, other)
-    return finish(spots, attended, pairs, held, twin)
+    mine, other = two_rings(attended)
+    held, twin, mine[5] = owned_columns(piece, seq, mine[5])
+    return finish(spots, mine, other, held, twin)
 
 
 def solution(mesh):

time: 173 us -> 179 us (1.035)
  starting transfers between devices: 55.6 us -> 66.6 us
  local copies, waits for them, and re-layouts: 18.1 us -> 13 us
  waiting for transfers between devices: 67.3 us -> 69.3 us
    ppermute x14 -> x21, starting transfers between devices: 24.1 us -> 33.6 us  [along_z(): lax.ppermute(value, 'head', [(i, i // 8 * 8 + (i + step) % 8) for i in ra...]
    ppermute x14 -> x21, waiting for transfers between devices: 36.4 us -> 43.5 us  [along_z(): lax.ppermute(value, 'head', [(i, i // 8 * 8 + (i + step) % 8) for i in ra...]
    ppermute x2, waiting for transfers between devices: 4.73 us -> 0.32 us  [along_seq(): return lax.ppermute(value, 'seq', [(i, i + step) for i in range(16 - step)])]
    ppermute x3, waiting for transfers between devices: 3.43 us -> 0.01 us  [round_x(): lax.ppermute(value, 'seq', [(i, (i + 4 * step) % 16) for i in range(16)])]
    dynamic_slice x1 -> x0, local copies, waits for them, and re-layouts: 3.06 us -> none  [body(): q_own = lax.dynamic_slice_in_dim(w_query, row * half, half, 0)]
    ppermute x5, waiting for transfers between devices: 14 us -> 16.2 us  [swap_rows(): return lax.ppermute(value, 'head', [(i, (i + 8) % 16) for i in range(16)])]
    dynamic_update_slice x3, local copies, waits for them, and re-layouts: 2.2 us -> 0.15 us  [owned_columns(): held = lax.dynamic_update_slice_in_dim(held, part[None], x - step & 3, 0)]
    unnamed x34 -> x10, local copies, waits for them, and re-layouts: 6.46 us -> 4.55 us
  transfers between devices with their start and end apart: 28 -> 35, of which waited for: 16 -> 18; matrix products, arithmetic and copies ran while one was open for 7% -> 4% of each run, Pallas kernels for 17% -> 16%
where the time goes in v3:
time: 179 us
  waiting for transfers between devices  69.3 us (39%)
  starting transfers between devices  66.6 us (37%)
  Pallas kernels  29.5 us (16%)
  local copies, waits for them, and re-layouts  13 us (7%)
    ppermute x21, waiting for transfers between devices, along_z(): lax.ppermute(value, 'head', [(i, i // 8 * 8 + (i + step) % 8) for i in ra...  43.5 us
    ppermute x21, starting transfers between devices, along_z(): lax.ppermute(value, 'head', [(i, i // 8 * 8 + (i + step) % 8) for i in ra...  33.6 us
    pallas_call x1, Pallas kernels, attend(): pl.pallas_call(attend_kernel, out_shape=jax.ShapeDtypeStruct(mine.shape,...  21.7 us
    ppermute x5, waiting for transfers between devices, swap_rows(): return lax.ppermute(value, 'head', [(i, (i + 8) % 16) for i in range(16)])  16.2 us
    all_to_all x1, waiting for transfers between devices, sent_to_row(): lax.all_to_all(jnp.broadcast_to(value[None], (8, *value.shape)), 'head',...  9.18 us
    ppermute x5, starting transfers between devices, swap_rows(): return lax.ppermute(value, 'head', [(i, (i + 8) % 16) for i in range(16)])  9.17 us
    all_to_all x1, starting transfers between devices, body(): piece = lax.all_to_all(piece, 'head', 0, 0, tiled=True)  8.09 us
    ppermute x2, starting transfers between devices, along_seq(): return lax.ppermute(value, 'seq', [(i, i + step) for i in range(16 - step)])  6.72 us
  transfers between devices with their start and end apart: 35, of which 18 were waited for; matrix products, arithmetic and copies ran while one was open for 4% of the time, Pallas kernels for 16%

profile of v3, /device:TPU:2, one launch (start us, length us, event | category | flops | bytes accessed | tf_op | source)
XLA Modules:
  0.0 178.7 jit_solution(5143460323489124590)
XLA Ops:
  0.0 1.3 constant_dynamic-slice_fusion
  1.3 1.7 collective-permute-start.8
  3.0 1.9 %collective-permute-start = (bf16[256,512]{1,0:T(8,128)(2,1)S(1)}, bf16[256,512]{1,0:T(8,128)(2,1)S(1)}, u32[]{:S(2)}, u32[]{:S(2)}) collective-permute-start(bf16[256,512]{1,0:T(8,128)(2,1)S(1)} %copy-done.1), channel_id=1, source_target_pairs={{0,1},{1,2},{2,3},{3,4},{4,5},{5,6},{6,7},{7,0},{8,9},{9,10},{10,1... | collective-permute-start | bytes 786440 | tf_op jit(solution)/shard_map/ppermute | solution.py:224
  4.9 3.9 %collective-permute-start.1 = (bf16[256,512]{1,0:T(8,128)(2,1)S(1)}, bf16[256,512]{1,0:T(8,128)(2,1)S(1)}, u32[]{:S(2)}, u32[]{:S(2)}) collective-permute-start(bf16[256,512]{1,0:T(8,128)(2,1)S(1)} %copy-done.1), channel_id=1, source_target_pairs={{0,7},{1,0},{2,1},{3,2},{4,3},{5,4},{6,5},{7,6},{8,15},{9,8},{10,9... | collective-permute-start | bytes 786440 | tf_op jit(solution)/shard_map/ppermute | solution.py:224
  8.9 6.0 %collective-permute-done.refs_1_ = bf16[256,512]{1,0:T(8,128)(2,1)S(1)} collective-permute-done((bf16[256,512]{1,0:T(8,128)(2,1)S(1)}, bf16[256,512]{1,0:T(8,128)(2,1)S(1)}, u32[]{:S(2)}, u32[]{:S(2)}) %collective-permute-start) | collective-permute-done | bytes 262176 | tf_op jit(solution)/shard_map/ppermute | solution.py:224
  14.9 0.0 collective-permute-start.2
  14.9 3.2 %collective-permute-start.3 = (bf16[256,512]{1,0:T(8,128)(2,1)S(1)}, bf16[256,512]{1,0:T(8,128)(2,1)S(1)}, u32[]{:S(2)}, u32[]{:S(2)}) collective-permute-start(bf16[256,512]{1,0:T(8,128)(2,1)S(1)} %collective-permute-done.1.refs_2_), channel_id=1, source_target_pairs={{0,7},{1,0},{2,1},{3,2},{4,3},{5,4},{6,5},{7,6},{8,15},{9,8},{10,9... | collective-permute-start | bytes 786440 | tf_op jit(solution)/shard_map/ppermute | solution.py:224
  18.1 5.2 %collective-permute-done.2.refs_3_ = bf16[256,512]{1,0:T(8,128)(2,1)S(1)} collective-permute-done((bf16[256,512]{1,0:T(8,128)(2,1)S(1)}, bf16[256,512]{1,0:T(8,128)(2,1)S(1)}, u32[]{:S(2)}, u32[]{:S(2)}) %collective-permute-start.2) | collective-permute-done | bytes 262176 | tf_op jit(solution)/shard_map/ppermute | solution.py:224
  23.3 0.0 collective-permute-done.3.refs_4_
  23.3 1.9 %collective-permute-start.4 = (bf16[256,512]{1,0:T(8,128)(2,1)S(1)}, bf16[256,512]{1,0:T(8,128)(2,1)}, u32[]{:S(2)}, u32[]{:S(2)}) collective-permute-start(bf16[256,512]{1,0:T(8,128)(2,1)S(1)} %collective-permute-done.2.refs_3_), channel_id=1, source_target_pairs={{0,1},{1,2},{2,3},{3,4},{4,5},{5,6},{6,7},{7,0},{8,9},{9,10},{10,1... | collective-permute-start | bytes 786440 | tf_op jit(solution)/shard_map/ppermute | solution.py:224
  25.2 1.3 collective-permute-start.5
  26.5 1.9 %constant_dynamic-slice_fusion.1 = bf16[32,8192]{1,0:T(8,128)(2,1)} fusion(bf16[256,8192]{1,0:T(8,128)(2,1)} %param.7, s32[]{:T(128)S(6)} %select_n.24), kind=kLoop, calls=%fused_computation.10 | loop fusion | bytes 1048580 | tf_op jit(solution)/shard_map/dynamic_slice | solution.py:270
  28.4 1.9 %copy.8 = bf16[4,16,8,512]{3,2,0,1:T(8,128)(2,1)} copy(bf16[4,16,8,512]{3,2,1,0:T(8,128)(2,1)} %bitcast.29) | data formatting | bytes 1048576 | tf_op jit(solution)/shard_map/reshape | solution.py:271
  30.3 0.7 collective-permute-done.4.refs_5_
  31.0 0.7 collective-permute-done.5.refs_6_
  31.7 8.1 %all-to-all-start = ((bf16[16,32,512]{2,1,0:T(8,128)(2,1)}), bf16[16,32,512]{2,1,0:T(8,128)(2,1)}, u32[]{:S(2)}, u32[]{:S(2)}) async-start(bf16[16,32,512]{2,1,0:T(8,128)(2,1)} %bitcast.28), calls=%async_computation | async-start | bytes 1048576 | tf_op jit(solution)/shard_map/all_to_all | solution.py:366
  39.8 1.1 dynamic-slice_bitcast_fusion
  40.8 2.0 %collective-permute-start.7 = (bf16[32,4096]{1,0:T(8,128)(2,1)S(1)}, bf16[32,4096]{1,0:T(8,128)(2,1)S(1)}, u32[]{:S(2)}, u32[]{:S(2)}) collective-permute-start(bf16[32,4096]{1,0:T(8,128)(2,1)S(1)} %get-tuple-element.69), channel_id=1, source_target_pairs={{0,8},{1,9},{2,10},{3,11},{4,12},{5,13},{6,14},{7,15},{8,0},{9,1},... | collective-permute-start | bytes 786440 | tf_op jit(solution)/shard_map/ppermute | solution.py:220
  42.8 1.5 collective-permute-start.6
  44.3 0.1 pad_add_fusion.spot_ref
  44.3 9.4 %collective-permute-done.7.refs_9_ = bf16[32,4096]{1,0:T(8,128)(2,1)S(1)} collective-permute-done((bf16[32,4096]{1,0:T(8,128)(2,1)S(1)}, bf16[32,4096]{1,0:T(8,128)(2,1)S(1)}, u32[]{:S(2)}, u32[]{:S(2)}) %collective-permute-start.7) | collective-permute-done | bytes 262176 | tf_op jit(solution)/shard_map/ppermute | solution.py:220
  53.7 7.0 %collective-permute-done.6.refs_7_ = bf16[256,512]{1,0:T(8,128)(2,1)S(1)} collective-permute-done((bf16[256,512]{1,0:T(8,128)(2,1)}, bf16[256,512]{1,0:T(8,128)(2,1)S(1)}, u32[]{:S(2)}, u32[]{:S(2)}) %collective-permute-start.6) | collective-permute-done | bytes 262176 | tf_op jit(solution)/shard_map/ppermute | solution.py:224
  60.7 2.2 %copy-done = bf16[8192,256]{1,0:T(8,128)(2,1)S(1)} copy-done((bf16[8192,256]{1,0:T(8,128)(2,1)S(1)}, bf16[8192,256]{1,0:T(8,128)(2,1)}, u32[]{:S(2)}) %copy-start) | copy-done | bytes 4194328
  62.9 5.1 %shard_map.46 = (f32[64,256]{1,0:T(8,128)S(1)}, f32[256,256]{1,0:T(8,128)S(1)}, f32[256,256]{1,0:T(8,128)S(1)}) custom-call(s32[2]{0:T(128)S(1)} %pad_add_fusion.spot_ref, bf16[256,512]{1,0:T(8,128)(2,1)S(1)} %copy-done.1, bf16[256,512]{1,0:T(8,128)(2,1)S(1)} %collective-permute-done.refs_1_, bf16[256,512]{1,0:T(8,128)(2,1)S(1)} %collective-permute-done.1.refs_2_, ...), custom_call_target="tpu_custom_call" | custom-call | tf_op jit(solution)/shard_map/pallas_call | solution.py:206
  68.0 0.0 copy-start.2
  68.0 0.7 copy-done.2
  68.7 0.7 copy-done.4
  69.4 1.5 collective-permute-start.11
  70.9 2.8 %collective-permute-done.11 = f32[64,256]{1,0:T(8,128)S(1)} collective-permute-done((f32[64,256]{1,0:T(8,128)S(1)}, f32[64,256]{1,0:T(8,128)S(1)}, u32[]{:S(2)}, u32[]{:S(2)}) %collective-permute-start.11) | collective-permute-done | bytes 65568 | tf_op jit(solution)/shard_map/ppermute | solution.py:220
  73.7 0.7 broadcast_in_dim.21
  74.4 4.5 %all-to-all-start.1 = ((bf16[8,64,256]{2,1,0:T(8,128)(2,1)}), bf16[8,64,256]{2,1,0:T(8,128)(2,1)S(1)}, u32[]{:S(2)}, u32[]{:S(2)}) async-start(bf16[8,64,256]{2,1,0:T(8,128)(2,1)} %broadcast_in_dim.21), calls=%async_computation.1 | async-start | bytes 524288 | tf_op jit(solution)/shard_map/all_to_all | solution.py:260
  79.0 1.5 collective-permute-start.10
  80.5 9.2 %all-to-all-done.1 = bf16[8,64,256]{2,1,0:T(8,128)(2,1)S(1)} async-done(((bf16[8,64,256]{2,1,0:T(8,128)(2,1)}), bf16[8,64,256]{2,1,0:T(8,128)(2,1)S(1)}, u32[]{:S(2)}, u32[]{:S(2)}) %all-to-all-start.1) | async-done | bytes 262176 | tf_op jit(solution)/shard_map/all_to_all | solution.py:260
  89.6 1.9 %collective-permute-start.13 = (bf16[8,2,32,256]{3,2,1,0:T(8,128)(2,1)S(1)}, bf16[8,2,32,256]{3,2,1,0:T(8,128)(2,1)S(1)}, u32[]{:S(2)}, u32[]{:S(2)}) collective-permute-start(bf16[8,2,32,256]{3,2,1,0:T(8,128)(2,1)S(1)} %bitcast.25), channel_id=1, source_target_pairs={{0,16},{16,32},{32,48},{48,64},{64,80},{80,96},{96,112},{112,128},... | collective-permute-start | bytes 786440 | tf_op jit(solution)/shard_map/ppermute | solution.py:230
  91.6 4.8 %collective-permute-start.12 = (bf16[8,32,256]{2,1,0:T(8,128)(2,1)S(1)}, bf16[8,32,256]{2,1,0:T(8,128)(2,1)S(1)}, u32[]{:S(2)}, u32[]{:S(2)}) collective-permute-start(bf16[8,32,256]{2,1,0:T(8,128)(2,1)S(1)} %slice_bitcast_fusion), channel_id=1, source_target_pairs={{0,32},{16,48},{32,64},{48,80},{64,96},{80,112},{96,128},{112,144}... | collective-permute-start | bytes 393224 | tf_op jit(solution)/shard_map/ppermute | solution.py:230
  96.4 1.7 collective-permute-start.18
  98.1 0.5 collective-permute-start.19
  98.7 2.1 %collective-permute-start.20 = (bf16[16,32,512]{2,1,0:T(8,128)(2,1)}, bf16[16,32,512]{2,1,0:T(8,128)(2,1)S(1)}, u32[]{:S(2)}, u32[]{:S(2)}) collective-permute-start(bf16[16,32,512]{2,1,0:T(8,128)(2,1)} %all-to-all-done), channel_id=1, source_target_pairs={{0,128},{16,144},{32,160},{48,176},{64,192},{80,208},{96,224},{112... | collective-permute-start | bytes 1572872 | tf_op jit(solution)/shard_map/ppermute | solution.py:234
  100.8 0.3 collective-permute-done.12.far_ref
  101.1 0.9 copy-done.3
  102.1 21.7 %shard_map.47.refs_0_ = bf16[256,256]{1,0:T(8,128)(2,1)S(1)} custom-call(s32[1]{0:T(128)} %bitcast.2.seq_ref, f32[256,256]{1,0:T(8,128)S(1)} %copy-done.3, f32[256,256]{1,0:T(8,128)S(1)} %collective-permute-done.10.sent_ref, bf16[8,32,256]{2,1,0:T(8,128)(2,1)S(1)} %collective-permute-done.12.far_ref, ...), custom_call_target="tpu_custom_call" | custom-call | tf_op jit(solution)/shard_map/pallas_call | solution.py:139
  123.8 0.6 collective-permute-start.14
  124.5 2.7 %collective-permute-start.15 = (bf16[256,256]{1,0:T(8,128)(2,1)S(1)}, bf16[256,256]{1,0:T(8,128)(2,1)S(1)}, u32[]{:S(2)}, u32[]{:S(2)}) collective-permute-start(bf16[256,256]{1,0:T(8,128)(2,1)S(1)} %shard_map.47.refs_0_), channel_id=1, source_target_pairs={{0,7},{1,0},{2,1},{3,2},{4,3},{5,4},{6,5},{7,6},{8,15},{9,8},{10,9... | collective-permute-start | bytes 393224 | tf_op jit(solution)/shard_map/ppermute | solution.py:224
  127.1 2.9 %collective-permute-done.14.refs_1_ = bf16[256,256]{1,0:T(8,128)(2,1)S(1)} collective-permute-done((bf16[256,256]{1,0:T(8,128)(2,1)S(1)}, bf16[256,256]{1,0:T(8,128)(2,1)S(1)}, u32[]{:S(2)}, u32[]{:S(2)}) %collective-permute-start.14) | collective-permute-done | bytes 131104 | tf_op jit(solution)/shard_map/ppermute | solution.py:224
  130.1 3.2 %collective-permute-start.17 = (bf16[256,256]{1,0:T(8,128)(2,1)S(1)}, bf16[256,256]{1,0:T(8,128)(2,1)S(1)}, u32[]{:S(2)}, u32[]{:S(2)}) collective-permute-start(bf16[256,256]{1,0:T(8,128)(2,1)S(1)} %collective-permute-done.15.refs_2_), channel_id=1, source_target_pairs={{0,7},{1,0},{2,1},{3,2},{4,3},{5,4},{6,5},{7,6},{8,15},{9,8},{10,9... | collective-permute-start | bytes 393224 | tf_op jit(solution)/shard_map/ppermute | solution.py:224
  133.3 3.5 %collective-permute-done.16.refs_3_ = bf16[256,256]{1,0:T(8,128)(2,1)S(1)} collective-permute-done((bf16[256,256]{1,0:T(8,128)(2,1)S(1)}, bf16[256,256]{1,0:T(8,128)(2,1)S(1)}, u32[]{:S(2)}, u32[]{:S(2)}) %collective-permute-start.16) | collective-permute-done | bytes 131104 | tf_op jit(solution)/shard_map/ppermute | solution.py:224
  136.8 3.5 %collective-permute-start.22 = (bf16[256,256]{1,0:T(8,128)(2,1)S(1)}, bf16[256,256]{1,0:T(8,128)(2,1)S(1)}, u32[]{:S(2)}, u32[]{:S(2)}) collective-permute-start(bf16[256,256]{1,0:T(8,128)(2,1)S(1)} %collective-permute-done.17.refs_4_), channel_id=1, source_target_pairs={{0,7},{1,0},{2,1},{3,2},{4,3},{5,4},{6,5},{7,6},{8,15},{9,8},{10,9... | collective-permute-start | bytes 393224 | tf_op jit(solution)/shard_map/ppermute | solution.py:224
  140.3 0.2 broadcast_in_dim.22
  140.6 1.1 bitcast_dynamic-update-slice_fusion.3
  141.7 2.7 %collective-permute-done.21.refs_5_ = bf16[256,256]{1,0:T(8,128)(2,1)S(1)} collective-permute-done((bf16[256,256]{1,0:T(8,128)(2,1)S(1)}, bf16[256,256]{1,0:T(8,128)(2,1)S(1)}, u32[]{:S(2)}, u32[]{:S(2)}) %collective-permute-start.21) | collective-permute-done | bytes 131104 | tf_op jit(solution)/shard_map/ppermute | solution.py:224
  144.6 0.1 collective-permute-start.31
  144.7 2.6 %collective-permute-start.24 = (bf16[256,256]{1,0:T(8,128)(2,1)S(1)}, bf16[256,256]{1,0:T(8,128)(2,1)S(1)}, u32[]{:S(2)}, u32[]{:S(2)}) collective-permute-start(bf16[256,256]{1,0:T(8,128)(2,1)S(1)} %shard_map.47.refs_0_), channel_id=1, source_target_pairs={{0,8},{1,9},{2,10},{3,11},{4,12},{5,13},{6,14},{7,15},{8,0},{9,1},... | collective-permute-start | bytes 393224 | tf_op jit(solution)/shard_map/ppermute | solution.py:220
  147.3 4.1 %collective-permute-done.24.refs_8_ = bf16[256,256]{1,0:T(8,128)(2,1)S(1)} collective-permute-done((bf16[256,256]{1,0:T(8,128)(2,1)S(1)}, bf16[256,256]{1,0:T(8,128)(2,1)S(1)}, u32[]{:S(2)}, u32[]{:S(2)}) %collective-permute-start.24) | collective-permute-done | bytes 131104 | tf_op jit(solution)/shard_map/ppermute | solution.py:220
  151.4 3.2 %collective-permute-start.26 = (bf16[256,256]{1,0:T(8,128)(2,1)S(1)}, bf16[256,256]{1,0:T(8,128)(2,1)S(1)}, u32[]{:S(2)}, u32[]{:S(2)}) collective-permute-start(bf16[256,256]{1,0:T(8,128)(2,1)S(1)} %collective-permute-done.24.refs_8_), channel_id=1, source_target_pairs={{0,7},{1,0},{2,1},{3,2},{4,3},{5,4},{6,5},{7,6},{8,15},{9,8},{10,9... | collective-permute-start | bytes 393224 | tf_op jit(solution)/shard_map/ppermute | solution.py:224
  154.6 3.2 %collective-permute-done.25.refs_9_ = bf16[256,256]{1,0:T(8,128)(2,1)S(1)} collective-permute-done((bf16[256,256]{1,0:T(8,128)(2,1)S(1)}, bf16[256,256]{1,0:T(8,128)(2,1)S(1)}, u32[]{:S(2)}, u32[]{:S(2)}) %collective-permute-start.25) | collective-permute-done | bytes 131104 | tf_op jit(solution)/shard_map/ppermute | solution.py:224
  157.8 3.2 %collective-permute-start.28 = (bf16[256,256]{1,0:T(8,128)(2,1)S(1)}, bf16[256,256]{1,0:T(8,128)(2,1)S(1)}, u32[]{:S(2)}, u32[]{:S(2)}) collective-permute-start(bf16[256,256]{1,0:T(8,128)(2,1)S(1)} %collective-permute-done.26.refs_10_), channel_id=1, source_target_pairs={{0,7},{1,0},{2,1},{3,2},{4,3},{5,4},{6,5},{7,6},{8,15},{9,8},{10,9... | collective-permute-start | bytes 393224 | tf_op jit(solution)/shard_map/ppermute | solution.py:224
  161.0 2.9 %collective-permute-done.27.refs_11_ = bf16[256,256]{1,0:T(8,128)(2,1)S(1)} collective-permute-done((bf16[256,256]{1,0:T(8,128)(2,1)S(1)}, bf16[256,256]{1,0:T(8,128)(2,1)S(1)}, u32[]{:S(2)}, u32[]{:S(2)}) %collective-permute-start.27) | collective-permute-done | bytes 131104 | tf_op jit(solution)/shard_map/ppermute | solution.py:224
  164.0 0.6 collective-permute-start.29
  164.6 2.7 %collective-permute-start.30 = (bf16[256,256]{1,0:T(8,128)(2,1)S(1)}, bf16[256,256]{1,0:T(8,128)(2,1)S(1)}, u32[]{:S(2)}, u32[]{:S(2)}) collective-permute-start(bf16[256,256]{1,0:T(8,128)(2,1)S(1)} %collective-permute-done.28.refs_12_), channel_id=1, source_target_pairs={{0,7},{1,0},{2,1},{3,2},{4,3},{5,4},{6,5},{7,6},{8,15},{9,8},{10,9... | collective-permute-start | bytes 393224 | tf_op jit(solution)/shard_map/ppermute | solution.py:224
  167.2 4.3 %collective-permute-done.29.refs_13_ = bf16[256,256]{1,0:T(8,128)(2,1)S(1)} collective-permute-done((bf16[256,256]{1,0:T(8,128)(2,1)S(1)}, bf16[256,256]{1,0:T(8,128)(2,1)S(1)}, u32[]{:S(2)}, u32[]{:S(2)}) %collective-permute-start.29) | collective-permute-done | bytes 131104 | tf_op jit(solution)/shard_map/ppermute | solution.py:224
  171.6 2.4 %collective-permute-done.23.refs_7_ = bf16[256,256]{1,0:T(8,128)(2,1)S(1)} collective-permute-done((bf16[256,256]{1,0:T(8,128)(2,1)S(1)}, bf16[256,256]{1,0:T(8,128)(2,1)S(1)}, u32[]{:S(2)}, u32[]{:S(2)}) %collective-permute-start.23) | collective-permute-done | bytes 131104 | tf_op jit(solution)/shard_map/ppermute | solution.py:224
  173.9 1.8 shard_map.48
  175.7 2.0 %collective-permute-done.32.last_ref = bf16[256,256]{1,0:T(8,128)(2,1)S(1)} collective-permute-done((bf16[256,256]{1,0:T(8,128)(2,1)S(1)}, bf16[256,256]{1,0:T(8,128)(2,1)S(1)}, u32[]{:S(2)}, u32[]{:S(2)}) %collective-permute-start.32) | collective-permute-done | bytes 131104 | tf_op jit(solution)/shard_map/ppermute | solution.py:224
  177.7 0.9 shard_map.49
  (33 shorter events, 0.2 us)
Async XLA Ops:
  0.0 3.0 %copy-start.1 = (bf16[256,512]{1,0:T(8,128)(2,1)S(1)}, bf16[256,512]{1,0:T(8,128)(2,1)}, u32[]{:S(2)}) copy-start(bf16[256,512]{1,0:T(8,128)(2,1)} %refs_0_.1) | copy-start | bytes 786436
  1.3 25.2 %collective-permute-start.8 = (bf16[2048,256]{1,0:T(8,128)(2,1)S(1)}, bf16[2048,256]{1,0:T(8,128)(2,1)S(1)}, u32[]{:S(2)}, u32[]{:S(2)}) collective-permute-start(bf16[2048,256]{1,0:T(8,128)(2,1)S(1)} %constant_dynamic-slice_fusion), channel_id=1, source_target_pairs={{0,8},{1,9},{2,10},{3,11},{4,12},{5,13},{6,14},{7,15},{8,0},{9,1},... | collective-permute-start | bytes 3145736 | tf_op jit(solution)/shard_map/ppermute | solution.py:220
  3.0 11.9 %collective-permute-start = (bf16[256,512]{1,0:T(8,128)(2,1)S(1)}, bf16[256,512]{1,0:T(8,128)(2,1)S(1)}, u32[]{:S(2)}, u32[]{:S(2)}) collective-permute-start(bf16[256,512]{1,0:T(8,128)(2,1)S(1)} %copy-done.1), channel_id=1, source_target_pairs={{0,1},{1,2},{2,3},{3,4},{4,5},{5,6},{6,7},{7,0},{8,9},{9,10},{10,1... | collective-permute-start | bytes 786440 | tf_op jit(solution)/shard_map/ppermute | solution.py:224
  4.9 10.0 %collective-permute-start.1 = (bf16[256,512]{1,0:T(8,128)(2,1)S(1)}, bf16[256,512]{1,0:T(8,128)(2,1)S(1)}, u32[]{:S(2)}, u32[]{:S(2)}) collective-permute-start(bf16[256,512]{1,0:T(8,128)(2,1)S(1)} %copy-done.1), channel_id=1, source_target_pairs={{0,7},{1,0},{2,1},{3,2},{4,3},{5,4},{6,5},{7,6},{8,15},{9,8},{10,9... | collective-permute-start | bytes 786440 | tf_op jit(solution)/shard_map/ppermute | solution.py:224
  14.9 8.4 %collective-permute-start.2 = (bf16[256,512]{1,0:T(8,128)(2,1)S(1)}, bf16[256,512]{1,0:T(8,128)(2,1)S(1)}, u32[]{:S(2)}, u32[]{:S(2)}) collective-permute-start(bf16[256,512]{1,0:T(8,128)(2,1)S(1)} %collective-permute-done.refs_1_), channel_id=1, source_target_pairs={{0,1},{1,2},{2,3},{3,4},{4,5},{5,6},{6,7},{7,0},{8,9},{9,10},{10,1... | collective-permute-start | bytes 786440 | tf_op jit(solution)/shard_map/ppermute | solution.py:224
  14.9 8.4 %collective-permute-start.3 = (bf16[256,512]{1,0:T(8,128)(2,1)S(1)}, bf16[256,512]{1,0:T(8,128)(2,1)S(1)}, u32[]{:S(2)}, u32[]{:S(2)}) collective-permute-start(bf16[256,512]{1,0:T(8,128)(2,1)S(1)} %collective-permute-done.1.refs_2_), channel_id=1, source_target_pairs={{0,7},{1,0},{2,1},{3,2},{4,3},{5,4},{6,5},{7,6},{8,15},{9,8},{10,9... | collective-permute-start | bytes 786440 | tf_op jit(solution)/shard_map/ppermute | solution.py:224
  23.3 7.7 %collective-permute-start.4 = (bf16[256,512]{1,0:T(8,128)(2,1)S(1)}, bf16[256,512]{1,0:T(8,128)(2,1)}, u32[]{:S(2)}, u32[]{:S(2)}) collective-permute-start(bf16[256,512]{1,0:T(8,128)(2,1)S(1)} %collective-permute-done.2.refs_3_), channel_id=1, source_target_pairs={{0,1},{1,2},{2,3},{3,4},{4,5},{5,6},{6,7},{7,0},{8,9},{9,10},{10,1... | collective-permute-start | bytes 786440 | tf_op jit(solution)/shard_map/ppermute | solution.py:224
  25.2 6.5 %collective-permute-start.5 = (bf16[256,512]{1,0:T(8,128)(2,1)S(1)}, bf16[256,512]{1,0:T(8,128)(2,1)}, u32[]{:S(2)}, u32[]{:S(2)}) collective-permute-start(bf16[256,512]{1,0:T(8,128)(2,1)S(1)} %collective-permute-done.3.refs_4_), channel_id=1, source_target_pairs={{0,7},{1,0},{2,1},{3,2},{4,3},{5,4},{6,5},{7,6},{8,15},{9,8},{10,9... | collective-permute-start | bytes 786440 | tf_op jit(solution)/shard_map/ppermute | solution.py:224
  26.5 34.2 %collective-permute-start.9 = (bf16[2048,256]{1,0:T(8,128)(2,1)S(1)}, bf16[2048,256]{1,0:T(8,128)(2,1)S(1)}, u32[]{:S(2)}, u32[]{:S(2)}) collective-permute-start(bf16[2048,256]{1,0:T(8,128)(2,1)S(1)} %collective-permute-done.8.refs_11_), channel_id=1, source_target_pairs={{0,16},{16,0},{32,48},{48,32},{64,80},{80,64},{96,112},{112,96},{1... | collective-permute-start | bytes 3145736 | tf_op jit(solution)/shard_map/ppermute | solution.py:238
  31.7 42.0 %all-to-all-start = ((bf16[16,32,512]{2,1,0:T(8,128)(2,1)}), bf16[16,32,512]{2,1,0:T(8,128)(2,1)}, u32[]{:S(2)}, u32[]{:S(2)}) async-start(bf16[16,32,512]{2,1,0:T(8,128)(2,1)} %bitcast.28), calls=%async_computation | async-start | bytes 1048576 | tf_op jit(solution)/shard_map/all_to_all | solution.py:366
  40.8 12.9 %collective-permute-start.7 = (bf16[32,4096]{1,0:T(8,128)(2,1)S(1)}, bf16[32,4096]{1,0:T(8,128)(2,1)S(1)}, u32[]{:S(2)}, u32[]{:S(2)}) collective-permute-start(bf16[32,4096]{1,0:T(8,128)(2,1)S(1)} %get-tuple-element.69), channel_id=1, source_target_pairs={{0,8},{1,9},{2,10},{3,11},{4,12},{5,13},{6,14},{7,15},{8,0},{9,1},... | collective-permute-start | bytes 786440 | tf_op jit(solution)/shard_map/ppermute | solution.py:220
  42.8 17.9 %collective-permute-start.6 = (bf16[256,512]{1,0:T(8,128)(2,1)}, bf16[256,512]{1,0:T(8,128)(2,1)S(1)}, u32[]{:S(2)}, u32[]{:S(2)}) collective-permute-start(bf16[256,512]{1,0:T(8,128)(2,1)} %collective-permute-done.4.refs_5_), channel_id=1, source_target_pairs={{0,1},{1,2},{2,3},{3,4},{4,5},{5,6},{6,7},{7,0},{8,9},{9,10},{10,1... | collective-permute-start | bytes 786440 | tf_op jit(solution)/shard_map/ppermute | solution.py:224
  60.7 2.2 %copy-start = (bf16[8192,256]{1,0:T(8,128)(2,1)S(1)}, bf16[8192,256]{1,0:T(8,128)(2,1)}, u32[]{:S(2)}) copy-start(bf16[8192,256]{1,0:T(8,128)(2,1)} %refs_10_.1) | copy-start | bytes 12582916
  68.0 0.7 copy-start.2
  68.7 0.7 copy-start.4
  69.4 4.3 %collective-permute-start.11 = (f32[64,256]{1,0:T(8,128)S(1)}, f32[64,256]{1,0:T(8,128)S(1)}, u32[]{:S(2)}, u32[]{:S(2)}) collective-permute-start(f32[64,256]{1,0:T(8,128)S(1)} %get-tuple-element.48), channel_id=1, source_target_pairs={{0,8},{1,9},{2,10},{3,11},{4,12},{5,13},{6,14},{7,15},{8,0},{9,1},... | collective-permute-start | bytes 196616 | tf_op jit(solution)/shard_map/ppermute | solution.py:220
  74.4 15.2 %all-to-all-start.1 = ((bf16[8,64,256]{2,1,0:T(8,128)(2,1)}), bf16[8,64,256]{2,1,0:T(8,128)(2,1)S(1)}, u32[]{:S(2)}, u32[]{:S(2)}) async-start(bf16[8,64,256]{2,1,0:T(8,128)(2,1)} %broadcast_in_dim.21), calls=%async_computation.1 | async-start | bytes 524288 | tf_op jit(solution)/shard_map/all_to_all | solution.py:260
  79.0 19.7 %collective-permute-start.10 = (f32[256,256]{1,0:T(8,128)}, f32[256,256]{1,0:T(8,128)S(1)}, u32[]{:S(2)}, u32[]{:S(2)}) collective-permute-start(f32[256,256]{1,0:T(8,128)} %copy-done.4), channel_id=1, source_target_pairs={{0,8},{1,9},{2,10},{3,11},{4,12},{5,13},{6,14},{7,15},{8,0},{9,1},... | collective-permute-start | bytes 786440 | tf_op jit(solution)/shard_map/ppermute | solution.py:220
  89.6 11.5 %collective-permute-start.13 = (bf16[8,2,32,256]{3,2,1,0:T(8,128)(2,1)S(1)}, bf16[8,2,32,256]{3,2,1,0:T(8,128)(2,1)S(1)}, u32[]{:S(2)}, u32[]{:S(2)}) collective-permute-start(bf16[8,2,32,256]{3,2,1,0:T(8,128)(2,1)S(1)} %bitcast.25), channel_id=1, source_target_pairs={{0,16},{16,32},{32,48},{48,64},{64,80},{80,96},{96,112},{112,128},... | collective-permute-start | bytes 786440 | tf_op jit(solution)/shard_map/ppermute | solution.py:230
  91.6 9.6 %collective-permute-start.12 = (bf16[8,32,256]{2,1,0:T(8,128)(2,1)S(1)}, bf16[8,32,256]{2,1,0:T(8,128)(2,1)S(1)}, u32[]{:S(2)}, u32[]{:S(2)}) collective-permute-start(bf16[8,32,256]{2,1,0:T(8,128)(2,1)S(1)} %slice_bitcast_fusion), channel_id=1, source_target_pairs={{0,32},{16,48},{32,64},{48,80},{64,96},{80,112},{96,128},{112,144}... | collective-permute-start | bytes 393224 | tf_op jit(solution)/shard_map/ppermute | solution.py:230
  96.4 48.0 %collective-permute-start.18 = (bf16[16,32,512]{2,1,0:T(8,128)(2,1)}, bf16[16,32,512]{2,1,0:T(8,128)(2,1)S(1)}, u32[]{:S(2)}, u32[]{:S(2)}) collective-permute-start(bf16[16,32,512]{2,1,0:T(8,128)(2,1)} %all-to-all-done), channel_id=1, source_target_pairs={{0,64},{16,80},{32,96},{48,112},{64,128},{80,144},{96,160},{112,17... | collective-permute-start | bytes 1572872 | tf_op jit(solution)/shard_map/ppermute | solution.py:234
  98.1 46.3 %collective-permute-start.19 = (bf16[16,32,512]{2,1,0:T(8,128)(2,1)}, bf16[16,32,512]{2,1,0:T(8,128)(2,1)S(1)}, u32[]{:S(2)}, u32[]{:S(2)}) collective-permute-start(bf16[16,32,512]{2,1,0:T(8,128)(2,1)} %all-to-all-done), channel_id=1, source_target_pairs={{0,192},{16,208},{32,224},{48,240},{64,0},{80,16},{96,32},{112,48}... | collective-permute-start | bytes 1572872 | tf_op jit(solution)/shard_map/ppermute | solution.py:234
  98.7 45.7 %collective-permute-start.20 = (bf16[16,32,512]{2,1,0:T(8,128)(2,1)}, bf16[16,32,512]{2,1,0:T(8,128)(2,1)S(1)}, u32[]{:S(2)}, u32[]{:S(2)}) collective-permute-start(bf16[16,32,512]{2,1,0:T(8,128)(2,1)} %all-to-all-done), channel_id=1, source_target_pairs={{0,128},{16,144},{32,160},{48,176},{64,192},{80,208},{96,224},{112... | collective-permute-start | bytes 1572872 | tf_op jit(solution)/shard_map/ppermute | solution.py:234
  101.1 1.0 copy-start.3
  123.8 6.3 %collective-permute-start.14 = (bf16[256,256]{1,0:T(8,128)(2,1)S(1)}, bf16[256,256]{1,0:T(8,128)(2,1)S(1)}, u32[]{:S(2)}, u32[]{:S(2)}) collective-permute-start(bf16[256,256]{1,0:T(8,128)(2,1)S(1)} %shard_map.47.refs_0_), channel_id=1, source_target_pairs={{0,1},{1,2},{2,3},{3,4},{4,5},{5,6},{6,7},{7,0},{8,9},{9,10},{10,1... | collective-permute-start | bytes 393224 | tf_op jit(solution)/shard_map/ppermute | solution.py:224
  124.5 5.6 %collective-permute-start.15 = (bf16[256,256]{1,0:T(8,128)(2,1)S(1)}, bf16[256,256]{1,0:T(8,128)(2,1)S(1)}, u32[]{:S(2)}, u32[]{:S(2)}) collective-permute-start(bf16[256,256]{1,0:T(8,128)(2,1)S(1)} %shard_map.47.refs_0_), channel_id=1, source_target_pairs={{0,7},{1,0},{2,1},{3,2},{4,3},{5,4},{6,5},{7,6},{8,15},{9,8},{10,9... | collective-permute-start | bytes 393224 | tf_op jit(solution)/shard_map/ppermute | solution.py:224
  130.1 6.7 %collective-permute-start.16 = (bf16[256,256]{1,0:T(8,128)(2,1)S(1)}, bf16[256,256]{1,0:T(8,128)(2,1)S(1)}, u32[]{:S(2)}, u32[]{:S(2)}) collective-permute-start(bf16[256,256]{1,0:T(8,128)(2,1)S(1)} %collective-permute-done.14.refs_1_), channel_id=1, source_target_pairs={{0,1},{1,2},{2,3},{3,4},{4,5},{5,6},{6,7},{7,0},{8,9},{9,10},{10,1... | collective-permute-start | bytes 393224 | tf_op jit(solution)/shard_map/ppermute | solution.py:224
  130.1 6.7 %collective-permute-start.17 = (bf16[256,256]{1,0:T(8,128)(2,1)S(1)}, bf16[256,256]{1,0:T(8,128)(2,1)S(1)}, u32[]{:S(2)}, u32[]{:S(2)}) collective-permute-start(bf16[256,256]{1,0:T(8,128)(2,1)S(1)} %collective-permute-done.15.refs_2_), channel_id=1, source_target_pairs={{0,7},{1,0},{2,1},{3,2},{4,3},{5,4},{6,5},{7,6},{8,15},{9,8},{10,9... | collective-permute-start | bytes 393224 | tf_op jit(solution)/shard_map/ppermute | solution.py:224
  136.8 7.6 %collective-permute-start.21 = (bf16[256,256]{1,0:T(8,128)(2,1)S(1)}, bf16[256,256]{1,0:T(8,128)(2,1)S(1)}, u32[]{:S(2)}, u32[]{:S(2)}) collective-permute-start(bf16[256,256]{1,0:T(8,128)(2,1)S(1)} %collective-permute-done.16.refs_3_), channel_id=1, source_target_pairs={{0,1},{1,2},{2,3},{3,4},{4,5},{5,6},{6,7},{7,0},{8,9},{9,10},{10,1... | collective-permute-start | bytes 393224 | tf_op jit(solution)/shard_map/ppermute | solution.py:224
  136.8 7.6 %collective-permute-start.22 = (bf16[256,256]{1,0:T(8,128)(2,1)S(1)}, bf16[256,256]{1,0:T(8,128)(2,1)S(1)}, u32[]{:S(2)}, u32[]{:S(2)}) collective-permute-start(bf16[256,256]{1,0:T(8,128)(2,1)S(1)} %collective-permute-done.17.refs_4_), channel_id=1, source_target_pairs={{0,7},{1,0},{2,1},{3,2},{4,3},{5,4},{6,5},{7,6},{8,15},{9,8},{10,9... | collective-permute-start | bytes 393224 | tf_op jit(solution)/shard_map/ppermute | solution.py:224
  144.6 29.3 %collective-permute-start.31 = (bf16[4,16,32,512]{3,2,1,0:T(8,128)(2,1)S(1)}, bf16[4,16,32,512]{3,2,1,0:T(8,128)(2,1)S(1)}, u32[]{:S(2)}, u32[]{:S(2)}) collective-permute-start(bf16[4,16,32,512]{3,2,1,0:T(8,128)(2,1)S(1)} %bitcast_dynamic-update-slice_fusion.refs_15_), channel_id=1, source_target_pairs={{0,16},{16,0},{32,48},{48,32},{64,80},{80,64},{96,112},{112,96},{1... | collective-permute-start | bytes 6291464 | tf_op jit(solution)/shard_map/ppermute | solution.py:238
  144.7 6.7 %collective-permute-start.24 = (bf16[256,256]{1,0:T(8,128)(2,1)S(1)}, bf16[256,256]{1,0:T(8,128)(2,1)S(1)}, u32[]{:S(2)}, u32[]{:S(2)}) collective-permute-start(bf16[256,256]{1,0:T(8,128)(2,1)S(1)} %shard_map.47.refs_0_), channel_id=1, source_target_pairs={{0,8},{1,9},{2,10},{3,11},{4,12},{5,13},{6,14},{7,15},{8,0},{9,1},... | collective-permute-start | bytes 393224 | tf_op jit(solution)/shard_map/ppermute | solution.py:220
  151.4 6.4 %collective-permute-start.25 = (bf16[256,256]{1,0:T(8,128)(2,1)S(1)}, bf16[256,256]{1,0:T(8,128)(2,1)S(1)}, u32[]{:S(2)}, u32[]{:S(2)}) collective-permute-start(bf16[256,256]{1,0:T(8,128)(2,1)S(1)} %collective-permute-done.24.refs_8_), channel_id=1, source_target_pairs={{0,1},{1,2},{2,3},{3,4},{4,5},{5,6},{6,7},{7,0},{8,9},{9,10},{10,1... | collective-permute-start | bytes 393224 | tf_op jit(solution)/shard_map/ppermute | solution.py:224
  151.4 6.4 %collective-permute-start.26 = (bf16[256,256]{1,0:T(8,128)(2,1)S(1)}, bf16[256,256]{1,0:T(8,128)(2,1)S(1)}, u32[]{:S(2)}, u32[]{:S(2)}) collective-permute-start(bf16[256,256]{1,0:T(8,128)(2,1)S(1)} %collective-permute-done.24.refs_8_), channel_id=1, source_target_pairs={{0,7},{1,0},{2,1},{3,2},{4,3},{5,4},{6,5},{7,6},{8,15},{9,8},{10,9... | collective-permute-start | bytes 393224 | tf_op jit(solution)/shard_map/ppermute | solution.py:224
  157.8 6.2 %collective-permute-start.27 = (bf16[256,256]{1,0:T(8,128)(2,1)S(1)}, bf16[256,256]{1,0:T(8,128)(2,1)S(1)}, u32[]{:S(2)}, u32[]{:S(2)}) collective-permute-start(bf16[256,256]{1,0:T(8,128)(2,1)S(1)} %collective-permute-done.25.refs_9_), channel_id=1, source_target_pairs={{0,1},{1,2},{2,3},{3,4},{4,5},{5,6},{6,7},{7,0},{8,9},{9,10},{10,1... | collective-permute-start | bytes 393224 | tf_op jit(solution)/shard_map/ppermute | solution.py:224
  157.8 6.2 %collective-permute-start.28 = (bf16[256,256]{1,0:T(8,128)(2,1)S(1)}, bf16[256,256]{1,0:T(8,128)(2,1)S(1)}, u32[]{:S(2)}, u32[]{:S(2)}) collective-permute-start(bf16[256,256]{1,0:T(8,128)(2,1)S(1)} %collective-permute-done.26.refs_10_), channel_id=1, source_target_pairs={{0,7},{1,0},{2,1},{3,2},{4,3},{5,4},{6,5},{7,6},{8,15},{9,8},{10,9... | collective-permute-start | bytes 393224 | tf_op jit(solution)/shard_map/ppermute | solution.py:224
  164.0 7.6 %collective-permute-start.29 = (bf16[256,256]{1,0:T(8,128)(2,1)S(1)}, bf16[256,256]{1,0:T(8,128)(2,1)S(1)}, u32[]{:S(2)}, u32[]{:S(2)}) collective-permute-start(bf16[256,256]{1,0:T(8,128)(2,1)S(1)} %collective-permute-done.27.refs_11_), channel_id=1, source_target_pairs={{0,1},{1,2},{2,3},{3,4},{4,5},{5,6},{6,7},{7,0},{8,9},{9,10},{10,1... | collective-permute-start | bytes 393224 | tf_op jit(solution)/shard_map/ppermute | solution.py:224
  164.6 7.0 %collective-permute-start.30 = (bf16[256,256]{1,0:T(8,128)(2,1)S(1)}, bf16[256,256]{1,0:T(8,128)(2,1)S(1)}, u32[]{:S(2)}, u32[]{:S(2)}) collective-permute-start(bf16[256,256]{1,0:T(8,128)(2,1)S(1)} %collective-permute-done.28.refs_12_), channel_id=1, source_target_pairs={{0,7},{1,0},{2,1},{3,2},{4,3},{5,4},{6,5},{7,6},{8,15},{9,8},{10,9... | collective-permute-start | bytes 393224 | tf_op jit(solution)/shard_map/ppermute | solution.py:224
  167.2 6.7 %collective-permute-start.23 = (bf16[256,256]{1,0:T(8,128)(2,1)S(1)}, bf16[256,256]{1,0:T(8,128)(2,1)S(1)}, u32[]{:S(2)}, u32[]{:S(2)}) collective-permute-start(bf16[256,256]{1,0:T(8,128)(2,1)S(1)} %collective-permute-done.21.refs_5_), channel_id=1, source_target_pairs={{0,1},{1,2},{2,3},{3,4},{4,5},{5,6},{6,7},{7,0},{8,9},{9,10},{10,1... | collective-permute-start | bytes 393224 | tf_op jit(solution)/shard_map/ppermute | solution.py:224
  171.6 6.2 %collective-permute-start.32 = (bf16[256,256]{1,0:T(8,128)(2,1)S(1)}, bf16[256,256]{1,0:T(8,128)(2,1)S(1)}, u32[]{:S(2)}, u32[]{:S(2)}) collective-permute-start(bf16[256,256]{1,0:T(8,128)(2,1)S(1)} %collective-permute-done.29.refs_13_), channel_id=1, source_target_pairs={{0,1},{1,2},{2,3},{3,4},{4,5},{5,6},{6,7},{7,0},{8,9},{9,10},{10,1... | collective-permute-start | bytes 393224 | tf_op jit(solution)/shard_map/ppermute | solution.py:224

commit v4 on v3

--- a/solution.py
+++ b/solution.py
@@ -10,21 +10,30 @@
 WIN1 = 512
 WIN2 = 32
 BLK = 128
-GROUP = 8
+GROUP = 16
+MIX = 16
 LOW = -1e30
 LANES = (((1,), (1,)), ((), ()))
 
 
-def pick(source, which, lanes):
+OWN, NEAR, FAR = 0, 2, 4
+
+
+def pick(gathered, source, which, lanes):
     places = slice((which % 2) * 4, (which % 2) * 4 + 4)
-    found = source[places, :, lanes] if len(source.shape) == 3 else source[places, which // 2, :, lanes]
-    return found.reshape(HEAD, BLK)
+    return gathered[places, source + which // 2, :, lanes].reshape(HEAD, BLK)
 
 
 def attend_kernel(
-    seq_ref, mine_ref, sent_ref, far_ref, near_ref, own_ref, out_ref,
-    k2f, v2f, ktile, vtile, kpair, vpair, s_scr, mx_scr, mcb_scr,
+    seq_ref, mine_any, sent_any, all_ref, out_ref,
+    k2f, v2f, ktile, vtile, kpair, vpair, s_scr, mx_scr, mcb_scr, mine_ref, sent_ref, sems,
 ):
+    fetches = [
+        pltpu.make_async_copy(source, target, sems.at[k])
+        for k, (source, target) in enumerate(((mine_any, mine_ref), (sent_any, sent_ref)))
+    ]
+    for fetch in fetches:
+        fetch.start()
     tok = mine_ref.shape[0]
     heads = mine_ref.shape[1] // HEAD
     blocks = tok // BLK
@@ -33,20 +42,22 @@
     start = seq == 0
 
     for t in range(6):
-        source = (far_ref, near_ref, own_ref)[t // 2]
+        source = (FAR, NEAR, OWN)[t // 2]
         lanes = slice((t % 2) * BLK, (t % 2 + 1) * BLK)
-        ktile[t] = pick(source, 0, lanes)
-        vtile[t] = pick(source, 1, lanes).astype(jnp.float32).T.astype(jnp.bfloat16)
+        ktile[t] = pick(all_ref, source, 0, lanes)
+        vtile[t] = pick(all_ref, source, 1, lanes).astype(jnp.float32).T.astype(jnp.bfloat16)
     for scr, which in ((k2f, 2), (v2f, 3)):
-        scr[:BLK] = pick(near_ref, which, slice(tok - BLK, tok)).astype(jnp.float32).T
+        scr[:BLK] = pick(all_ref, NEAR, which, slice(tok - BLK, tok)).astype(jnp.float32).T
         for t in range(blocks):
-            scr[(t + 1) * BLK:(t + 2) * BLK] = pick(own_ref, which, slice(t * BLK, (t + 1) * BLK)).astype(jnp.float32).T
+            scr[(t + 1) * BLK:(t + 2) * BLK] = pick(all_ref, OWN, which, slice(t * BLK, (t + 1) * BLK)).astype(jnp.float32).T
 
     @pl.when(start)
     def _():
         k2f[:BLK] = jnp.broadcast_to(k2f[BLK:BLK + 1], (BLK, HEAD))
         v2f[:BLK] = jnp.zeros((BLK, HEAD), jnp.float32)
 
+    for fetch in fetches:
+        fetch.wait()
     row = lax.broadcasted_iota(jnp.int32, (BLK, BLK), 0)
     col = lax.broadcasted_iota(jnp.int32, (BLK, BLK), 1)
     early = col > row
@@ -108,18 +119,21 @@
                 for p in range(4)
             ]
 
-        def mix(lag, carry):
+        def mix(step, carry):
             acc, tot = carry
-            raised = raised_at(lag)
-            tot = tot + ((raised[0] + raised[1]) + (raised[2] + raised[3]))
-            split = [jnp.where(early, raised[0], 0.0), jnp.where(early, 0.0, raised[0])]
-            w = jnp.concatenate([part.astype(jnp.bfloat16) for part in split + raised[1:]], axis=1)
-            m = jnp.dot(w, vpair[...], preferred_element_type=jnp.float32)
-            acc = acc + m * v2f[pl.ds(BLK + base - lag, BLK), :]
+            ws = []
+            for g in range(MIX):
+                raised = raised_at(step * MIX + g)
+                tot = tot + ((raised[0] + raised[1]) + (raised[2] + raised[3]))
+                split = [jnp.where(early, raised[0], 0.0), jnp.where(early, 0.0, raised[0])]
+                ws.append(jnp.concatenate([part.astype(jnp.bfloat16) for part in split + raised[1:]], axis=1))
+            m = jnp.dot(jnp.concatenate(ws, axis=0), vpair[...], preferred_element_type=jnp.float32)
+            for g in range(MIX):
+                acc = acc + m[g * BLK:(g + 1) * BLK] * v2f[pl.ds(BLK + base - step * MIX - g, BLK), :]
             return acc, tot
 
         zero = jnp.zeros((BLK, HEAD), jnp.float32)
-        acc, tot = lax.fori_loop(0, WIN2, mix, (zero, zero), unroll=4)
+        acc, tot = lax.fori_loop(0, WIN2 // MIX, mix, (zero, zero))
         last = raised_at(WIN2 - 1)
         spare = jnp.where(jnp.logical_and(start, b == 0), jnp.maximum(WIN2 - 1 - row, 0), 0)
         tot = tot - spare.astype(jnp.float32) * ((last[0] + last[1]) + (last[2] + last[3]))
@@ -134,12 +148,14 @@
     return [pl.BlockSpec(memory_space=pltpu.VMEM)] * count
 
 
-def attend(seq, mine, sent, far, near, own):
+def attend(seq, mine, sent, gathered):
     tok = mine.shape[0]
     return pl.pallas_call(
         attend_kernel,
         out_shape=jax.ShapeDtypeStruct(mine.shape, jnp.bfloat16),
-        in_specs=[pl.BlockSpec(memory_space=pltpu.SMEM)] + in_vmem(5),
+        in_specs=[pl.BlockSpec(memory_space=pltpu.SMEM)]
+        + [pl.BlockSpec(memory_space=pltpu.HBM)] * 2
+        + in_vmem(1),
         out_specs=in_vmem(1)[0],
         scratch_shapes=[
             pltpu.VMEM((BLK + tok, HEAD), jnp.float32),
@@ -151,29 +167,40 @@
             pltpu.VMEM((WIN2, BLK, 4 * BLK), jnp.float32),
             pltpu.VMEM((4, BLK, BLK), jnp.float32),
             pltpu.VMEM((4, BLK, BLK), jnp.float32),
+            pltpu.VMEM(mine.shape, jnp.float32),
+            pltpu.VMEM(mine.shape, jnp.float32),
+            pltpu.SemaphoreType.DMA((2,)),
         ],
         compiler_params=pltpu.CompilerParams(vmem_limit_bytes=24 * 1024 * 1024),
-    )(seq, mine, sent, far, near, own)
+    )(seq, mine, sent, gathered)
 
 
 OFFSETS = (0, -1, 1, -2, 2, -3, 3, -4)
+OWN_WEIGHTS = 10
 
 
 def project_kernel(spot_ref, *refs):
-    shards, kv_own, kv_part, own_any, same_ref, twin_ref = refs[:8], *refs[8:13]
-    kv_out, mine_out, theirs_out, own_ref, sem = refs[13:]
+    sources = refs[:13]
+    kv_out, mine_any, theirs_any = refs[13:16]
+    held = refs[16:29]
+    mine_out, theirs_out, sems = refs[29:]
+    shards, kv_own, kv_part, own_ref, same_ref, twin_ref = held[:8], *held[8:]
     depth = shards[0].shape[1]
     half = own_ref.shape[0]
     row, core = spot_ref[0] >> 3, spot_ref[1]
-    fetch = pltpu.make_async_copy(
-        own_any.at[pl.ds(pl.multiple_of(row * half, half), half), :], own_ref, sem
-    )
-    fetch.start()
+    fetches = []
+    for k, (source, target) in enumerate(zip(sources, held)):
+        if k == OWN_WEIGHTS:
+            source = source.at[pl.ds(pl.multiple_of(row * half, half), half), :]
+        fetches.append(pltpu.make_async_copy(source, target, sems.at[k]))
+        fetches[k].start()
 
     def from_place(offset, count):
         spot = (spot_ref[0] + offset) & (count - 1)
         return pl.ds(pl.multiple_of(spot * depth, depth), depth)
 
+    for k in range(OWN_WEIGHTS):
+        fetches[k].wait()
     parts = kv_own.shape[0]
     for weight, side in ((kv_own, row), (kv_part, 1 - row)):
         total = None
@@ -182,6 +209,8 @@
             new = lax.dot_general(cols, shard[...], LANES, preferred_element_type=jnp.float32)
             total = new if total is None else total + new
         kv_out[pl.ds(pl.multiple_of(side * parts, parts), parts), :] = total
+    for k in range(OWN_WEIGHTS, len(held)):
+        fetches[k].wait()
     theirs_out[...] = jnp.zeros(theirs_out.shape, jnp.float32)
     for offset, shard in zip(OFFSETS, shards):
         low = from_place(offset, 4)
@@ -191,28 +220,33 @@
             @pl.when(upper == side)
             def _():
                 theirs_out[...] += jnp.dot(shard[...], ref[low, :], preferred_element_type=jnp.float32)
-    fetch.wait()
+    send = pltpu.make_async_copy(theirs_out, theirs_any, sems.at[len(held)])
+    send.start()
     total = None
     for offset, shard in zip(OFFSETS, shards):
         new = jnp.dot(shard[...], own_ref[from_place(offset, 8), :], preferred_element_type=jnp.float32)
         total = new if total is None else total + new
     mine_out[...] = total
+    keep = pltpu.make_async_copy(mine_out, mine_any, sems.at[len(held) + 1])
+    keep.start()
+    send.wait()
+    keep.wait()
 
 
 def project(spots, arrays, shapes):
-    specs = in_vmem(len(arrays))
-    specs[10] = pl.BlockSpec(memory_space=pl.ANY)
-    own = arrays[10]
+    far_off = pl.BlockSpec(memory_space=pltpu.HBM)
+    own = arrays[OWN_WEIGHTS]
+    kept = [array.shape for array in arrays]
+    kept[OWN_WEIGHTS] = (own.shape[0] // 2, own.shape[1])
     return pl.pallas_call(
         project_kernel,
         out_shape=tuple(jax.ShapeDtypeStruct(shape, jnp.float32) for shape in shapes),
-        in_specs=[pl.BlockSpec(memory_space=pltpu.SMEM)] + specs,
-        out_specs=tuple(in_vmem(len(shapes))),
-        scratch_shapes=[
-            pltpu.VMEM((own.shape[0] // 2, own.shape[1]), own.dtype),
-            pltpu.SemaphoreType.DMA,
-        ],
-        compiler_params=pltpu.CompilerParams(vmem_limit_bytes=24 * 1024 * 1024),
+        in_specs=[pl.BlockSpec(memory_space=pltpu.SMEM)] + [far_off] * len(arrays),
+        out_specs=(in_vmem(1)[0], far_off, far_off),
+        scratch_shapes=[pltpu.VMEM(shape, own.dtype) for shape in kept]
+        + [pltpu.VMEM(shape, jnp.float32) for shape in shapes[1:]]
+        + [pltpu.SemaphoreType.DMA((len(arrays) + 2,))],
+        compiler_params=pltpu.CompilerParams(vmem_limit_bytes=60 * 1024 * 1024),
     )(spots, *arrays)
 
 
@@ -268,7 +302,7 @@
     rows, width = w_out.shape
     part = rows // 8
     piece = lax.dynamic_slice_in_dim(w_out, (2 * x + core) * part, part, 0)
-    return piece.reshape(part, 16, width // 16).transpose(1, 0, 2)
+    return piece.reshape(part, 2, 8, width // 16).transpose(2, 1, 0, 3)
 
 
 def owned_columns(piece, seq, tie):
@@ -282,66 +316,67 @@
     return held, other_core(held), tie
 
 
-def two_rings(value):
-    other = swap_rows(value)
-    rings = []
-    for start in (value, other):
-        rings.append(z_ring(start))
-    return rings
-
-
-def gather_rows(spot_ref, held, twin, place, out, slot):
+def gather_rows(spot_ref, held, twin, spot, out, slot):
     core = spot_ref[1]
-    part = held.shape[2]
+    part = held.shape[3]
+    cols = held.shape[4]
     for x in range(4):
         for source, side in ((held, core), (twin, 1 - core)):
             low = pl.multiple_of(x * 2 * part + side * part, part)
-            out[slot, pl.ds(low, part), :] = source[x, place]
+            for half in range(2):
+                out[slot, pl.ds(low, part), half * cols:(half + 1) * cols] = source[x, spot, half]
 
 
 def finish_kernel(spot_ref, *refs):
-    mine, other, held, twin = refs[:8], refs[8:15], refs[15], refs[16]
-    part_out, tail_out, w_scr = refs[17:]
+    values, held, twin = refs[:7], refs[7], refs[8]
+    part_out, tail_out, w_scr = refs[9:]
     total = None
-    for side, values in enumerate((mine, other)):
-        for k, value in enumerate(values):
-            place = ((spot_ref[0] & 8) ^ (8 * side)) | ((spot_ref[0] + OFFSETS[k]) & 7)
-            slot = 8 * side + k
-            gather_rows(spot_ref, held, twin, place, w_scr, slot)
-            new = jnp.dot(value[...], w_scr[slot], preferred_element_type=jnp.float32)
-            total = new if total is None else total + new
+    for k, value in enumerate(values):
+        gather_rows(spot_ref, held, twin, (spot_ref[0] + OFFSETS[k]) & 7, w_scr, k)
+        new = jnp.dot(value[...], w_scr[k], preferred_element_type=jnp.float32)
+        total = new if total is None else total + new
     part_out[...] = total
-    place = ((spot_ref[0] & 8) ^ 8) | ((spot_ref[0] + OFFSETS[7]) & 7)
-    gather_rows(spot_ref, held, twin, place, tail_out, 0)
-
-
-def close_kernel(part_ref, tail_ref, last_ref, out_ref):
+    gather_rows(spot_ref, held, twin, (spot_ref[0] + OFFSETS[7]) & 7, tail_out, 0)
+
+
+def close_kernel(spot_ref, part_ref, tail_ref, last_ref, mine_out, theirs_out):
     total = part_ref[...] + jnp.dot(last_ref[...], tail_ref[0], preferred_element_type=jnp.float32)
-    out_ref[...] = total.astype(jnp.bfloat16)
-
-
-def finish(spots, mine, other, held, twin):
-    tok, feats = mine[0].shape
+    cols = mine_out.shape[1]
+    for row in range(2):
+
+        @pl.when((spot_ref[0] >> 3) == row)
+        def _():
+            mine_out[...] = total[:, row * cols:(row + 1) * cols]
+            theirs_out[...] = total[:, (1 - row) * cols:(2 - row) * cols].astype(jnp.bfloat16)
+
+
+def finish(spots, values, held, twin):
+    tok, feats = values[0].shape
     cols = held.shape[-1]
     limit = pltpu.CompilerParams(vmem_limit_bytes=24 * 1024 * 1024)
+    smem = [pl.BlockSpec(memory_space=pltpu.SMEM)]
     part, tail = pl.pallas_call(
         finish_kernel,
         out_shape=(
+            jax.ShapeDtypeStruct((tok, 2 * cols), jnp.float32),
+            jax.ShapeDtypeStruct((1, feats, 2 * cols), held.dtype),
+        ),
+        in_specs=smem + in_vmem(9),
+        out_specs=tuple(in_vmem(2)),
+        scratch_shapes=[pltpu.VMEM((7, feats, 2 * cols), held.dtype)],
+        compiler_params=limit,
+    )(spots, *values[:7], held, twin)
+    mine, theirs = pl.pallas_call(
+        close_kernel,
+        out_shape=(
             jax.ShapeDtypeStruct((tok, cols), jnp.float32),
-            jax.ShapeDtypeStruct((1, feats, cols), held.dtype),
+            jax.ShapeDtypeStruct((tok, cols), jnp.bfloat16),
         ),
-        in_specs=[pl.BlockSpec(memory_space=pltpu.SMEM)] + in_vmem(17),
+        in_specs=smem + in_vmem(3),
         out_specs=tuple(in_vmem(2)),
-        scratch_shapes=[pltpu.VMEM((15, feats, cols), held.dtype)],
         compiler_params=limit,
-    )(spots, *mine, *other[:7], held, twin)
-    return pl.pallas_call(
-        close_kernel,
-        out_shape=jax.ShapeDtypeStruct((tok, cols), jnp.bfloat16),
-        in_specs=in_vmem(3),
-        out_specs=in_vmem(1)[0],
-        compiler_params=limit,
-    )(part, tail, other[7])
+    )(spots, part, tail, values[7])
+    return (mine + swap_rows(theirs).astype(jnp.float32)).astype(jnp.bfloat16)
 
 
 def body(tokens, w_query, w_keyval, w_out):
@@ -363,7 +398,7 @@
     piece, shards[5], shards[6] = lax.optimization_barrier(
         (owned_piece(w_out, seq), shards[5], shards[6])
     )
-    piece = lax.all_to_all(piece, "head", 0, 0, tiled=True)
+    piece = lax.all_to_all(piece, "head", 0, 0, tiled=True, axis_index_groups=ROWS)
     kv_part, q_mine, q_theirs = project(
         spots,
         (*shards, kv_own, kv_part, w_query, q_same, q_twin),
@@ -372,13 +407,14 @@
     kv = (kv_part + swap_rows(kv_part)).astype(jnp.bfloat16)
     piece, kv = lax.optimization_barrier((piece, kv))
     q_sent = swap_rows(q_theirs)
-    keyval = sent_to_row(kv).reshape(8, 2, kv_flat.shape[0], tok_rows)
-    near = along_seq(keyval, 1)
-    far = along_seq(keyval[:, 0], 2)
-    attended = attend(seq.reshape(1), q_mine, q_sent, far, near, keyval)
-    mine, other = two_rings(attended)
-    held, twin, mine[5] = owned_columns(piece, seq, mine[5])
-    return finish(spots, mine, other, held, twin)
+    near = along_seq(kv, 1)
+    far = along_seq(kv[:kv_flat.shape[0]], 2)
+    keyval = sent_to_row(jnp.concatenate([kv, near, far], axis=0))
+    keyval = keyval.reshape(8, 5, kv_flat.shape[0], tok_rows)
+    attended = attend(seq.reshape(1), q_mine, q_sent, keyval)
+    values = z_ring(attended)
+    held, twin, values[3] = owned_columns(piece, seq, values[3])
+    return finish(spots, values, held, twin)
 
 
 def solution(mesh):

time: 179 us -> 162 us (0.905)
  starting transfers between devices: 66.6 us -> 54 us
  local copies, waits for them, and re-layouts: 13 us -> 6.86 us
  Pallas kernels: 29.5 us -> 26.8 us
  waiting for transfers between devices: 69.3 us -> 71.6 us
  other arithmetic: 0.08 us -> 2.24 us
    ppermute x21 -> x14, starting transfers between devices: 33.6 us -> 24.3 us  [along_z(): lax.ppermute(value, 'head', [(i, i // 8 * 8 + (i + step) % 8) for i in ra...]
    pallas_call x1, Pallas kernels: 21.7 us -> 16.4 us  [attend(): pl.pallas_call(attend_kernel, out_shape=jax.ShapeDtypeStruct(mine.shape,...]
    all_to_all x1, waiting for transfers between devices: 9.18 us -> 13 us  [sent_to_row(): lax.all_to_all(jnp.broadcast_to(value[None], (8, *value.shape)), 'head',...]
    unnamed x10 -> x21, local copies, waits for them, and re-layouts: 4.55 us -> 0.89 us
    ppermute x21 -> x14, waiting for transfers between devices: 43.5 us -> 40.4 us  [along_z(): lax.ppermute(value, 'head', [(i, i // 8 * 8 + (i + step) % 8) for i in ra...]
    pallas_call x1, Pallas kernels: 5.09 us -> 7.71 us  [project(): pl.pallas_call(project_kernel, out_shape=tuple((jax.ShapeDtypeStruct(shap...]
    ppermute x2, waiting for transfers between devices: 0.32 us -> 2.93 us  [along_seq(): return lax.ppermute(value, 'seq', [(i, i + step) for i in range(16 - step)])]
    all_to_all x1, starting transfers between devices: 8.09 us -> 5.55 us  [body(): lax.all_to_all(piece, 'head', 0, 0, tiled=True, axis_index_groups=ROWS)]
  transfers between devices with their start and end apart: 35 -> 28, of which waited for: 18 -> 15; matrix products, arithmetic and copies ran while one was open for 4% -> 3% of each run, Pallas kernels for 16% -> 16%
where the time goes in v4:
time: 162 us
  waiting for transfers between devices  71.6 us (44%)
  starting transfers between devices  54 us (33%)
  Pallas kernels  26.8 us (17%)
  local copies, waits for them, and re-layouts  6.86 us (4%)
  other arithmetic  2.24 us (1%)
    ppermute x14, waiting for transfers between devices, along_z(): lax.ppermute(value, 'head', [(i, i // 8 * 8 + (i + step) % 8) for i in ra...  40.4 us
    ppermute x14, starting transfers between devices, along_z(): lax.ppermute(value, 'head', [(i, i // 8 * 8 + (i + step) % 8) for i in ra...  24.3 us
    pallas_call x1, Pallas kernels, attend(): pl.pallas_call(attend_kernel, out_shape=jax.ShapeDtypeStruct(mine.shape,...  16.4 us
    ppermute x5, waiting for transfers between devices, swap_rows(): return lax.ppermute(value, 'head', [(i, (i + 8) % 16) for i in range(16)])  15.1 us
    all_to_all x1, waiting for transfers between devices, sent_to_row(): lax.all_to_all(jnp.broadcast_to(value[None], (8, *value.shape)), 'head',...  13 us
    ppermute x5, starting transfers between devices, swap_rows(): return lax.ppermute(value, 'head', [(i, (i + 8) % 16) for i in range(16)])  8.26 us
    pallas_call x1, Pallas kernels, project(): pl.pallas_call(project_kernel, out_shape=tuple((jax.ShapeDtypeStruct(shap...  7.71 us
    ppermute x2, starting transfers between devices, along_seq(): return lax.ppermute(value, 'seq', [(i, i + step) for i in range(16 - step)])  7.03 us
  transfers between devices with their start and end apart: 28, of which 15 were waited for; matrix products, arithmetic and copies ran while one was open for 3% of the time, Pallas kernels for 16%

profile of v4, /device:TPU:2, one launch (start us, length us, event | category | flops | bytes accessed | tf_op | source)
XLA Modules:
  0.0 161.7 jit_solution(5336797276938039598)
XLA Ops:
  0.0 1.3 constant_dynamic-slice_fusion
  1.3 1.7 %collective-permute-start.8 = (bf16[2048,256]{1,0:T(8,128)(2,1)S(1)}, bf16[2048,256]{1,0:T(8,128)(2,1)S(1)}, u32[]{:S(2)}, u32[]{:S(2)}) collective-permute-start(bf16[2048,256]{1,0:T(8,128)(2,1)S(1)} %constant_dynamic-slice_fusion), channel_id=1, source_target_pairs={{0,8},{1,9},{2,10},{3,11},{4,12},{5,13},{6,14},{7,15},{8,0},{9,1},... | collective-permute-start | bytes 3145736 | tf_op jit(solution)/shard_map/ppermute | solution.py:254
  3.0 1.9 %collective-permute-start = (bf16[256,512]{1,0:T(8,128)(2,1)S(1)}, bf16[256,512]{1,0:T(8,128)(2,1)S(1)}, u32[]{:S(2)}, u32[]{:S(2)}) collective-permute-start(bf16[256,512]{1,0:T(8,128)(2,1)S(1)} %copy-done.4), channel_id=1, source_target_pairs={{0,1},{1,2},{2,3},{3,4},{4,5},{5,6},{6,7},{7,0},{8,9},{9,10},{10,1... | collective-permute-start | bytes 786440 | tf_op jit(solution)/shard_map/ppermute | solution.py:258
  4.9 3.9 %collective-permute-start.1 = (bf16[256,512]{1,0:T(8,128)(2,1)S(1)}, bf16[256,512]{1,0:T(8,128)(2,1)S(1)}, u32[]{:S(2)}, u32[]{:S(2)}) collective-permute-start(bf16[256,512]{1,0:T(8,128)(2,1)S(1)} %copy-done.4), channel_id=1, source_target_pairs={{0,7},{1,0},{2,1},{3,2},{4,3},{5,4},{6,5},{7,6},{8,15},{9,8},{10,9... | collective-permute-start | bytes 786440 | tf_op jit(solution)/shard_map/ppermute | solution.py:258
  8.9 6.0 %collective-permute-done.refs_1_ = bf16[256,512]{1,0:T(8,128)(2,1)S(1)} collective-permute-done((bf16[256,512]{1,0:T(8,128)(2,1)S(1)}, bf16[256,512]{1,0:T(8,128)(2,1)S(1)}, u32[]{:S(2)}, u32[]{:S(2)}) %collective-permute-start) | collective-permute-done | bytes 262176 | tf_op jit(solution)/shard_map/ppermute | solution.py:258
  14.9 0.1 collective-permute-start.2
  15.0 3.2 %collective-permute-start.3 = (bf16[256,512]{1,0:T(8,128)(2,1)S(1)}, bf16[256,512]{1,0:T(8,128)(2,1)}, u32[]{:S(2)}, u32[]{:S(2)}) collective-permute-start(bf16[256,512]{1,0:T(8,128)(2,1)S(1)} %collective-permute-done.1.refs_2_), channel_id=1, source_target_pairs={{0,7},{1,0},{2,1},{3,2},{4,3},{5,4},{6,5},{7,6},{8,15},{9,8},{10,9... | collective-permute-start | bytes 786440 | tf_op jit(solution)/shard_map/ppermute | solution.py:258
  18.2 5.2 %collective-permute-done.2.refs_3_ = bf16[256,512]{1,0:T(8,128)(2,1)S(1)} collective-permute-done((bf16[256,512]{1,0:T(8,128)(2,1)S(1)}, bf16[256,512]{1,0:T(8,128)(2,1)S(1)}, u32[]{:S(2)}, u32[]{:S(2)}) %collective-permute-start.2) | collective-permute-done | bytes 262176 | tf_op jit(solution)/shard_map/ppermute | solution.py:258
  23.4 0.0 collective-permute-done.3.refs_4_
  23.4 1.9 %collective-permute-start.4 = (bf16[256,512]{1,0:T(8,128)(2,1)S(1)}, bf16[256,512]{1,0:T(8,128)(2,1)}, u32[]{:S(2)}, u32[]{:S(2)}) collective-permute-start(bf16[256,512]{1,0:T(8,128)(2,1)S(1)} %collective-permute-done.2.refs_3_), channel_id=1, source_target_pairs={{0,1},{1,2},{2,3},{3,4},{4,5},{5,6},{6,7},{7,0},{8,9},{9,10},{10,1... | collective-permute-start | bytes 786440 | tf_op jit(solution)/shard_map/ppermute | solution.py:258
  25.3 1.3 collective-permute-start.5
  26.6 0.0 collective-permute-done.8.refs_11_
  26.6 0.0 collective-permute-start.9
  26.6 1.5 constant_dynamic-slice_fusion.1
  28.1 0.2 copy.6
  28.3 1.1 copy.8
  29.4 1.7 %collective-permute-done.4.refs_5_ = bf16[256,512]{1,0:T(8,128)(2,1)} collective-permute-done((bf16[256,512]{1,0:T(8,128)(2,1)S(1)}, bf16[256,512]{1,0:T(8,128)(2,1)}, u32[]{:S(2)}, u32[]{:S(2)}) %collective-permute-start.4) | collective-permute-done | bytes 262176 | tf_op jit(solution)/shard_map/ppermute | solution.py:258
  31.1 0.9 collective-permute-done.5.refs_6_
  32.0 5.6 %all-to-all-start = ((bf16[8,2,32,512]{3,2,1,0:T(8,128)(2,1)}), bf16[8,2,32,512]{3,2,1,0:T(8,128)(2,1)S(1)}, u32[]{:S(2)}, u32[]{:S(2)}) async-start(bf16[8,2,32,512]{3,2,1,0:T(8,128)(2,1)} %bitcast.21), calls=%async_computation | async-start | bytes 1048576 | tf_op jit(solution)/shard_map/all_to_all | solution.py:401
  37.6 0.8 dynamic-slice_bitcast_fusion
  38.3 1.6 collective-permute-start.7
  39.9 2.0 %collective-permute-start.6 = (bf16[256,512]{1,0:T(8,128)(2,1)}, bf16[256,512]{1,0:T(8,128)(2,1)S(1)}, u32[]{:S(2)}, u32[]{:S(2)}) collective-permute-start(bf16[256,512]{1,0:T(8,128)(2,1)} %collective-permute-done.4.refs_5_), channel_id=1, source_target_pairs={{0,1},{1,2},{2,3},{3,4},{4,5},{5,6},{6,7},{7,0},{8,9},{9,10},{10,1... | collective-permute-start | bytes 786440 | tf_op jit(solution)/shard_map/ppermute | solution.py:258
  41.9 0.6 pad_add_fusion.spot_ref
  42.5 3.9 %collective-permute-done.7.refs_9_ = bf16[32,4096]{1,0:T(8,128)(2,1)S(1)} collective-permute-done((bf16[32,4096]{1,0:T(8,128)(2,1)S(1)}, bf16[32,4096]{1,0:T(8,128)(2,1)S(1)}, u32[]{:S(2)}, u32[]{:S(2)}) %collective-permute-start.7) | collective-permute-done | bytes 262176 | tf_op jit(solution)/shard_map/ppermute | solution.py:254
  46.4 11.9 %collective-permute-done.6.refs_7_ = bf16[256,512]{1,0:T(8,128)(2,1)S(1)} collective-permute-done((bf16[256,512]{1,0:T(8,128)(2,1)}, bf16[256,512]{1,0:T(8,128)(2,1)S(1)}, u32[]{:S(2)}, u32[]{:S(2)}) %collective-permute-start.6) | collective-permute-done | bytes 262176 | tf_op jit(solution)/shard_map/ppermute | solution.py:258
  58.3 0.0 collective-permute-done.9.refs_12_
  58.3 0.7 copy-done.9
  59.0 7.7 %shard_map.46 = (f32[64,256]{1,0:T(8,128)}, f32[256,256]{1,0:T(8,128)}, f32[256,256]{1,0:T(8,128)}) custom-call(s32[2]{0:T(128)} %pad_add_fusion.spot_ref, bf16[256,512]{1,0:T(8,128)(2,1)} %refs_0_.1, bf16[256,512]{1,0:T(8,128)(2,1)} %copy-done.5, bf16[256,512]{1,0:T(8,128)(2,1)} %copy-done.6, bf16[256,512]{1,0:T(8,128)(2,1)} %copy-done.7, ...), custom_call_target="tpu_custom_call" | custom-call | tf_op jit(solution)/shard_map/pallas_call | solution.py:241
  66.7 1.7 %collective-permute-start.11 = (f32[64,256]{1,0:T(8,128)}, f32[64,256]{1,0:T(8,128)S(1)}, u32[]{:S(2)}, u32[]{:S(2)}) collective-permute-start(f32[64,256]{1,0:T(8,128)} %get-tuple-element.44), channel_id=1, source_target_pairs={{0,8},{1,9},{2,10},{3,11},{4,12},{5,13},{6,14},{7,15},{8,0},{9,1},... | collective-permute-start | bytes 196616 | tf_op jit(solution)/shard_map/ppermute | solution.py:254
  68.4 2.9 %collective-permute-done.11 = f32[64,256]{1,0:T(8,128)S(1)} collective-permute-done((f32[64,256]{1,0:T(8,128)}, f32[64,256]{1,0:T(8,128)S(1)}, u32[]{:S(2)}, u32[]{:S(2)}) %collective-permute-start.11) | collective-permute-done | bytes 65568 | tf_op jit(solution)/shard_map/ppermute | solution.py:254
  71.3 0.8 add_convert_fusion.1
  72.1 0.0 all-to-all-done
  72.2 1.9 %collective-permute-start.12 = (bf16[64,256]{1,0:T(8,128)(2,1)S(1)}, bf16[64,256]{1,0:T(8,128)(2,1)S(1)}, u32[]{:S(2)}, u32[]{:S(2)}) collective-permute-start(bf16[64,256]{1,0:T(8,128)(2,1)S(1)} %add_convert_fusion.1), channel_id=1, source_target_pairs={{0,16},{16,32},{32,48},{48,64},{64,80},{80,96},{96,112},{112,128},... | collective-permute-start | bytes 98312 | tf_op jit(solution)/shard_map/ppermute | solution.py:264
  74.1 5.1 %collective-permute-start.13 = (bf16[32,256]{1,0:T(8,128)(2,1)S(1)}, bf16[32,256]{1,0:T(8,128)(2,1)S(1)}, u32[]{:S(2)}, u32[]{:S(2)}) collective-permute-start(bf16[32,256]{1,0:T(8,128)(2,1)S(1)} %slice.3), channel_id=1, source_target_pairs={{0,32},{16,48},{32,64},{48,80},{64,96},{80,112},{96,128},{112,144}... | collective-permute-start | bytes 49160 | tf_op jit(solution)/shard_map/ppermute | solution.py:264
  79.2 2.9 %collective-permute-done.13 = bf16[32,256]{1,0:T(8,128)(2,1)S(1)} collective-permute-done((bf16[32,256]{1,0:T(8,128)(2,1)S(1)}, bf16[32,256]{1,0:T(8,128)(2,1)S(1)}, u32[]{:S(2)}, u32[]{:S(2)}) %collective-permute-start.13) | collective-permute-done | bytes 16416 | tf_op jit(solution)/shard_map/ppermute | solution.py:264
  82.1 0.0 collective-permute-done.12
  82.1 0.9 broadcast_in_dim.21
  83.0 4.5 %all-to-all-start.1 = ((bf16[8,160,256]{2,1,0:T(8,128)(2,1)}), bf16[8,160,256]{2,1,0:T(8,128)(2,1)S(1)}, u32[]{:S(2)}, u32[]{:S(2)}) async-start(bf16[8,160,256]{2,1,0:T(8,128)(2,1)} %broadcast_in_dim.21), calls=%async_computation.1 | async-start | bytes 1310720 | tf_op jit(solution)/shard_map/all_to_all | solution.py:294
  87.6 1.6 collective-permute-start.10
  89.1 1.5 collective-permute-start.16
  90.6 0.5 collective-permute-start.17
  91.2 2.1 %collective-permute-start.18 = (bf16[8,2,32,512]{3,2,1,0:T(8,128)(2,1)S(1)}, bf16[8,2,32,512]{3,2,1,0:T(8,128)(2,1)S(1)}, u32[]{:S(2)}, u32[]{:S(2)}) collective-permute-start(bf16[8,2,32,512]{3,2,1,0:T(8,128)(2,1)S(1)} %all-to-all-done), channel_id=1, source_target_pairs={{0,128},{16,144},{32,160},{48,176},{64,192},{80,208},{96,224},{112... | collective-permute-start | bytes 1572872 | tf_op jit(solution)/shard_map/ppermute | solution.py:268
  93.3 2.8 %collective-permute-done.10.sent_any = f32[256,256]{1,0:T(8,128)S(1)} collective-permute-done((f32[256,256]{1,0:T(8,128)}, f32[256,256]{1,0:T(8,128)S(1)}, u32[]{:S(2)}, u32[]{:S(2)}) %collective-permute-start.10) | collective-permute-done | bytes 262176 | tf_op jit(solution)/shard_map/ppermute | solution.py:254
  96.1 13.0 %all-to-all-done.1 = bf16[8,160,256]{2,1,0:T(8,128)(2,1)S(1)} async-done(((bf16[8,160,256]{2,1,0:T(8,128)(2,1)}), bf16[8,160,256]{2,1,0:T(8,128)(2,1)S(1)}, u32[]{:S(2)}, u32[]{:S(2)}) %all-to-all-start.1) | async-done | bytes 655392 | tf_op jit(solution)/shard_map/all_to_all | solution.py:294
  109.2 16.4 %shard_map.47.refs_0_ = bf16[256,256]{1,0:T(8,128)(2,1)S(1)} custom-call(s32[1]{0:T(128)} %bitcast.2.seq_ref, f32[256,256]{1,0:T(8,128)S(1)} %copy-done, f32[256,256]{1,0:T(8,128)S(1)} %collective-permute-done.10.sent_any, bf16[8,5,32,256]{3,2,1,0:T(8,128)(2,1)S(1)} %bitcast.22), custom_call_target="tpu_custom_call" | custom-call | tf_op jit(solution)/shard_map/pallas_call | solution.py:153
  125.6 0.1 collective-permute-start.14
  125.7 3.2 %collective-permute-start.15 = (bf16[256,256]{1,0:T(8,128)(2,1)S(1)}, bf16[256,256]{1,0:T(8,128)(2,1)S(1)}, u32[]{:S(2)}, u32[]{:S(2)}) collective-permute-start(bf16[256,256]{1,0:T(8,128)(2,1)S(1)} %shard_map.47.refs_0_), channel_id=1, source_target_pairs={{0,7},{1,0},{2,1},{3,2},{4,3},{5,4},{6,5},{7,6},{8,15},{9,8},{10,9... | collective-permute-start | bytes 393224 | tf_op jit(solution)/shard_map/ppermute | solution.py:258
  129.0 3.5 %collective-permute-done.14.refs_1_ = bf16[256,256]{1,0:T(8,128)(2,1)S(1)} collective-permute-done((bf16[256,256]{1,0:T(8,128)(2,1)S(1)}, bf16[256,256]{1,0:T(8,128)(2,1)S(1)}, u32[]{:S(2)}, u32[]{:S(2)}) %collective-permute-start.14) | collective-permute-done | bytes 131104 | tf_op jit(solution)/shard_map/ppermute | solution.py:258
  132.5 3.2 %collective-permute-start.20 = (bf16[256,256]{1,0:T(8,128)(2,1)S(1)}, bf16[256,256]{1,0:T(8,128)(2,1)S(1)}, u32[]{:S(2)}, u32[]{:S(2)}) collective-permute-start(bf16[256,256]{1,0:T(8,128)(2,1)S(1)} %collective-permute-done.15.refs_2_), channel_id=1, source_target_pairs={{0,7},{1,0},{2,1},{3,2},{4,3},{5,4},{6,5},{7,6},{8,15},{9,8},{10,9... | collective-permute-start | bytes 393224 | tf_op jit(solution)/shard_map/ppermute | solution.py:258
  135.7 0.2 broadcast_in_dim.22
  136.0 2.6 %collective-permute-done.19.refs_3_ = bf16[256,256]{1,0:T(8,128)(2,1)S(1)} collective-permute-done((bf16[256,256]{1,0:T(8,128)(2,1)S(1)}, bf16[256,256]{1,0:T(8,128)(2,1)S(1)}, u32[]{:S(2)}, u32[]{:S(2)}) %collective-permute-start.19) | collective-permute-done | bytes 131104 | tf_op jit(solution)/shard_map/ppermute | solution.py:258
  138.6 0.0 collective-permute-done.17
  138.6 0.0 collective-permute-done.18
  138.8 0.1 collective-permute-start.23
  138.9 0.1 collective-permute-start.21
  139.0 3.3 %collective-permute-start.22 = (bf16[256,256]{1,0:T(8,128)(2,1)S(1)}, bf16[256,256]{1,0:T(8,128)(2,1)S(1)}, u32[]{:S(2)}, u32[]{:S(2)}) collective-permute-start(bf16[256,256]{1,0:T(8,128)(2,1)S(1)} %collective-permute-done.20.refs_4_), channel_id=1, source_target_pairs={{0,7},{1,0},{2,1},{3,2},{4,3},{5,4},{6,5},{7,6},{8,15},{9,8},{10,9... | collective-permute-start | bytes 393224 | tf_op jit(solution)/shard_map/ppermute | solution.py:258
  142.3 4.0 %collective-permute-done.21.refs_5_ = bf16[256,256]{1,0:T(8,128)(2,1)S(1)} collective-permute-done((bf16[256,256]{1,0:T(8,128)(2,1)S(1)}, bf16[256,256]{1,0:T(8,128)(2,1)S(1)}, u32[]{:S(2)}, u32[]{:S(2)}) %collective-permute-start.21) | collective-permute-done | bytes 131104 | tf_op jit(solution)/shard_map/ppermute | solution.py:258
  146.3 0.0 collective-permute-start.24
  146.3 1.8 %shard_map.48 = (f32[256,1024]{1,0:T(8,128)S(1)}, bf16[1,256,1024]{2,1,0:T(8,128)(2,1)S(1)}) custom-call(s32[2]{0:T(128)S(1)} %copy-done.1, bf16[256,256]{1,0:T(8,128)(2,1)S(1)} %shard_map.47.refs_0_, bf16[256,256]{1,0:T(8,128)(2,1)S(1)} %collective-permute-done.14.refs_1_, bf16[256,256]{1,0:T(8,128)(2,1)S(1)} %collective-permute-done.15.refs_2_, ...), custom_call_target="tpu_custom_call" | custom-call | tf_op jit(solution)/shard_map/pallas_call | solution.py:358
  148.1 4.6 %collective-permute-done.24.last_ref = bf16[256,256]{1,0:T(8,128)(2,1)S(1)} collective-permute-done((bf16[256,256]{1,0:T(8,128)(2,1)S(1)}, bf16[256,256]{1,0:T(8,128)(2,1)S(1)}, u32[]{:S(2)}, u32[]{:S(2)}) %collective-permute-start.24) | collective-permute-done | bytes 131104 | tf_op jit(solution)/shard_map/ppermute | solution.py:258
  152.8 0.9 shard_map.49
  153.7 1.8 %collective-permute-start.25 = (bf16[256,512]{1,0:T(8,128)(2,1)S(1)}, bf16[256,512]{1,0:T(8,128)(2,1)S(1)}, u32[]{:S(2)}, u32[]{:S(2)}) collective-permute-start(bf16[256,512]{1,0:T(8,128)(2,1)S(1)} %get-tuple-element.60), channel_id=1, source_target_pairs={{0,8},{1,9},{2,10},{3,11},{4,12},{5,13},{6,14},{7,15},{8,0},{9,1},... | collective-permute-start | bytes 786440 | tf_op jit(solution)/shard_map/ppermute | solution.py:254
  155.4 5.5 %collective-permute-done.25 = bf16[256,512]{1,0:T(8,128)(2,1)S(1)} collective-permute-done((bf16[256,512]{1,0:T(8,128)(2,1)S(1)}, bf16[256,512]{1,0:T(8,128)(2,1)S(1)}, u32[]{:S(2)}, u32[]{:S(2)}) %collective-permute-start.25) | collective-permute-done | bytes 262176 | tf_op jit(solution)/shard_map/ppermute | solution.py:254
  160.9 0.8 add_convert_fusion
  (32 shorter events, 0.3 us)
Async XLA Ops:
  0.0 3.0 %copy-start.4 = (bf16[256,512]{1,0:T(8,128)(2,1)S(1)}, bf16[256,512]{1,0:T(8,128)(2,1)}, u32[]{:S(2)}) copy-start(bf16[256,512]{1,0:T(8,128)(2,1)} %refs_0_.1) | copy-start | bytes 786436
  1.3 25.3 %collective-permute-start.8 = (bf16[2048,256]{1,0:T(8,128)(2,1)S(1)}, bf16[2048,256]{1,0:T(8,128)(2,1)S(1)}, u32[]{:S(2)}, u32[]{:S(2)}) collective-permute-start(bf16[2048,256]{1,0:T(8,128)(2,1)S(1)} %constant_dynamic-slice_fusion), channel_id=1, source_target_pairs={{0,8},{1,9},{2,10},{3,11},{4,12},{5,13},{6,14},{7,15},{8,0},{9,1},... | collective-permute-start | bytes 3145736 | tf_op jit(solution)/shard_map/ppermute | solution.py:254
  3.0 11.9 %collective-permute-start = (bf16[256,512]{1,0:T(8,128)(2,1)S(1)}, bf16[256,512]{1,0:T(8,128)(2,1)S(1)}, u32[]{:S(2)}, u32[]{:S(2)}) collective-permute-start(bf16[256,512]{1,0:T(8,128)(2,1)S(1)} %copy-done.4), channel_id=1, source_target_pairs={{0,1},{1,2},{2,3},{3,4},{4,5},{5,6},{6,7},{7,0},{8,9},{9,10},{10,1... | collective-permute-start | bytes 786440 | tf_op jit(solution)/shard_map/ppermute | solution.py:258
  4.9 10.0 %collective-permute-start.1 = (bf16[256,512]{1,0:T(8,128)(2,1)S(1)}, bf16[256,512]{1,0:T(8,128)(2,1)S(1)}, u32[]{:S(2)}, u32[]{:S(2)}) collective-permute-start(bf16[256,512]{1,0:T(8,128)(2,1)S(1)} %copy-done.4), channel_id=1, source_target_pairs={{0,7},{1,0},{2,1},{3,2},{4,3},{5,4},{6,5},{7,6},{8,15},{9,8},{10,9... | collective-permute-start | bytes 786440 | tf_op jit(solution)/shard_map/ppermute | solution.py:258
  14.9 17.1 %copy-start.5 = (bf16[256,512]{1,0:T(8,128)(2,1)}, bf16[256,512]{1,0:T(8,128)(2,1)S(1)}, u32[]{:S(2)}) copy-start(bf16[256,512]{1,0:T(8,128)(2,1)S(1)} %collective-permute-done.refs_1_) | copy-start | bytes 786436
  14.9 17.1 %copy-start.6 = (bf16[256,512]{1,0:T(8,128)(2,1)}, bf16[256,512]{1,0:T(8,128)(2,1)S(1)}, u32[]{:S(2)}) copy-start(bf16[256,512]{1,0:T(8,128)(2,1)S(1)} %collective-permute-done.1.refs_2_) | copy-start | bytes 786436
  14.9 8.5 %collective-permute-start.2 = (bf16[256,512]{1,0:T(8,128)(2,1)S(1)}, bf16[256,512]{1,0:T(8,128)(2,1)S(1)}, u32[]{:S(2)}, u32[]{:S(2)}) collective-permute-start(bf16[256,512]{1,0:T(8,128)(2,1)S(1)} %collective-permute-done.refs_1_), channel_id=1, source_target_pairs={{0,1},{1,2},{2,3},{3,4},{4,5},{5,6},{6,7},{7,0},{8,9},{9,10},{10,1... | collective-permute-start | bytes 786440 | tf_op jit(solution)/shard_map/ppermute | solution.py:258
  15.0 8.4 %collective-permute-start.3 = (bf16[256,512]{1,0:T(8,128)(2,1)S(1)}, bf16[256,512]{1,0:T(8,128)(2,1)}, u32[]{:S(2)}, u32[]{:S(2)}) collective-permute-start(bf16[256,512]{1,0:T(8,128)(2,1)S(1)} %collective-permute-done.1.refs_2_), channel_id=1, source_target_pairs={{0,7},{1,0},{2,1},{3,2},{4,3},{5,4},{6,5},{7,6},{8,15},{9,8},{10,9... | collective-permute-start | bytes 786440 | tf_op jit(solution)/shard_map/ppermute | solution.py:258
  18.2 19.4 %copy-start.3 = (bf16[8192,32]{0,1:T(8,128)(2,1)S(1)}, bf16[8192,32]{0,1:T(8,128)(2,1)}, u32[]{:S(2)}) copy-start(bf16[8192,32]{0,1:T(8,128)(2,1)} %param.6) | copy-start | bytes 1572868
  23.4 8.6 %copy-start.7 = (bf16[256,512]{1,0:T(8,128)(2,1)}, bf16[256,512]{1,0:T(8,128)(2,1)S(1)}, u32[]{:S(2)}) copy-start(bf16[256,512]{1,0:T(8,128)(2,1)S(1)} %collective-permute-done.2.refs_3_) | copy-start | bytes 786436
  23.4 7.7 %collective-permute-start.4 = (bf16[256,512]{1,0:T(8,128)(2,1)S(1)}, bf16[256,512]{1,0:T(8,128)(2,1)}, u32[]{:S(2)}, u32[]{:S(2)}) collective-permute-start(bf16[256,512]{1,0:T(8,128)(2,1)S(1)} %collective-permute-done.2.refs_3_), channel_id=1, source_target_pairs={{0,1},{1,2},{2,3},{3,4},{4,5},{5,6},{6,7},{7,0},{8,9},{9,10},{10,1... | collective-permute-start | bytes 786440 | tf_op jit(solution)/shard_map/ppermute | solution.py:258
  25.3 6.7 %collective-permute-start.5 = (bf16[256,512]{1,0:T(8,128)(2,1)}, bf16[256,512]{1,0:T(8,128)(2,1)}, u32[]{:S(2)}, u32[]{:S(2)}) collective-permute-start(bf16[256,512]{1,0:T(8,128)(2,1)} %collective-permute-done.3.refs_4_), channel_id=1, source_target_pairs={{0,7},{1,0},{2,1},{3,2},{4,3},{5,4},{6,5},{7,6},{8,15},{9,8},{10,9... | collective-permute-start | bytes 786440 | tf_op jit(solution)/shard_map/ppermute | solution.py:258
  26.6 5.4 %copy-start.2 = (bf16[2048,256]{1,0:T(8,128)(2,1)}, bf16[2048,256]{1,0:T(8,128)(2,1)S(1)}, u32[]{:S(2)}) copy-start(bf16[2048,256]{1,0:T(8,128)(2,1)S(1)} %collective-permute-done.8.refs_11_) | copy-start | bytes 3145732
  26.6 31.7 %collective-permute-start.9 = (bf16[2048,256]{1,0:T(8,128)(2,1)S(1)}, bf16[2048,256]{1,0:T(8,128)(2,1)}, u32[]{:S(2)}, u32[]{:S(2)}) collective-permute-start(bf16[2048,256]{1,0:T(8,128)(2,1)S(1)} %collective-permute-done.8.refs_11_), channel_id=1, source_target_pairs={{0,16},{16,0},{32,48},{48,32},{64,80},{80,64},{96,112},{112,96},{1... | collective-permute-start | bytes 3145736 | tf_op jit(solution)/shard_map/ppermute | solution.py:272
  32.0 40.1 %all-to-all-start = ((bf16[8,2,32,512]{3,2,1,0:T(8,128)(2,1)}), bf16[8,2,32,512]{3,2,1,0:T(8,128)(2,1)S(1)}, u32[]{:S(2)}, u32[]{:S(2)}) async-start(bf16[8,2,32,512]{3,2,1,0:T(8,128)(2,1)} %bitcast.21), calls=%async_computation | async-start | bytes 1048576 | tf_op jit(solution)/shard_map/all_to_all | solution.py:401
  38.3 8.1 %collective-permute-start.7 = (bf16[32,4096]{1,0:T(8,128)(2,1)S(1)}, bf16[32,4096]{1,0:T(8,128)(2,1)S(1)}, u32[]{:S(2)}, u32[]{:S(2)}) collective-permute-start(bf16[32,4096]{1,0:T(8,128)(2,1)S(1)} %get-tuple-element.61), channel_id=1, source_target_pairs={{0,8},{1,9},{2,10},{3,11},{4,12},{5,13},{6,14},{7,15},{8,0},{9,1},... | collective-permute-start | bytes 786440 | tf_op jit(solution)/shard_map/ppermute | solution.py:254
  39.9 18.4 %collective-permute-start.6 = (bf16[256,512]{1,0:T(8,128)(2,1)}, bf16[256,512]{1,0:T(8,128)(2,1)S(1)}, u32[]{:S(2)}, u32[]{:S(2)}) collective-permute-start(bf16[256,512]{1,0:T(8,128)(2,1)} %collective-permute-done.4.refs_5_), channel_id=1, source_target_pairs={{0,1},{1,2},{2,3},{3,4},{4,5},{5,6},{6,7},{7,0},{8,9},{9,10},{10,1... | collective-permute-start | bytes 786440 | tf_op jit(solution)/shard_map/ppermute | solution.py:258
  46.4 11.9 %copy-start.8 = (bf16[32,4096]{1,0:T(8,128)(2,1)}, bf16[32,4096]{1,0:T(8,128)(2,1)S(1)}, u32[]{:S(2)}) copy-start(bf16[32,4096]{1,0:T(8,128)(2,1)S(1)} %collective-permute-done.7.refs_9_) | copy-start | bytes 786436
  58.3 0.7 copy-start.9
  66.7 42.5 %copy-start = (f32[256,256]{1,0:T(8,128)S(1)}, f32[256,256]{1,0:T(8,128)}, u32[]{:S(2)}) copy-start(f32[256,256]{1,0:T(8,128)} %get-tuple-element.41.mine_any) | copy-start | bytes 786436
  66.7 4.6 %collective-permute-start.11 = (f32[64,256]{1,0:T(8,128)}, f32[64,256]{1,0:T(8,128)S(1)}, u32[]{:S(2)}, u32[]{:S(2)}) collective-permute-start(f32[64,256]{1,0:T(8,128)} %get-tuple-element.44), channel_id=1, source_target_pairs={{0,8},{1,9},{2,10},{3,11},{4,12},{5,13},{6,14},{7,15},{8,0},{9,1},... | collective-permute-start | bytes 196616 | tf_op jit(solution)/shard_map/ppermute | solution.py:254
  72.2 10.0 %collective-permute-start.12 = (bf16[64,256]{1,0:T(8,128)(2,1)S(1)}, bf16[64,256]{1,0:T(8,128)(2,1)S(1)}, u32[]{:S(2)}, u32[]{:S(2)}) collective-permute-start(bf16[64,256]{1,0:T(8,128)(2,1)S(1)} %add_convert_fusion.1), channel_id=1, source_target_pairs={{0,16},{16,32},{32,48},{48,64},{64,80},{80,96},{96,112},{112,128},... | collective-permute-start | bytes 98312 | tf_op jit(solution)/shard_map/ppermute | solution.py:264
  74.1 8.0 %collective-permute-start.13 = (bf16[32,256]{1,0:T(8,128)(2,1)S(1)}, bf16[32,256]{1,0:T(8,128)(2,1)S(1)}, u32[]{:S(2)}, u32[]{:S(2)}) collective-permute-start(bf16[32,256]{1,0:T(8,128)(2,1)S(1)} %slice.3), channel_id=1, source_target_pairs={{0,32},{16,48},{32,64},{48,80},{64,96},{80,112},{96,128},{112,144}... | collective-permute-start | bytes 49160 | tf_op jit(solution)/shard_map/ppermute | solution.py:264
  83.0 26.2 %all-to-all-start.1 = ((bf16[8,160,256]{2,1,0:T(8,128)(2,1)}), bf16[8,160,256]{2,1,0:T(8,128)(2,1)S(1)}, u32[]{:S(2)}, u32[]{:S(2)}) async-start(bf16[8,160,256]{2,1,0:T(8,128)(2,1)} %broadcast_in_dim.21), calls=%async_computation.1 | async-start | bytes 1310720 | tf_op jit(solution)/shard_map/all_to_all | solution.py:294
  87.6 8.6 %collective-permute-start.10 = (f32[256,256]{1,0:T(8,128)}, f32[256,256]{1,0:T(8,128)S(1)}, u32[]{:S(2)}, u32[]{:S(2)}) collective-permute-start(f32[256,256]{1,0:T(8,128)} %get-tuple-element.42), channel_id=1, source_target_pairs={{0,8},{1,9},{2,10},{3,11},{4,12},{5,13},{6,14},{7,15},{8,0},{9,1},... | collective-permute-start | bytes 786440 | tf_op jit(solution)/shard_map/ppermute | solution.py:254
  89.1 49.5 %collective-permute-start.16 = (bf16[8,2,32,512]{3,2,1,0:T(8,128)(2,1)S(1)}, bf16[8,2,32,512]{3,2,1,0:T(8,128)(2,1)S(1)}, u32[]{:S(2)}, u32[]{:S(2)}) collective-permute-start(bf16[8,2,32,512]{3,2,1,0:T(8,128)(2,1)S(1)} %all-to-all-done), channel_id=1, source_target_pairs={{0,64},{16,80},{32,96},{48,112},{64,128},{80,144},{96,160},{112,17... | collective-permute-start | bytes 1572872 | tf_op jit(solution)/shard_map/ppermute | solution.py:268
  90.6 48.0 %collective-permute-start.17 = (bf16[8,2,32,512]{3,2,1,0:T(8,128)(2,1)S(1)}, bf16[8,2,32,512]{3,2,1,0:T(8,128)(2,1)S(1)}, u32[]{:S(2)}, u32[]{:S(2)}) collective-permute-start(bf16[8,2,32,512]{3,2,1,0:T(8,128)(2,1)S(1)} %all-to-all-done), channel_id=1, source_target_pairs={{0,192},{16,208},{32,224},{48,240},{64,0},{80,16},{96,32},{112,48}... | collective-permute-start | bytes 1572872 | tf_op jit(solution)/shard_map/ppermute | solution.py:268
  91.2 47.5 %collective-permute-start.18 = (bf16[8,2,32,512]{3,2,1,0:T(8,128)(2,1)S(1)}, bf16[8,2,32,512]{3,2,1,0:T(8,128)(2,1)S(1)}, u32[]{:S(2)}, u32[]{:S(2)}) collective-permute-start(bf16[8,2,32,512]{3,2,1,0:T(8,128)(2,1)S(1)} %all-to-all-done), channel_id=1, source_target_pairs={{0,128},{16,144},{32,160},{48,176},{64,192},{80,208},{96,224},{112... | collective-permute-start | bytes 1572872 | tf_op jit(solution)/shard_map/ppermute | solution.py:268
  125.6 6.8 %collective-permute-start.14 = (bf16[256,256]{1,0:T(8,128)(2,1)S(1)}, bf16[256,256]{1,0:T(8,128)(2,1)S(1)}, u32[]{:S(2)}, u32[]{:S(2)}) collective-permute-start(bf16[256,256]{1,0:T(8,128)(2,1)S(1)} %shard_map.47.refs_0_), channel_id=1, source_target_pairs={{0,1},{1,2},{2,3},{3,4},{4,5},{5,6},{6,7},{7,0},{8,9},{9,10},{10,1... | collective-permute-start | bytes 393224 | tf_op jit(solution)/shard_map/ppermute | solution.py:258
  125.7 6.7 %collective-permute-start.15 = (bf16[256,256]{1,0:T(8,128)(2,1)S(1)}, bf16[256,256]{1,0:T(8,128)(2,1)S(1)}, u32[]{:S(2)}, u32[]{:S(2)}) collective-permute-start(bf16[256,256]{1,0:T(8,128)(2,1)S(1)} %shard_map.47.refs_0_), channel_id=1, source_target_pairs={{0,7},{1,0},{2,1},{3,2},{4,3},{5,4},{6,5},{7,6},{8,15},{9,8},{10,9... | collective-permute-start | bytes 393224 | tf_op jit(solution)/shard_map/ppermute | solution.py:258
  132.5 6.2 %collective-permute-start.19 = (bf16[256,256]{1,0:T(8,128)(2,1)S(1)}, bf16[256,256]{1,0:T(8,128)(2,1)S(1)}, u32[]{:S(2)}, u32[]{:S(2)}) collective-permute-start(bf16[256,256]{1,0:T(8,128)(2,1)S(1)} %collective-permute-done.14.refs_1_), channel_id=1, source_target_pairs={{0,1},{1,2},{2,3},{3,4},{4,5},{5,6},{6,7},{7,0},{8,9},{9,10},{10,1... | collective-permute-start | bytes 393224 | tf_op jit(solution)/shard_map/ppermute | solution.py:258
  132.5 6.2 %collective-permute-start.20 = (bf16[256,256]{1,0:T(8,128)(2,1)S(1)}, bf16[256,256]{1,0:T(8,128)(2,1)S(1)}, u32[]{:S(2)}, u32[]{:S(2)}) collective-permute-start(bf16[256,256]{1,0:T(8,128)(2,1)S(1)} %collective-permute-done.15.refs_2_), channel_id=1, source_target_pairs={{0,7},{1,0},{2,1},{3,2},{4,3},{5,4},{6,5},{7,6},{8,15},{9,8},{10,9... | collective-permute-start | bytes 393224 | tf_op jit(solution)/shard_map/ppermute | solution.py:258
  135.9 10.4 %copy-start.1 = (s32[2]{0:T(128)S(1)}, s32[2]{0:T(128)}, u32[]{:S(2)}) copy-start(s32[2]{0:T(128)} %pad_add_fusion.spot_ref) | copy-start | bytes 28
  138.8 7.5 %collective-permute-start.23 = (bf16[4,8,2,32,512]{4,3,2,1,0:T(8,128)(2,1)S(1)}, bf16[4,8,2,32,512]{4,3,2,1,0:T(8,128)(2,1)S(1)}, u32[]{:S(2)}, u32[]{:S(2)}) collective-permute-start(bf16[4,8,2,32,512]{4,3,2,1,0:T(8,128)(2,1)S(1)} %bitcast_dynamic-update-slice_fusion.refs_7_), channel_id=1, source_target_pairs={{0,16},{16,0},{32,48},{48,32},{64,80},{80,64},{96,112},{112,96},{1... | collective-permute-start | bytes 6291464 | tf_op jit(solution)/shard_map/ppermute | solution.py:272
  138.9 7.4 %collective-permute-start.21 = (bf16[256,256]{1,0:T(8,128)(2,1)S(1)}, bf16[256,256]{1,0:T(8,128)(2,1)S(1)}, u32[]{:S(2)}, u32[]{:S(2)}) collective-permute-start(bf16[256,256]{1,0:T(8,128)(2,1)S(1)} %collective-permute-done.19.refs_3_), channel_id=1, source_target_pairs={{0,1},{1,2},{2,3},{3,4},{4,5},{5,6},{6,7},{7,0},{8,9},{9,10},{10,1... | collective-permute-start | bytes 393224 | tf_op jit(solution)/shard_map/ppermute | solution.py:258
  139.0 7.3 %collective-permute-start.22 = (bf16[256,256]{1,0:T(8,128)(2,1)S(1)}, bf16[256,256]{1,0:T(8,128)(2,1)S(1)}, u32[]{:S(2)}, u32[]{:S(2)}) collective-permute-start(bf16[256,256]{1,0:T(8,128)(2,1)S(1)} %collective-permute-done.20.refs_4_), channel_id=1, source_target_pairs={{0,7},{1,0},{2,1},{3,2},{4,3},{5,4},{6,5},{7,6},{8,15},{9,8},{10,9... | collective-permute-start | bytes 393224 | tf_op jit(solution)/shard_map/ppermute | solution.py:258
  146.3 6.4 %collective-permute-start.24 = (bf16[256,256]{1,0:T(8,128)(2,1)S(1)}, bf16[256,256]{1,0:T(8,128)(2,1)S(1)}, u32[]{:S(2)}, u32[]{:S(2)}) collective-permute-start(bf16[256,256]{1,0:T(8,128)(2,1)S(1)} %collective-permute-done.21.refs_5_), channel_id=1, source_target_pairs={{0,1},{1,2},{2,3},{3,4},{4,5},{5,6},{6,7},{7,0},{8,9},{9,10},{10,1... | collective-permute-start | bytes 393224 | tf_op jit(solution)/shard_map/ppermute | solution.py:258
  153.7 7.3 %collective-permute-start.25 = (bf16[256,512]{1,0:T(8,128)(2,1)S(1)}, bf16[256,512]{1,0:T(8,128)(2,1)S(1)}, u32[]{:S(2)}, u32[]{:S(2)}) collective-permute-start(bf16[256,512]{1,0:T(8,128)(2,1)S(1)} %get-tuple-element.60), channel_id=1, source_target_pairs={{0,8},{1,9},{2,10},{3,11},{4,12},{5,13},{6,14},{7,15},{8,0},{9,1},... | collective-permute-start | bytes 786440 | tf_op jit(solution)/shard_map/ppermute | solution.py:254

commit v5 on v4

--- a/solution.py
+++ b/solution.py
@@ -16,16 +16,14 @@
 LANES = (((1,), (1,)), ((), ()))
 
 
-OWN, NEAR, FAR = 0, 2, 4
-
-
-def pick(gathered, source, which, lanes):
+def pick(source, which, lanes):
     places = slice((which % 2) * 4, (which % 2) * 4 + 4)
-    return gathered[places, source + which // 2, :, lanes].reshape(HEAD, BLK)
+    found = source[places, :, lanes] if len(source.shape) == 3 else source[places, which // 2, :, lanes]
+    return found.reshape(HEAD, BLK)
 
 
 def attend_kernel(
-    seq_ref, mine_any, sent_any, all_ref, out_ref,
+    seq_ref, mine_any, sent_any, far_ref, near_ref, own_ref, out_ref,
     k2f, v2f, ktile, vtile, kpair, vpair, s_scr, mx_scr, mcb_scr, mine_ref, sent_ref, sems,
 ):
     fetches = [
@@ -42,14 +40,14 @@
     start = seq == 0
 
     for t in range(6):
-        source = (FAR, NEAR, OWN)[t // 2]
+        source = (far_ref, near_ref, own_ref)[t // 2]
         lanes = slice((t % 2) * BLK, (t % 2 + 1) * BLK)
-        ktile[t] = pick(all_ref, source, 0, lanes)
-        vtile[t] = pick(all_ref, source, 1, lanes).astype(jnp.float32).T.astype(jnp.bfloat16)
+        ktile[t] = pick(source, 0, lanes)
+        vtile[t] = pick(source, 1, lanes).astype(jnp.float32).T.astype(jnp.bfloat16)
     for scr, which in ((k2f, 2), (v2f, 3)):
-        scr[:BLK] = pick(all_ref, NEAR, which, slice(tok - BLK, tok)).astype(jnp.float32).T
+        scr[:BLK] = pick(near_ref, which, slice(tok - BLK, tok)).astype(jnp.float32).T
         for t in range(blocks):
-            scr[(t + 1) * BLK:(t + 2) * BLK] = pick(all_ref, OWN, which, slice(t * BLK, (t + 1) * BLK)).astype(jnp.float32).T
+            scr[(t + 1) * BLK:(t + 2) * BLK] = pick(own_ref, which, slice(t * BLK, (t + 1) * BLK)).astype(jnp.float32).T
 
     @pl.when(start)
     def _():
@@ -148,14 +146,14 @@
     return [pl.BlockSpec(memory_space=pltpu.VMEM)] * count
 
 
-def attend(seq, mine, sent, gathered):
+def attend(seq, mine, sent, far, near, own):
     tok = mine.shape[0]
     return pl.pallas_call(
         attend_kernel,
         out_shape=jax.ShapeDtypeStruct(mine.shape, jnp.bfloat16),
         in_specs=[pl.BlockSpec(memory_space=pltpu.SMEM)]
         + [pl.BlockSpec(memory_space=pltpu.HBM)] * 2
-        + in_vmem(1),
+        + in_vmem(3),
         out_specs=in_vmem(1)[0],
         scratch_shapes=[
             pltpu.VMEM((BLK + tok, HEAD), jnp.float32),
@@ -172,72 +170,70 @@
             pltpu.SemaphoreType.DMA((2,)),
         ],
         compiler_params=pltpu.CompilerParams(vmem_limit_bytes=24 * 1024 * 1024),
-    )(seq, mine, sent, gathered)
+    )(seq, mine, sent, far, near, own)
 
 
 OFFSETS = (0, -1, 1, -2, 2, -3, 3, -4)
-OWN_WEIGHTS = 10
 
 
 def project_kernel(spot_ref, *refs):
-    sources = refs[:13]
+    shards_any, kv_any, own_any, parts_any = refs[:8], refs[8:10], refs[10], refs[11:13]
     kv_out, mine_any, theirs_any = refs[13:16]
-    held = refs[16:29]
-    mine_out, theirs_out, sems = refs[29:]
-    shards, kv_own, kv_part, own_ref, same_ref, twin_ref = held[:8], *held[8:]
-    depth = shards[0].shape[1]
+    shards, kv_ref, own_ref, part_ref, mine_out, theirs_out, sems = refs[16:]
+    depth = shards.shape[2]
     half = own_ref.shape[0]
     row, core = spot_ref[0] >> 3, spot_ref[1]
-    fetches = []
-    for k, (source, target) in enumerate(zip(sources, held)):
-        if k == OWN_WEIGHTS:
-            source = source.at[pl.ds(pl.multiple_of(row * half, half), half), :]
-        fetches.append(pltpu.make_async_copy(source, target, sems.at[k]))
-        fetches[k].start()
-
-    def from_place(offset, count):
-        spot = (spot_ref[0] + offset) & (count - 1)
-        return pl.ds(pl.multiple_of(spot * depth, depth), depth)
-
-    for k in range(OWN_WEIGHTS):
-        fetches[k].wait()
-    parts = kv_own.shape[0]
-    for weight, side in ((kv_own, row), (kv_part, 1 - row)):
+    parts = kv_ref.shape[0] // 2
+
+    def rows_at(place, count):
+        return pl.ds(pl.multiple_of(place * count, count), count)
+
+    moves = [(source, shards.at[k]) for k, source in enumerate(shards_any)]
+    for source, side in zip(kv_any, (row, 1 - row)):
+        moves.append((source, kv_ref.at[rows_at(side, parts), :]))
+    moves.append((own_any.at[rows_at(row, half), :], own_ref))
+    for source, side in zip(parts_any, (core, 1 - core)):
+        moves.append((source, part_ref.at[rows_at(side, half // 2), :]))
+    fetches = [
+        pltpu.make_async_copy(source, target, sems.at[k])
+        for k, (source, target) in enumerate(moves)
+    ]
+    for fetch in fetches:
+        fetch.start()
+    spots = [(spot_ref[0] + offset) & 7 for offset in OFFSETS]
+    for fetch in fetches[:10]:
+        fetch.wait()
+    total = None
+    for k, spot in enumerate(spots):
+        cols = kv_ref[:, rows_at(spot, depth)]
+        new = lax.dot_general(cols, shards[k], LANES, preferred_element_type=jnp.float32)
+        total = new if total is None else total + new
+    kv_out[...] = total
+
+    def whole_sum(weights, out, target, sem):
         total = None
-        for offset, shard in zip(OFFSETS, shards):
-            cols = weight[:, from_place(offset, 8)]
-            new = lax.dot_general(cols, shard[...], LANES, preferred_element_type=jnp.float32)
+        for k, spot in enumerate(spots):
+            new = jnp.dot(shards[k], weights[rows_at(spot, depth), :], preferred_element_type=jnp.float32)
             total = new if total is None else total + new
-        kv_out[pl.ds(pl.multiple_of(side * parts, parts), parts), :] = total
-    for k in range(OWN_WEIGHTS, len(held)):
-        fetches[k].wait()
-    theirs_out[...] = jnp.zeros(theirs_out.shape, jnp.float32)
-    for offset, shard in zip(OFFSETS, shards):
-        low = from_place(offset, 4)
-        upper = ((spot_ref[0] + offset) & 7) >> 2
-        for ref, side in ((same_ref, core), (twin_ref, 1 - core)):
-
-            @pl.when(upper == side)
-            def _():
-                theirs_out[...] += jnp.dot(shard[...], ref[low, :], preferred_element_type=jnp.float32)
-    send = pltpu.make_async_copy(theirs_out, theirs_any, sems.at[len(held)])
-    send.start()
-    total = None
-    for offset, shard in zip(OFFSETS, shards):
-        new = jnp.dot(shard[...], own_ref[from_place(offset, 8), :], preferred_element_type=jnp.float32)
-        total = new if total is None else total + new
-    mine_out[...] = total
-    keep = pltpu.make_async_copy(mine_out, mine_any, sems.at[len(held) + 1])
-    keep.start()
+        out[...] = total
+        move = pltpu.make_async_copy(out, target, sem)
+        move.start()
+        return move
+
+    fetches[10].wait()
+    keep = whole_sum(own_ref, mine_out, mine_any, sems.at[13])
+    for fetch in fetches[11:]:
+        fetch.wait()
+    send = whole_sum(part_ref, theirs_out, theirs_any, sems.at[14])
+    keep.wait()
     send.wait()
-    keep.wait()
 
 
 def project(spots, arrays, shapes):
     far_off = pl.BlockSpec(memory_space=pltpu.HBM)
-    own = arrays[OWN_WEIGHTS]
-    kept = [array.shape for array in arrays]
-    kept[OWN_WEIGHTS] = (own.shape[0] // 2, own.shape[1])
+    own = arrays[10]
+    half = (own.shape[0] // 2, own.shape[1])
+    kept = [(8, *arrays[0].shape), (2 * arrays[8].shape[0], arrays[8].shape[1]), half, half]
     return pl.pallas_call(
         project_kernel,
         out_shape=tuple(jax.ShapeDtypeStruct(shape, jnp.float32) for shape in shapes),
@@ -245,7 +241,7 @@
         out_specs=(in_vmem(1)[0], far_off, far_off),
         scratch_shapes=[pltpu.VMEM(shape, own.dtype) for shape in kept]
         + [pltpu.VMEM(shape, jnp.float32) for shape in shapes[1:]]
-        + [pltpu.SemaphoreType.DMA((len(arrays) + 2,))],
+        + [pltpu.SemaphoreType.DMA((15,))],
         compiler_params=pltpu.CompilerParams(vmem_limit_bytes=60 * 1024 * 1024),
     )(spots, *arrays)
 
@@ -272,7 +268,7 @@
     return lax.ppermute(value, "seq", [(i, i ^ 1) for i in range(16)])
 
 
-def z_ring(value):
+def z_ring(value, extra=None):
     found = [value]
     up = down = value
     for step in range(1, 5):
@@ -280,11 +276,14 @@
         if step < 4:
             down = along_z(down, -1)
         if step < 4:
-            up, down = lax.optimization_barrier((up, down))
+            if extra is not None and step == 2:
+                up, down, extra = lax.optimization_barrier((up, down, extra))
+            else:
+                up, down = lax.optimization_barrier((up, down))
             found += [up, down]
         else:
             found.append(up)
-    return found
+    return found if extra is None else (found, extra)
 
 
 ROWS = [list(range(8)), list(range(8, 16))]
@@ -394,10 +393,8 @@
     )
     q_twin = other_core(q_same)
     kv_own = lax.dynamic_slice_in_dim(kv_flat, row * half, half, 1)
-    shards = z_ring(tokens)
-    piece, shards[5], shards[6] = lax.optimization_barrier(
-        (owned_piece(w_out, seq), shards[5], shards[6])
-    )
+    shards, piece = z_ring(tokens, owned_piece(w_out, seq))
+    piece, shards[5], shards[6] = lax.optimization_barrier((piece, shards[5], shards[6]))
     piece = lax.all_to_all(piece, "head", 0, 0, tiled=True, axis_index_groups=ROWS)
     kv_part, q_mine, q_theirs = project(
         spots,
@@ -407,11 +404,10 @@
     kv = (kv_part + swap_rows(kv_part)).astype(jnp.bfloat16)
     piece, kv = lax.optimization_barrier((piece, kv))
     q_sent = swap_rows(q_theirs)
-    near = along_seq(kv, 1)
-    far = along_seq(kv[:kv_flat.shape[0]], 2)
-    keyval = sent_to_row(jnp.concatenate([kv, near, far], axis=0))
-    keyval = keyval.reshape(8, 5, kv_flat.shape[0], tok_rows)
-    attended = attend(seq.reshape(1), q_mine, q_sent, keyval)
+    keyval = sent_to_row(kv).reshape(8, 2, kv_flat.shape[0], tok_rows)
+    near = along_seq(keyval, 1)
+    far = along_seq(keyval[:, 0], 2)
+    attended = attend(seq.reshape(1), q_mine, q_sent, far, near, keyval)
     values = z_ring(attended)
     held, twin, values[3] = owned_columns(piece, seq, values[3])
     return finish(spots, values, held, twin)

time: 162 us -> 174 us (1.074)
  waiting for transfers between devices: 71.6 us -> 79.2 us
  starting transfers between devices: 54 us -> 57.4 us
    ppermute x2, waiting for transfers between devices: 2.93 us -> 14.8 us  [along_seq(): return lax.ppermute(value, 'seq', [(i, i + step) for i in range(16 - step)])]
    all_to_all x1, waiting for transfers between devices: 13 us -> 4.75 us  [sent_to_row(): lax.all_to_all(jnp.broadcast_to(value[None], (8, *value.shape)), 'head',...]
    ppermute x5, waiting for transfers between devices: 15.1 us -> 20.3 us  [swap_rows(): return lax.ppermute(value, 'head', [(i, (i + 8) % 16) for i in range(16)])]
    ppermute x14, starting transfers between devices: 24.3 us -> 28.8 us  [along_z(): lax.ppermute(value, 'head', [(i, i // 8 * 8 + (i + step) % 8) for i in ra...]
  transfers between devices with their start and end apart: 28 -> 28, of which waited for: 15 -> 16; matrix products, arithmetic and copies ran while one was open for 3% -> 3% of each run, Pallas kernels for 16% -> 15%
where the time goes in v5:
time: 174 us; the launch traced here: 173 us
  waiting for transfers between devices  79.2 us (46%)
  starting transfers between devices  57.4 us (33%)
  Pallas kernels  26.1 us (15%)
  local copies, waits for them, and re-layouts  7.97 us (5%)
  other arithmetic  2.2 us (1%)
    ppermute x14, waiting for transfers between devices, along_z(): lax.ppermute(value, 'head', [(i, i // 8 * 8 + (i + step) % 8) for i in ra...  39.4 us
    ppermute x14, starting transfers between devices, along_z(): lax.ppermute(value, 'head', [(i, i // 8 * 8 + (i + step) % 8) for i in ra...  28.8 us
    ppermute x5, waiting for transfers between devices, swap_rows(): return lax.ppermute(value, 'head', [(i, (i + 8) % 16) for i in range(16)])  20.3 us
    pallas_call x1, Pallas kernels, attend(): pl.pallas_call(attend_kernel, out_shape=jax.ShapeDtypeStruct(mine.shape,...  16.4 us
    ppermute x2, waiting for transfers between devices, along_seq(): return lax.ppermute(value, 'seq', [(i, i + step) for i in range(16 - step)])  14.8 us
    ppermute x2, starting transfers between devices, along_seq(): return lax.ppermute(value, 'seq', [(i, i + step) for i in range(16 - step)])  7.01 us
    pallas_call x1, Pallas kernels, project(): pl.pallas_call(project_kernel, out_shape=tuple((jax.ShapeDtypeStruct(shap...  6.99 us
    ppermute x5, starting transfers between devices, swap_rows(): return lax.ppermute(value, 'head', [(i, (i + 8) % 16) for i in range(16)])  6.71 us
  transfers between devices with their start and end apart: 28, of which 16 were waited for; matrix products, arithmetic and copies ran while one was open for 3% of the time, Pallas kernels for 15%

profile of v5, /device:TPU:2, one launch (start us, length us, event | category | flops | bytes accessed | tf_op | source)
XLA Modules:
  0.0 173.1 jit_solution(15564374484388623773)
XLA Ops:
  0.0 1.3 constant_dynamic-slice_fusion
  1.3 1.7 collective-permute-start.8
  3.0 1.9 %collective-permute-start = (bf16[256,512]{1,0:T(8,128)(2,1)S(1)}, bf16[256,512]{1,0:T(8,128)(2,1)S(1)}, u32[]{:S(2)}, u32[]{:S(2)}) collective-permute-start(bf16[256,512]{1,0:T(8,128)(2,1)S(1)} %copy-done.5), channel_id=1, source_target_pairs={{0,1},{1,2},{2,3},{3,4},{4,5},{5,6},{6,7},{7,0},{8,9},{9,10},{10,1... | collective-permute-start | bytes 786440 | tf_op jit(solution)/shard_map/ppermute | solution.py:254
  4.9 3.9 %collective-permute-start.1 = (bf16[256,512]{1,0:T(8,128)(2,1)S(1)}, bf16[256,512]{1,0:T(8,128)(2,1)S(1)}, u32[]{:S(2)}, u32[]{:S(2)}) collective-permute-start(bf16[256,512]{1,0:T(8,128)(2,1)S(1)} %copy-done.5), channel_id=1, source_target_pairs={{0,7},{1,0},{2,1},{3,2},{4,3},{5,4},{6,5},{7,6},{8,15},{9,8},{10,9... | collective-permute-start | bytes 786440 | tf_op jit(solution)/shard_map/ppermute | solution.py:254
  8.9 6.0 %collective-permute-done.refs_1_ = bf16[256,512]{1,0:T(8,128)(2,1)S(1)} collective-permute-done((bf16[256,512]{1,0:T(8,128)(2,1)S(1)}, bf16[256,512]{1,0:T(8,128)(2,1)S(1)}, u32[]{:S(2)}, u32[]{:S(2)}) %collective-permute-start) | collective-permute-done | bytes 262176 | tf_op jit(solution)/shard_map/ppermute | solution.py:254
  14.9 0.1 collective-permute-start.2
  15.0 3.2 %collective-permute-start.3 = (bf16[256,512]{1,0:T(8,128)(2,1)S(1)}, bf16[256,512]{1,0:T(8,128)(2,1)}, u32[]{:S(2)}, u32[]{:S(2)}) collective-permute-start(bf16[256,512]{1,0:T(8,128)(2,1)S(1)} %collective-permute-done.1.refs_2_), channel_id=1, source_target_pairs={{0,7},{1,0},{2,1},{3,2},{4,3},{5,4},{6,5},{7,6},{8,15},{9,8},{10,9... | collective-permute-start | bytes 786440 | tf_op jit(solution)/shard_map/ppermute | solution.py:254
  18.2 8.1 %collective-permute-done.8.refs_11_ = bf16[2048,256]{1,0:T(8,128)(2,1)S(1)} collective-permute-done((bf16[2048,256]{1,0:T(8,128)(2,1)S(1)}, bf16[2048,256]{1,0:T(8,128)(2,1)S(1)}, u32[]{:S(2)}, u32[]{:S(2)}) %collective-permute-start.8) | collective-permute-done | bytes 1048608 | tf_op jit(solution)/shard_map/ppermute | solution.py:250
  26.3 0.0 collective-permute-start.9
  26.3 1.4 constant_dynamic-slice_fusion.1
  27.8 0.2 copy.6
  27.9 1.1 copy.8
  29.0 0.0 collective-permute-done.2.refs_3_
  29.1 2.0 %collective-permute-start.4 = (bf16[256,512]{1,0:T(8,128)(2,1)S(1)}, bf16[256,512]{1,0:T(8,128)(2,1)}, u32[]{:S(2)}, u32[]{:S(2)}) collective-permute-start(bf16[256,512]{1,0:T(8,128)(2,1)S(1)} %collective-permute-done.2.refs_3_), channel_id=1, source_target_pairs={{0,1},{1,2},{2,3},{3,4},{4,5},{5,6},{6,7},{7,0},{8,9},{9,10},{10,1... | collective-permute-start | bytes 786440 | tf_op jit(solution)/shard_map/ppermute | solution.py:254
  31.0 4.0 %collective-permute-start.5 = (bf16[256,512]{1,0:T(8,128)(2,1)}, bf16[256,512]{1,0:T(8,128)(2,1)}, u32[]{:S(2)}, u32[]{:S(2)}) collective-permute-start(bf16[256,512]{1,0:T(8,128)(2,1)} %collective-permute-done.3.refs_4_), channel_id=1, source_target_pairs={{0,7},{1,0},{2,1},{3,2},{4,3},{5,4},{6,5},{7,6},{8,15},{9,8},{10,9... | collective-permute-start | bytes 786440 | tf_op jit(solution)/shard_map/ppermute | solution.py:254
  35.1 6.6 %collective-permute-done.4.refs_5_ = bf16[256,512]{1,0:T(8,128)(2,1)} collective-permute-done((bf16[256,512]{1,0:T(8,128)(2,1)S(1)}, bf16[256,512]{1,0:T(8,128)(2,1)}, u32[]{:S(2)}, u32[]{:S(2)}) %collective-permute-start.4) | collective-permute-done | bytes 262176 | tf_op jit(solution)/shard_map/ppermute | solution.py:254
  41.7 6.1 %all-to-all-start = ((bf16[8,2,32,512]{3,2,1,0:T(8,128)(2,1)}), bf16[8,2,32,512]{3,2,1,0:T(8,128)(2,1)S(1)}, u32[]{:S(2)}, u32[]{:S(2)}) async-start(bf16[8,2,32,512]{3,2,1,0:T(8,128)(2,1)} %bitcast.23), calls=%async_computation | async-start | bytes 1048576 | tf_op jit(solution)/shard_map/all_to_all | solution.py:398
  47.8 0.8 dynamic-slice_bitcast_fusion
  48.5 1.6 collective-permute-start.7
  50.1 2.0 %collective-permute-start.6 = (bf16[256,512]{1,0:T(8,128)(2,1)}, bf16[256,512]{1,0:T(8,128)(2,1)S(1)}, u32[]{:S(2)}, u32[]{:S(2)}) collective-permute-start(bf16[256,512]{1,0:T(8,128)(2,1)} %collective-permute-done.4.refs_5_), channel_id=1, source_target_pairs={{0,1},{1,2},{2,3},{3,4},{4,5},{5,6},{6,7},{7,0},{8,9},{9,10},{10,1... | collective-permute-start | bytes 786440 | tf_op jit(solution)/shard_map/ppermute | solution.py:254
  52.1 0.6 pad_add_fusion.spot_ref
  52.7 2.8 %collective-permute-done.7.refs_9_ = bf16[32,4096]{1,0:T(8,128)(2,1)S(1)} collective-permute-done((bf16[32,4096]{1,0:T(8,128)(2,1)S(1)}, bf16[32,4096]{1,0:T(8,128)(2,1)S(1)}, u32[]{:S(2)}, u32[]{:S(2)}) %collective-permute-start.7) | collective-permute-done | bytes 262176 | tf_op jit(solution)/shard_map/ppermute | solution.py:250
  55.5 11.9 %collective-permute-done.6.refs_7_ = bf16[256,512]{1,0:T(8,128)(2,1)S(1)} collective-permute-done((bf16[256,512]{1,0:T(8,128)(2,1)}, bf16[256,512]{1,0:T(8,128)(2,1)S(1)}, u32[]{:S(2)}, u32[]{:S(2)}) %collective-permute-start.6) | collective-permute-done | bytes 262176 | tf_op jit(solution)/shard_map/ppermute | solution.py:254
  67.4 0.7 copy-done.10
  68.1 0.3 copy-done.3
  68.5 7.0 %shard_map.46 = (f32[64,256]{1,0:T(8,128)}, f32[256,256]{1,0:T(8,128)}, f32[256,256]{1,0:T(8,128)}) custom-call(s32[2]{0:T(128)} %pad_add_fusion.spot_ref, bf16[256,512]{1,0:T(8,128)(2,1)} %refs_0_.1, bf16[256,512]{1,0:T(8,128)(2,1)} %copy-done.6, bf16[256,512]{1,0:T(8,128)(2,1)} %copy-done.7, bf16[256,512]{1,0:T(8,128)(2,1)} %copy-done.8, ...), custom_call_target="tpu_custom_call" | custom-call | tf_op jit(solution)/shard_map/pallas_call | solution.py:237
  75.4 1.7 collective-permute-start.11
  77.1 2.9 %collective-permute-done.11 = f32[64,256]{1,0:T(8,128)S(1)} collective-permute-done((f32[64,256]{1,0:T(8,128)}, f32[64,256]{1,0:T(8,128)S(1)}, u32[]{:S(2)}, u32[]{:S(2)}) %collective-permute-start.11) | collective-permute-done | bytes 65568 | tf_op jit(solution)/shard_map/ppermute | solution.py:250
  80.0 0.9 add_convert_fusion.1
  80.9 0.0 all-to-all-done
  80.9 0.7 broadcast_in_dim.21
  81.6 4.5 %all-to-all-start.1 = ((bf16[8,64,256]{2,1,0:T(8,128)(2,1)}), bf16[8,64,256]{2,1,0:T(8,128)(2,1)S(1)}, u32[]{:S(2)}, u32[]{:S(2)}) async-start(bf16[8,64,256]{2,1,0:T(8,128)(2,1)} %broadcast_in_dim.21), calls=%async_computation.1 | async-start | bytes 524288 | tf_op jit(solution)/shard_map/all_to_all | solution.py:293
  86.1 1.6 collective-permute-start.10
  87.7 1.5 collective-permute-start.16
  89.2 0.5 collective-permute-start.17
  89.7 2.1 %collective-permute-start.18 = (bf16[8,2,32,512]{3,2,1,0:T(8,128)(2,1)S(1)}, bf16[8,2,32,512]{3,2,1,0:T(8,128)(2,1)S(1)}, u32[]{:S(2)}, u32[]{:S(2)}) collective-permute-start(bf16[8,2,32,512]{3,2,1,0:T(8,128)(2,1)S(1)} %all-to-all-done), channel_id=1, source_target_pairs={{0,128},{16,144},{32,160},{48,176},{64,192},{80,208},{96,224},{112... | collective-permute-start | bytes 1572872 | tf_op jit(solution)/shard_map/ppermute | solution.py:264
  91.9 4.8 %all-to-all-done.1 = bf16[8,64,256]{2,1,0:T(8,128)(2,1)S(1)} async-done(((bf16[8,64,256]{2,1,0:T(8,128)(2,1)}), bf16[8,64,256]{2,1,0:T(8,128)(2,1)S(1)}, u32[]{:S(2)}, u32[]{:S(2)}) %all-to-all-start.1) | async-done | bytes 262176 | tf_op jit(solution)/shard_map/all_to_all | solution.py:293
  96.6 1.9 %collective-permute-start.13 = (bf16[8,2,32,256]{3,2,1,0:T(8,128)(2,1)S(1)}, bf16[8,2,32,256]{3,2,1,0:T(8,128)(2,1)S(1)}, u32[]{:S(2)}, u32[]{:S(2)}) collective-permute-start(bf16[8,2,32,256]{3,2,1,0:T(8,128)(2,1)S(1)} %bitcast.24), channel_id=1, source_target_pairs={{0,16},{16,32},{32,48},{48,64},{64,80},{80,96},{96,112},{112,128},... | collective-permute-start | bytes 786440 | tf_op jit(solution)/shard_map/ppermute | solution.py:260
  98.5 0.0 collective-permute-done.10.sent_any
  98.6 5.1 %collective-permute-start.12 = (bf16[8,32,256]{2,1,0:T(8,128)(2,1)S(1)}, bf16[8,32,256]{2,1,0:T(8,128)(2,1)S(1)}, u32[]{:S(2)}, u32[]{:S(2)}) collective-permute-start(bf16[8,32,256]{2,1,0:T(8,128)(2,1)S(1)} %slice_bitcast_fusion), channel_id=1, source_target_pairs={{0,32},{16,48},{32,64},{48,80},{64,96},{80,112},{96,128},{112,144}... | collective-permute-start | bytes 393224 | tf_op jit(solution)/shard_map/ppermute | solution.py:260
  103.7 14.8 %collective-permute-done.12.far_ref = bf16[8,32,256]{2,1,0:T(8,128)(2,1)S(1)} collective-permute-done((bf16[8,32,256]{2,1,0:T(8,128)(2,1)S(1)}, bf16[8,32,256]{2,1,0:T(8,128)(2,1)S(1)}, u32[]{:S(2)}, u32[]{:S(2)}) %collective-permute-start.12) | collective-permute-done | bytes 131104 | tf_op jit(solution)/shard_map/ppermute | solution.py:260
  118.4 0.9 copy-done
  119.4 16.4 %shard_map.47.refs_0_ = bf16[256,256]{1,0:T(8,128)(2,1)S(1)} custom-call(s32[1]{0:T(128)} %bitcast.2.seq_ref, f32[256,256]{1,0:T(8,128)S(1)} %copy-done, f32[256,256]{1,0:T(8,128)S(1)} %collective-permute-done.10.sent_any, bf16[8,32,256]{2,1,0:T(8,128)(2,1)S(1)} %collective-permute-done.12.far_ref, ...), custom_call_target="tpu_custom_call" | custom-call | tf_op jit(solution)/shard_map/pallas_call | solution.py:151
  135.8 1.8 %collective-permute-start.14 = (bf16[256,256]{1,0:T(8,128)(2,1)S(1)}, bf16[256,256]{1,0:T(8,128)(2,1)S(1)}, u32[]{:S(2)}, u32[]{:S(2)}) collective-permute-start(bf16[256,256]{1,0:T(8,128)(2,1)S(1)} %shard_map.47.refs_0_), channel_id=1, source_target_pairs={{0,1},{1,2},{2,3},{3,4},{4,5},{5,6},{6,7},{7,0},{8,9},{9,10},{10,1... | collective-permute-start | bytes 393224 | tf_op jit(solution)/shard_map/ppermute | solution.py:254
  137.6 1.5 collective-permute-start.15
  139.1 3.0 %collective-permute-done.14.refs_1_ = bf16[256,256]{1,0:T(8,128)(2,1)S(1)} collective-permute-done((bf16[256,256]{1,0:T(8,128)(2,1)S(1)}, bf16[256,256]{1,0:T(8,128)(2,1)S(1)}, u32[]{:S(2)}, u32[]{:S(2)}) %collective-permute-start.14) | collective-permute-done | bytes 131104 | tf_op jit(solution)/shard_map/ppermute | solution.py:254
  142.1 0.5 collective-permute-done.15.refs_2_
  142.6 1.5 collective-permute-start.19
  144.1 1.8 %collective-permute-start.20 = (bf16[256,256]{1,0:T(8,128)(2,1)S(1)}, bf16[256,256]{1,0:T(8,128)(2,1)S(1)}, u32[]{:S(2)}, u32[]{:S(2)}) collective-permute-start(bf16[256,256]{1,0:T(8,128)(2,1)S(1)} %collective-permute-done.15.refs_2_), channel_id=1, source_target_pairs={{0,7},{1,0},{2,1},{3,2},{4,3},{5,4},{6,5},{7,6},{8,15},{9,8},{10,9... | collective-permute-start | bytes 393224 | tf_op jit(solution)/shard_map/ppermute | solution.py:254
  145.8 0.2 broadcast_in_dim.22
  146.2 2.6 %collective-permute-done.19.refs_3_ = bf16[256,256]{1,0:T(8,128)(2,1)S(1)} collective-permute-done((bf16[256,256]{1,0:T(8,128)(2,1)S(1)}, bf16[256,256]{1,0:T(8,128)(2,1)S(1)}, u32[]{:S(2)}, u32[]{:S(2)}) %collective-permute-start.19) | collective-permute-done | bytes 131104 | tf_op jit(solution)/shard_map/ppermute | solution.py:254
  148.8 0.4 collective-permute-done.20.refs_4_
  149.3 0.1 collective-permute-start.23
  149.4 3.3 %collective-permute-start.21 = (bf16[256,256]{1,0:T(8,128)(2,1)S(1)}, bf16[256,256]{1,0:T(8,128)(2,1)S(1)}, u32[]{:S(2)}, u32[]{:S(2)}) collective-permute-start(bf16[256,256]{1,0:T(8,128)(2,1)S(1)} %collective-permute-done.19.refs_3_), channel_id=1, source_target_pairs={{0,1},{1,2},{2,3},{3,4},{4,5},{5,6},{6,7},{7,0},{8,9},{9,10},{10,1... | collective-permute-start | bytes 393224 | tf_op jit(solution)/shard_map/ppermute | solution.py:254
  152.7 0.0 collective-permute-start.22
  152.7 3.8 %collective-permute-done.21.refs_5_ = bf16[256,256]{1,0:T(8,128)(2,1)S(1)} collective-permute-done((bf16[256,256]{1,0:T(8,128)(2,1)S(1)}, bf16[256,256]{1,0:T(8,128)(2,1)S(1)}, u32[]{:S(2)}, u32[]{:S(2)}) %collective-permute-start.21) | collective-permute-done | bytes 131104 | tf_op jit(solution)/shard_map/ppermute | solution.py:254
  156.5 2.0 %collective-permute-done.22.refs_6_ = bf16[256,256]{1,0:T(8,128)(2,1)S(1)} collective-permute-done((bf16[256,256]{1,0:T(8,128)(2,1)S(1)}, bf16[256,256]{1,0:T(8,128)(2,1)S(1)}, u32[]{:S(2)}, u32[]{:S(2)}) %collective-permute-start.22) | collective-permute-done | bytes 131104 | tf_op jit(solution)/shard_map/ppermute | solution.py:254
  158.5 1.7 %collective-permute-start.24 = (bf16[256,256]{1,0:T(8,128)(2,1)S(1)}, bf16[256,256]{1,0:T(8,128)(2,1)S(1)}, u32[]{:S(2)}, u32[]{:S(2)}) collective-permute-start(bf16[256,256]{1,0:T(8,128)(2,1)S(1)} %collective-permute-done.21.refs_5_), channel_id=1, source_target_pairs={{0,1},{1,2},{2,3},{3,4},{4,5},{5,6},{6,7},{7,0},{8,9},{9,10},{10,1... | collective-permute-start | bytes 393224 | tf_op jit(solution)/shard_map/ppermute | solution.py:254
  160.3 1.8 %shard_map.48 = (f32[256,1024]{1,0:T(8,128)S(1)}, bf16[1,256,1024]{2,1,0:T(8,128)(2,1)S(1)}) custom-call(s32[2]{0:T(128)S(1)} %copy-done.1, bf16[256,256]{1,0:T(8,128)(2,1)S(1)} %shard_map.47.refs_0_, bf16[256,256]{1,0:T(8,128)(2,1)S(1)} %collective-permute-done.14.refs_1_, bf16[256,256]{1,0:T(8,128)(2,1)S(1)} %collective-permute-done.15.refs_2_, ...), custom_call_target="tpu_custom_call" | custom-call | tf_op jit(solution)/shard_map/pallas_call | solution.py:357
  162.1 2.6 %collective-permute-done.24.last_ref = bf16[256,256]{1,0:T(8,128)(2,1)S(1)} collective-permute-done((bf16[256,256]{1,0:T(8,128)(2,1)S(1)}, bf16[256,256]{1,0:T(8,128)(2,1)S(1)}, u32[]{:S(2)}, u32[]{:S(2)}) %collective-permute-start.24) | collective-permute-done | bytes 131104 | tf_op jit(solution)/shard_map/ppermute | solution.py:254
  164.7 0.9 shard_map.49
  165.6 0.2 collective-permute-start.25
  165.9 6.5 %collective-permute-done.25 = bf16[256,512]{1,0:T(8,128)(2,1)S(1)} collective-permute-done((bf16[256,512]{1,0:T(8,128)(2,1)S(1)}, bf16[256,512]{1,0:T(8,128)(2,1)S(1)}, u32[]{:S(2)}, u32[]{:S(2)}) %collective-permute-start.25) | collective-permute-done | bytes 262176 | tf_op jit(solution)/shard_map/ppermute | solution.py:250
  172.3 0.8 add_convert_fusion
  (33 shorter events, 0.3 us)
Async XLA Ops:
  0.0 3.0 %copy-start.5 = (bf16[256,512]{1,0:T(8,128)(2,1)S(1)}, bf16[256,512]{1,0:T(8,128)(2,1)}, u32[]{:S(2)}) copy-start(bf16[256,512]{1,0:T(8,128)(2,1)} %refs_0_.1) | copy-start | bytes 786436
  1.3 25.0 %collective-permute-start.8 = (bf16[2048,256]{1,0:T(8,128)(2,1)S(1)}, bf16[2048,256]{1,0:T(8,128)(2,1)S(1)}, u32[]{:S(2)}, u32[]{:S(2)}) collective-permute-start(bf16[2048,256]{1,0:T(8,128)(2,1)S(1)} %constant_dynamic-slice_fusion), channel_id=1, source_target_pairs={{0,8},{1,9},{2,10},{3,11},{4,12},{5,13},{6,14},{7,15},{8,0},{9,1},... | collective-permute-start | bytes 3145736 | tf_op jit(solution)/shard_map/ppermute | solution.py:250
  3.0 11.9 %collective-permute-start = (bf16[256,512]{1,0:T(8,128)(2,1)S(1)}, bf16[256,512]{1,0:T(8,128)(2,1)S(1)}, u32[]{:S(2)}, u32[]{:S(2)}) collective-permute-start(bf16[256,512]{1,0:T(8,128)(2,1)S(1)} %copy-done.5), channel_id=1, source_target_pairs={{0,1},{1,2},{2,3},{3,4},{4,5},{5,6},{6,7},{7,0},{8,9},{9,10},{10,1... | collective-permute-start | bytes 786440 | tf_op jit(solution)/shard_map/ppermute | solution.py:254
  4.9 10.0 %collective-permute-start.1 = (bf16[256,512]{1,0:T(8,128)(2,1)S(1)}, bf16[256,512]{1,0:T(8,128)(2,1)S(1)}, u32[]{:S(2)}, u32[]{:S(2)}) collective-permute-start(bf16[256,512]{1,0:T(8,128)(2,1)S(1)} %copy-done.5), channel_id=1, source_target_pairs={{0,7},{1,0},{2,1},{3,2},{4,3},{5,4},{6,5},{7,6},{8,15},{9,8},{10,9... | collective-permute-start | bytes 786440 | tf_op jit(solution)/shard_map/ppermute | solution.py:254
  8.9 38.9 %copy-start.4 = (bf16[8192,32]{0,1:T(8,128)(2,1)S(1)}, bf16[8192,32]{0,1:T(8,128)(2,1)}, u32[]{:S(2)}) copy-start(bf16[8192,32]{0,1:T(8,128)(2,1)} %param.6) | copy-start | bytes 1572868
  14.9 26.8 %copy-start.6 = (bf16[256,512]{1,0:T(8,128)(2,1)}, bf16[256,512]{1,0:T(8,128)(2,1)S(1)}, u32[]{:S(2)}) copy-start(bf16[256,512]{1,0:T(8,128)(2,1)S(1)} %collective-permute-done.refs_1_) | copy-start | bytes 786436
  14.9 26.8 %copy-start.7 = (bf16[256,512]{1,0:T(8,128)(2,1)}, bf16[256,512]{1,0:T(8,128)(2,1)S(1)}, u32[]{:S(2)}) copy-start(bf16[256,512]{1,0:T(8,128)(2,1)S(1)} %collective-permute-done.1.refs_2_) | copy-start | bytes 786436
  14.9 14.1 %collective-permute-start.2 = (bf16[256,512]{1,0:T(8,128)(2,1)S(1)}, bf16[256,512]{1,0:T(8,128)(2,1)S(1)}, u32[]{:S(2)}, u32[]{:S(2)}) collective-permute-start(bf16[256,512]{1,0:T(8,128)(2,1)S(1)} %collective-permute-done.refs_1_), channel_id=1, source_target_pairs={{0,1},{1,2},{2,3},{3,4},{4,5},{5,6},{6,7},{7,0},{8,9},{9,10},{10,1... | collective-permute-start | bytes 786440 | tf_op jit(solution)/shard_map/ppermute | solution.py:254
  15.0 14.1 %collective-permute-start.3 = (bf16[256,512]{1,0:T(8,128)(2,1)S(1)}, bf16[256,512]{1,0:T(8,128)(2,1)}, u32[]{:S(2)}, u32[]{:S(2)}) collective-permute-start(bf16[256,512]{1,0:T(8,128)(2,1)S(1)} %collective-permute-done.1.refs_2_), channel_id=1, source_target_pairs={{0,7},{1,0},{2,1},{3,2},{4,3},{5,4},{6,5},{7,6},{8,15},{9,8},{10,9... | collective-permute-start | bytes 786440 | tf_op jit(solution)/shard_map/ppermute | solution.py:254
  26.3 15.4 %copy-start.2 = (bf16[2048,256]{1,0:T(8,128)(2,1)}, bf16[2048,256]{1,0:T(8,128)(2,1)S(1)}, u32[]{:S(2)}) copy-start(bf16[2048,256]{1,0:T(8,128)(2,1)S(1)} %collective-permute-done.8.refs_11_) | copy-start | bytes 3145732
  26.3 41.1 %collective-permute-start.9 = (bf16[2048,256]{1,0:T(8,128)(2,1)S(1)}, bf16[2048,256]{1,0:T(8,128)(2,1)S(1)}, u32[]{:S(2)}, u32[]{:S(2)}) collective-permute-start(bf16[2048,256]{1,0:T(8,128)(2,1)S(1)} %collective-permute-done.8.refs_11_), channel_id=1, source_target_pairs={{0,16},{16,0},{32,48},{48,32},{64,80},{80,64},{96,112},{112,96},{1... | collective-permute-start | bytes 3145736 | tf_op jit(solution)/shard_map/ppermute | solution.py:268
  29.0 38.4 %copy-start.8 = (bf16[256,512]{1,0:T(8,128)(2,1)}, bf16[256,512]{1,0:T(8,128)(2,1)S(1)}, u32[]{:S(2)}) copy-start(bf16[256,512]{1,0:T(8,128)(2,1)S(1)} %collective-permute-done.2.refs_3_) | copy-start | bytes 786436
  29.1 12.7 %collective-permute-start.4 = (bf16[256,512]{1,0:T(8,128)(2,1)S(1)}, bf16[256,512]{1,0:T(8,128)(2,1)}, u32[]{:S(2)}, u32[]{:S(2)}) collective-permute-start(bf16[256,512]{1,0:T(8,128)(2,1)S(1)} %collective-permute-done.2.refs_3_), channel_id=1, source_target_pairs={{0,1},{1,2},{2,3},{3,4},{4,5},{5,6},{6,7},{7,0},{8,9},{9,10},{10,1... | collective-permute-start | bytes 786440 | tf_op jit(solution)/shard_map/ppermute | solution.py:254
  31.0 10.7 %collective-permute-start.5 = (bf16[256,512]{1,0:T(8,128)(2,1)}, bf16[256,512]{1,0:T(8,128)(2,1)}, u32[]{:S(2)}, u32[]{:S(2)}) collective-permute-start(bf16[256,512]{1,0:T(8,128)(2,1)} %collective-permute-done.3.refs_4_), channel_id=1, source_target_pairs={{0,7},{1,0},{2,1},{3,2},{4,3},{5,4},{6,5},{7,6},{8,15},{9,8},{10,9... | collective-permute-start | bytes 786440 | tf_op jit(solution)/shard_map/ppermute | solution.py:254
  41.7 39.1 %all-to-all-start = ((bf16[8,2,32,512]{3,2,1,0:T(8,128)(2,1)}), bf16[8,2,32,512]{3,2,1,0:T(8,128)(2,1)S(1)}, u32[]{:S(2)}, u32[]{:S(2)}) async-start(bf16[8,2,32,512]{3,2,1,0:T(8,128)(2,1)} %bitcast.23), calls=%async_computation | async-start | bytes 1048576 | tf_op jit(solution)/shard_map/all_to_all | solution.py:398
  48.5 6.9 %collective-permute-start.7 = (bf16[32,4096]{1,0:T(8,128)(2,1)S(1)}, bf16[32,4096]{1,0:T(8,128)(2,1)S(1)}, u32[]{:S(2)}, u32[]{:S(2)}) collective-permute-start(bf16[32,4096]{1,0:T(8,128)(2,1)S(1)} %get-tuple-element.63), channel_id=1, source_target_pairs={{0,8},{1,9},{2,10},{3,11},{4,12},{5,13},{6,14},{7,15},{8,0},{9,1},... | collective-permute-start | bytes 786440 | tf_op jit(solution)/shard_map/ppermute | solution.py:250
  50.1 17.3 %collective-permute-start.6 = (bf16[256,512]{1,0:T(8,128)(2,1)}, bf16[256,512]{1,0:T(8,128)(2,1)S(1)}, u32[]{:S(2)}, u32[]{:S(2)}) collective-permute-start(bf16[256,512]{1,0:T(8,128)(2,1)} %collective-permute-done.4.refs_5_), channel_id=1, source_target_pairs={{0,1},{1,2},{2,3},{3,4},{4,5},{5,6},{6,7},{7,0},{8,9},{9,10},{10,1... | collective-permute-start | bytes 786440 | tf_op jit(solution)/shard_map/ppermute | solution.py:254
  55.5 11.9 %copy-start.9 = (bf16[32,4096]{1,0:T(8,128)(2,1)}, bf16[32,4096]{1,0:T(8,128)(2,1)S(1)}, u32[]{:S(2)}) copy-start(bf16[32,4096]{1,0:T(8,128)(2,1)S(1)} %collective-permute-done.7.refs_9_) | copy-start | bytes 786436
  67.4 0.7 copy-start.10
  67.4 1.1 copy-start.3
  75.4 4.6 %collective-permute-start.11 = (f32[64,256]{1,0:T(8,128)}, f32[64,256]{1,0:T(8,128)S(1)}, u32[]{:S(2)}, u32[]{:S(2)}) collective-permute-start(f32[64,256]{1,0:T(8,128)} %get-tuple-element.46), channel_id=1, source_target_pairs={{0,8},{1,9},{2,10},{3,11},{4,12},{5,13},{6,14},{7,15},{8,0},{9,1},... | collective-permute-start | bytes 196616 | tf_op jit(solution)/shard_map/ppermute | solution.py:250
  81.6 15.0 %all-to-all-start.1 = ((bf16[8,64,256]{2,1,0:T(8,128)(2,1)}), bf16[8,64,256]{2,1,0:T(8,128)(2,1)S(1)}, u32[]{:S(2)}, u32[]{:S(2)}) async-start(bf16[8,64,256]{2,1,0:T(8,128)(2,1)} %broadcast_in_dim.21), calls=%async_computation.1 | async-start | bytes 524288 | tf_op jit(solution)/shard_map/all_to_all | solution.py:293
  86.1 12.4 %collective-permute-start.10 = (f32[256,256]{1,0:T(8,128)}, f32[256,256]{1,0:T(8,128)S(1)}, u32[]{:S(2)}, u32[]{:S(2)}) collective-permute-start(f32[256,256]{1,0:T(8,128)} %get-tuple-element.44), channel_id=1, source_target_pairs={{0,8},{1,9},{2,10},{3,11},{4,12},{5,13},{6,14},{7,15},{8,0},{9,1},... | collective-permute-start | bytes 786440 | tf_op jit(solution)/shard_map/ppermute | solution.py:250
  87.7 61.4 %collective-permute-start.16 = (bf16[8,2,32,512]{3,2,1,0:T(8,128)(2,1)S(1)}, bf16[8,2,32,512]{3,2,1,0:T(8,128)(2,1)S(1)}, u32[]{:S(2)}, u32[]{:S(2)}) collective-permute-start(bf16[8,2,32,512]{3,2,1,0:T(8,128)(2,1)S(1)} %all-to-all-done), channel_id=1, source_target_pairs={{0,64},{16,80},{32,96},{48,112},{64,128},{80,144},{96,160},{112,17... | collective-permute-start | bytes 1572872 | tf_op jit(solution)/shard_map/ppermute | solution.py:264
  89.2 59.9 %collective-permute-start.17 = (bf16[8,2,32,512]{3,2,1,0:T(8,128)(2,1)S(1)}, bf16[8,2,32,512]{3,2,1,0:T(8,128)(2,1)S(1)}, u32[]{:S(2)}, u32[]{:S(2)}) collective-permute-start(bf16[8,2,32,512]{3,2,1,0:T(8,128)(2,1)S(1)} %all-to-all-done), channel_id=1, source_target_pairs={{0,192},{16,208},{32,224},{48,240},{64,0},{80,16},{96,32},{112,48}... | collective-permute-start | bytes 1572872 | tf_op jit(solution)/shard_map/ppermute | solution.py:264
  89.7 59.4 %collective-permute-start.18 = (bf16[8,2,32,512]{3,2,1,0:T(8,128)(2,1)S(1)}, bf16[8,2,32,512]{3,2,1,0:T(8,128)(2,1)S(1)}, u32[]{:S(2)}, u32[]{:S(2)}) collective-permute-start(bf16[8,2,32,512]{3,2,1,0:T(8,128)(2,1)S(1)} %all-to-all-done), channel_id=1, source_target_pairs={{0,128},{16,144},{32,160},{48,176},{64,192},{80,208},{96,224},{112... | collective-permute-start | bytes 1572872 | tf_op jit(solution)/shard_map/ppermute | solution.py:264
  96.6 21.8 %collective-permute-start.13 = (bf16[8,2,32,256]{3,2,1,0:T(8,128)(2,1)S(1)}, bf16[8,2,32,256]{3,2,1,0:T(8,128)(2,1)S(1)}, u32[]{:S(2)}, u32[]{:S(2)}) collective-permute-start(bf16[8,2,32,256]{3,2,1,0:T(8,128)(2,1)S(1)} %bitcast.24), channel_id=1, source_target_pairs={{0,16},{16,32},{32,48},{48,64},{64,80},{80,96},{96,112},{112,128},... | collective-permute-start | bytes 786440 | tf_op jit(solution)/shard_map/ppermute | solution.py:260
  98.6 19.9 %collective-permute-start.12 = (bf16[8,32,256]{2,1,0:T(8,128)(2,1)S(1)}, bf16[8,32,256]{2,1,0:T(8,128)(2,1)S(1)}, u32[]{:S(2)}, u32[]{:S(2)}) collective-permute-start(bf16[8,32,256]{2,1,0:T(8,128)(2,1)S(1)} %slice_bitcast_fusion), channel_id=1, source_target_pairs={{0,32},{16,48},{32,64},{48,80},{64,96},{80,112},{96,128},{112,144}... | collective-permute-start | bytes 393224 | tf_op jit(solution)/shard_map/ppermute | solution.py:260
  118.4 1.0 copy-start
  135.8 6.3 %collective-permute-start.14 = (bf16[256,256]{1,0:T(8,128)(2,1)S(1)}, bf16[256,256]{1,0:T(8,128)(2,1)S(1)}, u32[]{:S(2)}, u32[]{:S(2)}) collective-permute-start(bf16[256,256]{1,0:T(8,128)(2,1)S(1)} %shard_map.47.refs_0_), channel_id=1, source_target_pairs={{0,1},{1,2},{2,3},{3,4},{4,5},{5,6},{6,7},{7,0},{8,9},{9,10},{10,1... | collective-permute-start | bytes 393224 | tf_op jit(solution)/shard_map/ppermute | solution.py:254
  137.6 5.0 %collective-permute-start.15 = (bf16[256,256]{1,0:T(8,128)(2,1)S(1)}, bf16[256,256]{1,0:T(8,128)(2,1)S(1)}, u32[]{:S(2)}, u32[]{:S(2)}) collective-permute-start(bf16[256,256]{1,0:T(8,128)(2,1)S(1)} %shard_map.47.refs_0_), channel_id=1, source_target_pairs={{0,7},{1,0},{2,1},{3,2},{4,3},{5,4},{6,5},{7,6},{8,15},{9,8},{10,9... | collective-permute-start | bytes 393224 | tf_op jit(solution)/shard_map/ppermute | solution.py:254
  142.6 6.2 %collective-permute-start.19 = (bf16[256,256]{1,0:T(8,128)(2,1)S(1)}, bf16[256,256]{1,0:T(8,128)(2,1)S(1)}, u32[]{:S(2)}, u32[]{:S(2)}) collective-permute-start(bf16[256,256]{1,0:T(8,128)(2,1)S(1)} %collective-permute-done.14.refs_1_), channel_id=1, source_target_pairs={{0,1},{1,2},{2,3},{3,4},{4,5},{5,6},{6,7},{7,0},{8,9},{9,10},{10,1... | collective-permute-start | bytes 393224 | tf_op jit(solution)/shard_map/ppermute | solution.py:254
  144.1 5.1 %collective-permute-start.20 = (bf16[256,256]{1,0:T(8,128)(2,1)S(1)}, bf16[256,256]{1,0:T(8,128)(2,1)S(1)}, u32[]{:S(2)}, u32[]{:S(2)}) collective-permute-start(bf16[256,256]{1,0:T(8,128)(2,1)S(1)} %collective-permute-done.15.refs_2_), channel_id=1, source_target_pairs={{0,7},{1,0},{2,1},{3,2},{4,3},{5,4},{6,5},{7,6},{8,15},{9,8},{10,9... | collective-permute-start | bytes 393224 | tf_op jit(solution)/shard_map/ppermute | solution.py:254
  146.1 14.2 %copy-start.1 = (s32[2]{0:T(128)S(1)}, s32[2]{0:T(128)}, u32[]{:S(2)}) copy-start(s32[2]{0:T(128)} %pad_add_fusion.spot_ref) | copy-start | bytes 28
  149.3 11.0 %collective-permute-start.23 = (bf16[4,8,2,32,512]{4,3,2,1,0:T(8,128)(2,1)S(1)}, bf16[4,8,2,32,512]{4,3,2,1,0:T(8,128)(2,1)S(1)}, u32[]{:S(2)}, u32[]{:S(2)}) collective-permute-start(bf16[4,8,2,32,512]{4,3,2,1,0:T(8,128)(2,1)S(1)} %bitcast_dynamic-update-slice_fusion.refs_7_), channel_id=1, source_target_pairs={{0,16},{16,0},{32,48},{48,32},{64,80},{80,64},{96,112},{112,96},{1... | collective-permute-start | bytes 6291464 | tf_op jit(solution)/shard_map/ppermute | solution.py:268
  149.4 7.1 %collective-permute-start.21 = (bf16[256,256]{1,0:T(8,128)(2,1)S(1)}, bf16[256,256]{1,0:T(8,128)(2,1)S(1)}, u32[]{:S(2)}, u32[]{:S(2)}) collective-permute-start(bf16[256,256]{1,0:T(8,128)(2,1)S(1)} %collective-permute-done.19.refs_3_), channel_id=1, source_target_pairs={{0,1},{1,2},{2,3},{3,4},{4,5},{5,6},{6,7},{7,0},{8,9},{9,10},{10,1... | collective-permute-start | bytes 393224 | tf_op jit(solution)/shard_map/ppermute | solution.py:254
  152.7 5.8 %collective-permute-start.22 = (bf16[256,256]{1,0:T(8,128)(2,1)S(1)}, bf16[256,256]{1,0:T(8,128)(2,1)S(1)}, u32[]{:S(2)}, u32[]{:S(2)}) collective-permute-start(bf16[256,256]{1,0:T(8,128)(2,1)S(1)} %collective-permute-done.20.refs_4_), channel_id=1, source_target_pairs={{0,7},{1,0},{2,1},{3,2},{4,3},{5,4},{6,5},{7,6},{8,15},{9,8},{10,9... | collective-permute-start | bytes 393224 | tf_op jit(solution)/shard_map/ppermute | solution.py:254
  158.5 6.2 %collective-permute-start.24 = (bf16[256,256]{1,0:T(8,128)(2,1)S(1)}, bf16[256,256]{1,0:T(8,128)(2,1)S(1)}, u32[]{:S(2)}, u32[]{:S(2)}) collective-permute-start(bf16[256,256]{1,0:T(8,128)(2,1)S(1)} %collective-permute-done.21.refs_5_), channel_id=1, source_target_pairs={{0,1},{1,2},{2,3},{3,4},{4,5},{5,6},{6,7},{7,0},{8,9},{9,10},{10,1... | collective-permute-start | bytes 393224 | tf_op jit(solution)/shard_map/ppermute | solution.py:254
  165.6 6.7 %collective-permute-start.25 = (bf16[256,512]{1,0:T(8,128)(2,1)S(1)}, bf16[256,512]{1,0:T(8,128)(2,1)S(1)}, u32[]{:S(2)}, u32[]{:S(2)}) collective-permute-start(bf16[256,512]{1,0:T(8,128)(2,1)S(1)} %get-tuple-element.62), channel_id=1, source_target_pairs={{0,8},{1,9},{2,10},{3,11},{4,12},{5,13},{6,14},{7,15},{8,0},{9,1},... | collective-permute-start | bytes 786440 | tf_op jit(solution)/shard_map/ppermute | solution.py:250

commit v6 on v5

--- a/solution.py
+++ b/solution.py
@@ -10,7 +10,7 @@
 WIN1 = 512
 WIN2 = 32
 BLK = 128
-GROUP = 16
+GROUP = 32
 MIX = 16
 LOW = -1e30
 LANES = (((1,), (1,)), ((), ()))
@@ -179,52 +179,41 @@
 def project_kernel(spot_ref, *refs):
     shards_any, kv_any, own_any, parts_any = refs[:8], refs[8:10], refs[10], refs[11:13]
     kv_out, mine_any, theirs_any = refs[13:16]
-    shards, kv_ref, own_ref, part_ref, mine_out, theirs_out, sems = refs[16:]
-    depth = shards.shape[2]
+    rows_ref, kv_ref, own_ref, part_ref, mine_out, theirs_out, sems = refs[16:]
+    depth = shards_any[0].shape[1]
     half = own_ref.shape[0]
     row, core = spot_ref[0] >> 3, spot_ref[1]
     parts = kv_ref.shape[0] // 2
 
-    def rows_at(place, count):
+    def at(place, count):
         return pl.ds(pl.multiple_of(place * count, count), count)
 
-    moves = [(source, shards.at[k]) for k, source in enumerate(shards_any)]
+    moves = []
+    for offset, source in zip(OFFSETS, shards_any):
+        moves.append((source, rows_ref.at[:, at((spot_ref[0] + offset) & 7, depth)]))
     for source, side in zip(kv_any, (row, 1 - row)):
-        moves.append((source, kv_ref.at[rows_at(side, parts), :]))
-    moves.append((own_any.at[rows_at(row, half), :], own_ref))
+        moves.append((source, kv_ref.at[at(side, parts), :]))
+    moves.append((own_any.at[at(row, half), :], own_ref))
     for source, side in zip(parts_any, (core, 1 - core)):
-        moves.append((source, part_ref.at[rows_at(side, half // 2), :]))
+        moves.append((source, part_ref.at[at(side, half // 2), :]))
     fetches = [
         pltpu.make_async_copy(source, target, sems.at[k])
         for k, (source, target) in enumerate(moves)
     ]
     for fetch in fetches:
         fetch.start()
-    spots = [(spot_ref[0] + offset) & 7 for offset in OFFSETS]
     for fetch in fetches[:10]:
         fetch.wait()
-    total = None
-    for k, spot in enumerate(spots):
-        cols = kv_ref[:, rows_at(spot, depth)]
-        new = lax.dot_general(cols, shards[k], LANES, preferred_element_type=jnp.float32)
-        total = new if total is None else total + new
-    kv_out[...] = total
-
-    def whole_sum(weights, out, target, sem):
-        total = None
-        for k, spot in enumerate(spots):
-            new = jnp.dot(shards[k], weights[rows_at(spot, depth), :], preferred_element_type=jnp.float32)
-            total = new if total is None else total + new
-        out[...] = total
-        move = pltpu.make_async_copy(out, target, sem)
-        move.start()
-        return move
-
+    kv_out[...] = lax.dot_general(kv_ref[...], rows_ref[...], LANES, preferred_element_type=jnp.float32)
     fetches[10].wait()
-    keep = whole_sum(own_ref, mine_out, mine_any, sems.at[13])
+    mine_out[...] = jnp.dot(rows_ref[...], own_ref[...], preferred_element_type=jnp.float32)
+    keep = pltpu.make_async_copy(mine_out, mine_any, sems.at[13])
+    keep.start()
     for fetch in fetches[11:]:
         fetch.wait()
-    send = whole_sum(part_ref, theirs_out, theirs_any, sems.at[14])
+    theirs_out[...] = jnp.dot(rows_ref[...], part_ref[...], preferred_element_type=jnp.float32)
+    send = pltpu.make_async_copy(theirs_out, theirs_any, sems.at[14])
+    send.start()
     keep.wait()
     send.wait()
 
@@ -233,7 +222,7 @@
     far_off = pl.BlockSpec(memory_space=pltpu.HBM)
     own = arrays[10]
     half = (own.shape[0] // 2, own.shape[1])
-    kept = [(8, *arrays[0].shape), (2 * arrays[8].shape[0], arrays[8].shape[1]), half, half]
+    kept = [(arrays[0].shape[0], half[0]), (2 * arrays[8].shape[0], arrays[8].shape[1]), half, half]
     return pl.pallas_call(
         project_kernel,
         out_shape=tuple(jax.ShapeDtypeStruct(shape, jnp.float32) for shape in shapes),
@@ -277,7 +266,7 @@
             down = along_z(down, -1)
         if step < 4:
             if extra is not None and step == 2:
-                up, down, extra = lax.optimization_barrier((up, down, extra))
+                up, down, *extra = lax.optimization_barrier((up, down, *extra))
             else:
                 up, down = lax.optimization_barrier((up, down))
             found += [up, down]
@@ -393,16 +382,16 @@
     )
     q_twin = other_core(q_same)
     kv_own = lax.dynamic_slice_in_dim(kv_flat, row * half, half, 1)
-    shards, piece = z_ring(tokens, owned_piece(w_out, seq))
-    piece, shards[5], shards[6] = lax.optimization_barrier((piece, shards[5], shards[6]))
+    shards, (piece, spots) = z_ring(tokens, (owned_piece(w_out, seq), spots))
     piece = lax.all_to_all(piece, "head", 0, 0, tiled=True, axis_index_groups=ROWS)
     kv_part, q_mine, q_theirs = project(
         spots,
         (*shards, kv_own, kv_part, w_query, q_same, q_twin),
         ((2 * kv_flat.shape[0], tok_rows),) + ((tok_rows, w_query.shape[1]),) * 2,
     )
-    kv = (kv_part + swap_rows(kv_part)).astype(jnp.bfloat16)
-    piece, kv = lax.optimization_barrier((piece, kv))
+    kv_sent = swap_rows(kv_part)
+    piece, kv_sent = lax.optimization_barrier((piece, kv_sent))
+    kv = (kv_part + kv_sent).astype(jnp.bfloat16)
     q_sent = swap_rows(q_theirs)
     keyval = sent_to_row(kv).reshape(8, 2, kv_flat.shape[0], tok_rows)
     near = along_seq(keyval, 1)

time: 174 us -> 172 us (0.989)
  starting transfers between devices: 57.4 us -> 55.6 us
    ppermute x14, waiting for transfers between devices: 39.4 us -> 44.4 us  [along_z(): lax.ppermute(value, 'head', [(i, i // 8 * 8 + (i + step) % 8) for i in ra...]
    ppermute x14, starting transfers between devices: 28.8 us -> 24.3 us  [along_z(): lax.ppermute(value, 'head', [(i, i // 8 * 8 + (i + step) % 8) for i in ra...]
    ppermute x5, waiting for transfers between devices: 20.3 us -> 17.5 us  [swap_rows(): return lax.ppermute(value, 'head', [(i, (i + 8) % 16) for i in range(16)])]
    all_to_all x1, starting transfers between devices: 6.06 us -> 8.48 us  [body(): lax.all_to_all(piece, 'head', 0, 0, tiled=True, axis_index_groups=ROWS)]
  transfers between devices with their start and end apart: 28 -> 28, of which waited for: 16 -> 15; matrix products, arithmetic and copies ran while one was open for 3% -> 3% of each run, Pallas kernels for 15% -> 14%
where the time goes in v6:
time: 172 us
  waiting for transfers between devices  80.6 us (47%)
  starting transfers between devices  55.6 us (32%)
  Pallas kernels  25.3 us (15%)
  local copies, waits for them, and re-layouts  7.95 us (5%)
  other arithmetic  2.22 us (1%)
    ppermute x14, waiting for transfers between devices, along_z(): lax.ppermute(value, 'head', [(i, i // 8 * 8 + (i + step) % 8) for i in ra...  44.4 us
    ppermute x14, starting transfers between devices, along_z(): lax.ppermute(value, 'head', [(i, i // 8 * 8 + (i + step) % 8) for i in ra...  24.3 us
    ppermute x5, waiting for transfers between devices, swap_rows(): return lax.ppermute(value, 'head', [(i, (i + 8) % 16) for i in range(16)])  17.5 us
    pallas_call x1, Pallas kernels, attend(): pl.pallas_call(attend_kernel, out_shape=jax.ShapeDtypeStruct(mine.shape,...  15.6 us
    ppermute x2, waiting for transfers between devices, along_seq(): return lax.ppermute(value, 'seq', [(i, i + step) for i in range(16 - step)])  14 us
    all_to_all x1, starting transfers between devices, body(): lax.all_to_all(piece, 'head', 0, 0, tiled=True, axis_index_groups=ROWS)  8.48 us
    ppermute x2, starting transfers between devices, along_seq(): return lax.ppermute(value, 'seq', [(i, i + step) for i in range(16 - step)])  7.01 us
    pallas_call x1, Pallas kernels, project(): pl.pallas_call(project_kernel, out_shape=tuple((jax.ShapeDtypeStruct(shap...  7 us
  transfers between devices with their start and end apart: 28, of which 15 were waited for; matrix products, arithmetic and copies ran while one was open for 3% of the time, Pallas kernels for 14%

profile of v6, /device:TPU:2, one launch (start us, length us, event | category | flops | bytes accessed | tf_op | source)
XLA Modules:
  0.0 172.0 jit_solution(3614030954495917111)
XLA Ops:
  0.0 1.3 constant_dynamic-slice_fusion
  1.3 1.7 collective-permute-start.8
  3.0 1.9 %collective-permute-start = (bf16[256,512]{1,0:T(8,128)(2,1)S(1)}, bf16[256,512]{1,0:T(8,128)(2,1)S(1)}, u32[]{:S(2)}, u32[]{:S(2)}) collective-permute-start(bf16[256,512]{1,0:T(8,128)(2,1)S(1)} %copy-done.5), channel_id=1, source_target_pairs={{0,1},{1,2},{2,3},{3,4},{4,5},{5,6},{6,7},{7,0},{8,9},{9,10},{10,1... | collective-permute-start | bytes 786440 | tf_op jit(solution)/shard_map/ppermute | solution.py:243
  4.9 3.9 %collective-permute-start.1 = (bf16[256,512]{1,0:T(8,128)(2,1)S(1)}, bf16[256,512]{1,0:T(8,128)(2,1)S(1)}, u32[]{:S(2)}, u32[]{:S(2)}) collective-permute-start(bf16[256,512]{1,0:T(8,128)(2,1)S(1)} %copy-done.5), channel_id=1, source_target_pairs={{0,7},{1,0},{2,1},{3,2},{4,3},{5,4},{6,5},{7,6},{8,15},{9,8},{10,9... | collective-permute-start | bytes 786440 | tf_op jit(solution)/shard_map/ppermute | solution.py:243
  8.9 6.0 %collective-permute-done.refs_1_ = bf16[256,512]{1,0:T(8,128)(2,1)S(1)} collective-permute-done((bf16[256,512]{1,0:T(8,128)(2,1)S(1)}, bf16[256,512]{1,0:T(8,128)(2,1)S(1)}, u32[]{:S(2)}, u32[]{:S(2)}) %collective-permute-start) | collective-permute-done | bytes 262176 | tf_op jit(solution)/shard_map/ppermute | solution.py:243
  14.9 0.1 collective-permute-start.2
  15.0 3.2 %collective-permute-start.3 = (bf16[256,512]{1,0:T(8,128)(2,1)S(1)}, bf16[256,512]{1,0:T(8,128)(2,1)}, u32[]{:S(2)}, u32[]{:S(2)}) collective-permute-start(bf16[256,512]{1,0:T(8,128)(2,1)S(1)} %collective-permute-done.1.refs_2_), channel_id=1, source_target_pairs={{0,7},{1,0},{2,1},{3,2},{4,3},{5,4},{6,5},{7,6},{8,15},{9,8},{10,9... | collective-permute-start | bytes 786440 | tf_op jit(solution)/shard_map/ppermute | solution.py:243
  18.2 8.1 %collective-permute-done.8.refs_11_ = bf16[2048,256]{1,0:T(8,128)(2,1)S(1)} collective-permute-done((bf16[2048,256]{1,0:T(8,128)(2,1)S(1)}, bf16[2048,256]{1,0:T(8,128)(2,1)S(1)}, u32[]{:S(2)}, u32[]{:S(2)}) %collective-permute-start.8) | collective-permute-done | bytes 1048608 | tf_op jit(solution)/shard_map/ppermute | solution.py:239
  26.3 0.0 collective-permute-start.9
  26.3 1.4 constant_dynamic-slice_fusion.1
  27.8 0.2 copy.6
  27.9 1.1 copy.8
  29.0 0.6 pad_add_fusion.spot_ref
  29.6 0.0 collective-permute-done.2.refs_3_
  29.6 0.0 collective-permute-done.3.refs_4_
  29.7 8.5 %all-to-all-start = ((bf16[8,2,32,512]{3,2,1,0:T(8,128)(2,1)}), bf16[8,2,32,512]{3,2,1,0:T(8,128)(2,1)S(1)}, u32[]{:S(2)}, u32[]{:S(2)}) async-start(bf16[8,2,32,512]{3,2,1,0:T(8,128)(2,1)} %bitcast.23), calls=%async_computation | async-start | bytes 1048576 | tf_op jit(solution)/shard_map/all_to_all | solution.py:386
  38.2 2.0 %collective-permute-start.4 = (bf16[256,512]{1,0:T(8,128)(2,1)S(1)}, bf16[256,512]{1,0:T(8,128)(2,1)S(1)}, u32[]{:S(2)}, u32[]{:S(2)}) collective-permute-start(bf16[256,512]{1,0:T(8,128)(2,1)S(1)} %collective-permute-done.2.refs_3_), channel_id=1, source_target_pairs={{0,1},{1,2},{2,3},{3,4},{4,5},{5,6},{6,7},{7,0},{8,9},{9,10},{10,1... | collective-permute-start | bytes 786440 | tf_op jit(solution)/shard_map/ppermute | solution.py:243
  40.2 1.2 collective-permute-start.5
  41.4 0.8 dynamic-slice_bitcast_fusion
  42.2 1.6 collective-permute-start.7
  43.7 15.1 %collective-permute-done.4.refs_5_ = bf16[256,512]{1,0:T(8,128)(2,1)S(1)} collective-permute-done((bf16[256,512]{1,0:T(8,128)(2,1)S(1)}, bf16[256,512]{1,0:T(8,128)(2,1)S(1)}, u32[]{:S(2)}, u32[]{:S(2)}) %collective-permute-start.4) | collective-permute-done | bytes 262176 | tf_op jit(solution)/shard_map/ppermute | solution.py:243
  58.9 0.2 collective-permute-start.6
  59.1 0.0 collective-permute-done.7.refs_9_
  59.1 8.4 %collective-permute-done.6.refs_7_ = bf16[256,512]{1,0:T(8,128)(2,1)S(1)} collective-permute-done((bf16[256,512]{1,0:T(8,128)(2,1)S(1)}, bf16[256,512]{1,0:T(8,128)(2,1)S(1)}, u32[]{:S(2)}, u32[]{:S(2)}) %collective-permute-start.6) | collective-permute-done | bytes 262176 | tf_op jit(solution)/shard_map/ppermute | solution.py:243
  67.5 0.0 collective-permute-done.9.refs_12_
  67.5 0.7 copy-done.12
  68.2 0.3 copy-done.3
  68.6 7.0 %shard_map.46 = (f32[64,256]{1,0:T(8,128)}, f32[256,256]{1,0:T(8,128)}, f32[256,256]{1,0:T(8,128)}) custom-call(s32[2]{0:T(128)} %pad_add_fusion.spot_ref, bf16[256,512]{1,0:T(8,128)(2,1)} %refs_0_.1, bf16[256,512]{1,0:T(8,128)(2,1)} %copy-done.6, bf16[256,512]{1,0:T(8,128)(2,1)} %copy-done.7, bf16[256,512]{1,0:T(8,128)(2,1)} %copy-done.8, ...), custom_call_target="tpu_custom_call" | custom-call | tf_op jit(solution)/shard_map/pallas_call | solution.py:226
  75.6 1.7 collective-permute-start.11
  77.2 2.9 %collective-permute-done.11 = f32[64,256]{1,0:T(8,128)S(1)} collective-permute-done((f32[64,256]{1,0:T(8,128)}, f32[64,256]{1,0:T(8,128)S(1)}, u32[]{:S(2)}, u32[]{:S(2)}) %collective-permute-start.11) | collective-permute-done | bytes 65568 | tf_op jit(solution)/shard_map/ppermute | solution.py:239
  80.1 0.8 add_convert_fusion.1
  81.0 0.7 broadcast_in_dim.21
  81.7 4.9 %all-to-all-start.1 = ((bf16[8,64,256]{2,1,0:T(8,128)(2,1)}), bf16[8,64,256]{2,1,0:T(8,128)(2,1)S(1)}, u32[]{:S(2)}, u32[]{:S(2)}) async-start(bf16[8,64,256]{2,1,0:T(8,128)(2,1)} %broadcast_in_dim.21), calls=%async_computation.1 | async-start | bytes 524288 | tf_op jit(solution)/shard_map/all_to_all | solution.py:282
  86.6 1.6 collective-permute-start.10
  88.2 1.5 collective-permute-start.16
  89.7 0.5 collective-permute-start.17
  90.2 2.1 %collective-permute-start.18 = (bf16[8,2,32,512]{3,2,1,0:T(8,128)(2,1)S(1)}, bf16[8,2,32,512]{3,2,1,0:T(8,128)(2,1)S(1)}, u32[]{:S(2)}, u32[]{:S(2)}) collective-permute-start(bf16[8,2,32,512]{3,2,1,0:T(8,128)(2,1)S(1)} %all-to-all-done), channel_id=1, source_target_pairs={{0,128},{16,144},{32,160},{48,176},{64,192},{80,208},{96,224},{112... | collective-permute-start | bytes 1572872 | tf_op jit(solution)/shard_map/ppermute | solution.py:253
  92.3 4.8 %all-to-all-done.1 = bf16[8,64,256]{2,1,0:T(8,128)(2,1)S(1)} async-done(((bf16[8,64,256]{2,1,0:T(8,128)(2,1)}), bf16[8,64,256]{2,1,0:T(8,128)(2,1)S(1)}, u32[]{:S(2)}, u32[]{:S(2)}) %all-to-all-start.1) | async-done | bytes 262176 | tf_op jit(solution)/shard_map/all_to_all | solution.py:282
  97.1 1.9 %collective-permute-start.13 = (bf16[8,2,32,256]{3,2,1,0:T(8,128)(2,1)S(1)}, bf16[8,2,32,256]{3,2,1,0:T(8,128)(2,1)S(1)}, u32[]{:S(2)}, u32[]{:S(2)}) collective-permute-start(bf16[8,2,32,256]{3,2,1,0:T(8,128)(2,1)S(1)} %bitcast.24), channel_id=1, source_target_pairs={{0,16},{16,32},{32,48},{48,64},{64,80},{80,96},{96,112},{112,128},... | collective-permute-start | bytes 786440 | tf_op jit(solution)/shard_map/ppermute | solution.py:249
  99.0 5.1 %collective-permute-start.12 = (bf16[8,32,256]{2,1,0:T(8,128)(2,1)S(1)}, bf16[8,32,256]{2,1,0:T(8,128)(2,1)S(1)}, u32[]{:S(2)}, u32[]{:S(2)}) collective-permute-start(bf16[8,32,256]{2,1,0:T(8,128)(2,1)S(1)} %slice_bitcast_fusion), channel_id=1, source_target_pairs={{0,32},{16,48},{32,64},{48,80},{64,96},{80,112},{96,128},{112,144}... | collective-permute-start | bytes 393224 | tf_op jit(solution)/shard_map/ppermute | solution.py:249
  104.1 14.0 %collective-permute-done.12.far_ref = bf16[8,32,256]{2,1,0:T(8,128)(2,1)S(1)} collective-permute-done((bf16[8,32,256]{2,1,0:T(8,128)(2,1)S(1)}, bf16[8,32,256]{2,1,0:T(8,128)(2,1)S(1)}, u32[]{:S(2)}, u32[]{:S(2)}) %collective-permute-start.12) | collective-permute-done | bytes 131104 | tf_op jit(solution)/shard_map/ppermute | solution.py:249
  118.1 0.9 copy-done
  119.1 15.6 %shard_map.47.refs_0_ = bf16[256,256]{1,0:T(8,128)(2,1)S(1)} custom-call(s32[1]{0:T(128)} %bitcast.3.seq_ref, f32[256,256]{1,0:T(8,128)S(1)} %copy-done, f32[256,256]{1,0:T(8,128)S(1)} %collective-permute-done.10.sent_any, bf16[8,32,256]{2,1,0:T(8,128)(2,1)S(1)} %collective-permute-done.12.far_ref, ...), custom_call_target="tpu_custom_call" | custom-call | tf_op jit(solution)/shard_map/pallas_call | solution.py:151
  134.7 1.8 %collective-permute-start.14 = (bf16[256,256]{1,0:T(8,128)(2,1)S(1)}, bf16[256,256]{1,0:T(8,128)(2,1)S(1)}, u32[]{:S(2)}, u32[]{:S(2)}) collective-permute-start(bf16[256,256]{1,0:T(8,128)(2,1)S(1)} %shard_map.47.refs_0_), channel_id=1, source_target_pairs={{0,1},{1,2},{2,3},{3,4},{4,5},{5,6},{6,7},{7,0},{8,9},{9,10},{10,1... | collective-permute-start | bytes 393224 | tf_op jit(solution)/shard_map/ppermute | solution.py:243
  136.5 1.5 collective-permute-start.15
  138.0 2.9 %collective-permute-done.14.refs_1_ = bf16[256,256]{1,0:T(8,128)(2,1)S(1)} collective-permute-done((bf16[256,256]{1,0:T(8,128)(2,1)S(1)}, bf16[256,256]{1,0:T(8,128)(2,1)S(1)}, u32[]{:S(2)}, u32[]{:S(2)}) %collective-permute-start.14) | collective-permute-done | bytes 131104 | tf_op jit(solution)/shard_map/ppermute | solution.py:243
  141.0 0.5 collective-permute-done.15.refs_2_
  141.5 1.5 collective-permute-start.19
  142.9 1.8 %collective-permute-start.20 = (bf16[256,256]{1,0:T(8,128)(2,1)S(1)}, bf16[256,256]{1,0:T(8,128)(2,1)S(1)}, u32[]{:S(2)}, u32[]{:S(2)}) collective-permute-start(bf16[256,256]{1,0:T(8,128)(2,1)S(1)} %collective-permute-done.15.refs_2_), channel_id=1, source_target_pairs={{0,7},{1,0},{2,1},{3,2},{4,3},{5,4},{6,5},{7,6},{8,15},{9,8},{10,9... | collective-permute-start | bytes 393224 | tf_op jit(solution)/shard_map/ppermute | solution.py:243
  144.7 0.2 broadcast_in_dim.22
  145.0 2.6 %collective-permute-done.19.refs_3_ = bf16[256,256]{1,0:T(8,128)(2,1)S(1)} collective-permute-done((bf16[256,256]{1,0:T(8,128)(2,1)S(1)}, bf16[256,256]{1,0:T(8,128)(2,1)S(1)}, u32[]{:S(2)}, u32[]{:S(2)}) %collective-permute-start.19) | collective-permute-done | bytes 131104 | tf_op jit(solution)/shard_map/ppermute | solution.py:243
  147.7 0.3 collective-permute-done.20.refs_4_
  148.2 0.1 collective-permute-start.23
  148.3 3.3 %collective-permute-start.21 = (bf16[256,256]{1,0:T(8,128)(2,1)S(1)}, bf16[256,256]{1,0:T(8,128)(2,1)S(1)}, u32[]{:S(2)}, u32[]{:S(2)}) collective-permute-start(bf16[256,256]{1,0:T(8,128)(2,1)S(1)} %collective-permute-done.19.refs_3_), channel_id=1, source_target_pairs={{0,1},{1,2},{2,3},{3,4},{4,5},{5,6},{6,7},{7,0},{8,9},{9,10},{10,1... | collective-permute-start | bytes 393224 | tf_op jit(solution)/shard_map/ppermute | solution.py:243
  151.6 0.0 collective-permute-start.22
  151.6 3.8 %collective-permute-done.21.refs_5_ = bf16[256,256]{1,0:T(8,128)(2,1)S(1)} collective-permute-done((bf16[256,256]{1,0:T(8,128)(2,1)S(1)}, bf16[256,256]{1,0:T(8,128)(2,1)S(1)}, u32[]{:S(2)}, u32[]{:S(2)}) %collective-permute-start.21) | collective-permute-done | bytes 131104 | tf_op jit(solution)/shard_map/ppermute | solution.py:243
  155.4 2.0 %collective-permute-done.22.refs_6_ = bf16[256,256]{1,0:T(8,128)(2,1)S(1)} collective-permute-done((bf16[256,256]{1,0:T(8,128)(2,1)S(1)}, bf16[256,256]{1,0:T(8,128)(2,1)S(1)}, u32[]{:S(2)}, u32[]{:S(2)}) %collective-permute-start.22) | collective-permute-done | bytes 131104 | tf_op jit(solution)/shard_map/ppermute | solution.py:243
  157.4 1.7 %collective-permute-start.24 = (bf16[256,256]{1,0:T(8,128)(2,1)S(1)}, bf16[256,256]{1,0:T(8,128)(2,1)S(1)}, u32[]{:S(2)}, u32[]{:S(2)}) collective-permute-start(bf16[256,256]{1,0:T(8,128)(2,1)S(1)} %collective-permute-done.21.refs_5_), channel_id=1, source_target_pairs={{0,1},{1,2},{2,3},{3,4},{4,5},{5,6},{6,7},{7,0},{8,9},{9,10},{10,1... | collective-permute-start | bytes 393224 | tf_op jit(solution)/shard_map/ppermute | solution.py:243
  159.2 1.8 %shard_map.48 = (f32[256,1024]{1,0:T(8,128)S(1)}, bf16[1,256,1024]{2,1,0:T(8,128)(2,1)S(1)}) custom-call(s32[2]{0:T(128)S(1)} %copy-done.1, bf16[256,256]{1,0:T(8,128)(2,1)S(1)} %shard_map.47.refs_0_, bf16[256,256]{1,0:T(8,128)(2,1)S(1)} %collective-permute-done.14.refs_1_, bf16[256,256]{1,0:T(8,128)(2,1)S(1)} %collective-permute-done.15.refs_2_, ...), custom_call_target="tpu_custom_call" | custom-call | tf_op jit(solution)/shard_map/pallas_call | solution.py:346
  161.0 2.6 %collective-permute-done.24.last_ref = bf16[256,256]{1,0:T(8,128)(2,1)S(1)} collective-permute-done((bf16[256,256]{1,0:T(8,128)(2,1)S(1)}, bf16[256,256]{1,0:T(8,128)(2,1)S(1)}, u32[]{:S(2)}, u32[]{:S(2)}) %collective-permute-start.24) | collective-permute-done | bytes 131104 | tf_op jit(solution)/shard_map/ppermute | solution.py:243
  163.6 0.9 shard_map.49
  164.5 0.2 collective-permute-start.25
  164.7 6.5 %collective-permute-done.25 = bf16[256,512]{1,0:T(8,128)(2,1)S(1)} collective-permute-done((bf16[256,512]{1,0:T(8,128)(2,1)S(1)}, bf16[256,512]{1,0:T(8,128)(2,1)S(1)}, u32[]{:S(2)}, u32[]{:S(2)}) %collective-permute-start.25) | collective-permute-done | bytes 262176 | tf_op jit(solution)/shard_map/ppermute | solution.py:239
  171.2 0.8 add_convert_fusion
  (37 shorter events, 0.3 us)
Async XLA Ops:
  0.0 3.0 %copy-start.5 = (bf16[256,512]{1,0:T(8,128)(2,1)S(1)}, bf16[256,512]{1,0:T(8,128)(2,1)}, u32[]{:S(2)}) copy-start(bf16[256,512]{1,0:T(8,128)(2,1)} %refs_0_.1) | copy-start | bytes 786436
  1.3 25.0 %collective-permute-start.8 = (bf16[2048,256]{1,0:T(8,128)(2,1)S(1)}, bf16[2048,256]{1,0:T(8,128)(2,1)S(1)}, u32[]{:S(2)}, u32[]{:S(2)}) collective-permute-start(bf16[2048,256]{1,0:T(8,128)(2,1)S(1)} %constant_dynamic-slice_fusion), channel_id=1, source_target_pairs={{0,8},{1,9},{2,10},{3,11},{4,12},{5,13},{6,14},{7,15},{8,0},{9,1},... | collective-permute-start | bytes 3145736 | tf_op jit(solution)/shard_map/ppermute | solution.py:239
  3.0 11.9 %collective-permute-start = (bf16[256,512]{1,0:T(8,128)(2,1)S(1)}, bf16[256,512]{1,0:T(8,128)(2,1)S(1)}, u32[]{:S(2)}, u32[]{:S(2)}) collective-permute-start(bf16[256,512]{1,0:T(8,128)(2,1)S(1)} %copy-done.5), channel_id=1, source_target_pairs={{0,1},{1,2},{2,3},{3,4},{4,5},{5,6},{6,7},{7,0},{8,9},{9,10},{10,1... | collective-permute-start | bytes 786440 | tf_op jit(solution)/shard_map/ppermute | solution.py:243
  4.9 10.0 %collective-permute-start.1 = (bf16[256,512]{1,0:T(8,128)(2,1)S(1)}, bf16[256,512]{1,0:T(8,128)(2,1)S(1)}, u32[]{:S(2)}, u32[]{:S(2)}) collective-permute-start(bf16[256,512]{1,0:T(8,128)(2,1)S(1)} %copy-done.5), channel_id=1, source_target_pairs={{0,7},{1,0},{2,1},{3,2},{4,3},{5,4},{6,5},{7,6},{8,15},{9,8},{10,9... | collective-permute-start | bytes 786440 | tf_op jit(solution)/shard_map/ppermute | solution.py:243
  8.9 32.5 %copy-start.4 = (bf16[8192,32]{0,1:T(8,128)(2,1)S(1)}, bf16[8192,32]{0,1:T(8,128)(2,1)}, u32[]{:S(2)}) copy-start(bf16[8192,32]{0,1:T(8,128)(2,1)} %param.6) | copy-start | bytes 1572868
  14.9 14.8 %copy-start.6 = (bf16[256,512]{1,0:T(8,128)(2,1)}, bf16[256,512]{1,0:T(8,128)(2,1)S(1)}, u32[]{:S(2)}) copy-start(bf16[256,512]{1,0:T(8,128)(2,1)S(1)} %collective-permute-done.refs_1_) | copy-start | bytes 786436
  14.9 14.8 %copy-start.7 = (bf16[256,512]{1,0:T(8,128)(2,1)}, bf16[256,512]{1,0:T(8,128)(2,1)S(1)}, u32[]{:S(2)}) copy-start(bf16[256,512]{1,0:T(8,128)(2,1)S(1)} %collective-permute-done.1.refs_2_) | copy-start | bytes 786436
  14.9 14.7 %collective-permute-start.2 = (bf16[256,512]{1,0:T(8,128)(2,1)S(1)}, bf16[256,512]{1,0:T(8,128)(2,1)S(1)}, u32[]{:S(2)}, u32[]{:S(2)}) collective-permute-start(bf16[256,512]{1,0:T(8,128)(2,1)S(1)} %collective-permute-done.refs_1_), channel_id=1, source_target_pairs={{0,1},{1,2},{2,3},{3,4},{4,5},{5,6},{6,7},{7,0},{8,9},{9,10},{10,1... | collective-permute-start | bytes 786440 | tf_op jit(solution)/shard_map/ppermute | solution.py:243
  15.0 14.7 %collective-permute-start.3 = (bf16[256,512]{1,0:T(8,128)(2,1)S(1)}, bf16[256,512]{1,0:T(8,128)(2,1)}, u32[]{:S(2)}, u32[]{:S(2)}) collective-permute-start(bf16[256,512]{1,0:T(8,128)(2,1)S(1)} %collective-permute-done.1.refs_2_), channel_id=1, source_target_pairs={{0,7},{1,0},{2,1},{3,2},{4,3},{5,4},{6,5},{7,6},{8,15},{9,8},{10,9... | collective-permute-start | bytes 786440 | tf_op jit(solution)/shard_map/ppermute | solution.py:243
  26.3 3.3 %copy-start.2 = (bf16[2048,256]{1,0:T(8,128)(2,1)}, bf16[2048,256]{1,0:T(8,128)(2,1)S(1)}, u32[]{:S(2)}) copy-start(bf16[2048,256]{1,0:T(8,128)(2,1)S(1)} %collective-permute-done.8.refs_11_) | copy-start | bytes 3145732
  26.3 41.2 %collective-permute-start.9 = (bf16[2048,256]{1,0:T(8,128)(2,1)S(1)}, bf16[2048,256]{1,0:T(8,128)(2,1)S(1)}, u32[]{:S(2)}, u32[]{:S(2)}) collective-permute-start(bf16[2048,256]{1,0:T(8,128)(2,1)S(1)} %collective-permute-done.8.refs_11_), channel_id=1, source_target_pairs={{0,16},{16,0},{32,48},{48,32},{64,80},{80,64},{96,112},{112,96},{1... | collective-permute-start | bytes 3145736 | tf_op jit(solution)/shard_map/ppermute | solution.py:257
  29.6 37.9 %copy-start.8 = (bf16[256,512]{1,0:T(8,128)(2,1)}, bf16[256,512]{1,0:T(8,128)(2,1)S(1)}, u32[]{:S(2)}) copy-start(bf16[256,512]{1,0:T(8,128)(2,1)S(1)} %collective-permute-done.2.refs_3_) | copy-start | bytes 786436
  29.7 47.6 %all-to-all-start = ((bf16[8,2,32,512]{3,2,1,0:T(8,128)(2,1)}), bf16[8,2,32,512]{3,2,1,0:T(8,128)(2,1)S(1)}, u32[]{:S(2)}, u32[]{:S(2)}) async-start(bf16[8,2,32,512]{3,2,1,0:T(8,128)(2,1)} %bitcast.23), calls=%async_computation | async-start | bytes 1048576 | tf_op jit(solution)/shard_map/all_to_all | solution.py:386
  38.2 20.7 %collective-permute-start.4 = (bf16[256,512]{1,0:T(8,128)(2,1)S(1)}, bf16[256,512]{1,0:T(8,128)(2,1)S(1)}, u32[]{:S(2)}, u32[]{:S(2)}) collective-permute-start(bf16[256,512]{1,0:T(8,128)(2,1)S(1)} %collective-permute-done.2.refs_3_), channel_id=1, source_target_pairs={{0,1},{1,2},{2,3},{3,4},{4,5},{5,6},{6,7},{7,0},{8,9},{9,10},{10,1... | collective-permute-start | bytes 786440 | tf_op jit(solution)/shard_map/ppermute | solution.py:243
  40.2 18.7 %collective-permute-start.5 = (bf16[256,512]{1,0:T(8,128)(2,1)}, bf16[256,512]{1,0:T(8,128)(2,1)S(1)}, u32[]{:S(2)}, u32[]{:S(2)}) collective-permute-start(bf16[256,512]{1,0:T(8,128)(2,1)} %collective-permute-done.3.refs_4_), channel_id=1, source_target_pairs={{0,7},{1,0},{2,1},{3,2},{4,3},{5,4},{6,5},{7,6},{8,15},{9,8},{10,9... | collective-permute-start | bytes 786440 | tf_op jit(solution)/shard_map/ppermute | solution.py:243
  42.2 17.0 %collective-permute-start.7 = (bf16[32,4096]{1,0:T(8,128)(2,1)S(1)}, bf16[32,4096]{1,0:T(8,128)(2,1)S(1)}, u32[]{:S(2)}, u32[]{:S(2)}) collective-permute-start(bf16[32,4096]{1,0:T(8,128)(2,1)S(1)} %get-tuple-element.59), channel_id=1, source_target_pairs={{0,8},{1,9},{2,10},{3,11},{4,12},{5,13},{6,14},{7,15},{8,0},{9,1},... | collective-permute-start | bytes 786440 | tf_op jit(solution)/shard_map/ppermute | solution.py:239
  58.9 8.6 %copy-start.9 = (bf16[256,512]{1,0:T(8,128)(2,1)}, bf16[256,512]{1,0:T(8,128)(2,1)S(1)}, u32[]{:S(2)}) copy-start(bf16[256,512]{1,0:T(8,128)(2,1)S(1)} %collective-permute-done.4.refs_5_) | copy-start | bytes 786436
  58.9 8.6 %copy-start.10 = (bf16[256,512]{1,0:T(8,128)(2,1)}, bf16[256,512]{1,0:T(8,128)(2,1)S(1)}, u32[]{:S(2)}) copy-start(bf16[256,512]{1,0:T(8,128)(2,1)S(1)} %collective-permute-done.5.refs_6_) | copy-start | bytes 786436
  58.9 8.6 %collective-permute-start.6 = (bf16[256,512]{1,0:T(8,128)(2,1)S(1)}, bf16[256,512]{1,0:T(8,128)(2,1)S(1)}, u32[]{:S(2)}, u32[]{:S(2)}) collective-permute-start(bf16[256,512]{1,0:T(8,128)(2,1)S(1)} %collective-permute-done.4.refs_5_), channel_id=1, source_target_pairs={{0,1},{1,2},{2,3},{3,4},{4,5},{5,6},{6,7},{7,0},{8,9},{9,10},{10,1... | collective-permute-start | bytes 786440 | tf_op jit(solution)/shard_map/ppermute | solution.py:243
  59.1 8.4 %copy-start.11 = (bf16[32,4096]{1,0:T(8,128)(2,1)}, bf16[32,4096]{1,0:T(8,128)(2,1)S(1)}, u32[]{:S(2)}) copy-start(bf16[32,4096]{1,0:T(8,128)(2,1)S(1)} %collective-permute-done.7.refs_9_) | copy-start | bytes 786436
  67.5 0.7 copy-start.12
  67.5 1.1 copy-start.3
  75.6 4.6 %collective-permute-start.11 = (f32[64,256]{1,0:T(8,128)}, f32[64,256]{1,0:T(8,128)S(1)}, u32[]{:S(2)}, u32[]{:S(2)}) collective-permute-start(f32[64,256]{1,0:T(8,128)} %get-tuple-element.41), channel_id=1, source_target_pairs={{0,8},{1,9},{2,10},{3,11},{4,12},{5,13},{6,14},{7,15},{8,0},{9,1},... | collective-permute-start | bytes 196616 | tf_op jit(solution)/shard_map/ppermute | solution.py:239
  81.7 15.4 %all-to-all-start.1 = ((bf16[8,64,256]{2,1,0:T(8,128)(2,1)}), bf16[8,64,256]{2,1,0:T(8,128)(2,1)S(1)}, u32[]{:S(2)}, u32[]{:S(2)}) async-start(bf16[8,64,256]{2,1,0:T(8,128)(2,1)} %broadcast_in_dim.21), calls=%async_computation.1 | async-start | bytes 524288 | tf_op jit(solution)/shard_map/all_to_all | solution.py:282
  86.6 12.4 %collective-permute-start.10 = (f32[256,256]{1,0:T(8,128)}, f32[256,256]{1,0:T(8,128)S(1)}, u32[]{:S(2)}, u32[]{:S(2)}) collective-permute-start(f32[256,256]{1,0:T(8,128)} %get-tuple-element.40), channel_id=1, source_target_pairs={{0,8},{1,9},{2,10},{3,11},{4,12},{5,13},{6,14},{7,15},{8,0},{9,1},... | collective-permute-start | bytes 786440 | tf_op jit(solution)/shard_map/ppermute | solution.py:239
  88.2 59.8 %collective-permute-start.16 = (bf16[8,2,32,512]{3,2,1,0:T(8,128)(2,1)S(1)}, bf16[8,2,32,512]{3,2,1,0:T(8,128)(2,1)S(1)}, u32[]{:S(2)}, u32[]{:S(2)}) collective-permute-start(bf16[8,2,32,512]{3,2,1,0:T(8,128)(2,1)S(1)} %all-to-all-done), channel_id=1, source_target_pairs={{0,64},{16,80},{32,96},{48,112},{64,128},{80,144},{96,160},{112,17... | collective-permute-start | bytes 1572872 | tf_op jit(solution)/shard_map/ppermute | solution.py:253
  89.7 58.3 %collective-permute-start.17 = (bf16[8,2,32,512]{3,2,1,0:T(8,128)(2,1)S(1)}, bf16[8,2,32,512]{3,2,1,0:T(8,128)(2,1)S(1)}, u32[]{:S(2)}, u32[]{:S(2)}) collective-permute-start(bf16[8,2,32,512]{3,2,1,0:T(8,128)(2,1)S(1)} %all-to-all-done), channel_id=1, source_target_pairs={{0,192},{16,208},{32,224},{48,240},{64,0},{80,16},{96,32},{112,48}... | collective-permute-start | bytes 1572872 | tf_op jit(solution)/shard_map/ppermute | solution.py:253
  90.2 57.8 %collective-permute-start.18 = (bf16[8,2,32,512]{3,2,1,0:T(8,128)(2,1)S(1)}, bf16[8,2,32,512]{3,2,1,0:T(8,128)(2,1)S(1)}, u32[]{:S(2)}, u32[]{:S(2)}) collective-permute-start(bf16[8,2,32,512]{3,2,1,0:T(8,128)(2,1)S(1)} %all-to-all-done), channel_id=1, source_target_pairs={{0,128},{16,144},{32,160},{48,176},{64,192},{80,208},{96,224},{112... | collective-permute-start | bytes 1572872 | tf_op jit(solution)/shard_map/ppermute | solution.py:253
  97.1 21.1 %collective-permute-start.13 = (bf16[8,2,32,256]{3,2,1,0:T(8,128)(2,1)S(1)}, bf16[8,2,32,256]{3,2,1,0:T(8,128)(2,1)S(1)}, u32[]{:S(2)}, u32[]{:S(2)}) collective-permute-start(bf16[8,2,32,256]{3,2,1,0:T(8,128)(2,1)S(1)} %bitcast.24), channel_id=1, source_target_pairs={{0,16},{16,32},{32,48},{48,64},{64,80},{80,96},{96,112},{112,128},... | collective-permute-start | bytes 786440 | tf_op jit(solution)/shard_map/ppermute | solution.py:249
  99.0 19.1 %collective-permute-start.12 = (bf16[8,32,256]{2,1,0:T(8,128)(2,1)S(1)}, bf16[8,32,256]{2,1,0:T(8,128)(2,1)S(1)}, u32[]{:S(2)}, u32[]{:S(2)}) collective-permute-start(bf16[8,32,256]{2,1,0:T(8,128)(2,1)S(1)} %slice_bitcast_fusion), channel_id=1, source_target_pairs={{0,32},{16,48},{32,64},{48,80},{64,96},{80,112},{96,128},{112,144}... | collective-permute-start | bytes 393224 | tf_op jit(solution)/shard_map/ppermute | solution.py:249
  118.1 1.0 copy-start
  134.7 6.3 %collective-permute-start.14 = (bf16[256,256]{1,0:T(8,128)(2,1)S(1)}, bf16[256,256]{1,0:T(8,128)(2,1)S(1)}, u32[]{:S(2)}, u32[]{:S(2)}) collective-permute-start(bf16[256,256]{1,0:T(8,128)(2,1)S(1)} %shard_map.47.refs_0_), channel_id=1, source_target_pairs={{0,1},{1,2},{2,3},{3,4},{4,5},{5,6},{6,7},{7,0},{8,9},{9,10},{10,1... | collective-permute-start | bytes 393224 | tf_op jit(solution)/shard_map/ppermute | solution.py:243
  136.5 5.0 %collective-permute-start.15 = (bf16[256,256]{1,0:T(8,128)(2,1)S(1)}, bf16[256,256]{1,0:T(8,128)(2,1)S(1)}, u32[]{:S(2)}, u32[]{:S(2)}) collective-permute-start(bf16[256,256]{1,0:T(8,128)(2,1)S(1)} %shard_map.47.refs_0_), channel_id=1, source_target_pairs={{0,7},{1,0},{2,1},{3,2},{4,3},{5,4},{6,5},{7,6},{8,15},{9,8},{10,9... | collective-permute-start | bytes 393224 | tf_op jit(solution)/shard_map/ppermute | solution.py:243
  141.5 6.2 %collective-permute-start.19 = (bf16[256,256]{1,0:T(8,128)(2,1)S(1)}, bf16[256,256]{1,0:T(8,128)(2,1)S(1)}, u32[]{:S(2)}, u32[]{:S(2)}) collective-permute-start(bf16[256,256]{1,0:T(8,128)(2,1)S(1)} %collective-permute-done.14.refs_1_), channel_id=1, source_target_pairs={{0,1},{1,2},{2,3},{3,4},{4,5},{5,6},{6,7},{7,0},{8,9},{9,10},{10,1... | collective-permute-start | bytes 393224 | tf_op jit(solution)/shard_map/ppermute | solution.py:243
  142.9 5.0 %collective-permute-start.20 = (bf16[256,256]{1,0:T(8,128)(2,1)S(1)}, bf16[256,256]{1,0:T(8,128)(2,1)S(1)}, u32[]{:S(2)}, u32[]{:S(2)}) collective-permute-start(bf16[256,256]{1,0:T(8,128)(2,1)S(1)} %collective-permute-done.15.refs_2_), channel_id=1, source_target_pairs={{0,7},{1,0},{2,1},{3,2},{4,3},{5,4},{6,5},{7,6},{8,15},{9,8},{10,9... | collective-permute-start | bytes 393224 | tf_op jit(solution)/shard_map/ppermute | solution.py:243
  145.0 14.2 %copy-start.1 = (s32[2]{0:T(128)S(1)}, s32[2]{0:T(128)}, u32[]{:S(2)}) copy-start(s32[2]{0:T(128)} %pad_add_fusion.spot_ref) | copy-start | bytes 28
  148.2 11.0 %collective-permute-start.23 = (bf16[4,8,2,32,512]{4,3,2,1,0:T(8,128)(2,1)S(1)}, bf16[4,8,2,32,512]{4,3,2,1,0:T(8,128)(2,1)S(1)}, u32[]{:S(2)}, u32[]{:S(2)}) collective-permute-start(bf16[4,8,2,32,512]{4,3,2,1,0:T(8,128)(2,1)S(1)} %bitcast_dynamic-update-slice_fusion.refs_7_), channel_id=1, source_target_pairs={{0,16},{16,0},{32,48},{48,32},{64,80},{80,64},{96,112},{112,96},{1... | collective-permute-start | bytes 6291464 | tf_op jit(solution)/shard_map/ppermute | solution.py:257
  148.3 7.1 %collective-permute-start.21 = (bf16[256,256]{1,0:T(8,128)(2,1)S(1)}, bf16[256,256]{1,0:T(8,128)(2,1)S(1)}, u32[]{:S(2)}, u32[]{:S(2)}) collective-permute-start(bf16[256,256]{1,0:T(8,128)(2,1)S(1)} %collective-permute-done.19.refs_3_), channel_id=1, source_target_pairs={{0,1},{1,2},{2,3},{3,4},{4,5},{5,6},{6,7},{7,0},{8,9},{9,10},{10,1... | collective-permute-start | bytes 393224 | tf_op jit(solution)/shard_map/ppermute | solution.py:243
  151.6 5.8 %collective-permute-start.22 = (bf16[256,256]{1,0:T(8,128)(2,1)S(1)}, bf16[256,256]{1,0:T(8,128)(2,1)S(1)}, u32[]{:S(2)}, u32[]{:S(2)}) collective-permute-start(bf16[256,256]{1,0:T(8,128)(2,1)S(1)} %collective-permute-done.20.refs_4_), channel_id=1, source_target_pairs={{0,7},{1,0},{2,1},{3,2},{4,3},{5,4},{6,5},{7,6},{8,15},{9,8},{10,9... | collective-permute-start | bytes 393224 | tf_op jit(solution)/shard_map/ppermute | solution.py:243
  157.4 6.2 %collective-permute-start.24 = (bf16[256,256]{1,0:T(8,128)(2,1)S(1)}, bf16[256,256]{1,0:T(8,128)(2,1)S(1)}, u32[]{:S(2)}, u32[]{:S(2)}) collective-permute-start(bf16[256,256]{1,0:T(8,128)(2,1)S(1)} %collective-permute-done.21.refs_5_), channel_id=1, source_target_pairs={{0,1},{1,2},{2,3},{3,4},{4,5},{5,6},{6,7},{7,0},{8,9},{9,10},{10,1... | collective-permute-start | bytes 393224 | tf_op jit(solution)/shard_map/ppermute | solution.py:243
  164.5 6.7 %collective-permute-start.25 = (bf16[256,512]{1,0:T(8,128)(2,1)S(1)}, bf16[256,512]{1,0:T(8,128)(2,1)S(1)}, u32[]{:S(2)}, u32[]{:S(2)}) collective-permute-start(bf16[256,512]{1,0:T(8,128)(2,1)S(1)} %get-tuple-element.58), channel_id=1, source_target_pairs={{0,8},{1,9},{2,10},{3,11},{4,12},{5,13},{6,14},{7,15},{8,0},{9,1},... | collective-permute-start | bytes 786440 | tf_op jit(solution)/shard_map/ppermute | solution.py:239

commit v7 on v6

--- a/solution.py
+++ b/solution.py
@@ -204,7 +204,9 @@
         fetch.start()
     for fetch in fetches[:10]:
         fetch.wait()
-    kv_out[...] = lax.dot_general(kv_ref[...], rows_ref[...], LANES, preferred_element_type=jnp.float32)
+    kv_out[...] = lax.dot_general(
+        rows_ref[...], kv_ref[...], LANES, preferred_element_type=jnp.float32
+    ).T
     fetches[10].wait()
     mine_out[...] = jnp.dot(rows_ref[...], own_ref[...], preferred_element_type=jnp.float32)
     keep = pltpu.make_async_copy(mine_out, mine_any, sems.at[13])
@@ -278,11 +280,21 @@
 ROWS = [list(range(8)), list(range(8, 16))]
 
 
-def sent_to_row(value):
-    return lax.all_to_all(
-        jnp.broadcast_to(value[None], (8, *value.shape)),
-        "head", 0, 0, tiled=True, axis_index_groups=ROWS,
-    )
+def copies_kernel(one_ref, two_ref, out_ref):
+    total = (one_ref[...] + two_ref[...]).astype(out_ref.dtype)
+    for k in range(out_ref.shape[0]):
+        out_ref[k] = total
+
+
+def sent_to_row(one, two):
+    copies = pl.pallas_call(
+        copies_kernel,
+        out_shape=jax.ShapeDtypeStruct((8, *one.shape), jnp.bfloat16),
+        in_specs=in_vmem(2),
+        out_specs=in_vmem(1)[0],
+        compiler_params=pltpu.CompilerParams(vmem_limit_bytes=8 * 1024 * 1024),
+    )(one, two)
+    return lax.all_to_all(copies, "head", 0, 0, tiled=True, axis_index_groups=ROWS)
 
 
 def owned_piece(w_out, seq):
@@ -391,9 +403,8 @@
     )
     kv_sent = swap_rows(kv_part)
     piece, kv_sent = lax.optimization_barrier((piece, kv_sent))
-    kv = (kv_part + kv_sent).astype(jnp.bfloat16)
     q_sent = swap_rows(q_theirs)
-    keyval = sent_to_row(kv).reshape(8, 2, kv_flat.shape[0], tok_rows)
+    keyval = sent_to_row(kv_part, kv_sent).reshape(8, 2, kv_flat.shape[0], tok_rows)
     near = along_seq(keyval, 1)
     far = along_seq(keyval[:, 0], 2)
     attended = attend(seq.reshape(1), q_mine, q_sent, far, near, keyval)

time: 172 us -> 172 us (level)
  no operation moved by 1% of the time
where the time goes in v7:
time: 172 us
  waiting for transfers between devices  80.7 us (47%)
  starting transfers between devices  55.6 us (32%)
  Pallas kernels  26 us (15%)
  local copies, waits for them, and re-layouts  8.09 us (5%)
    ppermute x14, waiting for transfers between devices, along_z(): lax.ppermute(value, 'head', [(i, i // 8 * 8 + (i + step) % 8) for i in ra...  44.4 us
    ppermute x14, starting transfers between devices, along_z(): lax.ppermute(value, 'head', [(i, i // 8 * 8 + (i + step) % 8) for i in ra...  24.3 us
    ppermute x5, waiting for transfers between devices, swap_rows(): return lax.ppermute(value, 'head', [(i, (i + 8) % 16) for i in range(16)])  17.5 us
    pallas_call x1, Pallas kernels, attend(): pl.pallas_call(attend_kernel, out_shape=jax.ShapeDtypeStruct(mine.shape,...  15.6 us
    ppermute x2, waiting for transfers between devices, along_seq(): return lax.ppermute(value, 'seq', [(i, i + step) for i in range(16 - step)])  14 us
    all_to_all x1, starting transfers between devices, body(): lax.all_to_all(piece, 'head', 0, 0, tiled=True, axis_index_groups=ROWS)  8.48 us
    ppermute x2, starting transfers between devices, along_seq(): return lax.ppermute(value, 'seq', [(i, i + step) for i in range(16 - step)])  7.01 us
    pallas_call x1, Pallas kernels, project(): pl.pallas_call(project_kernel, out_shape=tuple((jax.ShapeDtypeStruct(shap...  6.96 us
  transfers between devices with their start and end apart: 28, of which 15 were waited for; matrix products, arithmetic and copies ran while one was open for 3% of the time, Pallas kernels for 14%

profile of v7, /device:TPU:2, one launch (start us, length us, event | category | flops | bytes accessed | tf_op | source)
XLA Modules:
  0.0 172.0 jit_solution(1902028292474002183)
XLA Ops:
  0.0 1.3 constant_dynamic-slice_fusion
  1.3 1.7 collective-permute-start.8
  3.0 1.9 %collective-permute-start = (bf16[256,512]{1,0:T(8,128)(2,1)S(1)}, bf16[256,512]{1,0:T(8,128)(2,1)S(1)}, u32[]{:S(2)}, u32[]{:S(2)}) collective-permute-start(bf16[256,512]{1,0:T(8,128)(2,1)S(1)} %copy-done.6), channel_id=1, source_target_pairs={{0,1},{1,2},{2,3},{3,4},{4,5},{5,6},{6,7},{7,0},{8,9},{9,10},{10,1... | collective-permute-start | bytes 786440 | tf_op jit(solution)/shard_map/ppermute | solution.py:245
  4.9 3.9 %collective-permute-start.1 = (bf16[256,512]{1,0:T(8,128)(2,1)S(1)}, bf16[256,512]{1,0:T(8,128)(2,1)S(1)}, u32[]{:S(2)}, u32[]{:S(2)}) collective-permute-start(bf16[256,512]{1,0:T(8,128)(2,1)S(1)} %copy-done.6), channel_id=1, source_target_pairs={{0,7},{1,0},{2,1},{3,2},{4,3},{5,4},{6,5},{7,6},{8,15},{9,8},{10,9... | collective-permute-start | bytes 786440 | tf_op jit(solution)/shard_map/ppermute | solution.py:245
  8.9 6.0 %collective-permute-done.refs_1_ = bf16[256,512]{1,0:T(8,128)(2,1)S(1)} collective-permute-done((bf16[256,512]{1,0:T(8,128)(2,1)S(1)}, bf16[256,512]{1,0:T(8,128)(2,1)S(1)}, u32[]{:S(2)}, u32[]{:S(2)}) %collective-permute-start) | collective-permute-done | bytes 262176 | tf_op jit(solution)/shard_map/ppermute | solution.py:245
  14.9 0.1 collective-permute-start.2
  15.0 3.2 %collective-permute-start.3 = (bf16[256,512]{1,0:T(8,128)(2,1)S(1)}, bf16[256,512]{1,0:T(8,128)(2,1)}, u32[]{:S(2)}, u32[]{:S(2)}) collective-permute-start(bf16[256,512]{1,0:T(8,128)(2,1)S(1)} %collective-permute-done.1.refs_2_), channel_id=1, source_target_pairs={{0,7},{1,0},{2,1},{3,2},{4,3},{5,4},{6,5},{7,6},{8,15},{9,8},{10,9... | collective-permute-start | bytes 786440 | tf_op jit(solution)/shard_map/ppermute | solution.py:245
  18.2 8.1 %collective-permute-done.8.refs_11_ = bf16[2048,256]{1,0:T(8,128)(2,1)S(1)} collective-permute-done((bf16[2048,256]{1,0:T(8,128)(2,1)S(1)}, bf16[2048,256]{1,0:T(8,128)(2,1)S(1)}, u32[]{:S(2)}, u32[]{:S(2)}) %collective-permute-start.8) | collective-permute-done | bytes 1048608 | tf_op jit(solution)/shard_map/ppermute | solution.py:241
  26.3 0.0 collective-permute-start.9
  26.3 1.4 constant_dynamic-slice_fusion.1
  27.8 0.2 copy.6
  27.9 1.1 copy.8
  29.0 0.6 pad_add_fusion.spot_ref
  29.7 0.0 collective-permute-done.2.refs_3_
  29.7 8.5 %all-to-all-start = ((bf16[8,2,32,512]{3,2,1,0:T(8,128)(2,1)}), bf16[8,2,32,512]{3,2,1,0:T(8,128)(2,1)S(1)}, u32[]{:S(2)}, u32[]{:S(2)}) async-start(bf16[8,2,32,512]{3,2,1,0:T(8,128)(2,1)} %bitcast.23), calls=%async_computation | async-start | bytes 1048576 | tf_op jit(solution)/shard_map/all_to_all | solution.py:398
  38.2 2.0 %collective-permute-start.4 = (bf16[256,512]{1,0:T(8,128)(2,1)S(1)}, bf16[256,512]{1,0:T(8,128)(2,1)S(1)}, u32[]{:S(2)}, u32[]{:S(2)}) collective-permute-start(bf16[256,512]{1,0:T(8,128)(2,1)S(1)} %collective-permute-done.2.refs_3_), channel_id=1, source_target_pairs={{0,1},{1,2},{2,3},{3,4},{4,5},{5,6},{6,7},{7,0},{8,9},{9,10},{10,1... | collective-permute-start | bytes 786440 | tf_op jit(solution)/shard_map/ppermute | solution.py:245
  40.2 1.2 collective-permute-start.5
  41.4 0.8 dynamic-slice_bitcast_fusion
  42.2 1.6 collective-permute-start.7
  43.8 15.1 %collective-permute-done.4.refs_5_ = bf16[256,512]{1,0:T(8,128)(2,1)S(1)} collective-permute-done((bf16[256,512]{1,0:T(8,128)(2,1)S(1)}, bf16[256,512]{1,0:T(8,128)(2,1)S(1)}, u32[]{:S(2)}, u32[]{:S(2)}) %collective-permute-start.4) | collective-permute-done | bytes 262176 | tf_op jit(solution)/shard_map/ppermute | solution.py:245
  58.9 0.2 collective-permute-start.6
  59.2 8.4 %collective-permute-done.6.refs_7_ = bf16[256,512]{1,0:T(8,128)(2,1)S(1)} collective-permute-done((bf16[256,512]{1,0:T(8,128)(2,1)S(1)}, bf16[256,512]{1,0:T(8,128)(2,1)S(1)}, u32[]{:S(2)}, u32[]{:S(2)}) %collective-permute-start.6) | collective-permute-done | bytes 262176 | tf_op jit(solution)/shard_map/ppermute | solution.py:245
  67.6 0.7 copy-done.13
  68.2 0.4 copy-done.4
  68.6 7.0 %shard_map.46 = (f32[64,256]{1,0:T(8,128)}, f32[256,256]{1,0:T(8,128)}, f32[256,256]{1,0:T(8,128)}) custom-call(s32[2]{0:T(128)} %pad_add_fusion.spot_ref, bf16[256,512]{1,0:T(8,128)(2,1)} %refs_0_.1, bf16[256,512]{1,0:T(8,128)(2,1)} %copy-done.7, bf16[256,512]{1,0:T(8,128)(2,1)} %copy-done.8, bf16[256,512]{1,0:T(8,128)(2,1)} %copy-done.9, ...), custom_call_target="tpu_custom_call" | custom-call | tf_op jit(solution)/shard_map/pallas_call | solution.py:228
  75.6 1.7 collective-permute-start.11
  77.2 0.0 all-to-all-done
  77.2 2.9 %collective-permute-done.11.two_ref = f32[64,256]{1,0:T(8,128)S(1)} collective-permute-done((f32[64,256]{1,0:T(8,128)}, f32[64,256]{1,0:T(8,128)S(1)}, u32[]{:S(2)}, u32[]{:S(2)}) %collective-permute-start.11) | collective-permute-done | bytes 65568 | tf_op jit(solution)/shard_map/ppermute | solution.py:241
  80.1 0.8 copy-done.1
  81.0 0.7 shard_map.47
  81.7 4.9 %all-to-all-start.1 = ((bf16[8,64,256]{2,1,0:T(8,128)(2,1)}), bf16[8,64,256]{2,1,0:T(8,128)(2,1)S(1)}, u32[]{:S(2)}, u32[]{:S(2)}) async-start(bf16[8,64,256]{2,1,0:T(8,128)(2,1)} %shard_map.47), calls=%async_computation.1 | async-start | bytes 524288 | tf_op jit(solution)/shard_map/all_to_all | solution.py:297
  86.6 1.6 collective-permute-start.10
  88.2 1.5 collective-permute-start.16
  89.6 0.5 collective-permute-start.17
  90.2 2.1 %collective-permute-start.18 = (bf16[8,2,32,512]{3,2,1,0:T(8,128)(2,1)S(1)}, bf16[8,2,32,512]{3,2,1,0:T(8,128)(2,1)S(1)}, u32[]{:S(2)}, u32[]{:S(2)}) collective-permute-start(bf16[8,2,32,512]{3,2,1,0:T(8,128)(2,1)S(1)} %all-to-all-done), channel_id=1, source_target_pairs={{0,128},{16,144},{32,160},{48,176},{64,192},{80,208},{96,224},{112... | collective-permute-start | bytes 1572872 | tf_op jit(solution)/shard_map/ppermute | solution.py:255
  92.3 4.8 %all-to-all-done.1 = bf16[8,64,256]{2,1,0:T(8,128)(2,1)S(1)} async-done(((bf16[8,64,256]{2,1,0:T(8,128)(2,1)}), bf16[8,64,256]{2,1,0:T(8,128)(2,1)S(1)}, u32[]{:S(2)}, u32[]{:S(2)}) %all-to-all-start.1) | async-done | bytes 262176 | tf_op jit(solution)/shard_map/all_to_all | solution.py:297
  97.1 1.9 %collective-permute-start.13 = (bf16[8,2,32,256]{3,2,1,0:T(8,128)(2,1)S(1)}, bf16[8,2,32,256]{3,2,1,0:T(8,128)(2,1)S(1)}, u32[]{:S(2)}, u32[]{:S(2)}) collective-permute-start(bf16[8,2,32,256]{3,2,1,0:T(8,128)(2,1)S(1)} %bitcast.24), channel_id=1, source_target_pairs={{0,16},{16,32},{32,48},{48,64},{64,80},{80,96},{96,112},{112,128},... | collective-permute-start | bytes 786440 | tf_op jit(solution)/shard_map/ppermute | solution.py:251
  99.0 0.0 collective-permute-done.10.sent_any
  99.0 5.1 %collective-permute-start.12 = (bf16[8,32,256]{2,1,0:T(8,128)(2,1)S(1)}, bf16[8,32,256]{2,1,0:T(8,128)(2,1)S(1)}, u32[]{:S(2)}, u32[]{:S(2)}) collective-permute-start(bf16[8,32,256]{2,1,0:T(8,128)(2,1)S(1)} %slice_bitcast_fusion), channel_id=1, source_target_pairs={{0,32},{16,48},{32,64},{48,80},{64,96},{80,112},{96,128},{112,144}... | collective-permute-start | bytes 393224 | tf_op jit(solution)/shard_map/ppermute | solution.py:251
  104.1 14.0 %collective-permute-done.12.far_ref = bf16[8,32,256]{2,1,0:T(8,128)(2,1)S(1)} collective-permute-done((bf16[8,32,256]{2,1,0:T(8,128)(2,1)S(1)}, bf16[8,32,256]{2,1,0:T(8,128)(2,1)S(1)}, u32[]{:S(2)}, u32[]{:S(2)}) %collective-permute-start.12) | collective-permute-done | bytes 131104 | tf_op jit(solution)/shard_map/ppermute | solution.py:251
  118.1 0.9 copy-done
  119.1 15.6 %shard_map.48.refs_0_ = bf16[256,256]{1,0:T(8,128)(2,1)S(1)} custom-call(s32[1]{0:T(128)} %bitcast.3.seq_ref, f32[256,256]{1,0:T(8,128)S(1)} %copy-done, f32[256,256]{1,0:T(8,128)S(1)} %collective-permute-done.10.sent_any, bf16[8,32,256]{2,1,0:T(8,128)(2,1)S(1)} %collective-permute-done.12.far_ref, ...), custom_call_target="tpu_custom_call" | custom-call | tf_op jit(solution)/shard_map/pallas_call | solution.py:151
  134.7 1.8 %collective-permute-start.14 = (bf16[256,256]{1,0:T(8,128)(2,1)S(1)}, bf16[256,256]{1,0:T(8,128)(2,1)S(1)}, u32[]{:S(2)}, u32[]{:S(2)}) collective-permute-start(bf16[256,256]{1,0:T(8,128)(2,1)S(1)} %shard_map.48.refs_0_), channel_id=1, source_target_pairs={{0,1},{1,2},{2,3},{3,4},{4,5},{5,6},{6,7},{7,0},{8,9},{9,10},{10,1... | collective-permute-start | bytes 393224 | tf_op jit(solution)/shard_map/ppermute | solution.py:245
  136.5 1.5 collective-permute-start.15
  138.0 2.9 %collective-permute-done.14.refs_1_ = bf16[256,256]{1,0:T(8,128)(2,1)S(1)} collective-permute-done((bf16[256,256]{1,0:T(8,128)(2,1)S(1)}, bf16[256,256]{1,0:T(8,128)(2,1)S(1)}, u32[]{:S(2)}, u32[]{:S(2)}) %collective-permute-start.14) | collective-permute-done | bytes 131104 | tf_op jit(solution)/shard_map/ppermute | solution.py:245
  140.9 0.5 collective-permute-done.15.refs_2_
  141.5 1.5 collective-permute-start.19
  142.9 1.8 %collective-permute-start.20 = (bf16[256,256]{1,0:T(8,128)(2,1)S(1)}, bf16[256,256]{1,0:T(8,128)(2,1)S(1)}, u32[]{:S(2)}, u32[]{:S(2)}) collective-permute-start(bf16[256,256]{1,0:T(8,128)(2,1)S(1)} %collective-permute-done.15.refs_2_), channel_id=1, source_target_pairs={{0,7},{1,0},{2,1},{3,2},{4,3},{5,4},{6,5},{7,6},{8,15},{9,8},{10,9... | collective-permute-start | bytes 393224 | tf_op jit(solution)/shard_map/ppermute | solution.py:245
  144.7 0.2 broadcast_in_dim.15
  145.0 2.6 %collective-permute-done.19.refs_3_ = bf16[256,256]{1,0:T(8,128)(2,1)S(1)} collective-permute-done((bf16[256,256]{1,0:T(8,128)(2,1)S(1)}, bf16[256,256]{1,0:T(8,128)(2,1)S(1)}, u32[]{:S(2)}, u32[]{:S(2)}) %collective-permute-start.19) | collective-permute-done | bytes 131104 | tf_op jit(solution)/shard_map/ppermute | solution.py:245
  147.7 0.4 collective-permute-done.20.refs_4_
  148.0 0.0 collective-permute-done.17
  148.2 0.1 collective-permute-start.23
  148.3 3.3 %collective-permute-start.21 = (bf16[256,256]{1,0:T(8,128)(2,1)S(1)}, bf16[256,256]{1,0:T(8,128)(2,1)S(1)}, u32[]{:S(2)}, u32[]{:S(2)}) collective-permute-start(bf16[256,256]{1,0:T(8,128)(2,1)S(1)} %collective-permute-done.19.refs_3_), channel_id=1, source_target_pairs={{0,1},{1,2},{2,3},{3,4},{4,5},{5,6},{6,7},{7,0},{8,9},{9,10},{10,1... | collective-permute-start | bytes 393224 | tf_op jit(solution)/shard_map/ppermute | solution.py:245
  151.6 0.0 collective-permute-start.22
  151.6 3.8 %collective-permute-done.21.refs_5_ = bf16[256,256]{1,0:T(8,128)(2,1)S(1)} collective-permute-done((bf16[256,256]{1,0:T(8,128)(2,1)S(1)}, bf16[256,256]{1,0:T(8,128)(2,1)S(1)}, u32[]{:S(2)}, u32[]{:S(2)}) %collective-permute-start.21) | collective-permute-done | bytes 131104 | tf_op jit(solution)/shard_map/ppermute | solution.py:245
  155.4 2.0 %collective-permute-done.22.refs_6_ = bf16[256,256]{1,0:T(8,128)(2,1)S(1)} collective-permute-done((bf16[256,256]{1,0:T(8,128)(2,1)S(1)}, bf16[256,256]{1,0:T(8,128)(2,1)S(1)}, u32[]{:S(2)}, u32[]{:S(2)}) %collective-permute-start.22) | collective-permute-done | bytes 131104 | tf_op jit(solution)/shard_map/ppermute | solution.py:245
  157.4 1.7 %collective-permute-start.24 = (bf16[256,256]{1,0:T(8,128)(2,1)S(1)}, bf16[256,256]{1,0:T(8,128)(2,1)S(1)}, u32[]{:S(2)}, u32[]{:S(2)}) collective-permute-start(bf16[256,256]{1,0:T(8,128)(2,1)S(1)} %collective-permute-done.21.refs_5_), channel_id=1, source_target_pairs={{0,1},{1,2},{2,3},{3,4},{4,5},{5,6},{6,7},{7,0},{8,9},{9,10},{10,1... | collective-permute-start | bytes 393224 | tf_op jit(solution)/shard_map/ppermute | solution.py:245
  159.2 1.8 %shard_map.49 = (f32[256,1024]{1,0:T(8,128)S(1)}, bf16[1,256,1024]{2,1,0:T(8,128)(2,1)S(1)}) custom-call(s32[2]{0:T(128)S(1)} %copy-done.2, bf16[256,256]{1,0:T(8,128)(2,1)S(1)} %shard_map.48.refs_0_, bf16[256,256]{1,0:T(8,128)(2,1)S(1)} %collective-permute-done.14.refs_1_, bf16[256,256]{1,0:T(8,128)(2,1)S(1)} %collective-permute-done.15.refs_2_, ...), custom_call_target="tpu_custom_call" | custom-call | tf_op jit(solution)/shard_map/pallas_call | solution.py:358
  161.0 2.6 %collective-permute-done.24.last_ref = bf16[256,256]{1,0:T(8,128)(2,1)S(1)} collective-permute-done((bf16[256,256]{1,0:T(8,128)(2,1)S(1)}, bf16[256,256]{1,0:T(8,128)(2,1)S(1)}, u32[]{:S(2)}, u32[]{:S(2)}) %collective-permute-start.24) | collective-permute-done | bytes 131104 | tf_op jit(solution)/shard_map/ppermute | solution.py:245
  163.6 0.9 shard_map.50
  164.5 0.2 collective-permute-start.25
  164.7 6.5 %collective-permute-done.25 = bf16[256,512]{1,0:T(8,128)(2,1)S(1)} collective-permute-done((bf16[256,512]{1,0:T(8,128)(2,1)S(1)}, bf16[256,512]{1,0:T(8,128)(2,1)S(1)}, u32[]{:S(2)}, u32[]{:S(2)}) %collective-permute-start.25) | collective-permute-done | bytes 262176 | tf_op jit(solution)/shard_map/ppermute | solution.py:241
  171.2 0.8 add_convert_fusion
  (38 shorter events, 0.3 us)
Async XLA Ops:
  0.0 3.0 %copy-start.6 = (bf16[256,512]{1,0:T(8,128)(2,1)S(1)}, bf16[256,512]{1,0:T(8,128)(2,1)}, u32[]{:S(2)}) copy-start(bf16[256,512]{1,0:T(8,128)(2,1)} %refs_0_.1) | copy-start | bytes 786436
  1.3 25.0 %collective-permute-start.8 = (bf16[2048,256]{1,0:T(8,128)(2,1)S(1)}, bf16[2048,256]{1,0:T(8,128)(2,1)S(1)}, u32[]{:S(2)}, u32[]{:S(2)}) collective-permute-start(bf16[2048,256]{1,0:T(8,128)(2,1)S(1)} %constant_dynamic-slice_fusion), channel_id=1, source_target_pairs={{0,8},{1,9},{2,10},{3,11},{4,12},{5,13},{6,14},{7,15},{8,0},{9,1},... | collective-permute-start | bytes 3145736 | tf_op jit(solution)/shard_map/ppermute | solution.py:241
  3.0 11.9 %collective-permute-start = (bf16[256,512]{1,0:T(8,128)(2,1)S(1)}, bf16[256,512]{1,0:T(8,128)(2,1)S(1)}, u32[]{:S(2)}, u32[]{:S(2)}) collective-permute-start(bf16[256,512]{1,0:T(8,128)(2,1)S(1)} %copy-done.6), channel_id=1, source_target_pairs={{0,1},{1,2},{2,3},{3,4},{4,5},{5,6},{6,7},{7,0},{8,9},{9,10},{10,1... | collective-permute-start | bytes 786440 | tf_op jit(solution)/shard_map/ppermute | solution.py:245
  4.9 10.0 %collective-permute-start.1 = (bf16[256,512]{1,0:T(8,128)(2,1)S(1)}, bf16[256,512]{1,0:T(8,128)(2,1)S(1)}, u32[]{:S(2)}, u32[]{:S(2)}) collective-permute-start(bf16[256,512]{1,0:T(8,128)(2,1)S(1)} %copy-done.6), channel_id=1, source_target_pairs={{0,7},{1,0},{2,1},{3,2},{4,3},{5,4},{6,5},{7,6},{8,15},{9,8},{10,9... | collective-permute-start | bytes 786440 | tf_op jit(solution)/shard_map/ppermute | solution.py:245
  8.9 32.6 %copy-start.5 = (bf16[8192,32]{0,1:T(8,128)(2,1)S(1)}, bf16[8192,32]{0,1:T(8,128)(2,1)}, u32[]{:S(2)}) copy-start(bf16[8192,32]{0,1:T(8,128)(2,1)} %param.6) | copy-start | bytes 1572868
  14.9 14.8 %copy-start.7 = (bf16[256,512]{1,0:T(8,128)(2,1)}, bf16[256,512]{1,0:T(8,128)(2,1)S(1)}, u32[]{:S(2)}) copy-start(bf16[256,512]{1,0:T(8,128)(2,1)S(1)} %collective-permute-done.refs_1_) | copy-start | bytes 786436
  14.9 14.8 %copy-start.8 = (bf16[256,512]{1,0:T(8,128)(2,1)}, bf16[256,512]{1,0:T(8,128)(2,1)S(1)}, u32[]{:S(2)}) copy-start(bf16[256,512]{1,0:T(8,128)(2,1)S(1)} %collective-permute-done.1.refs_2_) | copy-start | bytes 786436
  14.9 14.8 %collective-permute-start.2 = (bf16[256,512]{1,0:T(8,128)(2,1)S(1)}, bf16[256,512]{1,0:T(8,128)(2,1)S(1)}, u32[]{:S(2)}, u32[]{:S(2)}) collective-permute-start(bf16[256,512]{1,0:T(8,128)(2,1)S(1)} %collective-permute-done.refs_1_), channel_id=1, source_target_pairs={{0,1},{1,2},{2,3},{3,4},{4,5},{5,6},{6,7},{7,0},{8,9},{9,10},{10,1... | collective-permute-start | bytes 786440 | tf_op jit(solution)/shard_map/ppermute | solution.py:245
  15.0 14.7 %collective-permute-start.3 = (bf16[256,512]{1,0:T(8,128)(2,1)S(1)}, bf16[256,512]{1,0:T(8,128)(2,1)}, u32[]{:S(2)}, u32[]{:S(2)}) collective-permute-start(bf16[256,512]{1,0:T(8,128)(2,1)S(1)} %collective-permute-done.1.refs_2_), channel_id=1, source_target_pairs={{0,7},{1,0},{2,1},{3,2},{4,3},{5,4},{6,5},{7,6},{8,15},{9,8},{10,9... | collective-permute-start | bytes 786440 | tf_op jit(solution)/shard_map/ppermute | solution.py:245
  26.3 3.4 %copy-start.3 = (bf16[2048,256]{1,0:T(8,128)(2,1)}, bf16[2048,256]{1,0:T(8,128)(2,1)S(1)}, u32[]{:S(2)}) copy-start(bf16[2048,256]{1,0:T(8,128)(2,1)S(1)} %collective-permute-done.8.refs_11_) | copy-start | bytes 3145732
  26.3 41.2 %collective-permute-start.9 = (bf16[2048,256]{1,0:T(8,128)(2,1)S(1)}, bf16[2048,256]{1,0:T(8,128)(2,1)S(1)}, u32[]{:S(2)}, u32[]{:S(2)}) collective-permute-start(bf16[2048,256]{1,0:T(8,128)(2,1)S(1)} %collective-permute-done.8.refs_11_), channel_id=1, source_target_pairs={{0,16},{16,0},{32,48},{48,32},{64,80},{80,64},{96,112},{112,96},{1... | collective-permute-start | bytes 3145736 | tf_op jit(solution)/shard_map/ppermute | solution.py:259
  29.7 37.9 %copy-start.9 = (bf16[256,512]{1,0:T(8,128)(2,1)}, bf16[256,512]{1,0:T(8,128)(2,1)S(1)}, u32[]{:S(2)}) copy-start(bf16[256,512]{1,0:T(8,128)(2,1)S(1)} %collective-permute-done.2.refs_3_) | copy-start | bytes 786436
  29.7 47.5 %all-to-all-start = ((bf16[8,2,32,512]{3,2,1,0:T(8,128)(2,1)}), bf16[8,2,32,512]{3,2,1,0:T(8,128)(2,1)S(1)}, u32[]{:S(2)}, u32[]{:S(2)}) async-start(bf16[8,2,32,512]{3,2,1,0:T(8,128)(2,1)} %bitcast.23), calls=%async_computation | async-start | bytes 1048576 | tf_op jit(solution)/shard_map/all_to_all | solution.py:398
  38.2 20.7 %collective-permute-start.4 = (bf16[256,512]{1,0:T(8,128)(2,1)S(1)}, bf16[256,512]{1,0:T(8,128)(2,1)S(1)}, u32[]{:S(2)}, u32[]{:S(2)}) collective-permute-start(bf16[256,512]{1,0:T(8,128)(2,1)S(1)} %collective-permute-done.2.refs_3_), channel_id=1, source_target_pairs={{0,1},{1,2},{2,3},{3,4},{4,5},{5,6},{6,7},{7,0},{8,9},{9,10},{10,1... | collective-permute-start | bytes 786440 | tf_op jit(solution)/shard_map/ppermute | solution.py:245
  40.2 18.7 %collective-permute-start.5 = (bf16[256,512]{1,0:T(8,128)(2,1)}, bf16[256,512]{1,0:T(8,128)(2,1)S(1)}, u32[]{:S(2)}, u32[]{:S(2)}) collective-permute-start(bf16[256,512]{1,0:T(8,128)(2,1)} %collective-permute-done.3.refs_4_), channel_id=1, source_target_pairs={{0,7},{1,0},{2,1},{3,2},{4,3},{5,4},{6,5},{7,6},{8,15},{9,8},{10,9... | collective-permute-start | bytes 786440 | tf_op jit(solution)/shard_map/ppermute | solution.py:245
  42.2 17.0 %collective-permute-start.7 = (bf16[32,4096]{1,0:T(8,128)(2,1)S(1)}, bf16[32,4096]{1,0:T(8,128)(2,1)S(1)}, u32[]{:S(2)}, u32[]{:S(2)}) collective-permute-start(bf16[32,4096]{1,0:T(8,128)(2,1)S(1)} %get-tuple-element.59), channel_id=1, source_target_pairs={{0,8},{1,9},{2,10},{3,11},{4,12},{5,13},{6,14},{7,15},{8,0},{9,1},... | collective-permute-start | bytes 786440 | tf_op jit(solution)/shard_map/ppermute | solution.py:241
  58.9 8.6 %copy-start.10 = (bf16[256,512]{1,0:T(8,128)(2,1)}, bf16[256,512]{1,0:T(8,128)(2,1)S(1)}, u32[]{:S(2)}) copy-start(bf16[256,512]{1,0:T(8,128)(2,1)S(1)} %collective-permute-done.4.refs_5_) | copy-start | bytes 786436
  58.9 8.6 %copy-start.11 = (bf16[256,512]{1,0:T(8,128)(2,1)}, bf16[256,512]{1,0:T(8,128)(2,1)S(1)}, u32[]{:S(2)}) copy-start(bf16[256,512]{1,0:T(8,128)(2,1)S(1)} %collective-permute-done.5.refs_6_) | copy-start | bytes 786436
  58.9 8.6 %collective-permute-start.6 = (bf16[256,512]{1,0:T(8,128)(2,1)S(1)}, bf16[256,512]{1,0:T(8,128)(2,1)S(1)}, u32[]{:S(2)}, u32[]{:S(2)}) collective-permute-start(bf16[256,512]{1,0:T(8,128)(2,1)S(1)} %collective-permute-done.4.refs_5_), channel_id=1, source_target_pairs={{0,1},{1,2},{2,3},{3,4},{4,5},{5,6},{6,7},{7,0},{8,9},{9,10},{10,1... | collective-permute-start | bytes 786440 | tf_op jit(solution)/shard_map/ppermute | solution.py:245
  59.2 8.4 %copy-start.12 = (bf16[32,4096]{1,0:T(8,128)(2,1)}, bf16[32,4096]{1,0:T(8,128)(2,1)S(1)}, u32[]{:S(2)}) copy-start(bf16[32,4096]{1,0:T(8,128)(2,1)S(1)} %collective-permute-done.7.refs_9_) | copy-start | bytes 786436
  67.5 0.7 copy-start.13
  67.5 1.1 copy-start.4
  75.6 4.6 %collective-permute-start.11 = (f32[64,256]{1,0:T(8,128)}, f32[64,256]{1,0:T(8,128)S(1)}, u32[]{:S(2)}, u32[]{:S(2)}) collective-permute-start(f32[64,256]{1,0:T(8,128)} %get-tuple-element.41.one_ref), channel_id=1, source_target_pairs={{0,8},{1,9},{2,10},{3,11},{4,12},{5,13},{6,14},{7,15},{8,0},{9,1},... | collective-permute-start | bytes 196616 | tf_op jit(solution)/shard_map/ppermute | solution.py:241
  80.1 0.8 copy-start.1
  81.7 15.4 %all-to-all-start.1 = ((bf16[8,64,256]{2,1,0:T(8,128)(2,1)}), bf16[8,64,256]{2,1,0:T(8,128)(2,1)S(1)}, u32[]{:S(2)}, u32[]{:S(2)}) async-start(bf16[8,64,256]{2,1,0:T(8,128)(2,1)} %shard_map.47), calls=%async_computation.1 | async-start | bytes 524288 | tf_op jit(solution)/shard_map/all_to_all | solution.py:297
  86.6 12.4 %collective-permute-start.10 = (f32[256,256]{1,0:T(8,128)}, f32[256,256]{1,0:T(8,128)S(1)}, u32[]{:S(2)}, u32[]{:S(2)}) collective-permute-start(f32[256,256]{1,0:T(8,128)} %get-tuple-element.40), channel_id=1, source_target_pairs={{0,8},{1,9},{2,10},{3,11},{4,12},{5,13},{6,14},{7,15},{8,0},{9,1},... | collective-permute-start | bytes 786440 | tf_op jit(solution)/shard_map/ppermute | solution.py:241
  88.2 59.9 %collective-permute-start.16 = (bf16[8,2,32,512]{3,2,1,0:T(8,128)(2,1)S(1)}, bf16[8,2,32,512]{3,2,1,0:T(8,128)(2,1)S(1)}, u32[]{:S(2)}, u32[]{:S(2)}) collective-permute-start(bf16[8,2,32,512]{3,2,1,0:T(8,128)(2,1)S(1)} %all-to-all-done), channel_id=1, source_target_pairs={{0,64},{16,80},{32,96},{48,112},{64,128},{80,144},{96,160},{112,17... | collective-permute-start | bytes 1572872 | tf_op jit(solution)/shard_map/ppermute | solution.py:255
  89.6 58.4 %collective-permute-start.17 = (bf16[8,2,32,512]{3,2,1,0:T(8,128)(2,1)S(1)}, bf16[8,2,32,512]{3,2,1,0:T(8,128)(2,1)S(1)}, u32[]{:S(2)}, u32[]{:S(2)}) collective-permute-start(bf16[8,2,32,512]{3,2,1,0:T(8,128)(2,1)S(1)} %all-to-all-done), channel_id=1, source_target_pairs={{0,192},{16,208},{32,224},{48,240},{64,0},{80,16},{96,32},{112,48}... | collective-permute-start | bytes 1572872 | tf_op jit(solution)/shard_map/ppermute | solution.py:255
  90.2 57.8 %collective-permute-start.18 = (bf16[8,2,32,512]{3,2,1,0:T(8,128)(2,1)S(1)}, bf16[8,2,32,512]{3,2,1,0:T(8,128)(2,1)S(1)}, u32[]{:S(2)}, u32[]{:S(2)}) collective-permute-start(bf16[8,2,32,512]{3,2,1,0:T(8,128)(2,1)S(1)} %all-to-all-done), channel_id=1, source_target_pairs={{0,128},{16,144},{32,160},{48,176},{64,192},{80,208},{96,224},{112... | collective-permute-start | bytes 1572872 | tf_op jit(solution)/shard_map/ppermute | solution.py:255
  97.1 21.1 %collective-permute-start.13 = (bf16[8,2,32,256]{3,2,1,0:T(8,128)(2,1)S(1)}, bf16[8,2,32,256]{3,2,1,0:T(8,128)(2,1)S(1)}, u32[]{:S(2)}, u32[]{:S(2)}) collective-permute-start(bf16[8,2,32,256]{3,2,1,0:T(8,128)(2,1)S(1)} %bitcast.24), channel_id=1, source_target_pairs={{0,16},{16,32},{32,48},{48,64},{64,80},{80,96},{96,112},{112,128},... | collective-permute-start | bytes 786440 | tf_op jit(solution)/shard_map/ppermute | solution.py:251
  99.0 19.1 %collective-permute-start.12 = (bf16[8,32,256]{2,1,0:T(8,128)(2,1)S(1)}, bf16[8,32,256]{2,1,0:T(8,128)(2,1)S(1)}, u32[]{:S(2)}, u32[]{:S(2)}) collective-permute-start(bf16[8,32,256]{2,1,0:T(8,128)(2,1)S(1)} %slice_bitcast_fusion), channel_id=1, source_target_pairs={{0,32},{16,48},{32,64},{48,80},{64,96},{80,112},{96,128},{112,144}... | collective-permute-start | bytes 393224 | tf_op jit(solution)/shard_map/ppermute | solution.py:251
  118.1 1.0 copy-start
  134.7 6.3 %collective-permute-start.14 = (bf16[256,256]{1,0:T(8,128)(2,1)S(1)}, bf16[256,256]{1,0:T(8,128)(2,1)S(1)}, u32[]{:S(2)}, u32[]{:S(2)}) collective-permute-start(bf16[256,256]{1,0:T(8,128)(2,1)S(1)} %shard_map.48.refs_0_), channel_id=1, source_target_pairs={{0,1},{1,2},{2,3},{3,4},{4,5},{5,6},{6,7},{7,0},{8,9},{9,10},{10,1... | collective-permute-start | bytes 393224 | tf_op jit(solution)/shard_map/ppermute | solution.py:245
  136.5 5.0 %collective-permute-start.15 = (bf16[256,256]{1,0:T(8,128)(2,1)S(1)}, bf16[256,256]{1,0:T(8,128)(2,1)S(1)}, u32[]{:S(2)}, u32[]{:S(2)}) collective-permute-start(bf16[256,256]{1,0:T(8,128)(2,1)S(1)} %shard_map.48.refs_0_), channel_id=1, source_target_pairs={{0,7},{1,0},{2,1},{3,2},{4,3},{5,4},{6,5},{7,6},{8,15},{9,8},{10,9... | collective-permute-start | bytes 393224 | tf_op jit(solution)/shard_map/ppermute | solution.py:245
  141.5 6.2 %collective-permute-start.19 = (bf16[256,256]{1,0:T(8,128)(2,1)S(1)}, bf16[256,256]{1,0:T(8,128)(2,1)S(1)}, u32[]{:S(2)}, u32[]{:S(2)}) collective-permute-start(bf16[256,256]{1,0:T(8,128)(2,1)S(1)} %collective-permute-done.14.refs_1_), channel_id=1, source_target_pairs={{0,1},{1,2},{2,3},{3,4},{4,5},{5,6},{6,7},{7,0},{8,9},{9,10},{10,1... | collective-permute-start | bytes 393224 | tf_op jit(solution)/shard_map/ppermute | solution.py:245
  142.9 5.1 %collective-permute-start.20 = (bf16[256,256]{1,0:T(8,128)(2,1)S(1)}, bf16[256,256]{1,0:T(8,128)(2,1)S(1)}, u32[]{:S(2)}, u32[]{:S(2)}) collective-permute-start(bf16[256,256]{1,0:T(8,128)(2,1)S(1)} %collective-permute-done.15.refs_2_), channel_id=1, source_target_pairs={{0,7},{1,0},{2,1},{3,2},{4,3},{5,4},{6,5},{7,6},{8,15},{9,8},{10,9... | collective-permute-start | bytes 393224 | tf_op jit(solution)/shard_map/ppermute | solution.py:245
  145.0 14.2 %copy-start.2 = (s32[2]{0:T(128)S(1)}, s32[2]{0:T(128)}, u32[]{:S(2)}) copy-start(s32[2]{0:T(128)} %pad_add_fusion.spot_ref) | copy-start | bytes 28
  148.2 11.0 %collective-permute-start.23 = (bf16[4,8,2,32,512]{4,3,2,1,0:T(8,128)(2,1)S(1)}, bf16[4,8,2,32,512]{4,3,2,1,0:T(8,128)(2,1)S(1)}, u32[]{:S(2)}, u32[]{:S(2)}) collective-permute-start(bf16[4,8,2,32,512]{4,3,2,1,0:T(8,128)(2,1)S(1)} %bitcast_dynamic-update-slice_fusion.refs_7_), channel_id=1, source_target_pairs={{0,16},{16,0},{32,48},{48,32},{64,80},{80,64},{96,112},{112,96},{1... | collective-permute-start | bytes 6291464 | tf_op jit(solution)/shard_map/ppermute | solution.py:259
  148.3 7.1 %collective-permute-start.21 = (bf16[256,256]{1,0:T(8,128)(2,1)S(1)}, bf16[256,256]{1,0:T(8,128)(2,1)S(1)}, u32[]{:S(2)}, u32[]{:S(2)}) collective-permute-start(bf16[256,256]{1,0:T(8,128)(2,1)S(1)} %collective-permute-done.19.refs_3_), channel_id=1, source_target_pairs={{0,1},{1,2},{2,3},{3,4},{4,5},{5,6},{6,7},{7,0},{8,9},{9,10},{10,1... | collective-permute-start | bytes 393224 | tf_op jit(solution)/shard_map/ppermute | solution.py:245
  151.6 5.8 %collective-permute-start.22 = (bf16[256,256]{1,0:T(8,128)(2,1)S(1)}, bf16[256,256]{1,0:T(8,128)(2,1)S(1)}, u32[]{:S(2)}, u32[]{:S(2)}) collective-permute-start(bf16[256,256]{1,0:T(8,128)(2,1)S(1)} %collective-permute-done.20.refs_4_), channel_id=1, source_target_pairs={{0,7},{1,0},{2,1},{3,2},{4,3},{5,4},{6,5},{7,6},{8,15},{9,8},{10,9... | collective-permute-start | bytes 393224 | tf_op jit(solution)/shard_map/ppermute | solution.py:245
  157.4 6.2 %collective-permute-start.24 = (bf16[256,256]{1,0:T(8,128)(2,1)S(1)}, bf16[256,256]{1,0:T(8,128)(2,1)S(1)}, u32[]{:S(2)}, u32[]{:S(2)}) collective-permute-start(bf16[256,256]{1,0:T(8,128)(2,1)S(1)} %collective-permute-done.21.refs_5_), channel_id=1, source_target_pairs={{0,1},{1,2},{2,3},{3,4},{4,5},{5,6},{6,7},{7,0},{8,9},{9,10},{10,1... | collective-permute-start | bytes 393224 | tf_op jit(solution)/shard_map/ppermute | solution.py:245
  164.5 6.7 %collective-permute-start.25 = (bf16[256,512]{1,0:T(8,128)(2,1)S(1)}, bf16[256,512]{1,0:T(8,128)(2,1)S(1)}, u32[]{:S(2)}, u32[]{:S(2)}) collective-permute-start(bf16[256,512]{1,0:T(8,128)(2,1)S(1)} %get-tuple-element.58), channel_id=1, source_target_pairs={{0,8},{1,9},{2,10},{3,11},{4,12},{5,13},{6,14},{7,15},{8,0},{9,1},... | collective-permute-start | bytes 786440 | tf_op jit(solution)/shard_map/ppermute | solution.py:241

commit v8 on v7

--- a/solution.py
+++ b/solution.py
@@ -176,65 +176,104 @@
 OFFSETS = (0, -1, 1, -2, 2, -3, 3, -4)
 
 
-def project_kernel(spot_ref, *refs):
-    shards_any, kv_any, own_any, parts_any = refs[:8], refs[8:10], refs[10], refs[11:13]
-    kv_out, mine_any, theirs_any = refs[13:16]
-    rows_ref, kv_ref, own_ref, part_ref, mine_out, theirs_out, sems = refs[16:]
-    depth = shards_any[0].shape[1]
-    half = own_ref.shape[0]
-    row, core = spot_ref[0] >> 3, spot_ref[1]
-    parts = kv_ref.shape[0] // 2
-
-    def at(place, count):
-        return pl.ds(pl.multiple_of(place * count, count), count)
-
-    moves = []
-    for offset, source in zip(OFFSETS, shards_any):
-        moves.append((source, rows_ref.at[:, at((spot_ref[0] + offset) & 7, depth)]))
-    for source, side in zip(kv_any, (row, 1 - row)):
-        moves.append((source, kv_ref.at[at(side, parts), :]))
-    moves.append((own_any.at[at(row, half), :], own_ref))
-    for source, side in zip(parts_any, (core, 1 - core)):
-        moves.append((source, part_ref.at[at(side, half // 2), :]))
+def at(place, count):
+    return pl.ds(pl.multiple_of(place * count, count), count)
+
+
+def fetch_all(moves, sems):
     fetches = [
         pltpu.make_async_copy(source, target, sems.at[k])
         for k, (source, target) in enumerate(moves)
     ]
     for fetch in fetches:
         fetch.start()
-    for fetch in fetches[:10]:
+    return fetches
+
+
+def into_rows(spot_ref, shards, rows_ref):
+    depth = shards[0].shape[1]
+    return [
+        (source, rows_ref.at[:, at((spot_ref[0] + offset) & 7, depth)])
+        for offset, source in zip(OFFSETS, shards)
+    ]
+
+
+def keyval_kernel(spot_ref, *refs):
+    shards, kv_any, kv_out, rows_ref, kv_ref, sems = refs[:8], refs[8:10], *refs[10:]
+    row = spot_ref[0] >> 3
+    parts = kv_ref.shape[0] // 2
+    moves = into_rows(spot_ref, shards, rows_ref)
+    for source, side in zip(kv_any, (row, 1 - row)):
+        moves.append((source, kv_ref.at[at(side, parts), :]))
+    for fetch in fetch_all(moves, sems):
         fetch.wait()
     kv_out[...] = lax.dot_general(
         rows_ref[...], kv_ref[...], LANES, preferred_element_type=jnp.float32
     ).T
-    fetches[10].wait()
+
+
+def query_kernel(spot_ref, *refs):
+    shards, own_any, parts_any = refs[:8], refs[8], refs[9:11]
+    mine_any, theirs_any, rows_ref, own_ref, part_ref, mine_out, theirs_out, sems = refs[11:]
+    half = own_ref.shape[0]
+    row, core = spot_ref[0] >> 3, spot_ref[1]
+    moves = into_rows(spot_ref, shards, rows_ref)
+    moves.append((own_any.at[at(row, half), :], own_ref))
+    for source, side in zip(parts_any, (core, 1 - core)):
+        moves.append((source, part_ref.at[at(side, half // 2), :]))
+    fetches = fetch_all(moves, sems)
+    for fetch in fetches[:9]:
+        fetch.wait()
     mine_out[...] = jnp.dot(rows_ref[...], own_ref[...], preferred_element_type=jnp.float32)
-    keep = pltpu.make_async_copy(mine_out, mine_any, sems.at[13])
+    keep = pltpu.make_async_copy(mine_out, mine_any, sems.at[11])
     keep.start()
-    for fetch in fetches[11:]:
+    for fetch in fetches[9:]:
         fetch.wait()
     theirs_out[...] = jnp.dot(rows_ref[...], part_ref[...], preferred_element_type=jnp.float32)
-    send = pltpu.make_async_copy(theirs_out, theirs_any, sems.at[14])
+    send = pltpu.make_async_copy(theirs_out, theirs_any, sems.at[12])
     send.start()
     keep.wait()
     send.wait()
 
 
-def project(spots, arrays, shapes):
+def project_keyval(spots, shards, kv_own, kv_part):
+    tok, depth = shards[0].shape
+    parts = kv_own.shape[0]
+    return pl.pallas_call(
+        keyval_kernel,
+        out_shape=jax.ShapeDtypeStruct((2 * parts, tok), jnp.float32),
+        in_specs=[pl.BlockSpec(memory_space=pltpu.SMEM)]
+        + [pl.BlockSpec(memory_space=pltpu.HBM)] * 10,
+        out_specs=in_vmem(1)[0],
+        scratch_shapes=[
+            pltpu.VMEM((tok, 8 * depth), kv_own.dtype),
+            pltpu.VMEM((2 * parts, 8 * depth), kv_own.dtype),
+            pltpu.SemaphoreType.DMA((10,)),
+        ],
+        compiler_params=pltpu.CompilerParams(vmem_limit_bytes=60 * 1024 * 1024),
+    )(spots, *shards, kv_own, kv_part)
+
+
+def project_query(spots, shards, own, same, twin):
+    tok, depth = shards[0].shape
     far_off = pl.BlockSpec(memory_space=pltpu.HBM)
-    own = arrays[10]
-    half = (own.shape[0] // 2, own.shape[1])
-    kept = [(arrays[0].shape[0], half[0]), (2 * arrays[8].shape[0], arrays[8].shape[1]), half, half]
+    half = (8 * depth, own.shape[1])
+    out = jax.ShapeDtypeStruct((tok, own.shape[1]), jnp.float32)
     return pl.pallas_call(
-        project_kernel,
-        out_shape=tuple(jax.ShapeDtypeStruct(shape, jnp.float32) for shape in shapes),
-        in_specs=[pl.BlockSpec(memory_space=pltpu.SMEM)] + [far_off] * len(arrays),
-        out_specs=(in_vmem(1)[0], far_off, far_off),
-        scratch_shapes=[pltpu.VMEM(shape, own.dtype) for shape in kept]
-        + [pltpu.VMEM(shape, jnp.float32) for shape in shapes[1:]]
-        + [pltpu.SemaphoreType.DMA((15,))],
+        query_kernel,
+        out_shape=(out, out),
+        in_specs=[pl.BlockSpec(memory_space=pltpu.SMEM)] + [far_off] * 11,
+        out_specs=(far_off, far_off),
+        scratch_shapes=[
+            pltpu.VMEM((tok, 8 * depth), own.dtype),
+            pltpu.VMEM(half, own.dtype),
+            pltpu.VMEM(half, own.dtype),
+            pltpu.VMEM(out.shape, jnp.float32),
+            pltpu.VMEM(out.shape, jnp.float32),
+            pltpu.SemaphoreType.DMA((13,)),
+        ],
         compiler_params=pltpu.CompilerParams(vmem_limit_bytes=60 * 1024 * 1024),
-    )(spots, *arrays)
+    )(spots, *shards, own, same, twin)
 
 
 def swap_rows(value):
@@ -396,11 +435,8 @@
     kv_own = lax.dynamic_slice_in_dim(kv_flat, row * half, half, 1)
     shards, (piece, spots) = z_ring(tokens, (owned_piece(w_out, seq), spots))
     piece = lax.all_to_all(piece, "head", 0, 0, tiled=True, axis_index_groups=ROWS)
-    kv_part, q_mine, q_theirs = project(
-        spots,
-        (*shards, kv_own, kv_part, w_query, q_same, q_twin),
-        ((2 * kv_flat.shape[0], tok_rows),) + ((tok_rows, w_query.shape[1]),) * 2,
-    )
+    kv_part = project_keyval(spots, shards, kv_own, kv_part)
+    q_mine, q_theirs = project_query(spots, shards, w_query, q_same, q_twin)
     kv_sent = swap_rows(kv_part)
     piece, kv_sent = lax.optimization_barrier((piece, kv_sent))
     q_sent = swap_rows(q_theirs)

time: 172 us -> 156 us (0.907)
  waiting for transfers between devices: 80.7 us -> 53.8 us
  blocking collectives: 0 us -> 15.7 us
  starting transfers between devices: 55.6 us -> 45.7 us
  Pallas kernels: 26 us -> 28.3 us
    all_to_all x0 -> x1, blocking collectives: none -> 15.7 us  [sent_to_row(): lax.all_to_all(copies, 'head', 0, 0, tiled=True, axis_index_groups=ROWS)]
    ppermute x2, waiting for transfers between devices: 14 us -> 0.01 us  [along_seq(): return lax.ppermute(value, 'seq', [(i, i + step) for i in range(16 - step)])]
    ppermute x14, waiting for transfers between devices: 44.4 us -> 38.3 us  [along_z(): lax.ppermute(value, 'head', [(i, i // 8 * 8 + (i + step) % 8) for i in ra...]
    all_to_all x1 -> x0, starting transfers between devices: 4.88 us -> none  [sent_to_row(): lax.all_to_all(copies, 'head', 0, 0, tiled=True, axis_index_groups=ROWS)]
    all_to_all x1 -> x0, waiting for transfers between devices: 4.75 us -> none  [sent_to_row(): lax.all_to_all(copies, 'head', 0, 0, tiled=True, axis_index_groups=ROWS)]
    pallas_call x1 -> x2, Pallas kernels: 6.96 us -> 9.96 us  [the longest x1 6.19 us: project_query(): pl.pallas_call(query_kernel, out_shape=(out, out), in_specs=[pl.BlockSpec...]
    all_to_all x1, starting transfers between devices: 8.48 us -> 5.66 us  [body(): lax.all_to_all(piece, 'head', 0, 0, tiled=True, axis_index_groups=ROWS)]
    ppermute x5, waiting for transfers between devices: 17.5 us -> 15.4 us  [swap_rows(): return lax.ppermute(value, 'head', [(i, (i + 8) % 16) for i in range(16)])]
  transfers between devices with their start and end apart: 28 -> 27, of which waited for: 15 -> 12; matrix products, arithmetic and copies ran while one was open for 3% -> 4% of each run, Pallas kernels for 14% -> 18%
where the time goes in v8:
time: 156 us; the launch traced here: 155 us
  waiting for transfers between devices  53.8 us (34%)
  starting transfers between devices  45.7 us (29%)
  Pallas kernels  28.3 us (18%)
  blocking collectives  15.7 us (10%)
  local copies, waits for them, and re-layouts  9.63 us (6%)
    ppermute x14, waiting for transfers between devices, along_z(): lax.ppermute(value, 'head', [(i, i // 8 * 8 + (i + step) % 8) for i in ra...  38.3 us
    ppermute x14, starting transfers between devices, along_z(): lax.ppermute(value, 'head', [(i, i // 8 * 8 + (i + step) % 8) for i in ra...  22.6 us
    all_to_all x1, blocking collectives, sent_to_row(): lax.all_to_all(copies, 'head', 0, 0, tiled=True, axis_index_groups=ROWS)  15.7 us
    pallas_call x1, Pallas kernels, attend(): pl.pallas_call(attend_kernel, out_shape=jax.ShapeDtypeStruct(mine.shape,...  15.6 us
    ppermute x5, waiting for transfers between devices, swap_rows(): return lax.ppermute(value, 'head', [(i, (i + 8) % 16) for i in range(16)])  15.4 us
    ppermute x2, starting transfers between devices, along_seq(): return lax.ppermute(value, 'seq', [(i, i + step) for i in range(16 - step)])  7.02 us
    ppermute x5, starting transfers between devices, swap_rows(): return lax.ppermute(value, 'head', [(i, (i + 8) % 16) for i in range(16)])  6.26 us
    pallas_call x1, Pallas kernels, project_query(): pl.pallas_call(query_kernel, out_shape=(out, out), in_specs=[pl.BlockSpec...  6.19 us
  transfers between devices with their start and end apart: 27, of which 12 were waited for; matrix products, arithmetic and copies ran while one was open for 4% of the time, Pallas kernels for 18%

profile of v8, /device:TPU:2, one launch (start us, length us, event | category | flops | bytes accessed | tf_op | source)
XLA Modules:
  0.0 154.8 jit_solution(2041956805570486035)
XLA Ops:
  0.0 1.9 %collective-permute-start = (bf16[256,512]{1,0:T(8,128)(2,1)}, bf16[256,512]{1,0:T(8,128)(2,1)S(1)}, u32[]{:S(2)}, u32[]{:S(2)}) collective-permute-start(bf16[256,512]{1,0:T(8,128)(2,1)} %refs_0_.3), channel_id=1, source_target_pairs={{0,1},{1,2},{2,3},{3,4},{4,5},{5,6},{6,7},{7,0},{8,9},{9,10},{10,1... | collective-permute-start | bytes 786440 | tf_op jit(solution)/shard_map/ppermute | solution.py:284
  1.9 3.9 %collective-permute-start.1 = (bf16[256,512]{1,0:T(8,128)(2,1)}, bf16[256,512]{1,0:T(8,128)(2,1)S(1)}, u32[]{:S(2)}, u32[]{:S(2)}) collective-permute-start(bf16[256,512]{1,0:T(8,128)(2,1)} %refs_0_.3), channel_id=1, source_target_pairs={{0,7},{1,0},{2,1},{3,2},{4,3},{5,4},{6,5},{7,6},{8,15},{9,8},{10,9... | collective-permute-start | bytes 786440 | tf_op jit(solution)/shard_map/ppermute | solution.py:284
  5.9 1.3 constant_dynamic-slice_fusion
  7.2 1.7 %collective-permute-start.7 = (bf16[2048,256]{1,0:T(8,128)(2,1)S(1)}, bf16[2048,256]{1,0:T(8,128)(2,1)S(1)}, u32[]{:S(2)}, u32[]{:S(2)}) collective-permute-start(bf16[2048,256]{1,0:T(8,128)(2,1)S(1)} %constant_dynamic-slice_fusion), channel_id=1, source_target_pairs={{0,8},{1,9},{2,10},{3,11},{4,12},{5,13},{6,14},{7,15},{8,0},{9,1},... | collective-permute-start | bytes 3145736 | tf_op jit(solution)/shard_map/ppermute | solution.py:280
  8.8 3.6 %collective-permute-done.refs_1_ = bf16[256,512]{1,0:T(8,128)(2,1)S(1)} collective-permute-done((bf16[256,512]{1,0:T(8,128)(2,1)}, bf16[256,512]{1,0:T(8,128)(2,1)S(1)}, u32[]{:S(2)}, u32[]{:S(2)}) %collective-permute-start) | collective-permute-done | bytes 262176 | tf_op jit(solution)/shard_map/ppermute | solution.py:284
  12.4 0.1 collective-permute-start.2
  12.5 3.2 %collective-permute-start.3 = (bf16[256,512]{1,0:T(8,128)(2,1)S(1)}, bf16[256,512]{1,0:T(8,128)(2,1)}, u32[]{:S(2)}, u32[]{:S(2)}) collective-permute-start(bf16[256,512]{1,0:T(8,128)(2,1)S(1)} %collective-permute-done.1.refs_2_), channel_id=1, source_target_pairs={{0,7},{1,0},{2,1},{3,2},{4,3},{5,4},{6,5},{7,6},{8,15},{9,8},{10,9... | collective-permute-start | bytes 786440 | tf_op jit(solution)/shard_map/ppermute | solution.py:284
  15.7 1.1 constant_dynamic-slice_fusion.1
  16.8 0.2 copy.6
  16.9 1.1 copy.8
  18.0 0.7 pad_add_fusion.spot_ref
  18.7 2.4 %collective-permute-done.2.refs_3_ = bf16[256,512]{1,0:T(8,128)(2,1)S(1)} collective-permute-done((bf16[256,512]{1,0:T(8,128)(2,1)S(1)}, bf16[256,512]{1,0:T(8,128)(2,1)S(1)}, u32[]{:S(2)}, u32[]{:S(2)}) %collective-permute-start.2) | collective-permute-done | bytes 262176 | tf_op jit(solution)/shard_map/ppermute | solution.py:284
  21.1 0.0 collective-permute-done.3.refs_4_
  21.2 5.7 %all-to-all-start = ((bf16[8,2,32,512]{3,2,1,0:T(8,128)(2,1)}), bf16[8,2,32,512]{3,2,1,0:T(8,128)(2,1)S(1)}, u32[]{:S(2)}, u32[]{:S(2)}) async-start(bf16[8,2,32,512]{3,2,1,0:T(8,128)(2,1)} %bitcast.23), calls=%async_computation | async-start | bytes 1048576 | tf_op jit(solution)/shard_map/all_to_all | solution.py:437
  26.8 2.0 %collective-permute-start.4 = (bf16[256,512]{1,0:T(8,128)(2,1)S(1)}, bf16[256,512]{1,0:T(8,128)(2,1)S(1)}, u32[]{:S(2)}, u32[]{:S(2)}) collective-permute-start(bf16[256,512]{1,0:T(8,128)(2,1)S(1)} %collective-permute-done.2.refs_3_), channel_id=1, source_target_pairs={{0,1},{1,2},{2,3},{3,4},{4,5},{5,6},{6,7},{7,0},{8,9},{9,10},{10,1... | collective-permute-start | bytes 786440 | tf_op jit(solution)/shard_map/ppermute | solution.py:284
  28.8 1.2 collective-permute-start.5
  30.1 1.8 %collective-permute-done.7.refs_9_ = bf16[2048,256]{1,0:T(8,128)(2,1)S(1)} collective-permute-done((bf16[2048,256]{1,0:T(8,128)(2,1)S(1)}, bf16[2048,256]{1,0:T(8,128)(2,1)S(1)}, u32[]{:S(2)}, u32[]{:S(2)}) %collective-permute-start.7) | collective-permute-done | bytes 1048608 | tf_op jit(solution)/shard_map/ppermute | solution.py:280
  31.9 2.1 %dynamic-slice_bitcast_fusion = (bf16[32,4096]{1,0:T(8,128)(2,1)S(1)}, bf16[32,4096]{1,0:T(8,128)(2,1)}) fusion(bf16[8192,32]{0,1:T(8,128)(2,1)} %param.6, s32[]{:T(128)S(6)} %select_n.27, s32[]{:T(128)S(6)} %select_n.26), kind=kLoop, calls=%fused_computation.6 | loop fusion | bytes 1048584 | tf_op jit(solution)/shard_map/dynamic_slice | solution.py:430
  34.0 1.6 %collective-permute-start.10 = (bf16[32,4096]{1,0:T(8,128)(2,1)S(1)}, bf16[32,4096]{1,0:T(8,128)(2,1)S(1)}, u32[]{:S(2)}, u32[]{:S(2)}) collective-permute-start(bf16[32,4096]{1,0:T(8,128)(2,1)S(1)} %get-tuple-element.57), channel_id=1, source_target_pairs={{0,8},{1,9},{2,10},{3,11},{4,12},{5,13},{6,14},{7,15},{8,0},{9,1},... | collective-permute-start | bytes 786440 | tf_op jit(solution)/shard_map/ppermute | solution.py:280
  35.6 9.7 %collective-permute-done.4.refs_5_ = bf16[256,512]{1,0:T(8,128)(2,1)S(1)} collective-permute-done((bf16[256,512]{1,0:T(8,128)(2,1)S(1)}, bf16[256,512]{1,0:T(8,128)(2,1)S(1)}, u32[]{:S(2)}, u32[]{:S(2)}) %collective-permute-start.4) | collective-permute-done | bytes 262176 | tf_op jit(solution)/shard_map/ppermute | solution.py:284
  45.2 0.0 collective-permute-done.5.refs_6_
  45.2 0.3 collective-permute-start.6
  45.5 0.0 collective-permute-done.10.refs_9_
  45.5 7.5 %collective-permute-done.6.refs_7_ = bf16[256,512]{1,0:T(8,128)(2,1)S(1)} collective-permute-done((bf16[256,512]{1,0:T(8,128)(2,1)S(1)}, bf16[256,512]{1,0:T(8,128)(2,1)S(1)}, u32[]{:S(2)}, u32[]{:S(2)}) %collective-permute-start.6) | collective-permute-done | bytes 262176 | tf_op jit(solution)/shard_map/ppermute | solution.py:284
  53.1 0.7 copy-done.10
  53.7 3.8 %shard_map.47.one_ref = f32[64,256]{1,0:T(8,128)} custom-call(s32[2]{0:T(128)} %pad_add_fusion.spot_ref, bf16[256,512]{1,0:T(8,128)(2,1)} %refs_0_.3, bf16[256,512]{1,0:T(8,128)(2,1)} %copy-done.5, bf16[256,512]{1,0:T(8,128)(2,1)} %copy-done.6, bf16[256,512]{1,0:T(8,128)(2,1)} %copy-done.7, bf16[256,512]{1,0:T(8,128)(2,1)} %collective-permute-done.3.refs_4_, ...), custom_call_target="tpu_custom_call" | custom-call | tf_op jit(solution)/shard_map/pallas_call | solution.py:242
  57.5 1.7 %collective-permute-start.11 = (f32[64,256]{1,0:T(8,128)}, f32[64,256]{1,0:T(8,128)S(1)}, u32[]{:S(2)}, u32[]{:S(2)}) collective-permute-start(f32[64,256]{1,0:T(8,128)} %shard_map.47.one_ref), channel_id=1, source_target_pairs={{0,8},{1,9},{2,10},{3,11},{4,12},{5,13},{6,14},{7,15},{8,0},{9,1},... | collective-permute-start | bytes 196616 | tf_op jit(solution)/shard_map/ppermute | solution.py:280
  59.2 2.9 %collective-permute-done.11.two_ref = f32[64,256]{1,0:T(8,128)S(1)} collective-permute-done((f32[64,256]{1,0:T(8,128)}, f32[64,256]{1,0:T(8,128)S(1)}, u32[]{:S(2)}, u32[]{:S(2)}) %collective-permute-start.11) | collective-permute-done | bytes 65568 | tf_op jit(solution)/shard_map/ppermute | solution.py:280
  62.1 0.0 all-to-all-done
  62.1 0.8 copy-done.1
  63.0 15.7 %all_to_all.10 = bf16[8,64,256]{2,1,0:T(8,128)(2,1)S(1)} all-to-all(bf16[8,64,256]{2,1,0:T(8,128)(2,1)S(1)} %shard_map.48), channel_id=1, replica_groups={{0,1,2,3,4,5,6,7},{8,9,10,11,12,13,14,15},{16,17,18,19,20,21,22,23},{24..., dimensions={0} | all-to-all | bytes 524288 | tf_op jit(solution)/shard_map/all_to_all | solution.py:336
  78.7 5.1 %collective-permute-start.12 = (bf16[8,32,256]{2,1,0:T(8,128)(2,1)S(1)}, bf16[8,32,256]{2,1,0:T(8,128)(2,1)S(1)}, u32[]{:S(2)}, u32[]{:S(2)}) collective-permute-start(bf16[8,32,256]{2,1,0:T(8,128)(2,1)S(1)} %slice_bitcast_fusion), channel_id=1, source_target_pairs={{0,32},{16,48},{32,64},{48,80},{64,96},{80,112},{96,128},{112,144}... | collective-permute-start | bytes 393224 | tf_op jit(solution)/shard_map/ppermute | solution.py:290
  83.8 1.9 %collective-permute-start.13 = (bf16[8,2,32,256]{3,2,1,0:T(8,128)(2,1)S(1)}, bf16[8,2,32,256]{3,2,1,0:T(8,128)(2,1)S(1)}, u32[]{:S(2)}, u32[]{:S(2)}) collective-permute-start(bf16[8,2,32,256]{3,2,1,0:T(8,128)(2,1)S(1)} %bitcast.25), channel_id=1, source_target_pairs={{0,16},{16,32},{32,48},{48,64},{64,80},{80,96},{96,112},{112,128},... | collective-permute-start | bytes 786440 | tf_op jit(solution)/shard_map/ppermute | solution.py:290
  85.7 0.0 collective-permute-done.8.refs_10_
  85.7 1.0 copy-done.4
  86.7 6.2 %shard_map.46 = (f32[256,256]{1,0:T(8,128)}, f32[256,256]{1,0:T(8,128)}) custom-call(s32[2]{0:T(128)} %pad_add_fusion.spot_ref, bf16[256,512]{1,0:T(8,128)(2,1)} %refs_0_.3, bf16[256,512]{1,0:T(8,128)(2,1)} %copy-done.5, bf16[256,512]{1,0:T(8,128)(2,1)} %copy-done.6, bf16[256,512]{1,0:T(8,128)(2,1)} %copy-done.7, ...), custom_call_target="tpu_custom_call" | custom-call | tf_op jit(solution)/shard_map/pallas_call | solution.py:262
  92.9 0.8 collective-permute-start.9
  93.7 1.5 collective-permute-start.16
  95.2 0.5 collective-permute-start.17
  95.7 0.0 collective-permute-done.12.far_ref
  95.7 2.1 %collective-permute-start.18 = (bf16[8,2,32,512]{3,2,1,0:T(8,128)(2,1)S(1)}, bf16[8,2,32,512]{3,2,1,0:T(8,128)(2,1)S(1)}, u32[]{:S(2)}, u32[]{:S(2)}) collective-permute-start(bf16[8,2,32,512]{3,2,1,0:T(8,128)(2,1)S(1)} %all-to-all-done), channel_id=1, source_target_pairs={{0,128},{16,144},{32,160},{48,176},{64,192},{80,208},{96,224},{112... | collective-permute-start | bytes 1572872 | tf_op jit(solution)/shard_map/ppermute | solution.py:294
  97.8 0.0 collective-permute-done.13.near_ref
  97.8 4.2 %collective-permute-done.9.sent_any = f32[256,256]{1,0:T(8,128)S(1)} collective-permute-done((f32[256,256]{1,0:T(8,128)}, f32[256,256]{1,0:T(8,128)S(1)}, u32[]{:S(2)}, u32[]{:S(2)}) %collective-permute-start.9) | collective-permute-done | bytes 262176 | tf_op jit(solution)/shard_map/ppermute | solution.py:280
  102.0 0.9 copy-done
  102.9 15.6 %shard_map.49.refs_0_ = bf16[256,256]{1,0:T(8,128)(2,1)S(1)} custom-call(s32[1]{0:T(128)} %bitcast.3.seq_ref, f32[256,256]{1,0:T(8,128)S(1)} %copy-done, f32[256,256]{1,0:T(8,128)S(1)} %collective-permute-done.9.sent_any, bf16[8,32,256]{2,1,0:T(8,128)(2,1)S(1)} %collective-permute-done.12.far_ref, ...), custom_call_target="tpu_custom_call" | custom-call | tf_op jit(solution)/shard_map/pallas_call | solution.py:151
  118.6 0.3 collective-permute-start.14
  118.8 3.0 %collective-permute-start.15 = (bf16[256,256]{1,0:T(8,128)(2,1)S(1)}, bf16[256,256]{1,0:T(8,128)(2,1)S(1)}, u32[]{:S(2)}, u32[]{:S(2)}) collective-permute-start(bf16[256,256]{1,0:T(8,128)(2,1)S(1)} %shard_map.49.refs_0_), channel_id=1, source_target_pairs={{0,7},{1,0},{2,1},{3,2},{4,3},{5,4},{6,5},{7,6},{8,15},{9,8},{10,9... | collective-permute-start | bytes 393224 | tf_op jit(solution)/shard_map/ppermute | solution.py:284
  121.9 3.9 %collective-permute-done.14.refs_1_ = bf16[256,256]{1,0:T(8,128)(2,1)S(1)} collective-permute-done((bf16[256,256]{1,0:T(8,128)(2,1)S(1)}, bf16[256,256]{1,0:T(8,128)(2,1)S(1)}, u32[]{:S(2)}, u32[]{:S(2)}) %collective-permute-start.14) | collective-permute-done | bytes 131104 | tf_op jit(solution)/shard_map/ppermute | solution.py:284
  125.8 0.0 collective-permute-done.15.refs_2_
  125.8 0.0 collective-permute-start.19
  125.8 3.2 %collective-permute-start.20 = (bf16[256,256]{1,0:T(8,128)(2,1)S(1)}, bf16[256,256]{1,0:T(8,128)(2,1)S(1)}, u32[]{:S(2)}, u32[]{:S(2)}) collective-permute-start(bf16[256,256]{1,0:T(8,128)(2,1)S(1)} %collective-permute-done.15.refs_2_), channel_id=1, source_target_pairs={{0,7},{1,0},{2,1},{3,2},{4,3},{5,4},{6,5},{7,6},{8,15},{9,8},{10,9... | collective-permute-start | bytes 393224 | tf_op jit(solution)/shard_map/ppermute | solution.py:284
  129.0 0.2 broadcast_in_dim.15
  129.3 2.7 %collective-permute-done.19.refs_3_ = bf16[256,256]{1,0:T(8,128)(2,1)S(1)} collective-permute-done((bf16[256,256]{1,0:T(8,128)(2,1)S(1)}, bf16[256,256]{1,0:T(8,128)(2,1)S(1)}, u32[]{:S(2)}, u32[]{:S(2)}) %collective-permute-start.19) | collective-permute-done | bytes 131104 | tf_op jit(solution)/shard_map/ppermute | solution.py:284
  132.0 0.0 collective-permute-done.16
  132.2 0.1 collective-permute-start.23
  132.3 0.1 collective-permute-start.21
  132.4 3.2 %collective-permute-start.22 = (bf16[256,256]{1,0:T(8,128)(2,1)S(1)}, bf16[256,256]{1,0:T(8,128)(2,1)S(1)}, u32[]{:S(2)}, u32[]{:S(2)}) collective-permute-start(bf16[256,256]{1,0:T(8,128)(2,1)S(1)} %collective-permute-done.20.refs_4_), channel_id=1, source_target_pairs={{0,7},{1,0},{2,1},{3,2},{4,3},{5,4},{6,5},{7,6},{8,15},{9,8},{10,9... | collective-permute-start | bytes 393224 | tf_op jit(solution)/shard_map/ppermute | solution.py:284
  135.6 4.0 %collective-permute-done.21.refs_5_ = bf16[256,256]{1,0:T(8,128)(2,1)S(1)} collective-permute-done((bf16[256,256]{1,0:T(8,128)(2,1)S(1)}, bf16[256,256]{1,0:T(8,128)(2,1)S(1)}, u32[]{:S(2)}, u32[]{:S(2)}) %collective-permute-start.21) | collective-permute-done | bytes 131104 | tf_op jit(solution)/shard_map/ppermute | solution.py:284
  139.6 1.8 %shard_map.50 = (f32[256,1024]{1,0:T(8,128)S(1)}, bf16[1,256,1024]{2,1,0:T(8,128)(2,1)S(1)}) custom-call(s32[2]{0:T(128)S(1)} %copy-done.2, bf16[256,256]{1,0:T(8,128)(2,1)S(1)} %shard_map.49.refs_0_, bf16[256,256]{1,0:T(8,128)(2,1)S(1)} %collective-permute-done.14.refs_1_, bf16[256,256]{1,0:T(8,128)(2,1)S(1)} %collective-permute-done.15.refs_2_, ...), custom_call_target="tpu_custom_call" | custom-call | tf_op jit(solution)/shard_map/pallas_call | solution.py:397
  141.5 4.5 %collective-permute-done.24.last_ref = bf16[256,256]{1,0:T(8,128)(2,1)S(1)} collective-permute-done((bf16[256,256]{1,0:T(8,128)(2,1)S(1)}, bf16[256,256]{1,0:T(8,128)(2,1)S(1)}, u32[]{:S(2)}, u32[]{:S(2)}) %collective-permute-start.24) | collective-permute-done | bytes 131104 | tf_op jit(solution)/shard_map/ppermute | solution.py:284
  146.0 0.9 shard_map.51
  146.9 0.6 collective-permute-start.25
  147.5 6.6 %collective-permute-done.25 = bf16[256,512]{1,0:T(8,128)(2,1)S(1)} collective-permute-done((bf16[256,512]{1,0:T(8,128)(2,1)S(1)}, bf16[256,512]{1,0:T(8,128)(2,1)S(1)}, u32[]{:S(2)}, u32[]{:S(2)}) %collective-permute-start.25) | collective-permute-done | bytes 262176 | tf_op jit(solution)/shard_map/ppermute | solution.py:280
  154.1 0.8 add_convert_fusion
  (34 shorter events, 0.3 us)
Async XLA Ops:
  0.0 12.4 %collective-permute-start = (bf16[256,512]{1,0:T(8,128)(2,1)}, bf16[256,512]{1,0:T(8,128)(2,1)S(1)}, u32[]{:S(2)}, u32[]{:S(2)}) collective-permute-start(bf16[256,512]{1,0:T(8,128)(2,1)} %refs_0_.3), channel_id=1, source_target_pairs={{0,1},{1,2},{2,3},{3,4},{4,5},{5,6},{6,7},{7,0},{8,9},{9,10},{10,1... | collective-permute-start | bytes 786440 | tf_op jit(solution)/shard_map/ppermute | solution.py:284
  1.9 10.5 %collective-permute-start.1 = (bf16[256,512]{1,0:T(8,128)(2,1)}, bf16[256,512]{1,0:T(8,128)(2,1)S(1)}, u32[]{:S(2)}, u32[]{:S(2)}) collective-permute-start(bf16[256,512]{1,0:T(8,128)(2,1)} %refs_0_.3), channel_id=1, source_target_pairs={{0,7},{1,0},{2,1},{3,2},{4,3},{5,4},{6,5},{7,6},{8,15},{9,8},{10,9... | collective-permute-start | bytes 786440 | tf_op jit(solution)/shard_map/ppermute | solution.py:284
  7.2 24.7 %collective-permute-start.7 = (bf16[2048,256]{1,0:T(8,128)(2,1)S(1)}, bf16[2048,256]{1,0:T(8,128)(2,1)S(1)}, u32[]{:S(2)}, u32[]{:S(2)}) collective-permute-start(bf16[2048,256]{1,0:T(8,128)(2,1)S(1)} %constant_dynamic-slice_fusion), channel_id=1, source_target_pairs={{0,8},{1,9},{2,10},{3,11},{4,12},{5,13},{6,14},{7,15},{8,0},{9,1},... | collective-permute-start | bytes 3145736 | tf_op jit(solution)/shard_map/ppermute | solution.py:280
  12.4 8.8 %copy-start.5 = (bf16[256,512]{1,0:T(8,128)(2,1)}, bf16[256,512]{1,0:T(8,128)(2,1)S(1)}, u32[]{:S(2)}) copy-start(bf16[256,512]{1,0:T(8,128)(2,1)S(1)} %collective-permute-done.refs_1_) | copy-start | bytes 786436
  12.4 8.8 %copy-start.6 = (bf16[256,512]{1,0:T(8,128)(2,1)}, bf16[256,512]{1,0:T(8,128)(2,1)S(1)}, u32[]{:S(2)}) copy-start(bf16[256,512]{1,0:T(8,128)(2,1)S(1)} %collective-permute-done.1.refs_2_) | copy-start | bytes 786436
  12.4 8.8 %collective-permute-start.2 = (bf16[256,512]{1,0:T(8,128)(2,1)S(1)}, bf16[256,512]{1,0:T(8,128)(2,1)S(1)}, u32[]{:S(2)}, u32[]{:S(2)}) collective-permute-start(bf16[256,512]{1,0:T(8,128)(2,1)S(1)} %collective-permute-done.refs_1_), channel_id=1, source_target_pairs={{0,1},{1,2},{2,3},{3,4},{4,5},{5,6},{6,7},{7,0},{8,9},{9,10},{10,1... | collective-permute-start | bytes 786440 | tf_op jit(solution)/shard_map/ppermute | solution.py:284
  12.5 8.7 %collective-permute-start.3 = (bf16[256,512]{1,0:T(8,128)(2,1)S(1)}, bf16[256,512]{1,0:T(8,128)(2,1)}, u32[]{:S(2)}, u32[]{:S(2)}) collective-permute-start(bf16[256,512]{1,0:T(8,128)(2,1)S(1)} %collective-permute-done.1.refs_2_), channel_id=1, source_target_pairs={{0,7},{1,0},{2,1},{3,2},{4,3},{5,4},{6,5},{7,6},{8,15},{9,8},{10,9... | collective-permute-start | bytes 786440 | tf_op jit(solution)/shard_map/ppermute | solution.py:284
  21.1 31.9 %copy-start.7 = (bf16[256,512]{1,0:T(8,128)(2,1)}, bf16[256,512]{1,0:T(8,128)(2,1)S(1)}, u32[]{:S(2)}) copy-start(bf16[256,512]{1,0:T(8,128)(2,1)S(1)} %collective-permute-done.2.refs_3_) | copy-start | bytes 786436
  21.2 40.9 %all-to-all-start = ((bf16[8,2,32,512]{3,2,1,0:T(8,128)(2,1)}), bf16[8,2,32,512]{3,2,1,0:T(8,128)(2,1)S(1)}, u32[]{:S(2)}, u32[]{:S(2)}) async-start(bf16[8,2,32,512]{3,2,1,0:T(8,128)(2,1)} %bitcast.23), calls=%async_computation | async-start | bytes 1048576 | tf_op jit(solution)/shard_map/all_to_all | solution.py:437
  26.8 18.4 %collective-permute-start.4 = (bf16[256,512]{1,0:T(8,128)(2,1)S(1)}, bf16[256,512]{1,0:T(8,128)(2,1)S(1)}, u32[]{:S(2)}, u32[]{:S(2)}) collective-permute-start(bf16[256,512]{1,0:T(8,128)(2,1)S(1)} %collective-permute-done.2.refs_3_), channel_id=1, source_target_pairs={{0,1},{1,2},{2,3},{3,4},{4,5},{5,6},{6,7},{7,0},{8,9},{9,10},{10,1... | collective-permute-start | bytes 786440 | tf_op jit(solution)/shard_map/ppermute | solution.py:284
  28.8 16.4 %collective-permute-start.5 = (bf16[256,512]{1,0:T(8,128)(2,1)}, bf16[256,512]{1,0:T(8,128)(2,1)S(1)}, u32[]{:S(2)}, u32[]{:S(2)}) collective-permute-start(bf16[256,512]{1,0:T(8,128)(2,1)} %collective-permute-done.3.refs_4_), channel_id=1, source_target_pairs={{0,7},{1,0},{2,1},{3,2},{4,3},{5,4},{6,5},{7,6},{8,15},{9,8},{10,9... | collective-permute-start | bytes 786440 | tf_op jit(solution)/shard_map/ppermute | solution.py:284
  31.9 46.8 %copy-start.3 = (bf16[2048,256]{1,0:T(8,128)(2,1)}, bf16[2048,256]{1,0:T(8,128)(2,1)S(1)}, u32[]{:S(2)}) copy-start(bf16[2048,256]{1,0:T(8,128)(2,1)S(1)} %collective-permute-done.7.refs_9_) | copy-start | bytes 3145732
  31.9 53.9 %collective-permute-start.8 = (bf16[2048,256]{1,0:T(8,128)(2,1)S(1)}, bf16[2048,256]{1,0:T(8,128)(2,1)S(1)}, u32[]{:S(2)}, u32[]{:S(2)}) collective-permute-start(bf16[2048,256]{1,0:T(8,128)(2,1)S(1)} %collective-permute-done.7.refs_9_), channel_id=1, source_target_pairs={{0,16},{16,0},{32,48},{48,32},{64,80},{80,64},{96,112},{112,96},{1... | collective-permute-start | bytes 3145736 | tf_op jit(solution)/shard_map/ppermute | solution.py:298
  34.0 11.5 %collective-permute-start.10 = (bf16[32,4096]{1,0:T(8,128)(2,1)S(1)}, bf16[32,4096]{1,0:T(8,128)(2,1)S(1)}, u32[]{:S(2)}, u32[]{:S(2)}) collective-permute-start(bf16[32,4096]{1,0:T(8,128)(2,1)S(1)} %get-tuple-element.57), channel_id=1, source_target_pairs={{0,8},{1,9},{2,10},{3,11},{4,12},{5,13},{6,14},{7,15},{8,0},{9,1},... | collective-permute-start | bytes 786440 | tf_op jit(solution)/shard_map/ppermute | solution.py:280
  45.2 7.8 %copy-start.8 = (bf16[256,512]{1,0:T(8,128)(2,1)}, bf16[256,512]{1,0:T(8,128)(2,1)S(1)}, u32[]{:S(2)}) copy-start(bf16[256,512]{1,0:T(8,128)(2,1)S(1)} %collective-permute-done.4.refs_5_) | copy-start | bytes 786436
  45.2 7.8 %copy-start.9 = (bf16[256,512]{1,0:T(8,128)(2,1)}, bf16[256,512]{1,0:T(8,128)(2,1)S(1)}, u32[]{:S(2)}) copy-start(bf16[256,512]{1,0:T(8,128)(2,1)S(1)} %collective-permute-done.5.refs_6_) | copy-start | bytes 786436
  45.2 7.8 %collective-permute-start.6 = (bf16[256,512]{1,0:T(8,128)(2,1)S(1)}, bf16[256,512]{1,0:T(8,128)(2,1)S(1)}, u32[]{:S(2)}, u32[]{:S(2)}) collective-permute-start(bf16[256,512]{1,0:T(8,128)(2,1)S(1)} %collective-permute-done.4.refs_5_), channel_id=1, source_target_pairs={{0,1},{1,2},{2,3},{3,4},{4,5},{5,6},{6,7},{7,0},{8,9},{9,10},{10,1... | collective-permute-start | bytes 786440 | tf_op jit(solution)/shard_map/ppermute | solution.py:284
  45.5 7.5 %copy-start.11 = (bf16[32,4096]{1,0:T(8,128)(2,1)}, bf16[32,4096]{1,0:T(8,128)(2,1)S(1)}, u32[]{:S(2)}) copy-start(bf16[32,4096]{1,0:T(8,128)(2,1)S(1)} %collective-permute-done.10.refs_9_) | copy-start | bytes 786436
  53.0 0.7 copy-start.10
  57.5 4.6 %collective-permute-start.11 = (f32[64,256]{1,0:T(8,128)}, f32[64,256]{1,0:T(8,128)S(1)}, u32[]{:S(2)}, u32[]{:S(2)}) collective-permute-start(f32[64,256]{1,0:T(8,128)} %shard_map.47.one_ref), channel_id=1, source_target_pairs={{0,8},{1,9},{2,10},{3,11},{4,12},{5,13},{6,14},{7,15},{8,0},{9,1},... | collective-permute-start | bytes 196616 | tf_op jit(solution)/shard_map/ppermute | solution.py:280
  62.1 0.8 copy-start.1
  78.7 17.0 %collective-permute-start.12 = (bf16[8,32,256]{2,1,0:T(8,128)(2,1)S(1)}, bf16[8,32,256]{2,1,0:T(8,128)(2,1)S(1)}, u32[]{:S(2)}, u32[]{:S(2)}) collective-permute-start(bf16[8,32,256]{2,1,0:T(8,128)(2,1)S(1)} %slice_bitcast_fusion), channel_id=1, source_target_pairs={{0,32},{16,48},{32,64},{48,80},{64,96},{80,112},{96,128},{112,144}... | collective-permute-start | bytes 393224 | tf_op jit(solution)/shard_map/ppermute | solution.py:290
  83.8 14.0 %collective-permute-start.13 = (bf16[8,2,32,256]{3,2,1,0:T(8,128)(2,1)S(1)}, bf16[8,2,32,256]{3,2,1,0:T(8,128)(2,1)S(1)}, u32[]{:S(2)}, u32[]{:S(2)}) collective-permute-start(bf16[8,2,32,256]{3,2,1,0:T(8,128)(2,1)S(1)} %bitcast.25), channel_id=1, source_target_pairs={{0,16},{16,32},{32,48},{48,64},{64,80},{80,96},{96,112},{112,128},... | collective-permute-start | bytes 786440 | tf_op jit(solution)/shard_map/ppermute | solution.py:290
  85.7 1.0 copy-start.4
  92.9 9.1 %collective-permute-start.9 = (f32[256,256]{1,0:T(8,128)}, f32[256,256]{1,0:T(8,128)S(1)}, u32[]{:S(2)}, u32[]{:S(2)}) collective-permute-start(f32[256,256]{1,0:T(8,128)} %get-tuple-element.39), channel_id=1, source_target_pairs={{0,8},{1,9},{2,10},{3,11},{4,12},{5,13},{6,14},{7,15},{8,0},{9,1},... | collective-permute-start | bytes 786440 | tf_op jit(solution)/shard_map/ppermute | solution.py:280
  93.7 38.4 %collective-permute-start.16 = (bf16[8,2,32,512]{3,2,1,0:T(8,128)(2,1)S(1)}, bf16[8,2,32,512]{3,2,1,0:T(8,128)(2,1)S(1)}, u32[]{:S(2)}, u32[]{:S(2)}) collective-permute-start(bf16[8,2,32,512]{3,2,1,0:T(8,128)(2,1)S(1)} %all-to-all-done), channel_id=1, source_target_pairs={{0,64},{16,80},{32,96},{48,112},{64,128},{80,144},{96,160},{112,17... | collective-permute-start | bytes 1572872 | tf_op jit(solution)/shard_map/ppermute | solution.py:294
  95.2 36.9 %collective-permute-start.17 = (bf16[8,2,32,512]{3,2,1,0:T(8,128)(2,1)S(1)}, bf16[8,2,32,512]{3,2,1,0:T(8,128)(2,1)S(1)}, u32[]{:S(2)}, u32[]{:S(2)}) collective-permute-start(bf16[8,2,32,512]{3,2,1,0:T(8,128)(2,1)S(1)} %all-to-all-done), channel_id=1, source_target_pairs={{0,192},{16,208},{32,224},{48,240},{64,0},{80,16},{96,32},{112,48}... | collective-permute-start | bytes 1572872 | tf_op jit(solution)/shard_map/ppermute | solution.py:294
  95.7 36.4 %collective-permute-start.18 = (bf16[8,2,32,512]{3,2,1,0:T(8,128)(2,1)S(1)}, bf16[8,2,32,512]{3,2,1,0:T(8,128)(2,1)S(1)}, u32[]{:S(2)}, u32[]{:S(2)}) collective-permute-start(bf16[8,2,32,512]{3,2,1,0:T(8,128)(2,1)S(1)} %all-to-all-done), channel_id=1, source_target_pairs={{0,128},{16,144},{32,160},{48,176},{64,192},{80,208},{96,224},{112... | collective-permute-start | bytes 1572872 | tf_op jit(solution)/shard_map/ppermute | solution.py:294
  102.0 1.0 copy-start
  118.6 7.2 %collective-permute-start.14 = (bf16[256,256]{1,0:T(8,128)(2,1)S(1)}, bf16[256,256]{1,0:T(8,128)(2,1)S(1)}, u32[]{:S(2)}, u32[]{:S(2)}) collective-permute-start(bf16[256,256]{1,0:T(8,128)(2,1)S(1)} %shard_map.49.refs_0_), channel_id=1, source_target_pairs={{0,1},{1,2},{2,3},{3,4},{4,5},{5,6},{6,7},{7,0},{8,9},{9,10},{10,1... | collective-permute-start | bytes 393224 | tf_op jit(solution)/shard_map/ppermute | solution.py:284
  118.8 6.9 %collective-permute-start.15 = (bf16[256,256]{1,0:T(8,128)(2,1)S(1)}, bf16[256,256]{1,0:T(8,128)(2,1)S(1)}, u32[]{:S(2)}, u32[]{:S(2)}) collective-permute-start(bf16[256,256]{1,0:T(8,128)(2,1)S(1)} %shard_map.49.refs_0_), channel_id=1, source_target_pairs={{0,7},{1,0},{2,1},{3,2},{4,3},{5,4},{6,5},{7,6},{8,15},{9,8},{10,9... | collective-permute-start | bytes 393224 | tf_op jit(solution)/shard_map/ppermute | solution.py:284
  125.8 6.3 %collective-permute-start.19 = (bf16[256,256]{1,0:T(8,128)(2,1)S(1)}, bf16[256,256]{1,0:T(8,128)(2,1)S(1)}, u32[]{:S(2)}, u32[]{:S(2)}) collective-permute-start(bf16[256,256]{1,0:T(8,128)(2,1)S(1)} %collective-permute-done.14.refs_1_), channel_id=1, source_target_pairs={{0,1},{1,2},{2,3},{3,4},{4,5},{5,6},{6,7},{7,0},{8,9},{9,10},{10,1... | collective-permute-start | bytes 393224 | tf_op jit(solution)/shard_map/ppermute | solution.py:284
  125.8 6.3 %collective-permute-start.20 = (bf16[256,256]{1,0:T(8,128)(2,1)S(1)}, bf16[256,256]{1,0:T(8,128)(2,1)S(1)}, u32[]{:S(2)}, u32[]{:S(2)}) collective-permute-start(bf16[256,256]{1,0:T(8,128)(2,1)S(1)} %collective-permute-done.15.refs_2_), channel_id=1, source_target_pairs={{0,7},{1,0},{2,1},{3,2},{4,3},{5,4},{6,5},{7,6},{8,15},{9,8},{10,9... | collective-permute-start | bytes 393224 | tf_op jit(solution)/shard_map/ppermute | solution.py:284
  129.3 10.4 %copy-start.2 = (s32[2]{0:T(128)S(1)}, s32[2]{0:T(128)}, u32[]{:S(2)}) copy-start(s32[2]{0:T(128)} %pad_add_fusion.spot_ref) | copy-start | bytes 28
  132.2 7.4 %collective-permute-start.23 = (bf16[4,8,2,32,512]{4,3,2,1,0:T(8,128)(2,1)S(1)}, bf16[4,8,2,32,512]{4,3,2,1,0:T(8,128)(2,1)S(1)}, u32[]{:S(2)}, u32[]{:S(2)}) collective-permute-start(bf16[4,8,2,32,512]{4,3,2,1,0:T(8,128)(2,1)S(1)} %bitcast_dynamic-update-slice_fusion.refs_7_), channel_id=1, source_target_pairs={{0,16},{16,0},{32,48},{48,32},{64,80},{80,64},{96,112},{112,96},{1... | collective-permute-start | bytes 6291464 | tf_op jit(solution)/shard_map/ppermute | solution.py:298
  132.3 7.3 %collective-permute-start.21 = (bf16[256,256]{1,0:T(8,128)(2,1)S(1)}, bf16[256,256]{1,0:T(8,128)(2,1)S(1)}, u32[]{:S(2)}, u32[]{:S(2)}) collective-permute-start(bf16[256,256]{1,0:T(8,128)(2,1)S(1)} %collective-permute-done.19.refs_3_), channel_id=1, source_target_pairs={{0,1},{1,2},{2,3},{3,4},{4,5},{5,6},{6,7},{7,0},{8,9},{9,10},{10,1... | collective-permute-start | bytes 393224 | tf_op jit(solution)/shard_map/ppermute | solution.py:284
  132.4 7.2 %collective-permute-start.22 = (bf16[256,256]{1,0:T(8,128)(2,1)S(1)}, bf16[256,256]{1,0:T(8,128)(2,1)S(1)}, u32[]{:S(2)}, u32[]{:S(2)}) collective-permute-start(bf16[256,256]{1,0:T(8,128)(2,1)S(1)} %collective-permute-done.20.refs_4_), channel_id=1, source_target_pairs={{0,7},{1,0},{2,1},{3,2},{4,3},{5,4},{6,5},{7,6},{8,15},{9,8},{10,9... | collective-permute-start | bytes 393224 | tf_op jit(solution)/shard_map/ppermute | solution.py:284
  139.6 6.4 %collective-permute-start.24 = (bf16[256,256]{1,0:T(8,128)(2,1)S(1)}, bf16[256,256]{1,0:T(8,128)(2,1)S(1)}, u32[]{:S(2)}, u32[]{:S(2)}) collective-permute-start(bf16[256,256]{1,0:T(8,128)(2,1)S(1)} %collective-permute-done.21.refs_5_), channel_id=1, source_target_pairs={{0,1},{1,2},{2,3},{3,4},{4,5},{5,6},{6,7},{7,0},{8,9},{9,10},{10,1... | collective-permute-start | bytes 393224 | tf_op jit(solution)/shard_map/ppermute | solution.py:284
  146.9 7.2 %collective-permute-start.25 = (bf16[256,512]{1,0:T(8,128)(2,1)S(1)}, bf16[256,512]{1,0:T(8,128)(2,1)S(1)}, u32[]{:S(2)}, u32[]{:S(2)}) collective-permute-start(bf16[256,512]{1,0:T(8,128)(2,1)S(1)} %get-tuple-element.56), channel_id=1, source_target_pairs={{0,8},{1,9},{2,10},{3,11},{4,12},{5,13},{6,14},{7,15},{8,0},{9,1},... | collective-permute-start | bytes 786440 | tf_op jit(solution)/shard_map/ppermute | solution.py:280
